TPU v7x, 32 devices: a whole 2x2x4 slice. The times are simulated.
32 devices in a mesh: dp: 4 (over y, x), fsdp: 8 (over z, core).
Axes of the slice: x: 2, y: 2, z: 4, core: 2. Of those that a mesh axis runs over, the one named last changes fastest.
Arguments:
- tokens: bfloat16 [32768, 768], P(('dp', 'fsdp')), may hold values from -11 to 11
- attention: bfloat16 [768, 3072], P(None, 'fsdp'), may hold values from -2 to 2
- attvector: bfloat16 [3840], P('fsdp'), may hold values from -2 to 2
- expand: bfloat16 [768, 3072], P(None, 'fsdp'), may hold values from -0.21875 to 0.21875
- contract: bfloat16 [3072, 768], P('fsdp'), may hold values from -0.109375 to 0.109375
- feedvector: bfloat16 [5376], P('fsdp'), may hold values from -2 to 2
- lengths: int32 [64], P(('dp', 'fsdp')), may hold values from 1 to 512, 19660 in all
- cotangent: bfloat16 [32768, 768], P(('dp', 'fsdp')), may hold values from -6 to 6
Outputs:
- layer_output: bfloat16 [32768, 768], P(('dp', 'fsdp'))
- input_grad: bfloat16 [32768, 768], P(('dp', 'fsdp'))
- attention_grad: float32 [768, 3072], P(None, 'fsdp')
- attvector_grad: float32 [3840], P('fsdp')
- expand_grad: float32 [768, 3072], P(None, 'fsdp')
- contract_grad: float32 [3072, 768], P('fsdp')
- feedvector_grad: float32 [5376], P('fsdp')
- root_squares: float32 [3], replicated
Inputs may be any that keep to these rules, and one draw needn't show every extreme that they name: `lengths`: some row is full.
All inputs are finite; a program needn't handle non-finite values. No bound on the sum of `lengths` on one device may be relied on, other than what follows from the above.
Results may differ from a plain program's by a relative error of at most 0.015.
Values may be sent and summed in bfloat16 or wider, within the bound.
No kernel may reach another device: no remote copies, remote signals or barrier semaphores. Data moves between devices by JAX's collectives and lax.ppermute only.
A program may use at most 192 MiB of HBM per device.

v0:
```python
import math

import jax
import jax.numpy as jnp
from jax import lax
from jax.sharding import PartitionSpec as P

HEAD_DIM = 64
FF = 3072


EPSILON = 1e-12
NEGATIVE = -1000000000.0


def norm_forward(residual, scale_gain, shift_bias):
    centered = residual - jnp.mean(residual, axis=-1, keepdims=True)
    inverse = lax.rsqrt(jnp.mean(centered * centered, axis=-1, keepdims=True) + EPSILON)
    normed = centered * inverse
    return (normed * scale_gain + shift_bias, normed, inverse)


def norm_backward(upstream, normed, inverse, scale_gain):
    gain_grad = jnp.sum(upstream * normed, axis=0)
    shift_grad = jnp.sum(upstream, axis=0)
    scaled = upstream * scale_gain
    mean_plain = jnp.mean(scaled, axis=-1, keepdims=True)
    mean_normed = jnp.mean(scaled * normed, axis=-1, keepdims=True)
    return (inverse * (scaled - mean_plain - normed * mean_normed), gain_grad, shift_grad)


def masked_scores(queries, key_rows, live_mask):
    scale_factor = 1.0 / math.sqrt(queries.shape[-1])
    scores = (
        jnp.einsum("qhd,khd->hqk", queries, key_rows, preferred_element_type=jnp.float32)
        * scale_factor
    )
    return jnp.where(live_mask[None, None, :], scores, NEGATIVE)


def attend(block_item):
    queries, key_rows, value_rows, live_mask = block_item
    scores = masked_scores(queries, key_rows, live_mask)
    peak_score = jnp.max(scores, axis=-1, keepdims=True)
    totals = jnp.sum(jnp.exp(scores - peak_score), axis=-1, keepdims=True)
    logsum = peak_score + jnp.log(totals)
    softmax_low = jnp.exp(scores - logsum).astype(jnp.bfloat16)
    context = jnp.einsum(
        "hqk,khd->qhd", softmax_low, value_rows, preferred_element_type=jnp.float32
    )
    return (context.astype(jnp.bfloat16), logsum[..., 0])


def attend_back(block_item):
    queries, key_rows, value_rows, live_mask, logsum, context_grad = block_item
    scale_factor = 1.0 / math.sqrt(queries.shape[-1])
    scores = masked_scores(queries, key_rows, live_mask)
    softmax_wide = jnp.exp(scores - logsum[..., None])
    softmax_low = softmax_wide.astype(jnp.bfloat16)
    value_grad = jnp.einsum(
        "hqk,qhd->khd", softmax_low, context_grad, preferred_element_type=jnp.float32
    )
    weight_grad = jnp.einsum(
        "qhd,khd->hqk", context_grad, value_rows, preferred_element_type=jnp.float32
    )
    row_total = jnp.sum(softmax_wide * weight_grad, axis=-1, keepdims=True)
    score_grad = (softmax_wide * (weight_grad - row_total)).astype(jnp.bfloat16)
    query_grad = (
        jnp.einsum("hqk,khd->qhd", score_grad, key_rows, preferred_element_type=jnp.float32)
        * scale_factor
    )
    key_grad = (
        jnp.einsum("hqk,qhd->khd", score_grad, queries, preferred_element_type=jnp.float32)
        * scale_factor
    )
    return (
        query_grad.astype(jnp.bfloat16),
        key_grad.astype(jnp.bfloat16),
        value_grad.astype(jnp.bfloat16),
    )


def gelu_slope(inner_act):
    cumulative = 0.5 * (1.0 + lax.erf(inner_act * (1.0 / math.sqrt(2.0))))
    density = jnp.exp(-0.5 * inner_act * inner_act) * (1.0 / math.sqrt(2.0 * math.pi))
    return cumulative + inner_act * density


def column_sum(values):
    return jnp.sum(values, axis=0, dtype=jnp.float32)


def per_device(tokens, attention, attvector, expand, contract, feedvector, lengths, cotangent):
    model_width = tokens.shape[1]
    row_count = lengths.shape[0]
    positions = tokens.shape[0] // row_count
    head_count = model_width // HEAD_DIM
    attn_whole, attvec_whole = (
        lax.all_gather(attention, "fsdp", axis=1, tiled=True),
        lax.all_gather(attvector, "fsdp", axis=0, tiled=True),
    )
    expand_whole, contract_whole, feedvec_whole = (
        lax.all_gather(expand, "fsdp", axis=1, tiled=True),
        lax.all_gather(contract, "fsdp", axis=0, tiled=True),
        lax.all_gather(feedvector, "fsdp", axis=0, tiled=True),
    )
    attvec_wide = attvec_whole.astype(jnp.float32)
    feedvec_wide = feedvec_whole.astype(jnp.float32)
    query_bias = attvec_wide[:model_width]
    value_bias = attvec_wide[model_width : 2 * model_width]
    output_bias = attvec_wide[2 * model_width : 3 * model_width]
    first_gain = attvec_wide[3 * model_width : 4 * model_width]
    first_shift = attvec_wide[4 * model_width :]
    inner_bias = feedvec_wide[:FF]
    outer_bias = feedvec_wide[FF : FF + model_width]
    second_gain = feedvec_wide[FF + model_width : FF + 2 * model_width]
    second_shift = feedvec_wide[FF + 2 * model_width :]
    tokens_wide = tokens.astype(jnp.float32)
    projected = jnp.dot(
        tokens, attn_whole[:, : 3 * model_width], preferred_element_type=jnp.float32
    )
    queries = (projected[:, :model_width] + query_bias).astype(jnp.bfloat16)
    key_rows = projected[:, model_width : 2 * model_width].astype(jnp.bfloat16)
    value_rows = (projected[:, 2 * model_width :] + value_bias).astype(jnp.bfloat16)
    shape_four = (row_count, positions, head_count, HEAD_DIM)
    live_mask = jnp.arange(positions, dtype=jnp.int32)[None, :] < lengths[:, None]
    query_four = queries.reshape(shape_four)
    key_four = key_rows.reshape(shape_four)
    value_four = value_rows.reshape(shape_four)
    context, logsum = lax.map(attend, (query_four, key_four, value_four, live_mask))
    context_flat = context.reshape(-1, model_width)
    branch_attn = (
        jnp.dot(context_flat, attn_whole[:, 3 * model_width :], preferred_element_type=jnp.float32)
        + output_bias
    )
    hidden, normed_one, inverse_one = norm_forward(
        tokens_wide + branch_attn, first_gain, first_shift
    )
    hidden_low = hidden.astype(jnp.bfloat16)
    inner_act = jnp.dot(hidden_low, expand_whole, preferred_element_type=jnp.float32) + inner_bias
    gelu_low = jax.nn.gelu(inner_act, approximate=False).astype(jnp.bfloat16)
    branch_feed = jnp.dot(gelu_low, contract_whole, preferred_element_type=jnp.float32) + outer_bias
    result, normed_two, inverse_two = norm_forward(hidden + branch_feed, second_gain, second_shift)
    live_column = live_mask.reshape(-1, 1).astype(jnp.float32)
    squares = jnp.stack(
        [
            jnp.sum(live_column * tokens_wide * tokens_wide),
            jnp.sum(live_column * branch_attn * branch_attn),
            jnp.sum(live_column * branch_feed * branch_feed),
        ]
    )
    count_sum = jnp.sum(lengths).astype(jnp.float32)
    square_sums, count_total = lax.psum((squares, count_sum), ("dp", "fsdp"))
    root_squares = jnp.sqrt(square_sums / (count_total * model_width))
    back_attention, back_attvec = (
        lax.all_gather(attention, "fsdp", axis=1, tiled=True),
        lax.all_gather(attvector, "fsdp", axis=0, tiled=True),
    )
    back_expand, back_contract, back_feedvec = (
        lax.all_gather(expand, "fsdp", axis=1, tiled=True),
        lax.all_gather(contract, "fsdp", axis=0, tiled=True),
        lax.all_gather(feedvector, "fsdp", axis=0, tiled=True),
    )
    first_gain_back = back_attvec[3 * model_width : 4 * model_width].astype(jnp.float32)
    second_gain_back = back_feedvec[FF + model_width : FF + 2 * model_width].astype(jnp.float32)
    grad_two, second_gain_grad, second_shift_grad = norm_backward(
        cotangent.astype(jnp.float32), normed_two, inverse_two, second_gain_back
    )
    feed_out_grad = grad_two.astype(jnp.bfloat16)
    outer_bias_grad = column_sum(feed_out_grad)
    contract_grad = jnp.einsum(
        "nf,nd->fd", gelu_low, feed_out_grad, preferred_element_type=jnp.float32
    )
    gelu_grad = jnp.einsum(
        "nd,fd->nf", feed_out_grad, back_contract, preferred_element_type=jnp.float32
    )
    inner_grad = (gelu_grad * gelu_slope(inner_act)).astype(jnp.bfloat16)
    inner_bias_grad = column_sum(inner_grad)
    expand_grad = jnp.einsum(
        "nd,nf->df", hidden_low, inner_grad, preferred_element_type=jnp.float32
    )
    feedvec_grad = jnp.concatenate(
        [inner_bias_grad, outer_bias_grad, second_gain_grad, second_shift_grad]
    )
    feed_shards = (
        lax.psum_scatter(expand_grad, "fsdp", scatter_dimension=1, tiled=True),
        lax.psum_scatter(contract_grad, "fsdp", scatter_dimension=0, tiled=True),
        lax.psum_scatter(feedvec_grad, "fsdp", scatter_dimension=0, tiled=True),
    )
    hidden_grad = grad_two + jnp.einsum(
        "nf,df->nd", inner_grad, back_expand, preferred_element_type=jnp.float32
    )
    grad_one, first_gain_grad, first_shift_grad = norm_backward(
        hidden_grad, normed_one, inverse_one, first_gain_back
    )
    attn_out_grad = grad_one.astype(jnp.bfloat16)
    output_bias_grad = column_sum(attn_out_grad)
    output_weight_grad = jnp.einsum(
        "nd,ne->de", context_flat, attn_out_grad, preferred_element_type=jnp.float32
    )
    context_grad = jnp.einsum(
        "ne,de->nd",
        attn_out_grad,
        back_attention[:, 3 * model_width :],
        preferred_element_type=jnp.float32,
    ).astype(jnp.bfloat16)
    query_grad, key_grad, value_grad = lax.map(
        attend_back,
        (query_four, key_four, value_four, live_mask, logsum, context_grad.reshape(shape_four)),
    )
    projected_grad = jnp.concatenate(
        [
            query_grad.reshape(-1, model_width),
            key_grad.reshape(-1, model_width),
            value_grad.reshape(-1, model_width),
        ],
        axis=1,
    )
    query_bias_grad = column_sum(projected_grad[:, :model_width])
    value_bias_grad = column_sum(projected_grad[:, 2 * model_width :])
    projection_grad = jnp.einsum(
        "nd,ne->de", tokens, projected_grad, preferred_element_type=jnp.float32
    )
    input_grad = grad_one + jnp.einsum(
        "ne,de->nd",
        projected_grad,
        back_attention[:, : 3 * model_width],
        preferred_element_type=jnp.float32,
    )
    attention_grad = jnp.concatenate([projection_grad, output_weight_grad], axis=1)
    attvec_grad = jnp.concatenate(
        [query_bias_grad, value_bias_grad, output_bias_grad, first_gain_grad, first_shift_grad]
    )
    attn_shards = (
        lax.psum_scatter(attention_grad, "fsdp", scatter_dimension=1, tiled=True),
        lax.psum_scatter(attvec_grad, "fsdp", scatter_dimension=0, tiled=True),
    )
    finished = (
        lax.psum(attn_shards[0].astype(jnp.bfloat16), "dp").astype(jnp.float32),
        lax.psum(attn_shards[1].astype(jnp.bfloat16), "dp").astype(jnp.float32),
        lax.psum(feed_shards[0].astype(jnp.bfloat16), "dp").astype(jnp.float32),
        lax.psum(feed_shards[1].astype(jnp.bfloat16), "dp").astype(jnp.float32),
        lax.psum(feed_shards[2].astype(jnp.bfloat16), "dp").astype(jnp.float32),
    )
    return (
        result.astype(jnp.bfloat16),
        input_grad.astype(jnp.bfloat16),
        finished[0],
        finished[1],
        finished[2],
        finished[3],
        finished[4],
        root_squares,
    )


def solution(mesh):
    return jax.shard_map(
        per_device,
        mesh=mesh,
        in_specs=(
            P(("dp", "fsdp"), None),
            P(None, "fsdp"),
            P("fsdp"),
            P(None, "fsdp"),
            P("fsdp", None),
            P("fsdp"),
            P(("dp", "fsdp")),
            P(("dp", "fsdp"), None),
        ),
        out_specs=(
            P(("dp", "fsdp"), None),
            P(("dp", "fsdp"), None),
            P(None, "fsdp"),
            P("fsdp"),
            P(None, "fsdp"),
            P("fsdp", None),
            P("fsdp"),
            P(),
        ),
        check_vma=False,
    )
```

profile of v0, /device:TPU:0, one launch (start us, length us, event | category | flops | bytes accessed | tf_op | source)
XLA Modules:
  0.0 590.2 jit_solution(3069860904495769675)
XLA Ops:
  13.8 32.2 %all-reduce.6 = (bf16[3840]{0:T(1024)(128)(2,1)S(1)}, bf16[5376]{0:T(1024)(128)(2,1)S(1)}) all-reduce(bf16[3840]{0:T(1024)(128)(2,1)S(1)} %dynamic-update-slice, bf16[5376]{0:T(1024)(128)(2,1)S(1)} %dynamic-update-slice.1), channel_id=1, replica_groups=mesh['dp'=4,'fsdp'=8] {'fsdp'}, use_global_device_ids=true, to_apply=%add | all-reduce | flops 9216 | bytes 36864
  52.8 11.5 %all-gather.4.cloned.1.call-done = bf16[768,3072]{1,0:T(8,128)(2,1)} async-done(((bf16[768,384]{1,0:T(8,128)(2,1)}), bf16[768,3072]{1,0:T(8,128)(2,1)}) %all-gather.4.cloned.1.call-update) | async-done | bytes 4718608 | tf_op jit(solution)/shard_map/all_gather | solution.py:99
  64.3 5.8 fusion.87
  80.3 3.9 reshape.147
  88.5 3.9 reshape.145
  96.6 19.5 %while.26 = (s32[]{:T(128)}, bf16[2,512,12,64]{1,3,2,0:T(8,128)(2,1)}, f32[2,12,512]{2,1,0:T(8,128)S(1)}, bf16[2,512,12,64]{1,3,2,0:T(8,128)(2,1)}, pred[2,512]{...) while((s32[]{:T(128)}, ...), condition=%wide.region_3.4_spmd, body=%wide.region_0.3_spmd.sunk | while | flops 840296448 | bytes 47428224 | solution.py:130
  102.8 3.8 fusion.145
  112.3 3.7 fusion.145
  116.1 4.2 copy.73
  120.8 5.1 fusion.105
  126.4 38.6 %fusion.59 = (bf16[1024,3072]{1,0:T(8,128)(2,1)}, f32[1024,3072]{1,0:T(8,128)}) fusion(f32[3072]{0:T(1024)S(1)} %slice.77, bf16[768,3072]{1,0:T(8,128)(2,1)} %all-gather.6.cloned.1.call-done, f32[1024,768]{0,1:T(8,128)S(1)} %get-tuple-element.245, f32[768]{0:T(1024)S(1)} %get-tuple-element.259, f32[768]{0:T(1024)S(1)} %get-tuple-element.258, ...), kind=kOutput, calls=%fused_computation.67 | convolution fusion | flops 5043388416 | bytes 26765312 | tf_op jit(solution)/shard_map/dot_general | solution.py:140
  167.6 12.3 %fusion.80 = (f32[]{:T(128)}, f32[]{:T(128)}, f32[]{:T(128)}, f32[1024]{0:T(1024)S(1)}, f32[1024,768]{0,1:T(8,128)S(1)}) fusion(bf16[1024,768]{0,1:T(8,128)(2,1)} %copy.66, f32[1024]{0:T(1024)S(1)} %bitcast.165, f32[1024,768]{0,1:T(8,128)} %get-tuple-element.267, f32[768]{0:T(1024)S(1)} %get-tuple-element.260, f32[768]{0:T(1024)S(1)} %copy-done.46, ...), kind=kOutput, calls=%fused_computation.106 | convolution fusion | flops 4845992960 | bytes 22048780 | tf_op jit(solution)/shard_map/dot_general | solution.py:142
  183.2 3.3 convert_reduce_fusion.2
  186.5 12.3 %convert_reduce_fusion = (f32[3072]{0:T(1024)}, bf16[1024,3072]{1,0:T(8,128)(2,1)S(1)}) fusion(f32[1024,3072]{1,0:T(8,128)S(1)} %copy-done.49, f32[3072]{0:T(1024)S(1)} %slice.77, bf16[1024,768]{0,1:T(8,128)(2,1)S(1)} %get-tuple-element.239, bf16[3072,768]{1,0:T(8,128)(2,1)S(1)} %bitcast.167), kind=kOutput, calls=%fused_computation.74 | convolution fusion | flops 4872729600 | bytes 25190400 | tf_op jit(solution)/shard_map/nd,fd->nf/dot_general | solution.py:174
  201.4 7.8 %fusion.99 = f32[768,3072]{1,0:T(8,128)} fusion(bf16[1024,3072]{1,0:T(8,128)(2,1)S(1)} %get-tuple-element.272, f32[1024,768]{0,1:T(8,128)S(1)} %copy-done.15, f32[768]{0:T(1024)S(1)} %get-tuple-element.259, f32[768]{0:T(1024)S(1)} %get-tuple-element.258, f32[1024]{0:T(1024)S(1)} %add_rsqrt_fusion.1, f32[1024]{0:T(1024)S(1)} %broadcast_multiply_fusion.5), kind=kOutput, calls=%fused_computation.169 | convolution fusion | flops 4835770368 | bytes 18888704 | tf_op jit(solution)/shard_map/nd,nf->df/dot_general | solution.py:179
  209.9 12.5 %multiply_reduce_fusion.1 = (f32[768]{0:T(1024)}, f32[1024]{0:T(1024)S(1)}, f32[1024]{0:T(1024)S(1)}, f32[768]{0:T(1024)}, f32[1024,768]{0,1:T(8,128)S(1)}) fusion(f32[1024,768]{0,1:T(8,128)} %copy-done.14, f32[1024]{0:T(1024)S(1)} %add_rsqrt_fusion.1, f32[1024]{0:T(1024)S(1)} %broadcast_multiply_fusion.5, f32[768]{0:T(1024)S(1)} %copy-done.36, ...), kind=kOutput, calls=%fused_computation.115 | convolution fusion | flops 4845989888 | bytes 22065152 | tf_op jit(solution)/shard_map/nf,df->nd/dot_general | solution.py:190
  235.9 48.5 %while.27 = (s32[]{:T(128)}, bf16[2,512,12,64]{1,3,2,0:T(8,128)(2,1)}, bf16[2,512,12,64]{1,3,2,0:T(8,128)(2,1)}, bf16[2,512,12,64]{1,3,2,0:T(8,128)(2,1)}, bf16[...) while((s32[]{:T(128)}, ...), condition=%wide.region_14.15_spmd, body=%wide.region_12.14_spmd.sunk | while | flops 2062411776 | bytes 152764272 | solution.py:207
  241.1 7.4 %multiply_reduce_fusion.7 = (f32[12,512]{1,0:T(8,128)S(1)}, f32[12,512,512]{1,2,0:T(8,128)}) fusion(f32[12,512,512]{1,2,0:T(8,128)S(1)} %fusion.154, f32[12,512]{1,0:T(8,128)S(1)} %dynamic-slice_bitcast_fusion.2, pred[512]{0:T(512)(128)(4,1)S(1)} %dynamic-slice_reduce_fusion.5, bf16[2,512,12,64]{1,3,2,0:T(8,128)(2,1)S(1)} %copy-done.5, ...), kind=kOutput, calls=%fused_computation.24.clone.1 | convolution fusion | flops 418375680 | bytes 26797568 | tf_op jit(solution)/shard_map/while/body/eval_jaxpr/qhd,khd->hqk/dot_general | solution.py:63
  248.5 7.3 %multiply_convert_fusion.4 = bf16[12,512,512]{1,2,0:T(8,128)(2,1)S(1)} fusion(f32[12,512,512]{1,2,0:T(8,128)} %get-tuple-element.389, f32[12,512,512]{1,2,0:T(8,128)S(1)} %fusion.154, f32[12,512]{1,0:T(8,128)S(1)} %get-tuple-element.390, f32[12,512]{1,0:T(8,128)S(1)} %dynamic-slice_bitcast_fusion.2, pred[512]{0:T(512)(128)(4,1)S(1)} %dynamic-slice_reduce_fusion.5), kind=kLoop, calls=%fused_computation.23.clone.1 | loop fusion | flops 18874368 | bytes 31506944 | tf_op jit(solution)/shard_map/while/body/eval_jaxpr/convert_element_type | solution.py:67
  265.2 7.4 %multiply_reduce_fusion.7 = (f32[12,512]{1,0:T(8,128)S(1)}, f32[12,512,512]{1,2,0:T(8,128)}) fusion(f32[12,512,512]{1,2,0:T(8,128)S(1)} %fusion.154, f32[12,512]{1,0:T(8,128)S(1)} %dynamic-slice_bitcast_fusion.2, pred[512]{0:T(512)(128)(4,1)S(1)} %dynamic-slice_reduce_fusion.5, bf16[2,512,12,64]{1,3,2,0:T(8,128)(2,1)S(1)} %copy-done.5, ...), kind=kOutput, calls=%fused_computation.24.clone.1 | convolution fusion | flops 418375680 | bytes 26797568 | tf_op jit(solution)/shard_map/while/body/eval_jaxpr/qhd,khd->hqk/dot_general | solution.py:63
  272.6 7.3 %multiply_convert_fusion.4 = bf16[12,512,512]{1,2,0:T(8,128)(2,1)S(1)} fusion(f32[12,512,512]{1,2,0:T(8,128)} %get-tuple-element.389, f32[12,512,512]{1,2,0:T(8,128)S(1)} %fusion.154, f32[12,512]{1,0:T(8,128)S(1)} %get-tuple-element.390, f32[12,512]{1,0:T(8,128)S(1)} %dynamic-slice_bitcast_fusion.2, pred[512]{0:T(512)(128)(4,1)S(1)} %dynamic-slice_reduce_fusion.5), kind=kLoop, calls=%fused_computation.23.clone.1 | loop fusion | flops 18874368 | bytes 31506944 | tf_op jit(solution)/shard_map/while/body/eval_jaxpr/convert_element_type | solution.py:67
  284.4 3.2 copy.83
  297.5 5.8 convolution_bitcast_fusion
  303.3 8.1 %pad_maximum_fusion = f32[768,3072]{0,1:T(8,128)} fusion(f32[768,768]{0,1:T(8,128)} %fusion.96, f32[768,2304]{0,1:T(8,128)} %convolution_bitcast_fusion), kind=kLoop, calls=%fused_computation.90 | loop fusion | flops 2359296 | bytes 18874368 | tf_op jit(solution)/shard_map/concatenate | solution.py:230
  311.5 10.1 %fusion.109 = f32[3072,768]{1,0:T(8,128)} fusion(bf16[1024,3072]{1,0:T(8,128)(2,1)} %get-tuple-element.268, bf16[1024,768]{0,1:T(8,128)(2,1)} %copy-done.27), kind=kOutput, calls=%fused_computation.176 | convolution fusion | flops 4831838208 | bytes 17301504 | tf_op jit(solution)/shard_map/nf,nd->fd/dot_general | solution.py:171
  326.8 40.2 %all-reduce.4 = (f32[3]{0:T(128)S(1)}, f32[]{:T(128)}) all-reduce(f32[3]{0:T(128)S(1)} %pad_maximum_fusion.2, f32[]{:T(128)S(6)} %convert_element_type.176), channel_id=1, replica_groups=mesh['dp'=4,'fsdp'=8] {'dp','fsdp'}, use_global_device_ids=true, to_apply=%region_37.38 | all-reduce | flops 4 | bytes 32 | tf_op jit(solution)/shard_map/psum | solution.py:153
  369.9 40.7 %reduce-scatter.4.cloned.1.call-done = f32[768,384]{0,1:T(8,128)} async-done(((f32[768,3072]{0,1:T(8,128)}), f32[768,384]{0,1:T(8,128)}) %reduce-scatter.4.cloned.1.call-update) | async-done | bytes 1179664 | tf_op jit(solution)/shard_map/reduce_scatter | solution.py:235
  412.7 97.9 %reduce-scatter.8.cloned.1.call-done = f32[384,768]{1,0:T(8,128)} async-done(((f32[3072,768]{1,0:T(8,128)}), f32[384,768]{1,0:T(8,128)}) %reduce-scatter.8.cloned.1.call-update) | async-done | bytes 1179664 | tf_op jit(solution)/shard_map/reduce_scatter | solution.py:187
  513.0 26.4 %all-reduce.5 = (bf16[3840]{0:T(1024)(128)(2,1)S(1)}, bf16[5376]{0:T(1024)(128)(2,1)S(1)}) all-reduce(f32[3840]{0:T(1024)S(1)} %constant_dynamic-update-slice_fusion.6, f32[5376]{0:T(1024)S(1)} %pad_maximum_fusion.1), channel_id=3, replica_groups=mesh['dp'=4,'fsdp'=8] {'fsdp'}, use_global_device_ids=true, to_apply=%region_22.23.clone | all-reduce | flops 9216 | bytes 55296
  539.5 9.9 %all-reduce.7 = (bf16[480]{0:T(512)(128)(2,1)S(1)}, bf16[672]{0:T(1024)(128)(2,1)S(1)}) all-reduce(bf16[480]{0:T(512)(128)(2,1)S(1)} %dynamic-slice.9, bf16[672]{0:T(1024)(128)(2,1)S(1)} %dynamic-slice.8), channel_id=1, replica_groups=mesh['dp'=4,'fsdp'=8] {'dp'}, use_global_device_ids=true, to_apply=%region_23.24 | all-reduce | flops 1152 | bytes 4608 | tf_op jit(solution)/shard_map/psum | solution.py:240
  552.2 8.3 %add_convert_fusion = bf16[1024,768]{0,1:T(8,128)(2,1)S(1)} fusion(f32[1024,768]{0,1:T(8,128)} %copy-done.20, bf16[1024,2304]{0,1:T(8,128)(2,1)} %copy-done.29, bf16[768,3072]{1,0:T(8,128)(2,1)} %all-gather.4.cloned.1.call-done), kind=kOutput, calls=%fused_computation.119 | convolution fusion | flops 3625451520 | bytes 12976128 | tf_op jit(solution)/shard_map/ne,de->nd/dot_general | solution.py:224
  563.2 14.3 %all-reduce.11.cloned.1.call-done = (bf16[768,384]{0,1:T(8,128)(2,1)}, bf16[768,384]{1,0:T(8,128)(2,1)}, bf16[384,768]{1,0:T(8,128)(2,1)}) async-done(((bf16[768,384]{0,1:T(8,128)(2,1)}, bf16[768,384]{1,0:T(8,128)(2,1)}, bf16[384,768]{1,0:T(8,128)(2,1)}), (bf16[768,384]{0,1:T(8,128)(2,1)}, bf16[768,384]{1,0:T(8,128)(2,1)}, bf16[384,768]{1,0:T(8,128)(2,1)})) %all-reduce.11.cloned.1.call-update) | async-done | bytes 1769488 | tf_op jit(solution)/shard_map/psum | solution.py:239
  (239 shorter events, 115.4 us)
Async XLA Ops:
  7.2 44.0 %copy-start.22 = (bf16[1024,768]{1,0:T(8,128)(2,1)S(1)}, bf16[1024,768]{1,0:T(8,128)(2,1)}, u32[]{:S(2)}) copy-start(bf16[1024,768]{1,0:T(8,128)(2,1)} %param.12) | copy-start | bytes 4718596
  7.2 57.1 %all-gather.4.cloned.1.call-start = ((), (), s32[]{:S(2)}) async-start(), calls=%async_computation.3 | async-start | bytes 5308416 | tf_op jit(solution)/shard_map/all_gather | solution.py:99
  7.9 118.4 %all-gather.6.cloned.1.call-start = ((), (), s32[]{:S(2)}) async-start(), calls=%async_computation.4 | async-start | bytes 5308416 | tf_op jit(solution)/shard_map/all_gather | solution.py:103
  8.7 158.9 %all-gather.8.cloned.1.call-start = ((), (), s32[]{:S(2)}) async-start(), calls=%async_computation.5 | async-start | bytes 5308416 | tf_op jit(solution)/shard_map/all_gather | solution.py:104
  9.4 358.3 %reduce-scatter.6.cloned.1.call-start = ((), (), s32[]{:S(2)}) async-start(), calls=%async_computation.7 | async-start | bytes 10616832 | tf_op jit(solution)/shard_map/reduce_scatter | solution.py:186
  116.1 4.7 copy-start.30
  116.1 4.7 copy-start.32
  116.1 4.7 copy-start.26
  120.8 5.1 copy-start.24
  125.9 39.0 %copy-start.14 = (f32[1024,768]{0,1:T(8,128)}, f32[1024,768]{0,1:T(8,128)S(1)}, u32[]{:S(2)}) copy-start(f32[1024,768]{0,1:T(8,128)S(1)} %get-tuple-element.245) | copy-start | bytes 9437188
  126.4 41.3 %copy-start.45 = (f32[1,4,2,128]{3,1,2,0:T(4,128)S(1)}, f32[1,4,2,128]{3,1,2,0:T(4,128)}, u32[]{:S(2)}) copy-start(f32[1,4,2,128]{3,1,2,0:T(4,128)} %copy.100) | copy-start | bytes 12292
  126.4 41.2 %copy-start.46 = (f32[768]{0:T(1024)S(1)}, f32[768]{0:T(1024)}, u32[]{:S(2)}) copy-start(f32[768]{0:T(1024)} %get-tuple-element.257) | copy-start | bytes 9220
  167.6 18.9 %copy-start.49 = (f32[1024,3072]{1,0:T(8,128)S(1)}, f32[1024,3072]{1,0:T(8,128)}, u32[]{:S(2)}) copy-start(f32[1024,3072]{1,0:T(8,128)} %get-tuple-element.269) | copy-start | bytes 37748740
  181.3 5.2 slice-start
  186.5 12.3 %copy-start.27 = (bf16[1024,768]{0,1:T(8,128)(2,1)}, bf16[1024,768]{0,1:T(8,128)(2,1)S(1)}, u32[]{:S(2)}) copy-start(bf16[1024,768]{0,1:T(8,128)(2,1)S(1)} %get-tuple-element.239) | copy-start | bytes 4718596
  186.5 14.9 %copy-start.15 = (f32[1024,768]{0,1:T(8,128)S(1)}, f32[1024,768]{0,1:T(8,128)}, u32[]{:S(2)}) copy-start(f32[1024,768]{0,1:T(8,128)} %copy-done.14) | copy-start | bytes 9437188
  209.2 201.4 %reduce-scatter.4.cloned.1.call-start = ((), (), s32[]{:S(2)}) async-start(), calls=%async_computation.6 | async-start | bytes 10616832 | tf_op jit(solution)/shard_map/reduce_scatter | solution.py:235
  209.9 12.5 %copy-start.16 = (f32[1024,768]{0,1:T(8,128)S(1)}, f32[1024,768]{0,1:T(8,128)}, u32[]{:S(2)}) copy-start(f32[1024,768]{0,1:T(8,128)} %copy-done.14) | copy-start | bytes 9437188
  241.1 7.4 %copy-start.8 = (bf16[2,512,12,64]{1,3,2,0:T(8,128)(2,1)}, bf16[2,512,12,64]{1,3,2,0:T(8,128)(2,1)S(1)}, u32[]{:S(2)}) copy-start(bf16[2,512,12,64]{1,3,2,0:T(8,128)(2,1)S(1)} %fusion.157) | copy-start | bytes 4718596 | tf_op jit(solution)/shard_map/while
  248.5 7.3 %copy-start.17 = (bf16[2,512,12,64]{1,3,2,0:T(8,128)(2,1)S(1)}, bf16[2,512,12,64]{1,3,2,0:T(8,128)(2,1)}, u32[]{:S(2)}) copy-start(bf16[2,512,12,64]{1,3,2,0:T(8,128)(2,1)} %get-tuple-element.428) | copy-start | bytes 4718596 | tf_op jit(solution)/shard_map/while
  265.2 7.4 %copy-start.8 = (bf16[2,512,12,64]{1,3,2,0:T(8,128)(2,1)}, bf16[2,512,12,64]{1,3,2,0:T(8,128)(2,1)S(1)}, u32[]{:S(2)}) copy-start(bf16[2,512,12,64]{1,3,2,0:T(8,128)(2,1)S(1)} %fusion.157) | copy-start | bytes 4718596 | tf_op jit(solution)/shard_map/while
  272.6 7.3 %copy-start.17 = (bf16[2,512,12,64]{1,3,2,0:T(8,128)(2,1)S(1)}, bf16[2,512,12,64]{1,3,2,0:T(8,128)(2,1)}, u32[]{:S(2)}) copy-start(bf16[2,512,12,64]{1,3,2,0:T(8,128)(2,1)} %get-tuple-element.428) | copy-start | bytes 4718596 | tf_op jit(solution)/shard_map/while
  311.4 199.3 %reduce-scatter.8.cloned.1.call-start = ((), (), s32[]{:S(2)}) async-start(), calls=%async_computation.8 | async-start | bytes 10616832 | tf_op jit(solution)/shard_map/reduce_scatter | solution.py:187
  321.6 255.9 %all-reduce.11.cloned.1.call-start = ((), (), s32[]{:S(2)}) async-start(), calls=%async_computation.9 | async-start | bytes 3538944 | tf_op jit(solution)/shard_map/psum | solution.py:239
  367.6 145.2 %copy-start.37 = (f32[768]{0:T(1024)S(1)}, f32[768]{0:T(1024)}, u32[]{:S(2)}) copy-start(f32[768]{0:T(1024)} %get-tuple-element.240) | copy-start | bytes 9220
  367.6 145.2 %copy-start.44 = (f32[768]{0:T(1024)S(1)}, f32[768]{0:T(1024)}, u32[]{:S(2)}) copy-start(f32[768]{0:T(1024)} %get-tuple-element.180) | copy-start | bytes 9220
  367.6 145.2 %copy-start.43 = (f32[768]{0:T(1024)S(1)}, f32[768]{0:T(1024)}, u32[]{:S(2)}) copy-start(f32[768]{0:T(1024)} %get-tuple-element.185) | copy-start | bytes 9220
  367.7 145.2 %copy-start.35 = (f32[768]{0:T(1024)S(1)}, f32[768]{0:T(1024)}, u32[]{:S(2)}) copy-start(f32[768]{0:T(1024)} %get-tuple-element.238) | copy-start | bytes 9220
  367.7 145.2 %copy-start.40 = (f32[768]{0:T(1024)S(1)}, f32[768]{0:T(1024)}, u32[]{:S(2)}) copy-start(f32[768]{0:T(1024)} %get-tuple-element.182) | copy-start | bytes 9220
  367.7 145.2 %copy-start.41 = (f32[768]{0:T(1024)S(1)}, f32[768]{0:T(1024)}, u32[]{:S(2)}) copy-start(f32[768]{0:T(1024)} %get-tuple-element.187) | copy-start | bytes 9220
  367.7 145.2 %copy-start.42 = (f32[3072]{0:T(1024)S(1)}, f32[3072]{0:T(1024)}, u32[]{:S(2)}) copy-start(f32[3072]{0:T(1024)} %get-tuple-element.271) | copy-start | bytes 36868
  369.9 180.7 %copy-start.19 = (bf16[1024,768]{0,1:T(8,128)(2,1)S(1)}, bf16[1024,768]{0,1:T(8,128)(2,1)}, u32[]{:S(2)}) copy-start(bf16[1024,768]{0,1:T(8,128)(2,1)} %get-tuple-element.252) | copy-start | bytes 4718596
  (36 other events, 90.8 us)
Sparse Core Ops, SparseCore 0:
  9.6 54.6 all-gather.3
  65.9 50.1 all-gather.5
  117.7 49.8 all-gather.7
  209.3 98.1 reduce-scatter.5
  311.5 99.0 reduce-scatter.3
  412.7 97.8 reduce-scatter.7
  514.7 62.7 all-reduce.10
where the time goes:
time: 598 us; the launch traced here: 590 us
  waiting for transfers between devices  169 us (28%)
  matrix products  169 us (28%)
  blocking collectives  109 us (18%)
  local copies, waits for them, and re-layouts  69.8 us (12%)
  other arithmetic  53.7 us (9%)
  between operations  18.9 us (3%)
    reduce_scatter x1, waiting for transfers between devices, per_device(): lax.psum_scatter(contract_grad, 'fsdp', scatter_dimension=0, tiled=True)  97.9 us
    unnamed x2, blocking collectives  58.6 us
    reduce_scatter x1, waiting for transfers between devices, per_device(): lax.psum_scatter(attention_grad, 'fsdp', scatter_dimension=1, tiled=True)  40.7 us
    psum x1, blocking collectives, per_device(): square_sums, count_total = lax.psum((squares, count_sum), ('dp', 'fsdp'))  40.2 us
    dot_general x1, matrix products, per_device(): jnp.dot(hidden_low, expand_whole, preferred_element_type=jnp.float32)  38.6 us
    unnamed x109, local copies, waits for them, and re-layouts  24.1 us
    dot_general x2, matrix products, attend_back(): jnp.einsum('qhd,khd->hqk', context_grad, value_rows, preferred_element_ty...  14.7 us
    convert_element_type x2, other arithmetic, attend_back(): score_grad = (softmax_wide * (weight_grad - row_total)).astype(jnp.bfloat16)  14.6 us
  transfers between devices with their start and end apart: 7, of which 5 were waited for; matrix products, arithmetic and copies ran while one was open for 40% of the time, Pallas kernels for 0%

commit v1 on v0

v1 whole, which is shorter than its diff:
```python
import math

import jax
import jax.numpy as jnp
from jax import lax
from jax.experimental import pallas as pl
from jax.experimental.pallas import tpu as pltpu
from jax.sharding import PartitionSpec as P

HEAD_DIM = 64
EPSILON = 1e-12
NEGATIVE = -1000000000.0
BF = jnp.bfloat16
F32 = jnp.float32
AXES = ("dp", "fsdp")


def norm_forward(residual, scale_gain, shift_bias):
    centered = residual - jnp.mean(residual, axis=-1, keepdims=True)
    inverse = lax.rsqrt(jnp.mean(centered * centered, axis=-1, keepdims=True) + EPSILON)
    normed = centered * inverse
    return (normed * scale_gain + shift_bias, normed, inverse)


def norm_backward(upstream, normed, inverse, scale_gain):
    gain_grad = jnp.sum(upstream * normed, axis=0)
    shift_grad = jnp.sum(upstream, axis=0)
    scaled = upstream * scale_gain
    mean_plain = jnp.mean(scaled, axis=-1, keepdims=True)
    mean_normed = jnp.mean(scaled * normed, axis=-1, keepdims=True)
    return (inverse * (scaled - mean_plain - normed * mean_normed), gain_grad, shift_grad)


def masked_scores(queries, key_rows, live_mask):
    scale_factor = 1.0 / math.sqrt(queries.shape[-1])
    scores = (
        jnp.einsum("qhd,khd->hqk", queries, key_rows, preferred_element_type=F32) * scale_factor
    )
    return jnp.where(live_mask[None, None, :], scores, NEGATIVE)


def attend(block_item):
    queries, key_rows, value_rows, live_mask = block_item
    scores = masked_scores(queries, key_rows, live_mask)
    peak_score = jnp.max(scores, axis=-1, keepdims=True)
    totals = jnp.sum(jnp.exp(scores - peak_score), axis=-1, keepdims=True)
    logsum = peak_score + jnp.log(totals)
    softmax_low = jnp.exp(scores - logsum).astype(BF)
    context = jnp.einsum("hqk,khd->qhd", softmax_low, value_rows, preferred_element_type=F32)
    return (context.astype(BF), logsum[..., 0])


def attend_back(block_item):
    queries, key_rows, value_rows, live_mask, logsum, context_grad = block_item
    scale_factor = 1.0 / math.sqrt(queries.shape[-1])
    scores = masked_scores(queries, key_rows, live_mask)
    softmax_wide = jnp.exp(scores - logsum[..., None])
    softmax_low = softmax_wide.astype(BF)
    value_grad = jnp.einsum("hqk,qhd->khd", softmax_low, context_grad, preferred_element_type=F32)
    weight_grad = jnp.einsum("qhd,khd->hqk", context_grad, value_rows, preferred_element_type=F32)
    row_total = jnp.sum(softmax_wide * weight_grad, axis=-1, keepdims=True)
    score_grad = (softmax_wide * (weight_grad - row_total)).astype(BF)
    query_grad = (
        jnp.einsum("hqk,khd->qhd", score_grad, key_rows, preferred_element_type=F32) * scale_factor
    )
    key_grad = (
        jnp.einsum("hqk,qhd->khd", score_grad, queries, preferred_element_type=F32) * scale_factor
    )
    return (query_grad.astype(BF), key_grad.astype(BF), value_grad.astype(BF))


def gelu_slope(inner_act):
    cumulative = 0.5 * (1.0 + lax.erf(inner_act * (1.0 / math.sqrt(2.0))))
    density = jnp.exp(-0.5 * inner_act * inner_act) * (1.0 / math.sqrt(2.0 * math.pi))
    return cumulative + inner_act * density


def column_sum(values):
    return jnp.sum(values, axis=0, dtype=F32)


def exchange(values, mask):
    size = lax.axis_size("dp") * lax.axis_size("fsdp")
    return lax.ppermute(values, AXES, [(i, i ^ mask) for i in range(size)])


class Places:
    def __init__(self):
        self.dp, self.fsdp = lax.axis_size("dp"), lax.axis_size("fsdp")
        self.zs = self.fsdp // 2
        self.my_dp, self.my_fsdp = lax.axis_index("dp"), lax.axis_index("fsdp")
        self.core_mask, self.dp_mask = 1, self.fsdp

    def z_mask(self, k):
        return 2 * k


def flip_axes(values, flips):
    for axis, bit in flips:
        values = jnp.where(bit == 1, jnp.flip(values, axis), values)
    return values


def bits_of(value, count):
    return [(value >> (count - 1 - i)) & 1 for i in range(count)]


def to_natural(values, places, with_dp):
    tail = values.shape[3 if with_dp else 2 :]
    zbits = places.zs.bit_length() - 1
    dbits = places.dp.bit_length() - 1 if with_dp else 0
    split = values.reshape((2,) + (2,) * dbits + (2,) * zbits + tail)
    flags = [places.my_fsdp & 1]
    flags += bits_of(places.my_dp, dbits) if with_dp else []
    flags += bits_of(places.my_fsdp >> 1, zbits)
    split = flip_axes(split, list(enumerate(flags)))
    lead = (2, places.dp, places.zs) if with_dp else (2, places.zs)
    whole = split.reshape(lead + tail)
    return jnp.moveaxis(whole, 2 if with_dp else 1, 0)


def to_exchange(values, places):
    moved = jnp.moveaxis(values, 0, 2)
    tail = moved.shape[3:]
    zbits, dbits = places.zs.bit_length() - 1, places.dp.bit_length() - 1
    split = moved.reshape((2,) + (2,) * dbits + (2,) * zbits + tail)
    flags = [places.my_fsdp & 1] + bits_of(places.my_dp, dbits) + bits_of(places.my_fsdp >> 1, zbits)
    split = flip_axes(split, list(enumerate(flags)))
    return split.reshape((2, places.dp, places.zs) + tail)


def gather_blocks(shard, places, extra=None):
    quarter = shard.shape[0] // places.dp
    mine = lax.dynamic_slice_in_dim(shard, places.my_dp * quarter, quarter, 0)
    if extra is not None:
        mine = jnp.concatenate([mine, extra], axis=0)
    over_z = [mine] + [exchange(mine, places.z_mask(k)) for k in range(1, places.zs)]
    extras = None
    if extra is not None:
        extras = jnp.concatenate([part[quarter:] for part in over_z], axis=0)
        over_z = [part[:quarter] for part in over_z]
    own = jnp.concatenate(over_z, axis=0)
    if places.dp == 4:
        half = own.shape[0] // 2
        one, two = exchange(own, places.dp_mask), exchange(own, 2 * places.dp_mask)
        three_a = exchange(one[:half], 2 * places.dp_mask)
        three_b = exchange(two[half:], places.dp_mask)
        parts = [own, one, two, three_a, three_b]
    else:
        parts = [own] + [exchange(own, m * places.dp_mask) for m in range(1, places.dp)]
    if extras is not None:
        parts.append(extras)
    ours = jnp.concatenate(parts, axis=0)
    theirs = exchange(ours, places.core_mask)
    rows = shard.shape[0] * places.zs
    whole = jnp.concatenate([ours[:rows], theirs[:rows]], axis=0)
    if extras is None:
        return whole, None
    return whole, jnp.stack([ours[rows:], theirs[rows:]])


def reduce_blocks(partial, places):
    rows, width = partial.shape
    half_rows = rows // 2
    quarter = half_rows // (places.dp * places.zs)

    def add(*parts):
        return sum(part.astype(F32) for part in parts)

    mine = add(partial[:half_rows], exchange(partial[half_rows:], places.core_mask)).astype(BF)
    block = half_rows // places.dp
    own = [mine[m * block : (m + 1) * block] for m in range(places.dp)]
    if places.dp == 4:
        half = block // 2
        three_a = exchange(own[3][:half], 2 * places.dp_mask)
        three_b = exchange(own[3][half:], places.dp_mask)
        one = jnp.concatenate([add(own[1][:half], three_a).astype(BF), own[1][half:]], axis=0)
        two = jnp.concatenate([own[2][:half], add(own[2][half:], three_b).astype(BF)], axis=0)
        got_one, got_two = exchange(one, places.dp_mask), exchange(two, 2 * places.dp_mask)
        summed = add(own[0], got_one, got_two).astype(BF)
    else:
        summed = add(own[0], *[exchange(own[m], m * places.dp_mask) for m in range(1, places.dp)]).astype(BF)
    pieces = [summed[k * quarter : (k + 1) * quarter] for k in range(places.zs)]
    final = add(pieces[0], *[exchange(pieces[k], places.z_mask(k)) for k in range(1, places.zs)]).astype(BF)
    stacked = jnp.stack([final] + [exchange(final, m * places.dp_mask) for m in range(1, places.dp)])
    dbits = places.dp.bit_length() - 1
    split = stacked.reshape((2,) * dbits + stacked.shape[1:])
    split = flip_axes(split, list(enumerate(bits_of(places.my_dp, dbits))))
    return split.reshape(places.dp * quarter, width).astype(F32)


def block_table(places):
    e = jnp.arange(2, dtype=jnp.int32)[:, None, None] ^ (places.my_fsdp & 1)
    m = jnp.arange(places.dp, dtype=jnp.int32)[None, :, None] ^ places.my_dp
    k = jnp.arange(places.zs, dtype=jnp.int32)[None, None, :] ^ (places.my_fsdp >> 1)
    return ((k * 2 + e) * places.dp + m).reshape(-1).astype(jnp.int32)


def reorder_kernel(table_ref, in_ref, out_ref, *, natural, size):
    def step(i, carry):
        here, there = pl.multiple_of(i * size, size), pl.multiple_of(table_ref[i] * size, size)
        if natural:
            out_ref[pl.ds(there, size), :] = in_ref[pl.ds(here, size), :]
        else:
            out_ref[pl.ds(here, size), :] = in_ref[pl.ds(there, size), :]
        return carry

    lax.fori_loop(0, in_ref.shape[0] // size, step, 0)


def reorder(values, places, natural):
    blocks = 2 * places.dp * places.zs
    size = values.shape[0] // blocks
    if size % 16:
        tail = values.shape[1:]
        if natural:
            return to_natural(values.reshape((2, places.dp, places.zs, size) + tail), places, True).reshape(values.shape)
        return to_exchange(values.reshape((places.zs, 2, places.dp, size) + tail), places).reshape(values.shape)
    import functools

    return pl.pallas_call(
        functools.partial(reorder_kernel, natural=natural, size=size),
        out_shape=jax.ShapeDtypeStruct(values.shape, values.dtype),
        in_specs=[pl.BlockSpec(memory_space=pltpu.SMEM), pl.BlockSpec(memory_space=pltpu.VMEM)],
        out_specs=pl.BlockSpec(memory_space=pltpu.VMEM),
        name="reorder",
    )(block_table(places), values)


def dot_nt(left, right):
    return lax.dot_general(left, right, (((1,), (1,)), ((), ())), preferred_element_type=F32)


def dot_nn(left, right):
    return jnp.dot(left, right, preferred_element_type=F32)


def dot_tn(left, right):
    return lax.dot_general(left, right, (((0,), (0,)), ((), ())), preferred_element_type=F32)


def per_device(tokens, attention, attvector, expand, contract, feedvector, lengths, cotangent):
    places = Places()
    width = tokens.shape[1]
    row_count = lengths.shape[0]
    positions = tokens.shape[0] // row_count
    head_count = width // HEAD_DIM
    fsdp = places.fsdp
    hidden = expand.shape[1] * fsdp
    att_len, feed_len = attvector.shape[0], feedvector.shape[0]

    extra_rows = 16
    vectors = jnp.concatenate([attvector, feedvector])
    extra = jnp.pad(vectors, (0, extra_rows * width - vectors.shape[0])).reshape(extra_rows, width)
    attn_blocks, extras = gather_blocks(attention.T, places, extra)
    expand_rows, _ = gather_blocks(expand.T, places)
    contract_rows, _ = gather_blocks(contract, places)
    attn_rows = reorder(attn_blocks, places, True)
    extras = extras.reshape(2, places.zs, extra_rows * width)[:, :, : vectors.shape[0]]
    vec_natural = to_natural(extras, places, False).reshape(fsdp, -1)
    attvec = vec_natural[:, :att_len].reshape(-1).astype(F32)
    feedvec = vec_natural[:, att_len:].reshape(-1).astype(F32)
    query_bias, value_bias, output_bias, first_gain, first_shift = (attvec[i * width : (i + 1) * width] for i in range(5))
    inner_natural = feedvec[:hidden]
    outer_bias, second_gain, second_shift = (feedvec[hidden + i * width : hidden + (i + 1) * width] for i in range(3))
    quarter = expand.shape[1] // places.dp
    inner_bias = to_exchange(inner_natural.reshape(places.zs, 2, places.dp, quarter), places).reshape(-1)

    tokens_wide = tokens.astype(F32)
    projected = dot_nt(tokens, attn_rows[: 3 * width])
    queries = (projected[:, :width] + query_bias).astype(BF)
    key_rows = projected[:, width : 2 * width].astype(BF)
    value_rows = (projected[:, 2 * width :] + value_bias).astype(BF)
    shape_four = (row_count, positions, head_count, HEAD_DIM)
    live_mask = jnp.arange(positions, dtype=jnp.int32)[None, :] < lengths[:, None]
    query_four = queries.reshape(shape_four)
    key_four = key_rows.reshape(shape_four)
    value_four = value_rows.reshape(shape_four)
    context, logsum = lax.map(attend, (query_four, key_four, value_four, live_mask))
    context_flat = context.reshape(-1, width)
    branch_attn = dot_nt(context_flat, attn_rows[3 * width :]) + output_bias
    hidden_state, normed_one, inverse_one = norm_forward(tokens_wide + branch_attn, first_gain, first_shift)
    hidden_low = hidden_state.astype(BF)
    inner_act = dot_nt(hidden_low, expand_rows) + inner_bias
    gelu_low = jax.nn.gelu(inner_act, approximate=False).astype(BF)
    branch_feed = dot_nn(gelu_low, contract_rows) + outer_bias
    result, normed_two, inverse_two = norm_forward(hidden_state + branch_feed, second_gain, second_shift)
    live_column = live_mask.reshape(-1, 1).astype(F32)
    scalars = jnp.stack(
        [
            jnp.sum(live_column * tokens_wide * tokens_wide),
            jnp.sum(live_column * branch_attn * branch_attn),
            jnp.sum(live_column * branch_feed * branch_feed),
            jnp.sum(lengths).astype(F32),
        ]
    )

    grad_two, second_gain_grad, second_shift_grad = norm_backward(
        cotangent.astype(F32), normed_two, inverse_two, second_gain
    )
    feed_out_grad = grad_two.astype(BF)
    outer_bias_grad = column_sum(feed_out_grad)
    contract_part = dot_tn(gelu_low, feed_out_grad).astype(BF)
    contract_sum = reduce_blocks(contract_part, places)
    inner_grad = (dot_nt(feed_out_grad, contract_rows) * gelu_slope(inner_act)).astype(BF)
    inner_bias_grad = column_sum(inner_grad)
    expand_part = dot_tn(inner_grad, hidden_low).astype(BF)
    expand_sum = reduce_blocks(expand_part, places)
    hidden_grad = grad_two + dot_nn(inner_grad, expand_rows)
    grad_one, first_gain_grad, first_shift_grad = norm_backward(hidden_grad, normed_one, inverse_one, first_gain)
    attn_out_grad = grad_one.astype(BF)
    output_bias_grad = column_sum(attn_out_grad)
    output_part = dot_tn(attn_out_grad, context_flat)
    context_grad = dot_nn(attn_out_grad, attn_rows[3 * width :]).astype(BF)
    query_grad, key_grad, value_grad = lax.map(
        attend_back,
        (query_four, key_four, value_four, live_mask, logsum, context_grad.reshape(shape_four)),
    )
    projected_grad = jnp.concatenate(
        [query_grad.reshape(-1, width), key_grad.reshape(-1, width), value_grad.reshape(-1, width)], axis=1
    )
    query_bias_grad = column_sum(projected_grad[:, :width])
    value_bias_grad = column_sum(projected_grad[:, 2 * width :])
    projection_part = dot_tn(projected_grad, tokens)
    attn_part = jnp.concatenate([projection_part.astype(BF), output_part.astype(BF)], axis=0)
    attn_sum = reduce_blocks(reorder(attn_part, places, False), places)
    input_grad = grad_one + dot_nn(projected_grad, attn_rows[: 3 * width])

    inner_bias_natural = to_natural(
        inner_bias_grad.reshape(2, places.dp, places.zs, quarter), places, True
    ).reshape(-1)
    vector_part = jnp.concatenate(
        [
            query_bias_grad, value_bias_grad, output_bias_grad, first_gain_grad, first_shift_grad,
            inner_bias_natural, outer_bias_grad, second_gain_grad, second_shift_grad, scalars,
        ]
    )
    count = vector_part.shape[0]
    small_rows = -(-count // (8 * width)) * 8
    vector_sum = jnp.pad(vector_part, (0, small_rows * width - count)).reshape(small_rows, width)
    step = 1
    while step < places.dp * fsdp:
        vector_sum = vector_sum + exchange(vector_sum, step)
        step *= 2
    vector_sum = vector_sum.reshape(-1)
    att_total, feed_total = att_len * fsdp, feed_len * fsdp
    att_sum = lax.dynamic_slice_in_dim(vector_sum[:att_total], places.my_fsdp * att_len, att_len, 0)
    feed_sum = lax.dynamic_slice_in_dim(vector_sum[att_total : att_total + feed_total], places.my_fsdp * feed_len, feed_len, 0)
    sums = vector_sum[att_total + feed_total : att_total + feed_total + 4]
    root_squares = jnp.sqrt(sums[:3] / (sums[3] * width))
    return (
        result.astype(BF),
        input_grad.astype(BF),
        attn_sum.T,
        att_sum,
        expand_sum.T,
        contract_sum,
        feed_sum,
        root_squares,
    )


def solution(mesh):
    return jax.shard_map(
        per_device,
        mesh=mesh,
        in_specs=(
            P(AXES, None),
            P(None, "fsdp"),
            P("fsdp"),
            P(None, "fsdp"),
            P("fsdp", None),
            P("fsdp"),
            P(AXES),
            P(AXES, None),
        ),
        out_specs=(
            P(AXES, None),
            P(AXES, None),
            P(None, "fsdp"),
            P("fsdp"),
            P(None, "fsdp"),
            P("fsdp", None),
            P("fsdp"),
            P(),
        ),
        check_vma=False,
    )
```

time: 598 us -> 536 us (0.90)
  blocking collectives: 109 us -> 0 us
  starting transfers between devices: 0.28 us -> 76.2 us
  waiting for transfers between devices: 169 us -> 99.9 us
  local copies, waits for them, and re-layouts: 69.8 us -> 133 us
  between operations: 18.9 us -> 3.34 us
  Pallas kernels: 0 us -> 10.4 us
  matrix products: 169 us -> 160 us
    reduce_scatter x3 -> x0, waiting for transfers between devices: 139 us -> none  [the longest x1 97.9 us: per_device(): lax.psum_scatter(contract_grad, 'fsdp', scatter_dimension=0, tiled=True)]
    ppermute x0 -> x62, waiting for transfers between devices: none -> 99.9 us  [exchange(): return lax.ppermute(values, AXES, [(i, i ^ mask) for i in range(size)])]
    ppermute x0 -> x62, starting transfers between devices: none -> 76.2 us  [exchange(): return lax.ppermute(values, AXES, [(i, i ^ mask) for i in range(size)])]
    unnamed x2 -> x0, blocking collectives: 58.6 us -> none
    psum x2 -> x0, blocking collectives: 50.1 us -> none  [the longest x1 40.2 us: per_device(): square_sums, count_total = lax.psum((squares, count_sum), ('dp', 'fsdp'))]
    concatenate x1 -> x6, local copies, waits for them, and re-layouts: 0.12 us -> 20 us  [the longest x3 14.9 us: gather_blocks(): whole = jnp.concatenate([ours[:rows], theirs[:rows]], axis=0)]
    slice x5 -> x27, local copies, waits for them, and re-layouts: 2.42 us -> 20.3 us  [the longest x3 10 us: reduce_blocks(): partial[half_rows:]]
    unnamed x109 -> x125, local copies, waits for them, and re-layouts: 24.1 us -> 41 us
  transfers between devices with their start and end apart: 7 -> 62, of which waited for: 5 -> 28; matrix products, arithmetic and copies ran while one was open for 40% -> 18% of each run, Pallas kernels for 0% -> 1%
where the time goes in v1:
time: 536 us; the launch traced here: 531 us
  matrix products  160 us (30%)
  local copies, waits for them, and re-layouts  133 us (25%)
  waiting for transfers between devices  99.9 us (19%)
  starting transfers between devices  76.2 us (14%)
  other arithmetic  48.1 us (9%)
  Pallas kernels  10.4 us (2%)
    ppermute x62, waiting for transfers between devices, exchange(): return lax.ppermute(values, AXES, [(i, i ^ mask) for i in range(size)])  99.9 us
    ppermute x62, starting transfers between devices, exchange(): return lax.ppermute(values, AXES, [(i, i ^ mask) for i in range(size)])  76.2 us
    dot_general x4, matrix products, dot_nt(): lax.dot_general(left, right, (((1,), (1,)), ((), ())), preferred_element_...  60.3 us
    unnamed x125, local copies, waits for them, and re-layouts  41 us
    dot_general x4, matrix products, dot_nn(): return jnp.dot(left, right, preferred_element_type=F32)  30.9 us
    dot_general x4, matrix products, dot_tn(): lax.dot_general(left, right, (((0,), (0,)), ((), ())), preferred_element_...  19.9 us
    concatenate x3, local copies, waits for them, and re-layouts, gather_blocks(): whole = jnp.concatenate([ours[:rows], theirs[:rows]], axis=0)  14.9 us
    dot_general x2, matrix products, attend_back(): jnp.einsum('qhd,khd->hqk', context_grad, value_rows, preferred_element_ty...  14.6 us
  transfers between devices with their start and end apart: 62, of which 28 were waited for; matrix products, arithmetic and copies ran while one was open for 18% of the time, Pallas kernels for 1%

profile of v1, /device:TPU:0, one launch (start us, length us, event | category | flops | bytes accessed | tf_op | source)
XLA Modules:
  0.0 531.3 jit_solution(18014842763521113510)
XLA Ops:
  1.8 5.1 collective-permute-start.10
  15.8 6.0 %collective-permute-start.16 = (bf16[96,768]{1,0:T(8,128)(2,1)S(1)}, bf16[96,768]{1,0:T(8,128)(2,1)S(1)}, u32[]{:S(2)}, u32[]{:S(2)}) collective-permute-start(bf16[96,768]{1,0:T(8,128)(2,1)S(1)} %get-tuple-element.234), channel_id=1, source_target_pairs={{0,2},{1,3},{2,0},{3,1},{4,6},{5,7},{6,4},{7,5},{8,10},{9,11},{10,... | collective-permute-start | bytes 442376 | tf_op jit(solution)/shard_map/ppermute | solution.py:84
  21.8 9.1 %collective-permute-done.9 = bf16[96,768]{0,1:T(8,128)(2,1)S(1)} collective-permute-done((bf16[96,768]{0,1:T(8,128)(2,1)S(1)}, bf16[96,768]{0,1:T(8,128)(2,1)S(1)}, u32[]{:S(2)}, u32[]{:S(2)}) %collective-permute-start.9) | collective-permute-done | bytes 147488 | tf_op jit(solution)/shard_map/ppermute | solution.py:84
  37.7 5.1 collective-permute-done.17
  63.7 5.6 %collective-permute-done.19 = bf16[384,768]{1,0:T(8,128)(2,1)S(1)} collective-permute-done((bf16[384,768]{1,0:T(8,128)(2,1)S(1)}, bf16[384,768]{1,0:T(8,128)(2,1)S(1)}, u32[]{:S(2)}, u32[]{:S(2)}) %collective-permute-start.19) | collective-permute-done | bytes 589856 | tf_op jit(solution)/shard_map/ppermute | solution.py:84
  74.8 7.1 %collective-permute-done.3 = bf16[384,768]{1,0:T(8,128)(2,1)S(1)} collective-permute-done((bf16[384,768]{1,0:T(8,128)(2,1)S(1)}, bf16[384,768]{1,0:T(8,128)(2,1)S(1)}, u32[]{:S(2)}, u32[]{:S(2)}) %collective-permute-start.3) | collective-permute-done | bytes 589856 | tf_op jit(solution)/shard_map/ppermute | solution.py:84
  115.6 8.3 %concatenate.79 = bf16[3072,768]{0,1:T(8,128)(2,1)} concatenate(bf16[96,768]{0,1:T(8,128)(2,1)S(1)} %dynamic-slice_bitcast_fusion.1, bf16[96,768]{0,1:T(8,128)(2,1)S(1)} %collective-permute-done.8, bf16[96,768]{0,1:T(8,128)(2,1)S(1)} %collective-permute-done.9, bf16[96,768]{0,1:T(8,128)(2,1)S(1)} %collective-permute-done.10, bf16[384,768]{0,1:T(8,128)(2,1)S(1)} %collective-permute-done.11, ...), dimensions={0} | concatenate | bytes 9437184 | tf_op jit(solution)/shard_map/concatenate | solution.py:156
  133.1 5.1 reorder.2
  138.2 6.1 %convolution_bitcast_fusion = f32[1024,2304]{0,1:T(8,128)S(1)} fusion(bf16[1024,768]{1,0:T(8,128)(2,1)S(1)} %copy-done.26, bf16[3072,768]{1,0:T(8,128)(2,1)} %reorder.2), kind=kOutput, calls=%fused_computation.90 | convolution fusion | flops 3623878656 | bytes 14548992 | tf_op jit(solution)/shard_map/dot_general | solution.py:231
  166.2 21.2 %while.26 = (s32[]{:T(128)}, bf16[2,512,12,64]{1,3,2,0:T(8,128)(2,1)}, f32[2,12,512]{2,1,0:T(8,128)S(1)}, bf16[2,512,12,64]{1,3,2,0:T(8,128)(2,1)}, pred[2,512]{...) while((s32[]{:T(128)}, ...), condition=%wide.region_3.4_spmd, body=%wide.region_0.3_spmd.sunk | while | flops 840296448 | bytes 47428224 | solution.py:279
  166.4 4.1 fusion.152
  176.9 4.0 fusion.152
  191.6 5.0 fusion.106
  197.0 36.7 %fusion.59 = (bf16[1024,3072]{1,0:T(8,128)(2,1)}, f32[1024,3072]{1,0:T(8,128)}) fusion(f32[3072]{0:T(1024)S(1)} %add.285, bf16[3072,768]{0,1:T(8,128)(2,1)S(1)} %bitcast.213, f32[1024,768]{0,1:T(8,128)S(1)} %get-tuple-element.236, f32[768]{0:T(1024)S(1)} %get-tuple-element.318, f32[768]{0:T(1024)S(1)} %get-tuple-element.317, f32[1024]{0:T(1024)S(1)} %add_rsqrt_fusion.1, ...), kind=kOutput, calls=%fused_computation.67 | convolution fusion | flops 5043388416 | bytes 26765312 | tf_op jit(solution)/shard_map/dot_general | solution.py:231
  233.7 11.2 %fusion.82 = (f32[]{:T(128)}, f32[]{:T(128)}, f32[]{:T(128)}, f32[1024]{0:T(1024)S(1)}, f32[1024,768]{0,1:T(8,128)S(1)}) fusion(f32[1024]{0:T(1024)S(1)} %bitcast.239, f32[768]{0:T(1024)S(1)} %copy-done.46, f32[1024,768]{0,1:T(8,128)} %get-tuple-element.324, f32[768]{0:T(1024)S(1)} %get-tuple-element.319, bf16[1024,768]{0,1:T(8,128)(2,1)S(1)} %copy-done.22, ...), kind=kOutput, calls=%fused_computation.114 | convolution fusion | flops 4845992960 | bytes 22048780 | tf_op jit(solution)/shard_map/dot_general | solution.py:235
  251.5 6.9 %convolution_convert_fusion = bf16[3072,768]{1,0:T(8,128)(2,1)} fusion(bf16[1024,3072]{1,0:T(8,128)(2,1)S(1)} %copy-done.48, bf16[1024,768]{0,1:T(8,128)(2,1)S(1)} %get-tuple-element.228), kind=kOutput, calls=%fused_computation.91 | convolution fusion | flops 4834197504 | bytes 12582912 | tf_op jit(solution)/shard_map/dot_general | solution.py:239
  258.4 12.6 %convert_reduce_fusion = (f32[3072]{0:T(1024)}, bf16[1024,3072]{1,0:T(8,128)(2,1)S(1)}) fusion(f32[1024,3072]{1,0:T(8,128)} %get-tuple-element.326, f32[3072]{0:T(1024)S(1)} %add.285, bf16[1024,768]{0,1:T(8,128)(2,1)S(1)} %get-tuple-element.228, bf16[3072,768]{1,0:T(8,128)(2,1)S(1)} %bitcast.238), kind=kOutput, calls=%fused_computation.74 | convolution fusion | flops 4872729600 | bytes 25190400 | tf_op jit(solution)/shard_map/dot_general | solution.py:231
  271.0 7.2 %multiply_reduce_fusion.1 = (f32[768]{0:T(1024)}, f32[1024]{0:T(1024)S(1)}, f32[1024]{0:T(1024)S(1)}, f32[768]{0:T(1024)}, f32[1024,768]{0,1:T(8,128)S(1)}) fusion(f32[1024,768]{0,1:T(8,128)S(1)} %get-tuple-element.236, f32[1024]{0:T(1024)S(1)} %add_rsqrt_fusion.1, f32[1024]{0:T(1024)S(1)} %broadcast_multiply_fusion.5, f32[768]{0:T(1024)S(1)} %get-tuple-element.317, ...), kind=kOutput, calls=%fused_computation.121 | convolution fusion | flops 4845989888 | bytes 22065152 | tf_op jit(solution)/shard_map/dot_general | solution.py:235
  278.2 7.6 %convolution_convert_fusion.1 = bf16[3072,768]{1,0:T(8,128)(2,1)} fusion(bf16[1024,3072]{1,0:T(8,128)(2,1)S(1)} %get-tuple-element.329, f32[1024,768]{0,1:T(8,128)S(1)} %get-tuple-element.236, f32[768]{0:T(1024)S(1)} %get-tuple-element.318, f32[768]{0:T(1024)S(1)} %get-tuple-element.317, f32[1024]{0:T(1024)S(1)} %add_rsqrt_fusion.1, ...), kind=kOutput, calls=%fused_computation.92 | convolution fusion | flops 4838129664 | bytes 14170112 | tf_op jit(solution)/shard_map/dot_general | solution.py:239
  304.4 50.6 %while.27 = (s32[]{:T(128)}, bf16[2,512,12,64]{1,3,2,0:T(8,128)(2,1)}, bf16[2,512,12,64]{1,3,2,0:T(8,128)(2,1)}, bf16[2,512,12,64]{1,3,2,0:T(8,128)(2,1)}, bf16[...) while((s32[]{:T(128)}, ...), condition=%wide.region_14.15_spmd, body=%wide.region_12.14_spmd.sunk | while | flops 2062411776 | bytes 159055760 | solution.py:315
  310.8 7.3 %multiply_reduce_fusion.7 = (f32[12,512]{1,0:T(8,128)S(1)}, f32[12,512,512]{1,2,0:T(8,128)}) fusion(f32[12,512,512]{1,2,0:T(8,128)S(1)} %fusion.162, f32[12,512]{1,0:T(8,128)S(1)} %dynamic-slice_bitcast_fusion.3, pred[512]{0:T(512)(128)(4,1)S(1)} %dynamic-slice_reduce_fusion.5, bf16[2,512,12,64]{1,3,2,0:T(8,128)(2,1)S(1)} %copy-done.6, ...), kind=kOutput, calls=%fused_computation.24.clone.1 | convolution fusion | flops 418375680 | bytes 26797568 | tf_op jit(solution)/shard_map/while/body/eval_jaxpr/qhd,khd->hqk/dot_general | solution.py:60
  318.1 7.2 %multiply_convert_fusion.4 = bf16[12,512,512]{1,2,0:T(8,128)(2,1)S(1)} fusion(f32[12,512,512]{1,2,0:T(8,128)} %get-tuple-element.448, f32[12,512,512]{1,2,0:T(8,128)S(1)} %fusion.162, f32[12,512]{1,0:T(8,128)S(1)} %get-tuple-element.449, f32[12,512]{1,0:T(8,128)S(1)} %dynamic-slice_bitcast_fusion.3, pred[512]{0:T(512)(128)(4,1)S(1)} %dynamic-slice_reduce_fusion.5), kind=kLoop, calls=%fused_computation.23.clone.1 | loop fusion | flops 18874368 | bytes 31506944 | tf_op jit(solution)/shard_map/while/body/eval_jaxpr/convert_element_type | solution.py:62
  336.0 7.3 %multiply_reduce_fusion.7 = (f32[12,512]{1,0:T(8,128)S(1)}, f32[12,512,512]{1,2,0:T(8,128)}) fusion(f32[12,512,512]{1,2,0:T(8,128)S(1)} %fusion.162, f32[12,512]{1,0:T(8,128)S(1)} %dynamic-slice_bitcast_fusion.3, pred[512]{0:T(512)(128)(4,1)S(1)} %dynamic-slice_reduce_fusion.5, bf16[2,512,12,64]{1,3,2,0:T(8,128)(2,1)S(1)} %copy-done.6, ...), kind=kOutput, calls=%fused_computation.24.clone.1 | convolution fusion | flops 418375680 | bytes 26797568 | tf_op jit(solution)/shard_map/while/body/eval_jaxpr/qhd,khd->hqk/dot_general | solution.py:60
  343.3 7.2 %multiply_convert_fusion.4 = bf16[12,512,512]{1,2,0:T(8,128)(2,1)S(1)} fusion(f32[12,512,512]{1,2,0:T(8,128)} %get-tuple-element.448, f32[12,512,512]{1,2,0:T(8,128)S(1)} %fusion.162, f32[12,512]{1,0:T(8,128)S(1)} %get-tuple-element.449, f32[12,512]{1,0:T(8,128)S(1)} %dynamic-slice_bitcast_fusion.3, pred[512]{0:T(512)(128)(4,1)S(1)} %dynamic-slice_reduce_fusion.5), kind=kLoop, calls=%fused_computation.23.clone.1 | loop fusion | flops 18874368 | bytes 31506944 | tf_op jit(solution)/shard_map/while/body/eval_jaxpr/convert_element_type | solution.py:62
  356.9 4.2 copy.89
  388.4 4.3 collective-permute-start.37
  399.8 5.3 reorder.3
  408.5 8.6 %add_convert_fusion.3 = bf16[1024,768]{0,1:T(8,128)(2,1)} fusion(f32[1024,768]{0,1:T(8,128)S(1)} %copy-done.25, bf16[1024,2304]{0,1:T(8,128)(2,1)} %copy-done.28, bf16[3072,768]{1,0:T(8,128)(2,1)} %reorder.2), kind=kOutput, calls=%fused_computation.125 | convolution fusion | flops 3625451520 | bytes 12976128 | tf_op jit(solution)/shard_map/dot_general | solution.py:235
  453.1 9.9 %collective-permute-done.55 = bf16[384,768]{1,0:T(8,128)(2,1)S(1)} collective-permute-done((bf16[384,768]{1,0:T(8,128)(2,1)S(1)}, bf16[384,768]{1,0:T(8,128)(2,1)S(1)}, u32[]{:S(2)}, u32[]{:S(2)}) %collective-permute-start.55) | collective-permute-done | bytes 589856 | tf_op jit(solution)/shard_map/ppermute | solution.py:84
  465.3 10.4 %collective-permute-done.44 = bf16[384,768]{1,0:T(8,128)(2,1)S(1)} collective-permute-done((bf16[384,768]{1,0:T(8,128)(2,1)S(1)}, bf16[384,768]{1,0:T(8,128)(2,1)S(1)}, u32[]{:S(2)}, u32[]{:S(2)}) %collective-permute-start.44) | collective-permute-done | bytes 589856 | tf_op jit(solution)/shard_map/ppermute | solution.py:84
  479.7 8.2 %collective-permute-done.28 = bf16[384,768]{1,0:T(8,128)(2,1)S(1)} collective-permute-done((bf16[384,768]{1,0:T(8,128)(2,1)S(1)}, bf16[384,768]{1,0:T(8,128)(2,1)S(1)}, u32[]{:S(2)}, u32[]{:S(2)}) %collective-permute-start.28) | collective-permute-done | bytes 589856 | tf_op jit(solution)/shard_map/ppermute | solution.py:84
  500.7 10.3 %collective-permute-done.46 = bf16[96,768]{1,0:T(8,128)(2,1)S(1)} collective-permute-done((bf16[96,768]{1,0:T(8,128)(2,1)S(1)}, bf16[96,768]{1,0:T(8,128)(2,1)S(1)}, u32[]{:S(2)}, u32[]{:S(2)}) %collective-permute-start.46) | collective-permute-done | bytes 147488 | tf_op jit(solution)/shard_map/ppermute | solution.py:84
  (462 shorter events, 284.1 us)
Async XLA Ops:
  7.0 24.0 %collective-permute-start.9 = (bf16[96,768]{0,1:T(8,128)(2,1)S(1)}, bf16[96,768]{0,1:T(8,128)(2,1)S(1)}, u32[]{:S(2)}, u32[]{:S(2)}) collective-permute-start(bf16[96,768]{0,1:T(8,128)(2,1)S(1)} %dynamic-slice_bitcast_fusion.1), channel_id=1, source_target_pairs={{0,4},{1,5},{2,6},{3,7},{4,0},{5,1},{6,2},{7,3},{8,12},{9,13},{10,... | collective-permute-start | bytes 442376 | tf_op jit(solution)/shard_map/ppermute | solution.py:84
  7.0 26.6 %collective-permute-start.8 = (bf16[96,768]{0,1:T(8,128)(2,1)S(1)}, bf16[96,768]{0,1:T(8,128)(2,1)S(1)}, u32[]{:S(2)}, u32[]{:S(2)}) collective-permute-start(bf16[96,768]{0,1:T(8,128)(2,1)S(1)} %dynamic-slice_bitcast_fusion.1), channel_id=1, source_target_pairs={{0,2},{1,3},{2,0},{3,1},{4,6},{5,7},{6,4},{7,5},{8,10},{9,11},{10,... | collective-permute-start | bytes 442376 | tf_op jit(solution)/shard_map/ppermute | solution.py:84
  9.2 24.8 %collective-permute-start.18 = (bf16[96,768]{1,0:T(8,128)(2,1)S(1)}, bf16[96,768]{1,0:T(8,128)(2,1)S(1)}, u32[]{:S(2)}, u32[]{:S(2)}) collective-permute-start(bf16[96,768]{1,0:T(8,128)(2,1)S(1)} %get-tuple-element.234), channel_id=1, source_target_pairs={{0,6},{1,7},{2,4},{3,5},{4,2},{5,3},{6,0},{7,1},{8,14},{9,15},{10,... | collective-permute-start | bytes 442376 | tf_op jit(solution)/shard_map/ppermute | solution.py:84
  13.0 29.9 %collective-permute-start.17 = (bf16[96,768]{1,0:T(8,128)(2,1)S(1)}, bf16[96,768]{1,0:T(8,128)(2,1)S(1)}, u32[]{:S(2)}, u32[]{:S(2)}) collective-permute-start(bf16[96,768]{1,0:T(8,128)(2,1)S(1)} %get-tuple-element.234), channel_id=1, source_target_pairs={{0,4},{1,5},{2,6},{3,7},{4,0},{5,1},{6,2},{7,3},{8,12},{9,13},{10,... | collective-permute-start | bytes 442376 | tf_op jit(solution)/shard_map/ppermute | solution.py:84
  15.8 28.5 %collective-permute-start.16 = (bf16[96,768]{1,0:T(8,128)(2,1)S(1)}, bf16[96,768]{1,0:T(8,128)(2,1)S(1)}, u32[]{:S(2)}, u32[]{:S(2)}) collective-permute-start(bf16[96,768]{1,0:T(8,128)(2,1)S(1)} %get-tuple-element.234), channel_id=1, source_target_pairs={{0,2},{1,3},{2,0},{3,1},{4,6},{5,7},{6,4},{7,5},{8,10},{9,11},{10,... | collective-permute-start | bytes 442376 | tf_op jit(solution)/shard_map/ppermute | solution.py:84
  30.9 22.4 %collective-permute-start.2 = (bf16[112,768]{1,0:T(8,128)(2,1)S(1)}, bf16[112,768]{1,0:T(8,128)(2,1)S(1)}, u32[]{:S(2)}, u32[]{:S(2)}) collective-permute-start(bf16[112,768]{1,0:T(8,128)(2,1)S(1)} %pad_maximum_fusion.13), channel_id=1, source_target_pairs={{0,6},{1,7},{2,4},{3,5},{4,2},{5,3},{6,0},{7,1},{8,14},{9,15},{10,... | collective-permute-start | bytes 516104 | tf_op jit(solution)/shard_map/ppermute | solution.py:84
  44.3 17.7 %collective-permute-start.11 = (bf16[384,768]{0,1:T(8,128)(2,1)S(1)}, bf16[384,768]{0,1:T(8,128)(2,1)S(1)}, u32[]{:S(2)}, u32[]{:S(2)}) collective-permute-start(bf16[384,768]{0,1:T(8,128)(2,1)S(1)} %pad_maximum_fusion.2), channel_id=1, source_target_pairs={{0,8},{1,9},{2,10},{3,11},{4,12},{5,13},{6,14},{7,15},{8,0},{9,1},... | collective-permute-start | bytes 1769480 | tf_op jit(solution)/shard_map/ppermute | solution.py:84
  45.9 25.8 %collective-permute-start.20 = (bf16[384,768]{1,0:T(8,128)(2,1)S(1)}, bf16[384,768]{1,0:T(8,128)(2,1)S(1)}, u32[]{:S(2)}, u32[]{:S(2)}) collective-permute-start(bf16[384,768]{1,0:T(8,128)(2,1)S(1)} %pad_maximum_fusion.3), channel_id=1, source_target_pairs={{0,16},{1,17},{2,18},{3,19},{4,20},{5,21},{6,22},{7,23},{8,24},{9,... | collective-permute-start | bytes 1769480 | tf_op jit(solution)/shard_map/ppermute | solution.py:84
  51.1 18.2 %collective-permute-start.19 = (bf16[384,768]{1,0:T(8,128)(2,1)S(1)}, bf16[384,768]{1,0:T(8,128)(2,1)S(1)}, u32[]{:S(2)}, u32[]{:S(2)}) collective-permute-start(bf16[384,768]{1,0:T(8,128)(2,1)S(1)} %pad_maximum_fusion.3), channel_id=1, source_target_pairs={{0,8},{1,9},{2,10},{3,11},{4,12},{5,13},{6,14},{7,15},{8,0},{9,1},... | collective-permute-start | bytes 1769480 | tf_op jit(solution)/shard_map/ppermute | solution.py:84
  54.1 27.8 %collective-permute-start.3 = (bf16[384,768]{1,0:T(8,128)(2,1)S(1)}, bf16[384,768]{1,0:T(8,128)(2,1)S(1)}, u32[]{:S(2)}, u32[]{:S(2)}) collective-permute-start(bf16[384,768]{1,0:T(8,128)(2,1)S(1)} %pad_maximum_fusion.1), channel_id=1, source_target_pairs={{0,8},{1,9},{2,10},{3,11},{4,12},{5,13},{6,14},{7,15},{8,0},{9,1},... | collective-permute-start | bytes 1769480 | tf_op jit(solution)/shard_map/ppermute | solution.py:84
  59.0 26.3 %collective-permute-start.4 = (bf16[384,768]{1,0:T(8,128)(2,1)S(1)}, bf16[384,768]{1,0:T(8,128)(2,1)S(1)}, u32[]{:S(2)}, u32[]{:S(2)}) collective-permute-start(bf16[384,768]{1,0:T(8,128)(2,1)S(1)} %pad_maximum_fusion.1), channel_id=1, source_target_pairs={{0,16},{1,17},{2,18},{3,19},{4,20},{5,21},{6,22},{7,23},{8,24},{9,... | collective-permute-start | bytes 1769480 | tf_op jit(solution)/shard_map/ppermute | solution.py:84
  62.1 28.3 %collective-permute-start.14 = (bf16[192,768]{0,1:T(8,128)(2,1)S(1)}, bf16[192,768]{0,1:T(8,128)(2,1)S(1)}, u32[]{:S(2)}, u32[]{:S(2)}) collective-permute-start(bf16[192,768]{0,1:T(8,128)(2,1)S(1)} %slice.363), channel_id=1, source_target_pairs={{0,8},{1,9},{2,10},{3,11},{4,12},{5,13},{6,14},{7,15},{8,0},{9,1},... | collective-permute-start | bytes 884744 | tf_op jit(solution)/shard_map/ppermute | solution.py:84
  69.3 23.4 %collective-permute-start.13 = (bf16[192,768]{0,1:T(8,128)(2,1)S(1)}, bf16[192,768]{0,1:T(8,128)(2,1)S(1)}, u32[]{:S(2)}, u32[]{:S(2)}) collective-permute-start(bf16[192,768]{0,1:T(8,128)(2,1)S(1)} %slice.362), channel_id=1, source_target_pairs={{0,16},{1,17},{2,18},{3,19},{4,20},{5,21},{6,22},{7,23},{8,24},{9,... | collective-permute-start | bytes 884744 | tf_op jit(solution)/shard_map/ppermute | solution.py:84
  71.7 25.0 %collective-permute-start.21 = (bf16[192,768]{1,0:T(8,128)(2,1)}, bf16[192,768]{1,0:T(8,128)(2,1)S(1)}, u32[]{:S(2)}, u32[]{:S(2)}) collective-permute-start(bf16[192,768]{1,0:T(8,128)(2,1)} %slice.366), channel_id=1, source_target_pairs={{0,16},{1,17},{2,18},{3,19},{4,20},{5,21},{6,22},{7,23},{8,24},{9,... | collective-permute-start | bytes 884744 | tf_op jit(solution)/shard_map/ppermute | solution.py:84
  95.9 19.7 %collective-permute-start.15 = (bf16[1536,768]{0,1:T(8,128)(2,1)}, bf16[1536,768]{0,1:T(8,128)(2,1)}, u32[]{:S(2)}, u32[]{:S(2)}) collective-permute-start(bf16[1536,768]{0,1:T(8,128)(2,1)} %concatenate.78), channel_id=1, source_target_pairs={{0,1},{1,0},{2,3},{3,2},{4,5},{5,4},{6,7},{7,6},{8,9},{9,8},{10,11... | collective-permute-start | bytes 7077896 | tf_op jit(solution)/shard_map/ppermute | solution.py:84
  99.4 24.5 %collective-permute-start.23 = (bf16[1536,768]{1,0:T(8,128)(2,1)}, bf16[1536,768]{1,0:T(8,128)(2,1)}, u32[]{:S(2)}, u32[]{:S(2)}) collective-permute-start(bf16[1536,768]{1,0:T(8,128)(2,1)} %get-tuple-element.281), channel_id=1, source_target_pairs={{0,1},{1,0},{2,3},{3,2},{4,5},{5,4},{6,7},{7,6},{8,9},{9,8},{10,11... | collective-permute-start | bytes 7077896 | tf_op jit(solution)/shard_map/ppermute | solution.py:84
  107.6 19.6 %collective-permute-start.7 = (bf16[1600,768]{1,0:T(8,128)(2,1)}, bf16[1600,768]{1,0:T(8,128)(2,1)}, u32[]{:S(2)}, u32[]{:S(2)}) collective-permute-start(bf16[1600,768]{1,0:T(8,128)(2,1)} %get-tuple-element.294), channel_id=1, source_target_pairs={{0,1},{1,0},{2,3},{3,2},{4,5},{5,4},{6,7},{7,6},{8,9},{9,8},{10,11... | collective-permute-start | bytes 7372808 | tf_op jit(solution)/shard_map/ppermute | solution.py:84
  381.9 42.5 %collective-permute-start.51 = (bf16[1536,768]{1,0:T(8,128)(2,1)}, bf16[1536,768]{1,0:T(8,128)(2,1)}, u32[]{:S(2)}, u32[]{:S(2)}) collective-permute-start(bf16[1536,768]{1,0:T(8,128)(2,1)} %slice.399), channel_id=1, source_target_pairs={{0,1},{1,0},{2,3},{3,2},{4,5},{5,4},{6,7},{7,6},{8,9},{9,8},{10,11... | collective-permute-start | bytes 7077896 | tf_op jit(solution)/shard_map/ppermute | solution.py:84
  381.9 48.4 %collective-permute-start.40 = (bf16[1536,768]{1,0:T(8,128)(2,1)}, bf16[1536,768]{1,0:T(8,128)(2,1)}, u32[]{:S(2)}, u32[]{:S(2)}) collective-permute-start(bf16[1536,768]{1,0:T(8,128)(2,1)} %slice.386), channel_id=1, source_target_pairs={{0,1},{1,0},{2,3},{3,2},{4,5},{5,4},{6,7},{7,6},{8,9},{9,8},{10,11... | collective-permute-start | bytes 7077896 | tf_op jit(solution)/shard_map/ppermute | solution.py:84
  408.4 25.9 %collective-permute-start.24 = (bf16[1536,768]{1,0:T(8,128)(2,1)}, bf16[1536,768]{1,0:T(8,128)(2,1)}, u32[]{:S(2)}, u32[]{:S(2)}) collective-permute-start(bf16[1536,768]{1,0:T(8,128)(2,1)} %slice.372), channel_id=1, source_target_pairs={{0,1},{1,0},{2,3},{3,2},{4,5},{5,4},{6,7},{7,6},{8,9},{9,8},{10,11... | collective-permute-start | bytes 7077896 | tf_op jit(solution)/shard_map/ppermute | solution.py:84
  439.8 23.2 %collective-permute-start.55 = (bf16[384,768]{1,0:T(8,128)(2,1)S(1)}, bf16[384,768]{1,0:T(8,128)(2,1)S(1)}, u32[]{:S(2)}, u32[]{:S(2)}) collective-permute-start(bf16[384,768]{1,0:T(8,128)(2,1)S(1)} %pad_maximum_fusion.11), channel_id=1, source_target_pairs={{0,16},{1,17},{2,18},{3,19},{4,20},{5,21},{6,22},{7,23},{8,24},{9,... | collective-permute-start | bytes 1769480 | tf_op jit(solution)/shard_map/ppermute | solution.py:84
  444.0 20.9 %collective-permute-start.53 = (bf16[384,768]{1,0:T(8,128)(2,1)S(1)}, bf16[384,768]{1,0:T(8,128)(2,1)S(1)}, u32[]{:S(2)}, u32[]{:S(2)}) collective-permute-start(bf16[384,768]{1,0:T(8,128)(2,1)S(1)} %pad_maximum_fusion.10), channel_id=1, source_target_pairs={{0,8},{1,9},{2,10},{3,11},{4,12},{5,13},{6,14},{7,15},{8,0},{9,1},... | collective-permute-start | bytes 1769480 | tf_op jit(solution)/shard_map/ppermute | solution.py:84
  446.1 29.5 %collective-permute-start.44 = (bf16[384,768]{1,0:T(8,128)(2,1)S(1)}, bf16[384,768]{1,0:T(8,128)(2,1)S(1)}, u32[]{:S(2)}, u32[]{:S(2)}) collective-permute-start(bf16[384,768]{1,0:T(8,128)(2,1)S(1)} %pad_maximum_fusion.8), channel_id=1, source_target_pairs={{0,16},{1,17},{2,18},{3,19},{4,20},{5,21},{6,22},{7,23},{8,24},{9,... | collective-permute-start | bytes 1769480 | tf_op jit(solution)/shard_map/ppermute | solution.py:84
  450.4 27.4 %collective-permute-start.42 = (bf16[384,768]{1,0:T(8,128)(2,1)S(1)}, bf16[384,768]{1,0:T(8,128)(2,1)S(1)}, u32[]{:S(2)}, u32[]{:S(2)}) collective-permute-start(bf16[384,768]{1,0:T(8,128)(2,1)S(1)} %pad_maximum_fusion.7), channel_id=1, source_target_pairs={{0,8},{1,9},{2,10},{3,11},{4,12},{5,13},{6,14},{7,15},{8,0},{9,1},... | collective-permute-start | bytes 1769480 | tf_op jit(solution)/shard_map/ppermute | solution.py:84
  452.5 35.3 %collective-permute-start.28 = (bf16[384,768]{1,0:T(8,128)(2,1)S(1)}, bf16[384,768]{1,0:T(8,128)(2,1)S(1)}, u32[]{:S(2)}, u32[]{:S(2)}) collective-permute-start(bf16[384,768]{1,0:T(8,128)(2,1)S(1)} %pad_maximum_fusion.5), channel_id=1, source_target_pairs={{0,16},{1,17},{2,18},{3,19},{4,20},{5,21},{6,22},{7,23},{8,24},{9,... | collective-permute-start | bytes 1769480 | tf_op jit(solution)/shard_map/ppermute | solution.py:84
  463.0 26.2 %collective-permute-start.26 = (bf16[384,768]{1,0:T(8,128)(2,1)S(1)}, bf16[384,768]{1,0:T(8,128)(2,1)S(1)}, u32[]{:S(2)}, u32[]{:S(2)}) collective-permute-start(bf16[384,768]{1,0:T(8,128)(2,1)S(1)} %pad_maximum_fusion.4), channel_id=1, source_target_pairs={{0,8},{1,9},{2,10},{3,11},{4,12},{5,13},{6,14},{7,15},{8,0},{9,1},... | collective-permute-start | bytes 1769480 | tf_op jit(solution)/shard_map/ppermute | solution.py:84
  465.2 26.4 %collective-permute-start.56 = (bf16[96,768]{1,0:T(8,128)(2,1)S(1)}, bf16[96,768]{1,0:T(8,128)(2,1)S(1)}, u32[]{:S(2)}, u32[]{:S(2)}) collective-permute-start(bf16[96,768]{1,0:T(8,128)(2,1)S(1)} %get-tuple-element.264), channel_id=1, source_target_pairs={{0,2},{1,3},{2,0},{3,1},{4,6},{5,7},{6,4},{7,5},{8,10},{9,11},{10,... | collective-permute-start | bytes 442376 | tf_op jit(solution)/shard_map/ppermute | solution.py:84
  491.6 19.5 %collective-permute-start.46 = (bf16[96,768]{1,0:T(8,128)(2,1)S(1)}, bf16[96,768]{1,0:T(8,128)(2,1)S(1)}, u32[]{:S(2)}, u32[]{:S(2)}) collective-permute-start(bf16[96,768]{1,0:T(8,128)(2,1)S(1)} %get-tuple-element.269), channel_id=1, source_target_pairs={{0,4},{1,5},{2,6},{3,7},{4,0},{5,1},{6,2},{7,3},{8,12},{9,13},{10,... | collective-permute-start | bytes 442376 | tf_op jit(solution)/shard_map/ppermute | solution.py:84
  491.6 21.3 %collective-permute-start.29 = (bf16[96,768]{1,0:T(8,128)(2,1)S(1)}, bf16[96,768]{1,0:T(8,128)(2,1)S(1)}, u32[]{:S(2)}, u32[]{:S(2)}) collective-permute-start(bf16[96,768]{1,0:T(8,128)(2,1)S(1)} %get-tuple-element.270), channel_id=1, source_target_pairs={{0,2},{1,3},{2,0},{3,1},{4,6},{5,7},{6,4},{7,5},{8,10},{9,11},{10,... | collective-permute-start | bytes 442376 | tf_op jit(solution)/shard_map/ppermute | solution.py:84
  493.9 19.7 %collective-permute-start.31 = (bf16[96,768]{1,0:T(8,128)(2,1)S(1)}, bf16[96,768]{1,0:T(8,128)(2,1)S(1)}, u32[]{:S(2)}, u32[]{:S(2)}) collective-permute-start(bf16[96,768]{1,0:T(8,128)(2,1)S(1)} %get-tuple-element.271), channel_id=1, source_target_pairs={{0,6},{1,7},{2,4},{3,5},{4,2},{5,3},{6,0},{7,1},{8,14},{9,15},{10,... | collective-permute-start | bytes 442376 | tf_op jit(solution)/shard_map/ppermute | solution.py:84
  496.1 20.4 %collective-permute-start.30 = (bf16[96,768]{1,0:T(8,128)(2,1)S(1)}, bf16[96,768]{1,0:T(8,128)(2,1)S(1)}, u32[]{:S(2)}, u32[]{:S(2)}) collective-permute-start(bf16[96,768]{1,0:T(8,128)(2,1)S(1)} %get-tuple-element.272), channel_id=1, source_target_pairs={{0,4},{1,5},{2,6},{3,7},{4,0},{5,1},{6,2},{7,3},{8,12},{9,13},{10,... | collective-permute-start | bytes 442376 | tf_op jit(solution)/shard_map/ppermute | solution.py:84
  499.1 19.0 %collective-permute-start.61 = (bf16[96,768]{1,0:T(8,128)(2,1)S(1)}, bf16[96,768]{1,0:T(8,128)(2,1)S(1)}, u32[]{:S(2)}, u32[]{:S(2)}) collective-permute-start(bf16[96,768]{1,0:T(8,128)(2,1)S(1)} %add_convert_fusion.14), channel_id=1, source_target_pairs={{0,24},{1,25},{2,26},{3,27},{4,28},{5,29},{6,30},{7,31},{8,16},{9,... | collective-permute-start | bytes 442376 | tf_op jit(solution)/shard_map/ppermute | solution.py:84
  (97 other events, 732.2 us)

commit v2 on v0

v2 whole, which is shorter than its diff:
```python
import functools
import math

import jax
import jax.numpy as jnp
from jax import lax
from jax.experimental import pallas as pl
from jax.experimental.pallas import tpu as pltpu
from jax.sharding import PartitionSpec as P

HEAD_DIM = 64
EPSILON = 1e-12
NEGATIVE = -1000000000.0
BF = jnp.bfloat16
F32 = jnp.float32
AXES = ("dp", "fsdp")
LOG2E = 1.0 / math.log(2.0)
SCALE = 1.0 / math.sqrt(HEAD_DIM)
TILE = 256
PAIR = 2 * HEAD_DIM


def dot_nt(left, right, precision=None):
    return lax.dot_general(
        left, right, (((1,), (1,)), ((), ())), precision=precision, preferred_element_type=F32
    )


def dot_nn(left, right):
    return jnp.dot(left, right, preferred_element_type=F32)


def dot_tn(left, right):
    return lax.dot_general(left, right, (((0,), (0,)), ((), ())), preferred_element_type=F32)


def resident(shape, *index):
    index = index or (0,) * len(shape)
    return pl.BlockSpec(shape, lambda *_: index)


def call(kernel, name, flops, bytes_moved, **kwargs):
    cost = pl.CostEstimate(flops=flops, bytes_accessed=bytes_moved, transcendentals=0)
    return pl.pallas_call(kernel, name=name, cost_estimate=cost, **kwargs)


SMEM = pl.BlockSpec(memory_space=pltpu.SMEM)


def project_kernel(table_ref, bias_ref, token_ref, *refs, starts, size):
    pieces, (out_ref, rows_ref) = refs[:-2], refs[-2:]

    @pl.when(pl.program_id(0) == 0)
    def _():
        for piece, start in zip(pieces, starts):
            for i in range(piece.shape[0] // size):
                there = pl.multiple_of(table_ref[start + i] * size, size)
                rows_ref[pl.ds(there, size), :] = piece[i * size : (i + 1) * size, :]

    width = token_ref.shape[1]
    for j in range(3):
        part = dot_nt(token_ref[...], rows_ref[j * width : (j + 1) * width, :])
        if j == 0:
            part = part + bias_ref[0:1, :]
        if j == 2:
            part = part + bias_ref[1:2, :]
        out_ref[j] = part.astype(BF)


def project(tokens, bias, table, pieces, starts, size):
    count, width = tokens.shape
    total = sum(piece.shape[0] for piece in pieces)
    return call(
        functools.partial(project_kernel, starts=starts, size=size),
        "project",
        2 * count * width * 3 * width,
        2 * (4 * count * width + 2 * total * width),
        grid=(count // TILE,),
        in_specs=[SMEM, resident(bias.shape), pl.BlockSpec((TILE, width), lambda t: (t, 0))]
        + [resident(piece.shape) for piece in pieces],
        out_specs=[
            pl.BlockSpec((3, TILE, width), lambda t: (0, t, 0)),
            resident((total, width)),
        ],
        out_shape=[
            jax.ShapeDtypeStruct((3, count, width), BF),
            jax.ShapeDtypeStruct((total, width), BF),
        ],
    )(table, bias, tokens, *pieces)


def head_lanes(values, head):
    lane = lax.broadcasted_iota(jnp.int32, values.shape, 1)
    return jnp.where((lane >= HEAD_DIM) == (head == 1), values, jnp.zeros_like(values))


def scores_of(keys, queries, length, head):
    scores = dot_nt(keys, head_lanes(queries, head))
    place = lax.broadcasted_iota(jnp.int32, scores.shape, 0)
    return jnp.where(place < length, scores, NEGATIVE / SCALE)


def attend_kernel(length_ref, q_ref, k_ref, v_ref, out_ref, log_ref):
    length = length_ref[pl.program_id(0)]
    keys = k_ref[0]
    values_t = v_ref[0].T
    halves = []
    for head in range(2):
        scores = scores_of(keys, q_ref[0], length, head)
        peak = jnp.max(scores, axis=0, keepdims=True) * (SCALE * LOG2E)
        weights = jnp.exp2(scores * (SCALE * LOG2E) - peak)
        total = jnp.sum(weights, axis=0, keepdims=True)
        part = dot_nn(values_t[head * HEAD_DIM : (head + 1) * HEAD_DIM, :], weights.astype(BF))
        halves.append(part * (1.0 / total))
        log_ref[0, 0, head : head + 1, :] = peak + jnp.log2(total)
    out_ref[...] = jnp.concatenate(halves, axis=0).T.astype(BF)


def attend(projected, lengths, positions):
    _, count, width = projected.shape
    rows, pairs = count // positions, width // PAIR
    block = (1, positions, PAIR)
    flops = 4 * rows * pairs * 2 * positions * positions * HEAD_DIM
    return call(
        attend_kernel,
        "attend",
        2 * flops,
        8 * count * width,
        grid_spec=pltpu.PrefetchScalarGridSpec(
            num_scalar_prefetch=1,
            grid=(rows, pairs),
            in_specs=[pl.BlockSpec(block, lambda r, p, _, j=j: (j, r, p)) for j in range(3)],
            out_specs=[
                pl.BlockSpec((positions, PAIR), lambda r, p, _: (r, p)),
                pl.BlockSpec((1, 1, 2, positions), lambda r, p, _: (r, p, 0, 0)),
            ],
        ),
        out_shape=[
            jax.ShapeDtypeStruct((count, width), BF),
            jax.ShapeDtypeStruct((rows, pairs, 2, positions), F32),
        ],
    )(lengths, projected, projected, projected)


def attend_back_kernel(length_ref, q_ref, k_ref, v_ref, grad_ref, ctx_ref, log_ref, out_ref, sum_ref):
    length = length_ref[pl.program_id(0)]
    queries, keys, values, grad = q_ref[0], k_ref[0], v_ref[0], grad_ref[...]
    keys_t = keys.T
    product = grad.astype(F32) * ctx_ref[...].astype(F32)
    key_grad, value_grad, query_halves = None, None, []
    for head in range(2):
        scores = scores_of(keys, queries, length, head)
        wide = jnp.exp2(scores * (SCALE * LOG2E) - log_ref[0, 0, head : head + 1, :])
        grad_head = head_lanes(grad, head)
        value_part = dot_nn(wide.astype(BF), grad_head)
        weight_grad = dot_nt(values, grad_head)
        ones = head_lanes(jnp.ones((8, PAIR), F32), head)
        row_total = dot_nt(ones, product, lax.Precision.HIGHEST)[0:1, :]
        score_grad = (wide * (weight_grad - row_total)).astype(BF)
        key_part = dot_nn(score_grad, head_lanes(queries, head))
        query_halves.append(dot_nn(keys_t[head * HEAD_DIM : (head + 1) * HEAD_DIM, :], score_grad))
        value_grad = value_part if head == 0 else value_grad + value_part
        key_grad = key_part if head == 0 else key_grad + key_part
    query_low = (jnp.concatenate(query_halves, axis=0) * SCALE).astype(F32).T.astype(BF)
    value_low = value_grad.astype(BF)
    out_ref[0] = query_low
    out_ref[1] = (key_grad * SCALE).astype(BF)
    out_ref[2] = value_low
    sum_ref[0, 0:1, :] = jnp.sum(query_low.astype(F32), axis=0, keepdims=True)
    sum_ref[0, 1:2, :] = jnp.sum(value_low.astype(F32), axis=0, keepdims=True)


def attend_back(projected, lengths, context_grad, context, logs, positions):
    _, count, width = projected.shape
    rows, pairs = count // positions, width // PAIR
    block = (1, positions, PAIR)
    flat = pl.BlockSpec((positions, PAIR), lambda r, p, _: (r, p))
    flops = 10 * rows * pairs * 2 * positions * positions * HEAD_DIM
    return call(
        attend_back_kernel,
        "attend_back",
        2 * flops,
        16 * count * width,
        grid_spec=pltpu.PrefetchScalarGridSpec(
            num_scalar_prefetch=1,
            grid=(rows, pairs),
            in_specs=[pl.BlockSpec(block, lambda r, p, _, j=j: (j, r, p)) for j in range(3)]
            + [flat, flat, pl.BlockSpec((1, 1, 2, positions), lambda r, p, _: (r, p, 0, 0))],
            out_specs=[
                pl.BlockSpec((3, positions, PAIR), lambda r, p, _: (0, r, p)),
                pl.BlockSpec((1, 2, PAIR), lambda r, p, _: (r, 0, p)),
            ],
        ),
        out_shape=[
            jax.ShapeDtypeStruct((3, count, width), BF),
            jax.ShapeDtypeStruct((rows, 2, width), F32),
        ],
    )(lengths, projected, projected, projected, context_grad, context, logs)


def normalize(residual):
    centered = residual - jnp.mean(residual, axis=-1, keepdims=True)
    inverse = lax.rsqrt(jnp.mean(centered * centered, axis=-1, keepdims=True) + EPSILON)
    return centered * inverse, inverse


def norm_back(upstream, normed, inverse, gain):
    scaled = upstream * gain
    mean_plain = jnp.mean(scaled, axis=-1, keepdims=True)
    mean_normed = jnp.mean(scaled * normed, axis=-1, keepdims=True)
    return inverse * (scaled - mean_plain - normed * mean_normed)


def live_tile(length_ref, positions, shape):
    first = pl.program_id(0) * TILE
    place = lax.broadcasted_iota(jnp.int32, shape, 0) + first % positions
    return place < length_ref[first // positions]


def add_rows(ref, rows):
    @pl.when(pl.program_id(0) == 0)
    def _():
        ref[...] = jnp.zeros_like(ref)

    for i, row in enumerate(rows):
        ref[i : i + 1, :] += jnp.sum(row, axis=0, keepdims=True)


def middle_kernel(length_ref, vec_ref, ctx_ref, weight_ref, token_ref, n_ref, s_ref, low_ref, sum_ref, *, positions):
    branch = dot_nt(ctx_ref[...], weight_ref[...]) + vec_ref[0:1, :]
    tokens = token_ref[...].astype(F32)
    normed, inverse = normalize(tokens + branch)
    n_ref[...] = normed
    s_ref[...] = jnp.broadcast_to(inverse, s_ref.shape)
    low_ref[...] = (normed * vec_ref[1:2, :] + vec_ref[2:3, :]).astype(BF)
    live = live_tile(length_ref, positions, tokens.shape)
    add_rows(sum_ref, [jnp.where(live, tokens * tokens, 0.0), jnp.where(live, branch * branch, 0.0)])


def tiles(width):
    return pl.BlockSpec((TILE, width), lambda t: (t, 0))


def middle(lengths, vectors, context, attn_rows, tokens, positions):
    count, width = tokens.shape
    return call(
        functools.partial(middle_kernel, positions=positions),
        "middle",
        2 * count * width * width,
        count * width * 12,
        grid=(count // TILE,),
        in_specs=[SMEM, resident(vectors.shape), tiles(width), resident((width, width), 3, 0), tiles(width)],
        out_specs=[tiles(width), tiles(128), tiles(width), resident((8, width))],
        out_shape=[
            jax.ShapeDtypeStruct((count, width), F32),
            jax.ShapeDtypeStruct((count, 128), F32),
            jax.ShapeDtypeStruct((count, width), BF),
            jax.ShapeDtypeStruct((8, width), F32),
        ],
    )(lengths, vectors, context, attn_rows, tokens)


def gelu_parts(inner):
    cumulative = 0.5 * (1.0 + lax.erf(inner * (1.0 / math.sqrt(2.0))))
    density = jnp.exp2(inner * inner * (-0.5 * LOG2E)) * (1.0 / math.sqrt(2.0 * math.pi))
    return inner * cumulative, cumulative + inner * density


def expand_kernel(bias_ref, low_ref, *refs):
    pieces, (gelu_ref, slope_ref) = refs[:-2], refs[-2:]
    low, at = low_ref[...], 0
    for piece in pieces:
        size = piece.shape[0]
        inner = dot_nt(low, piece[...]) + bias_ref[0:1, at : at + size]
        gelu, slope = gelu_parts(inner)
        gelu_ref[:, at : at + size] = gelu.astype(BF)
        slope_ref[:, at : at + size] = slope.astype(BF)
        at += size


def picked(piece, width):
    array, start, size = piece
    return pl.BlockSpec((size, width), lambda *_, at=start // size: (at, 0))


def expand_call(low, bias, pieces):
    count, width = low.shape
    hidden = bias.shape[1]
    return call(
        expand_kernel,
        "expand_gelu",
        2 * count * width * hidden,
        count * hidden * 4,
        grid=(count // TILE,),
        in_specs=[resident(bias.shape), tiles(width)] + [picked(piece, width) for piece in pieces],
        out_specs=[tiles(hidden), tiles(hidden)],
        out_shape=[jax.ShapeDtypeStruct((count, hidden), BF)] * 2,
    )(bias, low, *[piece[0] for piece in pieces])


def contract_kernel(length_ref, vec_ref, gelu_ref, n_ref, cot_ref, *refs, positions):
    pieces, (out_ref, grad_ref, low_ref, sum_ref) = refs[:-4], refs[-4:]
    branch, at = vec_ref[3:4, :], 0
    for piece in pieces:
        size = piece.shape[0]
        branch = branch + dot_nn(gelu_ref[:, at : at + size], piece[...])
        at += size
    first = n_ref[...] * vec_ref[1:2, :] + vec_ref[2:3, :]
    normed, inverse = normalize(first + branch)
    out_ref[...] = (normed * vec_ref[4:5, :] + vec_ref[5:6, :]).astype(BF)
    upstream = cot_ref[...].astype(F32)
    grad = norm_back(upstream, normed, inverse, vec_ref[4:5, :])
    low = grad.astype(BF)
    grad_ref[...] = grad
    low_ref[...] = low
    live = live_tile(length_ref, positions, branch.shape)
    add_rows(
        sum_ref, [jnp.where(live, branch * branch, 0.0), low.astype(F32), upstream * normed, upstream]
    )


def contract_call(lengths, vectors, gelu, normed, cotangent, pieces, positions):
    count, width = cotangent.shape
    hidden = gelu.shape[1]
    return call(
        functools.partial(contract_kernel, positions=positions),
        "contract_norm",
        2 * count * width * hidden,
        count * hidden * 2 + count * width * 14,
        grid=(count // TILE,),
        in_specs=[SMEM, resident(vectors.shape), tiles(hidden), tiles(width), tiles(width)]
        + [picked(piece, width) for piece in pieces],
        out_specs=[tiles(width), tiles(width), tiles(width), resident((8, width))],
        out_shape=[
            jax.ShapeDtypeStruct((count, width), BF),
            jax.ShapeDtypeStruct((count, width), F32),
            jax.ShapeDtypeStruct((count, width), BF),
            jax.ShapeDtypeStruct((8, width), F32),
        ],
    )(lengths, vectors, gelu, normed, cotangent, *[piece[0] for piece in pieces])


def inner_kernel(low_ref, slope_ref, grad_ref, *refs, count):
    contracts, expands, (inner_ref, out_ref, sum_ref) = refs[:count], refs[count : 2 * count], refs[2 * count :]

    @pl.when(pl.program_id(0) == 0)
    def _():
        sum_ref[...] = jnp.zeros_like(sum_ref)

    low, total, at = low_ref[...], grad_ref[...], 0
    for contract, expand in zip(contracts, expands):
        span = slice(at, at + contract.shape[0])
        inner = (dot_nt(low, contract[...]) * slope_ref[:, span].astype(F32)).astype(BF)
        inner_ref[:, span] = inner
        sum_ref[0:1, span] += jnp.sum(inner.astype(F32), axis=0, keepdims=True)
        total = total + dot_nn(inner, expand[...])
        at += contract.shape[0]
    out_ref[...] = total


def inner_back(low, slope, grad, contracts, expands):
    count, width = low.shape
    hidden = slope.shape[1]
    return call(
        functools.partial(inner_kernel, count=len(contracts)),
        "inner_back",
        4 * count * width * hidden,
        count * hidden * 4 + count * width * 10,
        grid=(count // TILE,),
        in_specs=[tiles(width), tiles(hidden), tiles(width)]
        + [picked(piece, width) for piece in contracts + expands],
        out_specs=[tiles(hidden), tiles(width), resident((8, hidden))],
        out_shape=[
            jax.ShapeDtypeStruct((count, hidden), BF),
            jax.ShapeDtypeStruct((count, width), F32),
            jax.ShapeDtypeStruct((8, hidden), F32),
        ],
    )(low, slope, grad, *[piece[0] for piece in contracts + expands])


def feed_weights_kernel(inner_ref, gelu_ref, low_ref, grad_ref, out_ref):
    size = inner_ref.shape[1]
    out_ref[0:size, :] = dot_tn(inner_ref[...], low_ref[...]).astype(BF)
    out_ref[size:, :] = dot_tn(gelu_ref[...], grad_ref[...]).astype(BF)


def feed_weights(inner, gelu, low, grad, half, blocks):
    count, width = low.shape
    size = inner.shape[1] // (2 * blocks)
    columns = pl.BlockSpec((count, size), lambda i: (0, half * blocks + i))
    return call(
        feed_weights_kernel,
        "feed_weights",
        4 * count * width * size * blocks,
        count * size * blocks * 4 + blocks * size * width * 4,
        grid=(blocks,),
        in_specs=[columns, columns, resident((count, width)), resident((count, width))],
        out_specs=pl.BlockSpec((2 * size, width), lambda i: (i, 0)),
        out_shape=jax.ShapeDtypeStruct((blocks * 2 * size, width), BF),
    )(inner, gelu, low, grad)


def middle_back_kernel(vec_ref, hid_ref, n_ref, s_ref, weight_ref, grad_ref, low_ref, ctx_ref, sum_ref):
    upstream, normed = hid_ref[...], n_ref[...]
    grad = norm_back(upstream, normed, s_ref[:, 0:1], vec_ref[1:2, :])
    low = grad.astype(BF)
    grad_ref[...] = grad
    low_ref[...] = low
    ctx_ref[...] = dot_nn(low, weight_ref[...]).astype(BF)
    add_rows(sum_ref, [low.astype(F32), upstream * normed, upstream])


def middle_back(vectors, hidden_grad, normed, inverse, attn_rows):
    count, width = hidden_grad.shape
    return call(
        middle_back_kernel,
        "middle_back",
        2 * count * width * width,
        count * width * 16,
        grid=(count // TILE,),
        in_specs=[resident(vectors.shape), tiles(width), tiles(width), tiles(128), resident((width, width), 3, 0)],
        out_specs=[tiles(width), tiles(width), tiles(width), resident((8, width))],
        out_shape=[
            jax.ShapeDtypeStruct((count, width), F32),
            jax.ShapeDtypeStruct((count, width), BF),
            jax.ShapeDtypeStruct((count, width), BF),
            jax.ShapeDtypeStruct((8, width), F32),
        ],
    )(vectors, hidden_grad, normed, inverse, attn_rows)


def attn_weights_kernel(table_ref, qkv_ref, low_ref, token_ref, ctx_ref, out_ref, *, quarters):
    def put(result):
        size = result.shape[0] // quarters
        for d in range(quarters):
            out_ref[d ^ table_ref[1], 0] = result[d * size : (d + 1) * size, :]

    @pl.when(pl.program_id(0) < 3)
    def _():
        put(dot_tn(qkv_ref[0], token_ref[...]).astype(BF))

    @pl.when(pl.program_id(0) == 3)
    def _():
        put(dot_tn(low_ref[...], ctx_ref[...]).astype(BF))


def attn_weights(table, qkv_grad, out_grad, tokens, context):
    count, width = tokens.shape
    half = width // 2
    return call(
        functools.partial(attn_weights_kernel, quarters=4),
        "attn_weights",
        4 * 2 * count * width * half,
        count * width * 8 + width * width * 4,
        grid_spec=pltpu.PrefetchScalarGridSpec(
            num_scalar_prefetch=1,
            grid=(4,),
            in_specs=[
                pl.BlockSpec((1, count, half), lambda i, t: (jnp.minimum(i, 2), 0, t[0])),
                pl.BlockSpec((count, half), lambda i, t: (0, t[0])),
                resident((count, width)),
                resident((count, width)),
            ],
            out_specs=pl.BlockSpec((4, 1, half // 4, width), lambda i, t: (0, i ^ t[2], 0, 0)),
        ),
        out_shape=jax.ShapeDtypeStruct((4, 4, half // 4, width), BF),
    )(table, qkv_grad, out_grad, tokens, context)


def input_kernel(qkv_ref, weight_ref, grad_ref, out_ref):
    width = out_ref.shape[1]
    total = grad_ref[...]
    for j in range(3):
        total = total + dot_nn(qkv_ref[j], weight_ref[j * width : (j + 1) * width, :])
    out_ref[...] = total.astype(BF)


def input_back(qkv_grad, attn_rows, grad):
    count, width = grad.shape
    return call(
        input_kernel,
        "input_back",
        6 * count * width * width,
        count * width * 12 + width * width * 6,
        grid=(count // TILE,),
        in_specs=[
            pl.BlockSpec((3, TILE, width), lambda t: (0, t, 0)),
            resident((3 * width, width)),
            tiles(width),
        ],
        out_specs=tiles(width),
        out_shape=jax.ShapeDtypeStruct((count, width), BF),
    )(qkv_grad, attn_rows, grad)


def tie(*values):
    return lax.optimization_barrier(values)


def add(*parts):
    return sum(part.astype(F32) for part in parts)


class Links:
    def __init__(self):
        self.dp, self.fsdp = lax.axis_size("dp"), lax.axis_size("fsdp")
        self.paired = (self.dp, self.fsdp) == (4, 8)
        my_dp, my_fsdp = lax.axis_index("dp"), lax.axis_index("fsdp")
        if self.paired:
            self.my_dp, self.my_core, self.my_z = my_dp, my_fsdp & 1, my_fsdp >> 1
        else:
            zero = jnp.zeros((), jnp.int32)
            self.my_dp, self.my_core, self.my_z = zero, zero, zero
        self.my_fsdp = my_fsdp

    def swap(self, values, core=0, dp=0, z=0):
        mask = core + 2 * z + self.fsdp * dp
        pairs = [(i, i ^ mask) for i in range(self.dp * self.fsdp)]
        return lax.ppermute(values, AXES, pairs)

    def table(self):
        e = jnp.arange(2, dtype=jnp.int32)[:, None, None]
        m = jnp.arange(4, dtype=jnp.int32)[None, :, None]
        k = jnp.arange(4, dtype=jnp.int32)[None, None, :]
        if not self.paired:
            return jnp.arange(32, dtype=jnp.int32)
        e, m, k = e ^ self.my_core, m ^ self.my_dp, k ^ self.my_z
        return ((k * 2 + e) * 4 + m).reshape(-1).astype(jnp.int32)

    def flip(self, values, axis, index):
        shape = values.shape
        bits = shape[axis].bit_length() - 1
        split = values.reshape(shape[:axis] + (2,) * bits + shape[axis + 1 :])
        for i in range(bits):
            bit = (index >> (bits - 1 - i)) & 1
            split = jnp.where(bit == 1, jnp.flip(split, axis + i), split)
        return split.reshape(shape)

    def to_exchange(self, natural):
        if not self.paired:
            return natural
        moved = natural.transpose(1, 2, 0, 3)
        return self.flip(self.flip(self.flip(moved, 0, self.my_core), 1, self.my_dp), 2, self.my_z)

    def to_natural(self, exchanged):
        if not self.paired:
            return exchanged
        moved = self.flip(self.flip(self.flip(exchanged, 0, self.my_core), 1, self.my_dp), 2, self.my_z)
        return moved.transpose(2, 0, 1, 3)


def spread_z(links, mine):
    return [mine] + [links.swap(mine, z=k) for k in range(1, 4)]


def spread_plane(links, own):
    one, two = links.swap(own, dp=1), links.swap(own, dp=2)
    return one, two


def spread_corner(links, one, two):
    half = one.shape[0] // 2
    return links.swap(one[:half], dp=2), links.swap(two[half:], dp=1)


def gather_plain(attention, attvector, expand, contract, feedvector):
    def whole(shard):
        return lax.all_gather(shard, "fsdp", axis=0, tiled=True)

    rows = [whole(attention.T), whole(expand.T), whole(contract)]
    return rows, whole(attvector).astype(F32), whole(feedvector).astype(F32)


def reduce_paired(links, near, far):
    mine = add(near, links.swap(far, core=1)).astype(BF)
    block = mine.shape[0] // 4
    half = block // 2
    own = [mine[m * block : (m + 1) * block] for m in range(4)]
    three_a, three_b = links.swap(own[3][:half], dp=2), links.swap(own[3][half:], dp=1)
    one = jnp.concatenate([add(own[1][:half], three_a).astype(BF), own[1][half:]], axis=0)
    two = jnp.concatenate([own[2][:half], add(own[2][half:], three_b).astype(BF)], axis=0)
    summed = add(own[0], links.swap(one, dp=1), links.swap(two, dp=2)).astype(BF)
    return summed


def reduce_z(links, summed, size):
    summed = summed.reshape(-1, 4, size, summed.shape[-1])
    pieces = [summed[:, k].reshape(-1, summed.shape[-1]) for k in range(4)]
    return add(pieces[0], *[links.swap(pieces[k], z=k) for k in range(1, 4)]).astype(BF)


def share_plane(links, final):
    stacked = jnp.stack([final] + [links.swap(final, dp=m) for m in range(1, 4)])
    return links.flip(stacked, 0, links.my_dp)


def per_device(tokens, attention, attvector, expand, contract, feedvector, lengths, cotangent):
    links = Links()
    width = tokens.shape[1]
    positions = tokens.shape[0] // lengths.shape[0]
    hidden = expand.shape[1] * links.fsdp
    att_len, feed_len = attvector.shape[0], feedvector.shape[0]
    size = width // 8
    quad = 4 * size

    if links.paired:
        vectors = jnp.concatenate([attvector, feedvector])
        extra = jnp.pad(vectors, (0, 16 * width - vectors.shape[0])).reshape(16, width)

        def quarter(shard):
            return lax.dynamic_slice_in_dim(shard, links.my_dp * size, size, 0)

        attn_z = spread_z(links, jnp.concatenate([quarter(attention.T), extra], axis=0))
        feed_mine = jnp.concatenate([quarter(expand.T), quarter(contract)], axis=0)
        feed_mine, *attn_z = tie(feed_mine, *attn_z)
        attn_own = jnp.concatenate([part[:size] for part in attn_z], axis=0)
        extras = jnp.concatenate([part[size:] for part in attn_z], axis=0)
        attn_one, attn_two = spread_plane(links, attn_own)
        feed_z = spread_z(links, feed_mine)
        attn_three = spread_corner(links, attn_one, attn_two)
        attn_near = [attn_own, attn_one, attn_two, *attn_three]
        attn_far = [links.swap(part, core=1) for part in attn_near]
        extras = jnp.stack([extras, links.swap(extras, core=1)])
        attn_pieces = attn_near + attn_far
        attn_starts = [0, 4, 8, 12, 14, 16, 20, 24, 28, 30]
        extras = extras.reshape(2, 1, 4, 16 * width)[..., : vectors.shape[0]]
        extras = links.flip(links.flip(extras, 0, links.my_core), 2, links.my_z)
        by_owner = extras.transpose(2, 0, 1, 3).reshape(links.fsdp, -1).astype(F32)
        attvec, feedvec = by_owner[:, :att_len].reshape(-1), by_owner[:, att_len:].reshape(-1)

        feed_own = jnp.concatenate([part[:size] for part in feed_z] + [part[size:] for part in feed_z], axis=0)
        feed_own, *_ = tie(feed_own, *attn_three)
        feed_one, feed_two = spread_plane(links, feed_own)
        feed_far = [links.swap(feed_own, core=1)]
    else:
        rows, attvec, feedvec = gather_plain(attention, attvector, expand, contract, feedvector)
        attn_pieces, attn_starts = [rows[0]], [0]
        expands = [(rows[1], i * quad, quad) for i in range(8)]
        contracts = [(rows[2], i * quad, quad) for i in range(8)]

    def row_of(vector, i, start=0):
        return vector[start + i * width : start + (i + 1) * width]

    project_bias = jnp.stack([row_of(attvec, 0), row_of(attvec, 1)])
    vec_rows = [row_of(attvec, i) for i in (2, 3, 4)] + [row_of(feedvec, i, hidden) for i in range(3)]
    vec_rows = jnp.stack(vec_rows + [jnp.zeros((width,), F32)] * 2)
    inner_bias = links.to_exchange(feedvec[:hidden].reshape(4, 2, 4, size)).reshape(1, hidden)

    projected, attn_rows = project(tokens, project_bias, links.table(), attn_pieces, attn_starts, size)
    context, logs = attend(projected, lengths, positions)
    if links.paired:
        context, feed_one, feed_two = tie(context, feed_one, feed_two)
        feed_three = spread_corner(links, feed_one, feed_two)
        feed_far += [links.swap(feed_one, core=1), links.swap(feed_two, core=1)]
    normed_one, inverse_one, hidden_low, sum_middle = middle(
        lengths, vec_rows, context, attn_rows, tokens, positions
    )
    if links.paired:
        hidden_low, *feed_three = tie(hidden_low, *feed_three)
        feed_near = [feed_own, feed_one, feed_two]
        far_three = [links.swap(part, core=1) for part in feed_three]
        expands = [(part, 0, quad) for part in feed_near] + [(feed_three[0], 0, quad)]
        expands += [(part, 0, quad) for part in feed_far] + [(far_three[0], 0, quad)]
        contracts = [(part, quad, quad) for part in feed_near] + [(feed_three[1], 0, quad)]
        contracts += [(part, quad, quad) for part in feed_far] + [(far_three[1], 0, quad)]
    gelu, slope = expand_call(hidden_low, inner_bias, expands)
    result, grad_two, grad_two_low, sum_two = contract_call(
        lengths, vec_rows, gelu, normed_one, cotangent, contracts, positions
    )
    inner_grad, hidden_grad, sum_inner = inner_back(grad_two_low, slope, grad_two, contracts, expands)
    feed_far_part = feed_weights(inner_grad, gelu, hidden_low, grad_two_low, 1, 4)
    feed_near_part = feed_weights(inner_grad, gelu, hidden_low, grad_two_low, 0, 4)
    grad_one, grad_one_low, context_grad, sum_one = middle_back(
        vec_rows, hidden_grad, normed_one, inverse_one, attn_rows
    )
    qkv_grad, sum_qkv = attend_back(projected, lengths, context_grad, context, logs, positions)

    def attn_part(e):
        table = jnp.stack([links.my_core ^ e, links.my_dp, links.my_z]).astype(jnp.int32)
        return attn_weights(table, qkv_grad, grad_one_low, tokens, context)

    attn_far_part, attn_near_part = attn_part(1), attn_part(0)
    input_grad = input_back(qkv_grad, attn_rows, grad_one)

    if links.paired:
        feed_sum = reduce_paired(links, feed_near_part, feed_far_part)
        feed_sum = share_plane(links, reduce_z(links, feed_sum, size))
        expand_sum = feed_sum[:, :size].reshape(quad, width).astype(F32).T
        contract_sum = feed_sum[:, size:].reshape(quad, width).astype(F32)
        attn_sum = reduce_paired(
            links, attn_near_part.reshape(-1, width), attn_far_part.reshape(-1, width)
        )
        attn_sum = share_plane(links, reduce_z(links, attn_sum, size)).reshape(quad, width).astype(F32).T
    else:
        def finish(natural):
            shard = lax.psum_scatter(natural, "fsdp", scatter_dimension=0, tiled=True)
            return lax.psum(shard, "dp").astype(F32)

        feed = jnp.concatenate([feed_near_part, feed_far_part], axis=0).reshape(8, 2, quad, width)
        expand_sum = finish(feed[:, 0].reshape(hidden, width)).T
        contract_sum = finish(feed[:, 1].reshape(hidden, width))
        both = jnp.stack([attn_near_part, attn_far_part])
        attn_sum = finish(both.transpose(2, 0, 1, 3, 4).reshape(4 * width, width)).T

    inner_sum = links.to_natural(sum_inner[0].reshape(2, 4, 4, size)).reshape(hidden // width, width)
    sum_rows = jnp.sum(sum_qkv, axis=0)
    count_row = jnp.pad(jnp.sum(lengths).astype(F32).reshape(1, 1), ((0, 0), (0, width - 1)))
    packed = jnp.concatenate(
        [sum_rows, sum_one[:3], inner_sum, sum_two[1:4], sum_middle[:2], sum_two[:1], count_row], axis=0
    )
    if links.paired:
        for step in ({"core": 1}, {"dp": 1}, {"dp": 2}, {"z": 1}, {"z": 2}):
            packed = packed + links.swap(packed, **step)
    else:
        packed = lax.psum(packed, AXES)
    flat = packed.reshape(-1)
    att_total, feed_total = att_len * links.fsdp, feed_len * links.fsdp
    att_sum = lax.dynamic_slice_in_dim(flat[:att_total], links.my_fsdp * att_len, att_len, 0)
    feed_vec_sum = lax.dynamic_slice_in_dim(
        flat[att_total : att_total + feed_total], links.my_fsdp * feed_len, feed_len, 0
    )
    squares = jnp.sum(packed[12:15], axis=1)
    root_squares = jnp.sqrt(squares / (packed[15, 0] * width))
    return (result, input_grad, attn_sum, att_sum, expand_sum, contract_sum, feed_vec_sum, root_squares)


def solution(mesh):
    return jax.shard_map(
        per_device,
        mesh=mesh,
        in_specs=(
            P(AXES, None),
            P(None, "fsdp"),
            P("fsdp"),
            P(None, "fsdp"),
            P("fsdp", None),
            P("fsdp"),
            P(AXES),
            P(AXES, None),
        ),
        out_specs=(
            P(AXES, None),
            P(AXES, None),
            P(None, "fsdp"),
            P("fsdp"),
            P(None, "fsdp"),
            P("fsdp", None),
            P("fsdp"),
            P(),
        ),
        check_vma=False,
    )
```

time: 598 us -> 379 us (0.63)
  Pallas kernels: 0 us -> 173 us
  matrix products: 169 us -> 0 us
  blocking collectives: 109 us -> 0 us
  waiting for transfers between devices: 169 us -> 81.7 us
  starting transfers between devices: 0.28 us -> 57.2 us
  local copies, waits for them, and re-layouts: 69.8 us -> 33.7 us
  other arithmetic: 53.7 us -> 28.6 us
  between operations: 18.9 us -> 2.72 us
    pallas_call x0 -> x13, Pallas kernels: none -> 173 us  [the longest x1 35.9 us: attend_back(): call(attend_back_kernel, 'attend_back', 2 * flops, 16 * count * width, gr...]
    dot_general x26 -> x0, matrix products: 169 us -> none  [the longest x1 38.6 us: per_device(): jnp.dot(hidden_low, expand_whole, preferred_element_type=jnp.float32)]
    reduce_scatter x3 -> x0, waiting for transfers between devices: 139 us -> none  [the longest x1 97.9 us: per_device(): lax.psum_scatter(contract_grad, 'fsdp', scatter_dimension=0, tiled=True)]
    ppermute x0 -> x52, waiting for transfers between devices: none -> 81.7 us  [swap(): return lax.ppermute(values, AXES, pairs)]
    unnamed x2 -> x0, blocking collectives: 58.6 us -> none
    ppermute x0 -> x52, starting transfers between devices: none -> 57.2 us  [swap(): return lax.ppermute(values, AXES, pairs)]
    psum x2 -> x0, blocking collectives: 50.1 us -> none  [the longest x1 40.2 us: per_device(): square_sums, count_total = lax.psum((squares, count_sum), ('dp', 'fsdp'))]
    while x44 -> x0, local copies, waits for them, and re-layouts: 20.9 us -> none  [the longest x4 10.5 us: per_device(): lax.map(attend, (query_four, key_four, value_four, live_mask))]
  transfers between devices with their start and end apart: 7 -> 52, of which waited for: 5 -> 19; matrix products, arithmetic and copies ran while one was open for 40% -> 14% of each run, Pallas kernels for 0% -> 33%
where the time goes in v2:
time: 379 us; the launch traced here: 377 us
  Pallas kernels  173 us (46%)
  waiting for transfers between devices  81.7 us (22%)
  starting transfers between devices  57.2 us (15%)
  local copies, waits for them, and re-layouts  33.7 us (9%)
  other arithmetic  28.6 us (8%)
    ppermute x52, waiting for transfers between devices, swap(): return lax.ppermute(values, AXES, pairs)  81.7 us
    ppermute x52, starting transfers between devices, swap(): return lax.ppermute(values, AXES, pairs)  57.2 us
    pallas_call x1, Pallas kernels, attend_back(): call(attend_back_kernel, 'attend_back', 2 * flops, 16 * count * width, gr...  35.9 us
    pallas_call x1, Pallas kernels, inner_back(): call(functools.partial(inner_kernel, count=len(contracts)), 'inner_back',...  23.7 us
    pallas_call x2, Pallas kernels, feed_weights(): call(feed_weights_kernel, 'feed_weights', 4 * count * width * size * bloc...  19.4 us
    pallas_call x1, Pallas kernels, attend(): call(attend_kernel, 'attend', 2 * flops, 8 * count * width, grid_spec=plt...  18.2 us
    pallas_call x2, Pallas kernels, attn_weights(): call(functools.partial(attn_weights_kernel, quarters=4), 'attn_weights',...  15.7 us
    pallas_call x1, Pallas kernels, contract_call(): call(functools.partial(contract_kernel, positions=positions), 'contract_n...  14.9 us
  transfers between devices with their start and end apart: 52, of which 19 were waited for; matrix products, arithmetic and copies ran while one was open for 14% of the time, Pallas kernels for 33%

profile of v2, /device:TPU:0, one launch (start us, length us, event | category | flops | bytes accessed | tf_op | source)
XLA Modules:
  0.0 377.1 jit_solution(17166835153185975169)
XLA Ops:
  3.0 5.1 %collective-permute-start.2 = (bf16[112,768]{1,0:T(8,128)(2,1)S(1)}, bf16[112,768]{1,0:T(8,128)(2,1)S(1)}, u32[]{:S(2)}, u32[]{:S(2)}) collective-permute-start(bf16[112,768]{1,0:T(8,128)(2,1)S(1)} %pad_maximum_fusion.8), channel_id=1, source_target_pairs={{0,6},{1,7},{2,4},{3,5},{4,2},{5,3},{6,0},{7,1},{8,14},{9,15},{10,... | collective-permute-start | bytes 516104 | tf_op jit(solution)/shard_map/ppermute | solution.py:519
  9.8 3.7 collective-permute-done.2
  13.5 9.3 %collective-permute-done.1 = bf16[112,768]{1,0:T(8,128)(2,1)S(1)} collective-permute-done((bf16[112,768]{1,0:T(8,128)(2,1)S(1)}, bf16[112,768]{1,0:T(8,128)(2,1)S(1)}, u32[]{:S(2)}, u32[]{:S(2)}) %collective-permute-start.1) | collective-permute-done | bytes 172064 | tf_op jit(solution)/shard_map/ppermute | solution.py:519
  23.0 2.5 collective-permute-start.15
  31.6 13.5 %collective-permute-done.13 = bf16[192,768]{1,0:T(8,128)(2,1)S(1)} collective-permute-done((bf16[192,768]{1,0:T(8,128)(2,1)S(1)}, bf16[192,768]{1,0:T(8,128)(2,1)S(1)}, u32[]{:S(2)}, u32[]{:S(2)}) %collective-permute-start.13) | collective-permute-done | bytes 294944 | tf_op jit(solution)/shard_map/ppermute | solution.py:519
  47.3 3.2 collective-permute-done.14
  55.7 5.6 %collective-permute-done.4.refs_1_ = bf16[384,768]{1,0:T(8,128)(2,1)S(1)} collective-permute-done((bf16[384,768]{1,0:T(8,128)(2,1)S(1)}, bf16[384,768]{1,0:T(8,128)(2,1)S(1)}, u32[]{:S(2)}, u32[]{:S(2)}) %collective-permute-start.4) | collective-permute-done | bytes 589856 | tf_op jit(solution)/shard_map/ppermute | solution.py:519
  74.3 10.0 %project.1 = (bf16[3,1024,768]{2,1,0:T(8,128)(2,1)}, bf16[3072,768]{1,0:T(8,128)(2,1)}) custom-call(s32[32]{0:T(128)} %add.120.table_ref, f32[2,768]{1,0:T(2,128)} %pad_maximum_fusion.11.bias_ref, bf16[1024,768]{1,0:T(8,128)(2,1)} %token_ref.7, bf16[384,768]{1,0:T(8,128)(2,1)} %copy-done.9, bf16[384,768]{1,0:T(8,128)(2,1)} %copy-done.10, ...), custom_call_target="tpu_custom_call" | custom-call | flops 3623878656 | bytes 15728640 | tf_op jit(solution)/shard_map/project/pallas_call | solution.py:73
  84.3 18.2 %attend.1 = (bf16[1024,768]{1,0:T(8,128)(2,1)}, f32[2,6,2,512]{3,2,1,0:T(2,128)}) custom-call(s32[2]{0:T(128)} %length_ref.7, bf16[3,1024,768]{2,1,0:T(8,128)(2,1)} %get-tuple-element.47.q_ref.k_ref.v_ref, bf16[3,1024,768]{2,1,0:T(8,128)(2,1)} %get-tuple-element.47.q_ref.k_ref.v_ref, bf16[3,1024,768]{2,1,0:T(8,128)(2,1)} %get-tuple-element.47.q_ref.k_ref.v_ref), custom_call_target="tpu_custom_call" | custom-call | flops 3221225472 | bytes 6291456 | tf_op jit(solution)/shard_map/attend/pallas_call | solution.py:124
  112.6 6.9 %middle.1 = (f32[1024,768]{1,0:T(8,128)}, f32[1024,128]{1,0:T(8,128)}, bf16[1024,768]{1,0:T(8,128)(2,1)}, f32[8,768]{1,0:T(8,128)}) custom-call(s32[2]{0:T(128)} %length_ref.7, f32[8,768]{1,0:T(8,128)} %stack.102.vec_ref, bf16[1024,768]{1,0:T(8,128)(2,1)} %get-tuple-element.51.ctx_ref, bf16[3072,768]{1,0:T(8,128)(2,1)} %get-tuple-element.52.weight_ref, ...), custom_call_target="tpu_custom_call" | custom-call | flops 1207959552 | bytes 9437184 | tf_op jit(solution)/shard_map/middle/pallas_call | solution.py:246
  122.8 12.0 %expand_gelu.1 = (bf16[1024,3072]{1,0:T(8,128)(2,1)}, bf16[1024,3072]{1,0:T(8,128)(2,1)}) custom-call(f32[1,3072]{1,0:T(1,128)} %reshape_reshape.11.bias_ref, bf16[1024,768]{1,0:T(8,128)(2,1)} %get-tuple-element.56.low_ref, bf16[768,768]{1,0:T(8,128)(2,1)} %slice_dynamic-update-slice_fusion.refs_0_.refs_8_, bf16[768,768]{1,0:T(8,128)(2,1)} %copy-done.4, ...), custom_call_target="tpu_custom_call" | custom-call | flops 4831838208 | bytes 12582912 | tf_op jit(solution)/shard_map/expand_gelu/pallas_call | solution.py:289
  135.6 14.9 %contract_norm.1 = (bf16[1024,768]{1,0:T(8,128)(2,1)}, f32[1024,768]{1,0:T(8,128)}, bf16[1024,768]{1,0:T(8,128)(2,1)}, f32[8,768]{1,0:T(8,128)}) custom-call(s32[2]{0:T(128)} %length_ref.7, f32[8,768]{1,0:T(8,128)} %stack.102.vec_ref, bf16[1024,3072]{1,0:T(8,128)(2,1)} %get-tuple-element.58.gelu_ref, f32[1024,768]{1,0:T(8,128)} %get-tuple-element.59.n_ref, ...), custom_call_target="tpu_custom_call" | custom-call | flops 4831838208 | bytes 17301504 | tf_op jit(solution)/shard_map/contract_norm/pallas_call | solution.py:325
  150.5 23.7 %inner_back.1 = (bf16[1024,3072]{1,0:T(8,128)(2,1)}, f32[1024,768]{1,0:T(8,128)}, f32[8,3072]{1,0:T(8,128)}) custom-call(bf16[1024,768]{1,0:T(8,128)(2,1)} %get-tuple-element.62.low_ref.grad_ref, bf16[1024,3072]{1,0:T(8,128)(2,1)} %get-tuple-element.63.slope_ref, f32[1024,768]{1,0:T(8,128)} %get-tuple-element.64.grad_ref, ...), custom_call_target="tpu_custom_call" | custom-call | flops 9663676416 | bytes 20447232 | tf_op jit(solution)/shard_map/inner_back/pallas_call | solution.py:364
  174.2 9.8 %feed_weights.3 = bf16[3072,768]{1,0:T(8,128)(2,1)} custom-call(bf16[1024,3072]{1,0:T(8,128)(2,1)} %get-tuple-element.77.inner_ref, bf16[1024,3072]{1,0:T(8,128)(2,1)} %get-tuple-element.58.gelu_ref, bf16[1024,768]{1,0:T(8,128)(2,1)} %get-tuple-element.56.low_ref, bf16[1024,768]{1,0:T(8,128)(2,1)} %get-tuple-element.62.low_ref.grad_ref), custom_call_target="tpu_custom_call" | custom-call | flops 4831838208 | bytes 11010048 | tf_op jit(solution)/shard_map/feed_weights/pallas_call | solution.py:391
  185.1 8.0 %middle_back.1 = (f32[1024,768]{1,0:T(8,128)}, bf16[1024,768]{1,0:T(8,128)(2,1)}, bf16[1024,768]{1,0:T(8,128)(2,1)}, f32[8,768]{1,0:T(8,128)}) custom-call(f32[8,768]{1,0:T(8,128)} %stack.102.vec_ref, f32[1024,768]{1,0:T(8,128)} %get-tuple-element.65.hid_ref, f32[1024,768]{1,0:T(8,128)} %get-tuple-element.59.n_ref, f32[1024,128]{1,0:T(8,128)} %get-tuple-element.66.s_ref, ...), custom_call_target="tpu_custom_call" | custom-call | flops 1207959552 | bytes 12582912 | tf_op jit(solution)/shard_map/middle_back/pallas_call | solution.py:415
  193.0 35.9 %attend_back.1 = (bf16[3,1024,768]{2,1,0:T(8,128)(2,1)}, f32[2,2,768]{2,1,0:T(2,128)}) custom-call(s32[2]{0:T(128)} %length_ref.7, bf16[3,1024,768]{2,1,0:T(8,128)(2,1)} %get-tuple-element.47.q_ref.k_ref.v_ref, bf16[3,1024,768]{2,1,0:T(8,128)(2,1)} %get-tuple-element.47.q_ref.k_ref.v_ref, bf16[3,1024,768]{2,1,0:T(8,128)(2,1)} %get-tuple-element.47.q_ref.k_ref.v_ref, ...), custom_call_target="tpu_custom_call" | custom-call | flops 8053063680 | bytes 12582912 | tf_op jit(solution)/shard_map/attend_back/pallas_call | solution.py:179
  229.0 7.9 %attn_weights.3 = bf16[4,4,96,768]{3,2,1,0:T(8,128)(2,1)} custom-call(s32[3]{0:T(128)} %add_add_fusion.1.table_ref, bf16[3,1024,768]{2,1,0:T(8,128)(2,1)} %get-tuple-element.69.qkv_ref, bf16[1024,768]{1,0:T(8,128)(2,1)} %get-tuple-element.71.low_ref, bf16[1024,768]{1,0:T(8,128)(2,1)} %token_ref.7, bf16[1024,768]{1,0:T(8,128)(2,1)} %get-tuple-element.51.ctx_ref), custom_call_target="tpu_custom_call" | custom-call | flops 2415919104 | bytes 8650752 | tf_op jit(solution)/shard_map/attn_weights/pallas_call | solution.py:450
  241.7 9.6 %feed_weights.2 = bf16[3072,768]{1,0:T(8,128)(2,1)} custom-call(bf16[1024,3072]{1,0:T(8,128)(2,1)} %get-tuple-element.77.inner_ref, bf16[1024,3072]{1,0:T(8,128)(2,1)} %get-tuple-element.58.gelu_ref, bf16[1024,768]{1,0:T(8,128)(2,1)} %get-tuple-element.56.low_ref, bf16[1024,768]{1,0:T(8,128)(2,1)} %get-tuple-element.62.low_ref.grad_ref), custom_call_target="tpu_custom_call" | custom-call | flops 4831838208 | bytes 11010048 | tf_op jit(solution)/shard_map/feed_weights/pallas_call | solution.py:391
  253.7 7.8 %attn_weights.2 = bf16[4,4,96,768]{3,2,1,0:T(8,128)(2,1)} custom-call(s32[3]{0:T(128)} %add_add_fusion.table_ref, bf16[3,1024,768]{2,1,0:T(8,128)(2,1)} %get-tuple-element.69.qkv_ref, bf16[1024,768]{1,0:T(8,128)(2,1)} %get-tuple-element.71.low_ref, bf16[1024,768]{1,0:T(8,128)(2,1)} %token_ref.7, bf16[1024,768]{1,0:T(8,128)(2,1)} %get-tuple-element.51.ctx_ref), custom_call_target="tpu_custom_call" | custom-call | flops 2415919104 | bytes 8650752 | tf_op jit(solution)/shard_map/attn_weights/pallas_call | solution.py:450
  263.0 3.0 fusion
  267.9 3.8 %add_convert_fusion = bf16[3072,768]{1,0:T(8,128)(2,1)S(1)} fusion(bf16[3072,768]{1,0:T(8,128)(2,1)} %collective-permute-done.41, bf16[3072,768]{1,0:T(8,128)(2,1)S(1)} %bitcast.72), kind=kLoop, calls=%fused_computation | loop fusion | flops 9437184 | bytes 14155776 | tf_op jit(solution)/shard_map/convert_element_type | solution.py:575
  278.0 3.1 collective-permute-start.39
  295.5 2.5 collective-permute-start.43
  298.0 8.4 %input_back.1 = bf16[1024,768]{1,0:T(8,128)(2,1)} custom-call(bf16[3,1024,768]{2,1,0:T(8,128)(2,1)} %get-tuple-element.69.qkv_ref, bf16[3072,768]{1,0:T(8,128)(2,1)} %get-tuple-element.52.weight_ref, f32[1024,768]{1,0:T(8,128)} %get-tuple-element.70.grad_ref), custom_call_target="tpu_custom_call" | custom-call | flops 3623878656 | bytes 12976128 | tf_op jit(solution)/shard_map/input_back/pallas_call | solution.py:480
  311.4 4.1 %collective-permute-start.30 = (bf16[96,768]{1,0:T(8,128)(2,1)S(1)}, bf16[96,768]{1,0:T(8,128)(2,1)S(1)}, u32[]{:S(2)}, u32[]{:S(2)}) collective-permute-start(bf16[96,768]{1,0:T(8,128)(2,1)S(1)} %get-tuple-element.104), channel_id=1, source_target_pairs={{0,2},{1,3},{2,0},{3,1},{4,6},{5,7},{6,4},{7,5},{8,10},{9,11},{10,... | collective-permute-start | bytes 442376 | tf_op jit(solution)/shard_map/ppermute | solution.py:519
  319.6 3.0 collective-permute-done.32
  322.6 2.7 collective-permute-done.31
  338.4 6.6 %collective-permute-done.48 = bf16[192,768]{1,0:T(8,128)(2,1)S(1)} collective-permute-done((bf16[192,768]{1,0:T(8,128)(2,1)S(1)}, bf16[192,768]{1,0:T(8,128)(2,1)S(1)}, u32[]{:S(2)}, u32[]{:S(2)}) %collective-permute-start.48) | collective-permute-done | bytes 294944 | tf_op jit(solution)/shard_map/ppermute | solution.py:519
  344.9 12.5 %collective-permute-done.47 = bf16[192,768]{1,0:T(8,128)(2,1)S(1)} collective-permute-done((bf16[192,768]{1,0:T(8,128)(2,1)S(1)}, bf16[192,768]{1,0:T(8,128)(2,1)S(1)}, u32[]{:S(2)}, u32[]{:S(2)}) %collective-permute-start.47) | collective-permute-done | bytes 294944 | tf_op jit(solution)/shard_map/ppermute | solution.py:519
  357.6 2.7 collective-permute-start.51
  363.2 5.3 %collective-permute-done.51 = bf16[192,768]{1,0:T(8,128)(2,1)S(1)} collective-permute-done((bf16[192,768]{1,0:T(8,128)(2,1)S(1)}, bf16[192,768]{1,0:T(8,128)(2,1)S(1)}, u32[]{:S(2)}, u32[]{:S(2)}) %collective-permute-start.51) | collective-permute-done | bytes 294944 | tf_op jit(solution)/shard_map/ppermute | solution.py:519
  368.5 5.3 %collective-permute-done.50 = bf16[192,768]{1,0:T(8,128)(2,1)S(1)} collective-permute-done((bf16[192,768]{1,0:T(8,128)(2,1)S(1)}, bf16[192,768]{1,0:T(8,128)(2,1)S(1)}, u32[]{:S(2)}, u32[]{:S(2)}) %collective-permute-start.50) | collective-permute-done | bytes 294944 | tf_op jit(solution)/shard_map/ppermute | solution.py:519
  (274 shorter events, 103.8 us)
Async XLA Ops:
  8.2 14.6 %collective-permute-start.1 = (bf16[112,768]{1,0:T(8,128)(2,1)S(1)}, bf16[112,768]{1,0:T(8,128)(2,1)S(1)}, u32[]{:S(2)}, u32[]{:S(2)}) collective-permute-start(bf16[112,768]{1,0:T(8,128)(2,1)S(1)} %pad_maximum_fusion.8), channel_id=1, source_target_pairs={{0,4},{1,5},{2,6},{3,7},{4,0},{5,1},{6,2},{7,3},{8,12},{9,13},{10,... | collective-permute-start | bytes 516104 | tf_op jit(solution)/shard_map/ppermute | solution.py:519
  8.2 14.6 %collective-permute-start = (bf16[112,768]{1,0:T(8,128)(2,1)S(1)}, bf16[112,768]{1,0:T(8,128)(2,1)S(1)}, u32[]{:S(2)}, u32[]{:S(2)}) collective-permute-start(bf16[112,768]{1,0:T(8,128)(2,1)S(1)} %pad_maximum_fusion.8), channel_id=1, source_target_pairs={{0,2},{1,3},{2,0},{3,1},{4,6},{5,7},{6,4},{7,5},{8,10},{9,11},{10,... | collective-permute-start | bytes 516104 | tf_op jit(solution)/shard_map/ppermute | solution.py:519
  23.0 28.1 %collective-permute-start.15 = (bf16[192,768]{1,0:T(8,128)(2,1)S(1)}, bf16[192,768]{1,0:T(8,128)(2,1)S(1)}, u32[]{:S(2)}, u32[]{:S(2)}) collective-permute-start(bf16[192,768]{1,0:T(8,128)(2,1)S(1)} %pad_maximum_fusion.7), channel_id=1, source_target_pairs={{0,6},{1,7},{2,4},{3,5},{4,2},{5,3},{6,0},{7,1},{8,14},{9,15},{10,... | collective-permute-start | bytes 884744 | tf_op jit(solution)/shard_map/ppermute | solution.py:519
  25.5 24.9 %collective-permute-start.14 = (bf16[192,768]{1,0:T(8,128)(2,1)S(1)}, bf16[192,768]{1,0:T(8,128)(2,1)S(1)}, u32[]{:S(2)}, u32[]{:S(2)}) collective-permute-start(bf16[192,768]{1,0:T(8,128)(2,1)S(1)} %pad_maximum_fusion.7), channel_id=1, source_target_pairs={{0,4},{1,5},{2,6},{3,7},{4,0},{5,1},{6,2},{7,3},{8,12},{9,13},{10,... | collective-permute-start | bytes 884744 | tf_op jit(solution)/shard_map/ppermute | solution.py:519
  25.5 19.6 %collective-permute-start.13 = (bf16[192,768]{1,0:T(8,128)(2,1)S(1)}, bf16[192,768]{1,0:T(8,128)(2,1)S(1)}, u32[]{:S(2)}, u32[]{:S(2)}) collective-permute-start(bf16[192,768]{1,0:T(8,128)(2,1)S(1)} %pad_maximum_fusion.7), channel_id=1, source_target_pairs={{0,2},{1,3},{2,0},{3,1},{4,6},{5,7},{6,4},{7,5},{8,10},{9,11},{10,... | collective-permute-start | bytes 884744 | tf_op jit(solution)/shard_map/ppermute | solution.py:519
  28.2 41.5 %collective-permute-start.8 = (bf16[384,768]{1,0:T(8,128)(2,1)S(1)}, bf16[384,768]{1,0:T(8,128)(2,1)S(1)}, u32[]{:S(2)}, u32[]{:S(2)}) collective-permute-start(bf16[384,768]{1,0:T(8,128)(2,1)S(1)} %pad_maximum_fusion.3.refs_0_), channel_id=1, source_target_pairs={{0,1},{1,0},{2,3},{3,2},{4,5},{5,4},{6,7},{7,6},{8,9},{9,8},{10,11... | collective-permute-start | bytes 1769480 | tf_op jit(solution)/shard_map/ppermute | solution.py:519
  28.3 24.2 %collective-permute-start.5 = (bf16[384,768]{1,0:T(8,128)(2,1)S(1)}, bf16[384,768]{1,0:T(8,128)(2,1)}, u32[]{:S(2)}, u32[]{:S(2)}) collective-permute-start(bf16[384,768]{1,0:T(8,128)(2,1)S(1)} %pad_maximum_fusion.3.refs_0_), channel_id=1, source_target_pairs={{0,16},{1,17},{2,18},{3,19},{4,20},{5,21},{6,22},{7,23},{8,24},{9,... | collective-permute-start | bytes 1769480 | tf_op jit(solution)/shard_map/ppermute | solution.py:519
  45.1 16.2 %collective-permute-start.4 = (bf16[384,768]{1,0:T(8,128)(2,1)S(1)}, bf16[384,768]{1,0:T(8,128)(2,1)S(1)}, u32[]{:S(2)}, u32[]{:S(2)}) collective-permute-start(bf16[384,768]{1,0:T(8,128)(2,1)S(1)} %pad_maximum_fusion.3.refs_0_), channel_id=1, source_target_pairs={{0,8},{1,9},{2,10},{3,11},{4,12},{5,13},{6,14},{7,15},{8,0},{9,1},... | collective-permute-start | bytes 1769480 | tf_op jit(solution)/shard_map/ppermute | solution.py:519
  53.5 12.8 %collective-permute-start.7 = (bf16[192,768]{1,0:T(8,128)(2,1)S(1)}, bf16[192,768]{1,0:T(8,128)(2,1)S(1)}, u32[]{:S(2)}, u32[]{:S(2)}) collective-permute-start(bf16[192,768]{1,0:T(8,128)(2,1)S(1)} %slice.302), channel_id=1, source_target_pairs={{0,8},{1,9},{2,10},{3,11},{4,12},{5,13},{6,14},{7,15},{8,0},{9,1},... | collective-permute-start | bytes 884744 | tf_op jit(solution)/shard_map/ppermute | solution.py:519
  68.2 34.4 %collective-permute-start.17 = (bf16[768,768]{1,0:T(8,128)(2,1)}, bf16[768,768]{1,0:T(8,128)(2,1)S(1)}, u32[]{:S(2)}, u32[]{:S(2)}) collective-permute-start(bf16[768,768]{1,0:T(8,128)(2,1)} %slice_dynamic-update-slice_fusion.refs_0_.refs_8_), channel_id=1, source_target_pairs={{0,16},{1,17},{2,18},{3,19},{4,20},{5,21},{6,22},{7,23},{8,24},{9,... | collective-permute-start | bytes 3538952 | tf_op jit(solution)/shard_map/ppermute | solution.py:519
  70.5 32.0 %collective-permute-start.16 = (bf16[768,768]{1,0:T(8,128)(2,1)}, bf16[768,768]{1,0:T(8,128)(2,1)S(1)}, u32[]{:S(2)}, u32[]{:S(2)}) collective-permute-start(bf16[768,768]{1,0:T(8,128)(2,1)} %slice_dynamic-update-slice_fusion.refs_0_.refs_8_), channel_id=1, source_target_pairs={{0,8},{1,9},{2,10},{3,11},{4,12},{5,13},{6,14},{7,15},{8,0},{9,1},... | collective-permute-start | bytes 3538952 | tf_op jit(solution)/shard_map/ppermute | solution.py:519
  103.5 16.0 %collective-permute-start.19 = (bf16[384,768]{1,0:T(8,128)(2,1)}, bf16[384,768]{1,0:T(8,128)(2,1)S(1)}, u32[]{:S(2)}, u32[]{:S(2)}) collective-permute-start(bf16[384,768]{1,0:T(8,128)(2,1)} %slice.254), channel_id=1, source_target_pairs={{0,8},{1,9},{2,10},{3,11},{4,12},{5,13},{6,14},{7,15},{8,0},{9,1},... | collective-permute-start | bytes 1769480 | tf_op jit(solution)/shard_map/ppermute | solution.py:519
  104.0 15.5 %collective-permute-start.18 = (bf16[384,768]{1,0:T(8,128)(2,1)S(1)}, bf16[384,768]{1,0:T(8,128)(2,1)}, u32[]{:S(2)}, u32[]{:S(2)}) collective-permute-start(bf16[384,768]{1,0:T(8,128)(2,1)S(1)} %slice.253), channel_id=1, source_target_pairs={{0,16},{1,17},{2,18},{3,19},{4,20},{5,21},{6,22},{7,23},{8,24},{9,... | collective-permute-start | bytes 1769480 | tf_op jit(solution)/shard_map/ppermute | solution.py:519
  108.1 14.7 %collective-permute-start.20 = (bf16[768,768]{1,0:T(8,128)(2,1)}, bf16[768,768]{1,0:T(8,128)(2,1)}, u32[]{:S(2)}, u32[]{:S(2)}) collective-permute-start(bf16[768,768]{1,0:T(8,128)(2,1)} %slice_dynamic-update-slice_fusion.refs_0_.refs_8_), channel_id=1, source_target_pairs={{0,1},{1,0},{2,3},{3,2},{4,5},{5,4},{6,7},{7,6},{8,9},{9,8},{10,11... | collective-permute-start | bytes 3538952 | tf_op jit(solution)/shard_map/ppermute | solution.py:519
  108.1 14.7 %collective-permute-start.21 = (bf16[768,768]{1,0:T(8,128)(2,1)S(1)}, bf16[768,768]{1,0:T(8,128)(2,1)}, u32[]{:S(2)}, u32[]{:S(2)}) collective-permute-start(bf16[768,768]{1,0:T(8,128)(2,1)S(1)} %collective-permute-done.16.refs_1_.refs_9_), channel_id=1, source_target_pairs={{0,1},{1,0},{2,3},{3,2},{4,5},{5,4},{6,7},{7,6},{8,9},{9,8},{10,11... | collective-permute-start | bytes 3538952 | tf_op jit(solution)/shard_map/ppermute | solution.py:519
  108.6 14.2 %collective-permute-start.22 = (bf16[768,768]{1,0:T(8,128)(2,1)S(1)}, bf16[768,768]{1,0:T(8,128)(2,1)}, u32[]{:S(2)}, u32[]{:S(2)}) collective-permute-start(bf16[768,768]{1,0:T(8,128)(2,1)S(1)} %collective-permute-done.17.refs_2_.refs_10_), channel_id=1, source_target_pairs={{0,1},{1,0},{2,3},{3,2},{4,5},{5,4},{6,7},{7,6},{8,9},{9,8},{10,11... | collective-permute-start | bytes 3538952 | tf_op jit(solution)/shard_map/ppermute | solution.py:519
  120.7 14.1 %collective-permute-start.24 = (bf16[384,768]{1,0:T(8,128)(2,1)S(1)}, bf16[384,768]{1,0:T(8,128)(2,1)S(1)}, u32[]{:S(2)}, u32[]{:S(2)}) collective-permute-start(bf16[384,768]{1,0:T(8,128)(2,1)S(1)} %collective-permute-done.19.refs_3_), channel_id=1, source_target_pairs={{0,1},{1,0},{2,3},{3,2},{4,5},{5,4},{6,7},{7,6},{8,9},{9,8},{10,11... | collective-permute-start | bytes 1769480 | tf_op jit(solution)/shard_map/ppermute | solution.py:519
  184.0 83.9 %collective-permute-start.41 = (bf16[3072,768]{1,0:T(8,128)(2,1)}, bf16[3072,768]{1,0:T(8,128)(2,1)}, u32[]{:S(2)}, u32[]{:S(2)}) collective-permute-start(bf16[3072,768]{1,0:T(8,128)(2,1)} %feed_weights.3), channel_id=1, source_target_pairs={{0,1},{1,0},{2,3},{3,2},{4,5},{5,4},{6,7},{7,6},{8,9},{9,8},{10,11... | collective-permute-start | bytes 14155784 | tf_op jit(solution)/shard_map/ppermute | solution.py:519
  237.0 26.0 %collective-permute-start.25 = (bf16[1536,768]{1,0:T(8,128)(2,1)}, bf16[1536,768]{1,0:T(8,128)(2,1)}, u32[]{:S(2)}, u32[]{:S(2)}) collective-permute-start(bf16[1536,768]{1,0:T(8,128)(2,1)} %bitcast.79), channel_id=1, source_target_pairs={{0,1},{1,0},{2,3},{3,2},{4,5},{5,4},{6,7},{7,6},{8,9},{9,8},{10,11... | collective-permute-start | bytes 7077896 | tf_op jit(solution)/shard_map/ppermute | solution.py:519
  261.5 15.9 %collective-permute-start.38 = (f32[16,768]{1,0:T(8,128)S(1)}, f32[16,768]{1,0:T(8,128)S(1)}, u32[]{:S(2)}, u32[]{:S(2)}) collective-permute-start(f32[16,768]{1,0:T(8,128)S(1)} %add.130), channel_id=1, source_target_pairs={{0,16},{1,17},{2,18},{3,19},{4,20},{5,21},{6,22},{7,23},{8,24},{9,... | collective-permute-start | bytes 147464 | tf_op jit(solution)/shard_map/ppermute | solution.py:519
  267.0 19.2 %collective-permute-start.26 = (bf16[192,768]{1,0:T(8,128)(2,1)}, bf16[192,768]{1,0:T(8,128)(2,1)}, u32[]{:S(2)}, u32[]{:S(2)}) collective-permute-start(bf16[192,768]{1,0:T(8,128)(2,1)} %get-tuple-element.94), channel_id=1, source_target_pairs={{0,16},{1,17},{2,18},{3,19},{4,20},{5,21},{6,22},{7,23},{8,24},{9,... | collective-permute-start | bytes 884744 | tf_op jit(solution)/shard_map/ppermute | solution.py:519
  267.9 18.3 %collective-permute-start.28 = (bf16[192,768]{1,0:T(8,128)(2,1)}, bf16[192,768]{1,0:T(8,128)(2,1)}, u32[]{:S(2)}, u32[]{:S(2)}) collective-permute-start(bf16[192,768]{1,0:T(8,128)(2,1)} %get-tuple-element.95), channel_id=1, source_target_pairs={{0,8},{1,9},{2,10},{3,11},{4,12},{5,13},{6,14},{7,15},{8,0},{9,1},... | collective-permute-start | bytes 884744 | tf_op jit(solution)/shard_map/ppermute | solution.py:519
  274.3 15.9 %collective-permute-start.42 = (bf16[384,768]{1,0:T(8,128)(2,1)}, bf16[384,768]{1,0:T(8,128)(2,1)}, u32[]{:S(2)}, u32[]{:S(2)}) collective-permute-start(bf16[384,768]{1,0:T(8,128)(2,1)} %get-tuple-element.88), channel_id=1, source_target_pairs={{0,16},{1,17},{2,18},{3,19},{4,20},{5,21},{6,22},{7,23},{8,24},{9,... | collective-permute-start | bytes 1769480 | tf_op jit(solution)/shard_map/ppermute | solution.py:519
  275.4 15.6 %collective-permute-start.44 = (bf16[384,768]{1,0:T(8,128)(2,1)}, bf16[384,768]{1,0:T(8,128)(2,1)}, u32[]{:S(2)}, u32[]{:S(2)}) collective-permute-start(bf16[384,768]{1,0:T(8,128)(2,1)} %get-tuple-element.89), channel_id=1, source_target_pairs={{0,8},{1,9},{2,10},{3,11},{4,12},{5,13},{6,14},{7,15},{8,0},{9,1},... | collective-permute-start | bytes 1769480 | tf_op jit(solution)/shard_map/ppermute | solution.py:519
  285.0 21.5 %collective-permute-start.40 = (f32[16,768]{1,0:T(8,128)}, f32[16,768]{1,0:T(8,128)}, u32[]{:S(2)}, u32[]{:S(2)}) collective-permute-start(f32[16,768]{1,0:T(8,128)} %add.132), channel_id=1, source_target_pairs={{0,4},{1,5},{2,6},{3,7},{4,0},{5,1},{6,2},{7,3},{8,12},{9,13},{10,... | collective-permute-start | bytes 147464 | tf_op jit(solution)/shard_map/ppermute | solution.py:519
  288.3 21.7 %collective-permute-start.29 = (bf16[384,768]{1,0:T(8,128)(2,1)}, bf16[384,768]{1,0:T(8,128)(2,1)}, u32[]{:S(2)}, u32[]{:S(2)}) collective-permute-start(bf16[384,768]{1,0:T(8,128)(2,1)} %pad_maximum_fusion.5), channel_id=1, source_target_pairs={{0,16},{1,17},{2,18},{3,19},{4,20},{5,21},{6,22},{7,23},{8,24},{9,... | collective-permute-start | bytes 1769480 | tf_op jit(solution)/shard_map/ppermute | solution.py:519
  290.2 19.7 %collective-permute-start.27 = (bf16[384,768]{1,0:T(8,128)(2,1)}, bf16[384,768]{1,0:T(8,128)(2,1)}, u32[]{:S(2)}, u32[]{:S(2)}) collective-permute-start(bf16[384,768]{1,0:T(8,128)(2,1)} %pad_maximum_fusion.4), channel_id=1, source_target_pairs={{0,8},{1,9},{2,10},{3,11},{4,12},{5,13},{6,14},{7,15},{8,0},{9,1},... | collective-permute-start | bytes 1769480 | tf_op jit(solution)/shard_map/ppermute | solution.py:519
  293.9 36.2 %collective-permute-start.45 = (bf16[768,768]{1,0:T(8,128)(2,1)}, bf16[768,768]{1,0:T(8,128)(2,1)}, u32[]{:S(2)}, u32[]{:S(2)}) collective-permute-start(bf16[768,768]{1,0:T(8,128)(2,1)} %pad_maximum_fusion.1), channel_id=1, source_target_pairs={{0,16},{1,17},{2,18},{3,19},{4,20},{5,21},{6,22},{7,23},{8,24},{9,... | collective-permute-start | bytes 3538952 | tf_op jit(solution)/shard_map/ppermute | solution.py:519
  295.5 35.7 %collective-permute-start.43 = (bf16[768,768]{1,0:T(8,128)(2,1)}, bf16[768,768]{1,0:T(8,128)(2,1)}, u32[]{:S(2)}, u32[]{:S(2)}) collective-permute-start(bf16[768,768]{1,0:T(8,128)(2,1)} %pad_maximum_fusion), channel_id=1, source_target_pairs={{0,8},{1,9},{2,10},{3,11},{4,12},{5,13},{6,14},{7,15},{8,0},{9,1},... | collective-permute-start | bytes 3538952 | tf_op jit(solution)/shard_map/ppermute | solution.py:519
  335.1 22.3 %collective-permute-start.47 = (bf16[192,768]{1,0:T(8,128)(2,1)S(1)}, bf16[192,768]{1,0:T(8,128)(2,1)S(1)}, u32[]{:S(2)}, u32[]{:S(2)}) collective-permute-start(bf16[192,768]{1,0:T(8,128)(2,1)S(1)} %bitcast.85), channel_id=1, source_target_pairs={{0,4},{1,5},{2,6},{3,7},{4,0},{5,1},{6,2},{7,3},{8,12},{9,13},{10,... | collective-permute-start | bytes 884744 | tf_op jit(solution)/shard_map/ppermute | solution.py:519
  337.2 20.2 %collective-permute-start.46 = (bf16[192,768]{1,0:T(8,128)(2,1)S(1)}, bf16[192,768]{1,0:T(8,128)(2,1)S(1)}, u32[]{:S(2)}, u32[]{:S(2)}) collective-permute-start(bf16[192,768]{1,0:T(8,128)(2,1)S(1)} %bitcast.84), channel_id=1, source_target_pairs={{0,2},{1,3},{2,0},{3,1},{4,6},{5,7},{6,4},{7,5},{8,10},{9,11},{10,... | collective-permute-start | bytes 884744 | tf_op jit(solution)/shard_map/ppermute | solution.py:519
  360.3 13.5 %collective-permute-start.50 = (bf16[192,768]{1,0:T(8,128)(2,1)S(1)}, bf16[192,768]{1,0:T(8,128)(2,1)S(1)}, u32[]{:S(2)}, u32[]{:S(2)}) collective-permute-start(bf16[192,768]{1,0:T(8,128)(2,1)S(1)} %fusion.3), channel_id=1, source_target_pairs={{0,16},{1,17},{2,18},{3,19},{4,20},{5,21},{6,22},{7,23},{8,24},{9,... | collective-permute-start | bytes 884744 | tf_op jit(solution)/shard_map/ppermute | solution.py:519
  (45 other events, 353.2 us)

commit v3 on v2

--- a/solution.py
+++ b/solution.py
@@ -142,7 +142,9 @@
     )(lengths, projected, projected, projected)
 
 
-def attend_back_kernel(length_ref, q_ref, k_ref, v_ref, grad_ref, ctx_ref, log_ref, out_ref, sum_ref):
+def attend_back_kernel(
+    length_ref, _, q_ref, k_ref, v_ref, grad_ref, ctx_ref, log_ref, out_ref, sum_ref
+):
     length = length_ref[pl.program_id(0)]
     queries, keys, values, grad = q_ref[0], k_ref[0], v_ref[0], grad_ref[...]
     keys_t = keys.T
@@ -161,7 +163,7 @@
         query_halves.append(dot_nn(keys_t[head * HEAD_DIM : (head + 1) * HEAD_DIM, :], score_grad))
         value_grad = value_part if head == 0 else value_grad + value_part
         key_grad = key_part if head == 0 else key_grad + key_part
-    query_low = (jnp.concatenate(query_halves, axis=0) * SCALE).astype(F32).T.astype(BF)
+    query_low = (jnp.concatenate(query_halves, axis=0) * SCALE).T.astype(BF)
     value_low = value_grad.astype(BF)
     out_ref[0] = query_low
     out_ref[1] = (key_grad * SCALE).astype(BF)
@@ -170,32 +172,38 @@
     sum_ref[0, 1:2, :] = jnp.sum(value_low.astype(F32), axis=0, keepdims=True)
 
 
-def attend_back(projected, lengths, context_grad, context, logs, positions):
+def attend_back(projected, lengths, side, context_grad, context, logs, positions):
     _, count, width = projected.shape
-    rows, pairs = count // positions, width // PAIR
+    rows, pairs = count // positions, width // PAIR // 2
     block = (1, positions, PAIR)
-    flat = pl.BlockSpec((positions, PAIR), lambda r, p, _: (r, p))
+    flat = pl.BlockSpec((positions, PAIR), lambda r, p, _, s: (r, s[0] * pairs + p))
     flops = 10 * rows * pairs * 2 * positions * positions * HEAD_DIM
     return call(
         attend_back_kernel,
         "attend_back",
         2 * flops,
-        16 * count * width,
+        8 * count * width,
         grid_spec=pltpu.PrefetchScalarGridSpec(
-            num_scalar_prefetch=1,
+            num_scalar_prefetch=2,
             grid=(rows, pairs),
-            in_specs=[pl.BlockSpec(block, lambda r, p, _, j=j: (j, r, p)) for j in range(3)]
-            + [flat, flat, pl.BlockSpec((1, 1, 2, positions), lambda r, p, _: (r, p, 0, 0))],
+            in_specs=[
+                pl.BlockSpec(block, lambda r, p, _, s, j=j: (j, r, s[0] * pairs + p)) for j in range(3)
+            ]
+            + [
+                flat,
+                flat,
+                pl.BlockSpec((1, 1, 2, positions), lambda r, p, _, s: (r, s[0] * pairs + p, 0, 0)),
+            ],
             out_specs=[
-                pl.BlockSpec((3, positions, PAIR), lambda r, p, _: (0, r, p)),
-                pl.BlockSpec((1, 2, PAIR), lambda r, p, _: (r, 0, p)),
+                pl.BlockSpec((3, positions, PAIR), lambda r, p, _, s: (0, r, p)),
+                pl.BlockSpec((1, 2, PAIR), lambda r, p, _, s: (r, 0, p)),
             ],
         ),
         out_shape=[
-            jax.ShapeDtypeStruct((3, count, width), BF),
-            jax.ShapeDtypeStruct((rows, 2, width), F32),
+            jax.ShapeDtypeStruct((3, count, width // 2), BF),
+            jax.ShapeDtypeStruct((rows, 2, width // 2), F32),
         ],
-    )(lengths, projected, projected, projected, context_grad, context, logs)
+    )(lengths, side, projected, projected, projected, context_grad, context, logs)
 
 
 def normalize(residual):
@@ -456,7 +464,7 @@
             num_scalar_prefetch=1,
             grid=(4,),
             in_specs=[
-                pl.BlockSpec((1, count, half), lambda i, t: (jnp.minimum(i, 2), 0, t[0])),
+                pl.BlockSpec((1, count, half), lambda i, t: (jnp.minimum(i, 2), 0, 0)),
                 pl.BlockSpec((count, half), lambda i, t: (0, t[0])),
                 resident((count, width)),
                 resident((count, width)),
@@ -467,30 +475,30 @@
     )(table, qkv_grad, out_grad, tokens, context)
 
 
-def input_kernel(qkv_ref, weight_ref, grad_ref, out_ref):
+def input_kernel(core_ref, near_ref, far_ref, weight_ref, grad_ref, out_ref):
     width = out_ref.shape[1]
+    near_first = core_ref[0] == 0
     total = grad_ref[...]
     for j in range(3):
-        total = total + dot_nn(qkv_ref[j], weight_ref[j * width : (j + 1) * width, :])
+        near, far = near_ref[j], far_ref[j]
+        whole = jnp.concatenate([jnp.where(near_first, near, far), jnp.where(near_first, far, near)], axis=1)
+        total = total + dot_nn(whole, weight_ref[j * width : (j + 1) * width, :])
     out_ref[...] = total.astype(BF)
 
 
-def input_back(qkv_grad, attn_rows, grad):
+def input_back(core, near, far, attn_rows, grad):
     count, width = grad.shape
+    half = pl.BlockSpec((3, TILE, width // 2), lambda t: (0, t, 0))
     return call(
         input_kernel,
         "input_back",
         6 * count * width * width,
         count * width * 12 + width * width * 6,
         grid=(count // TILE,),
-        in_specs=[
-            pl.BlockSpec((3, TILE, width), lambda t: (0, t, 0)),
-            resident((3 * width, width)),
-            tiles(width),
-        ],
+        in_specs=[SMEM, half, half, resident((3 * width, width)), tiles(width)],
         out_specs=tiles(width),
         out_shape=jax.ShapeDtypeStruct((count, width), BF),
-    )(qkv_grad, attn_rows, grad)
+    )(core, near, far, attn_rows, grad)
 
 
 def tie(*values):
@@ -571,22 +579,30 @@
     return rows, whole(attvector).astype(F32), whole(feedvector).astype(F32)
 
 
-def reduce_paired(links, near, far):
-    mine = add(near, links.swap(far, core=1)).astype(BF)
+def reduce_core(links, near, far_got):
+    return add(near, far_got).astype(BF)
+
+
+def reduce_corner(links, mine):
     block = mine.shape[0] // 4
     half = block // 2
-    own = [mine[m * block : (m + 1) * block] for m in range(4)]
-    three_a, three_b = links.swap(own[3][:half], dp=2), links.swap(own[3][half:], dp=1)
-    one = jnp.concatenate([add(own[1][:half], three_a).astype(BF), own[1][half:]], axis=0)
-    two = jnp.concatenate([own[2][:half], add(own[2][half:], three_b).astype(BF)], axis=0)
-    summed = add(own[0], links.swap(one, dp=1), links.swap(two, dp=2)).astype(BF)
-    return summed
+    corner = mine[3 * block :]
+    return links.swap(corner[:half], dp=2), links.swap(corner[half:], dp=1)
+
+
+def reduce_sides(mine, corners):
+    block = mine.shape[0] // 4
+    half = block // 2
+    own, one, two = (mine[m * block : (m + 1) * block] for m in range(3))
+    one = jnp.concatenate([add(one[:half], corners[0]).astype(BF), one[half:]], axis=0)
+    two = jnp.concatenate([two[:half], add(two[half:], corners[1]).astype(BF)], axis=0)
+    return own, one, two
 
 
 def reduce_z(links, summed, size):
     summed = summed.reshape(-1, 4, size, summed.shape[-1])
     pieces = [summed[:, k].reshape(-1, summed.shape[-1]) for k in range(4)]
-    return add(pieces[0], *[links.swap(pieces[k], z=k) for k in range(1, 4)]).astype(BF)
+    return pieces[0], [links.swap(pieces[k], z=k) for k in range(1, 4)]
 
 
 def share_plane(links, final):
@@ -668,47 +684,90 @@
         lengths, vec_rows, gelu, normed_one, cotangent, contracts, positions
     )
     inner_grad, hidden_grad, sum_inner = inner_back(grad_two_low, slope, grad_two, contracts, expands)
-    feed_far_part = feed_weights(inner_grad, gelu, hidden_low, grad_two_low, 1, 4)
-    feed_near_part = feed_weights(inner_grad, gelu, hidden_low, grad_two_low, 0, 4)
+    feed_far = feed_weights(inner_grad, gelu, hidden_low, grad_two_low, 1, 4)
+    inner_grad, feed_far = tie(inner_grad, feed_far)
+    feed_near = feed_weights(inner_grad, gelu, hidden_low, grad_two_low, 0, 4)
+    if links.paired:
+        feed_far = links.swap(feed_far, core=1)
+        feed_mine = reduce_core(links, feed_near, feed_far)
+        hidden_grad, feed_mine = tie(hidden_grad, feed_mine)
+        feed_corners = reduce_corner(links, feed_mine)
+    else:
+        hidden_grad, feed_near, feed_far = tie(hidden_grad, feed_near, feed_far)
     grad_one, grad_one_low, context_grad, sum_one = middle_back(
         vec_rows, hidden_grad, normed_one, inverse_one, attn_rows
     )
-    qkv_grad, sum_qkv = attend_back(projected, lengths, context_grad, context, logs, positions)
-
-    def attn_part(e):
+    if links.paired:
+        context_grad, *feed_corners = tie(context_grad, *feed_corners)
+        feed_own, feed_one, feed_two = reduce_sides(feed_mine, feed_corners)
+        context_grad, feed_one, feed_two = tie(context_grad, feed_one, feed_two)
+        feed_one, feed_two = links.swap(feed_one, dp=1), links.swap(feed_two, dp=2)
+
+    def attn_part(e, context_grad):
         table = jnp.stack([links.my_core ^ e, links.my_dp, links.my_z]).astype(jnp.int32)
-        return attn_weights(table, qkv_grad, grad_one_low, tokens, context)
-
-    attn_far_part, attn_near_part = attn_part(1), attn_part(0)
-    input_grad = input_back(qkv_grad, attn_rows, grad_one)
-
+        qkv_grad, sums = attend_back(
+            projected, lengths, table[:1], context_grad, context, logs, positions
+        )
+        return qkv_grad, attn_weights(table, qkv_grad, grad_one_low, tokens, context), sums
+
+    qkv_far, attn_far, sum_far = attn_part(1, context_grad)
     if links.paired:
-        feed_sum = reduce_paired(links, feed_near_part, feed_far_part)
-        feed_sum = share_plane(links, reduce_z(links, feed_sum, size))
-        expand_sum = feed_sum[:, :size].reshape(quad, width).astype(F32).T
-        contract_sum = feed_sum[:, size:].reshape(quad, width).astype(F32)
-        attn_sum = reduce_paired(
-            links, attn_near_part.reshape(-1, width), attn_far_part.reshape(-1, width)
-        )
-        attn_sum = share_plane(links, reduce_z(links, attn_sum, size)).reshape(quad, width).astype(F32).T
+        context_grad, feed_one, feed_two, attn_far = tie(context_grad, feed_one, feed_two, attn_far)
+        feed_sum = add(feed_own, feed_one, feed_two).astype(BF)
+        context_grad, feed_sum = tie(context_grad, feed_sum)
+        feed_piece, feed_z = reduce_z(links, feed_sum, size)
+        attn_far = links.swap(attn_far.reshape(-1, width), core=1)
     else:
+        context_grad, attn_far = tie(context_grad, attn_far)
+    qkv_near, sum_near = attend_back(
+        projected, lengths, links.my_core.reshape(1).astype(jnp.int32), context_grad, context, logs, positions
+    )
+    table = jnp.stack([links.my_core, links.my_dp, links.my_z]).astype(jnp.int32)
+    if links.paired:
+        qkv_near, *feed_z = tie(qkv_near, *feed_z)
+        feed_final = add(feed_piece, *feed_z).astype(BF)
+        qkv_near, feed_final = tie(qkv_near, feed_final)
+        feed_shared = share_plane(links, feed_final)
+    attn_near = attn_weights(table, qkv_near, grad_one_low, tokens, context)
+    if links.paired:
+        attn_mine = reduce_core(links, attn_near.reshape(-1, width), attn_far)
+        qkv_last, attn_mine = tie(qkv_near, attn_mine)
+        input_grad = input_back(table[:1], qkv_last, qkv_far, attn_rows, grad_one)
+        corners = reduce_corner(links, attn_mine)
+        attn_own, attn_one, attn_two = reduce_sides(attn_mine, corners)
+        attn_one, attn_two = links.swap(attn_one, dp=1), links.swap(attn_two, dp=2)
+        attn_sum = add(attn_own, attn_one, attn_two).astype(BF)
+        attn_sum, input_grad = tie(attn_sum, input_grad)
+        attn_piece, attn_z = reduce_z(links, attn_sum, size)
+        attn_final = add(attn_piece, *attn_z).astype(BF)
+        attn_sum = share_plane(links, attn_final).reshape(quad, width).astype(F32).T
+        expand_sum = feed_shared[:, :size].reshape(quad, width).astype(F32).T
+        contract_sum = feed_shared[:, size:].reshape(quad, width).astype(F32)
+    else:
+        input_grad = input_back(table[:1], qkv_near, qkv_far, attn_rows, grad_one)
+
         def finish(natural):
             shard = lax.psum_scatter(natural, "fsdp", scatter_dimension=0, tiled=True)
             return lax.psum(shard, "dp").astype(F32)
 
-        feed = jnp.concatenate([feed_near_part, feed_far_part], axis=0).reshape(8, 2, quad, width)
+        feed = jnp.concatenate([feed_near, feed_far], axis=0).reshape(8, 2, quad, width)
         expand_sum = finish(feed[:, 0].reshape(hidden, width)).T
         contract_sum = finish(feed[:, 1].reshape(hidden, width))
-        both = jnp.stack([attn_near_part, attn_far_part])
+        both = jnp.stack([attn_near, attn_far])
         attn_sum = finish(both.transpose(2, 0, 1, 3, 4).reshape(4 * width, width)).T
 
+    sums = [jnp.sum(part, axis=0) for part in (sum_near, sum_far)]
+    near_first = links.my_core == 0
+    sum_rows = jnp.concatenate(
+        [jnp.where(near_first, *sums), jnp.where(near_first, sums[1], sums[0])], axis=1
+    )
     inner_sum = links.to_natural(sum_inner[0].reshape(2, 4, 4, size)).reshape(hidden // width, width)
-    sum_rows = jnp.sum(sum_qkv, axis=0)
     count_row = jnp.pad(jnp.sum(lengths).astype(F32).reshape(1, 1), ((0, 0), (0, width - 1)))
     packed = jnp.concatenate(
         [sum_rows, sum_one[:3], inner_sum, sum_two[1:4], sum_middle[:2], sum_two[:1], count_row], axis=0
     )
     if links.paired:
+        packed, attn_mine = tie(packed, attn_mine)
         for step in ({"core": 1}, {"dp": 1}, {"dp": 2}, {"z": 1}, {"z": 2}):
             packed = packed + links.swap(packed, **step)
     else:

time: 379 us -> 365 us (0.963)
  waiting for transfers between devices: 81.7 us -> 67.3 us
  starting transfers between devices: 57.2 us -> 51.8 us
  local copies, waits for them, and re-layouts: 33.7 us -> 38.9 us
  Pallas kernels: 173 us -> 177 us
    ppermute x52, waiting for transfers between devices: 81.7 us -> 67.3 us  [swap(): return lax.ppermute(values, AXES, pairs)]
    ppermute x52, starting transfers between devices: 57.2 us -> 51.8 us  [swap(): return lax.ppermute(values, AXES, pairs)]
    pallas_call x1 -> x2, Pallas kernels: 35.9 us -> 39.4 us  [attend_back(): call(attend_back_kernel, 'attend_back', 2 * flops, 8 * count * width, gri...]
  transfers between devices with their start and end apart: 52 -> 52, of which waited for: 19 -> 15; matrix products, arithmetic and copies ran while one was open for 14% -> 12% of each run, Pallas kernels for 33% -> 35%
where the time goes in v3:
time: 365 us; the launch traced here: 363 us
  Pallas kernels  177 us (48%)
  waiting for transfers between devices  67.3 us (18%)
  starting transfers between devices  51.8 us (14%)
  local copies, waits for them, and re-layouts  38.9 us (11%)
  other arithmetic  25.6 us (7%)
    ppermute x52, waiting for transfers between devices, swap(): return lax.ppermute(values, AXES, pairs)  67.3 us
    ppermute x52, starting transfers between devices, swap(): return lax.ppermute(values, AXES, pairs)  51.8 us
    pallas_call x2, Pallas kernels, attend_back(): call(attend_back_kernel, 'attend_back', 2 * flops, 8 * count * width, gri...  39.4 us
    pallas_call x1, Pallas kernels, inner_back(): call(functools.partial(inner_kernel, count=len(contracts)), 'inner_back',...  23.7 us
    pallas_call x2, Pallas kernels, feed_weights(): call(feed_weights_kernel, 'feed_weights', 4 * count * width * size * bloc...  19.4 us
    pallas_call x1, Pallas kernels, attend(): call(attend_kernel, 'attend', 2 * flops, 8 * count * width, grid_spec=plt...  18.2 us
    pallas_call x2, Pallas kernels, attn_weights(): call(functools.partial(attn_weights_kernel, quarters=4), 'attn_weights',...  15.7 us
    pallas_call x1, Pallas kernels, contract_call(): call(functools.partial(contract_kernel, positions=positions), 'contract_n...  14.8 us
  transfers between devices with their start and end apart: 52, of which 15 were waited for; matrix products, arithmetic and copies ran while one was open for 12% of the time, Pallas kernels for 35%

profile of v3, /device:TPU:0, one launch (start us, length us, event | category | flops | bytes accessed | tf_op | source)
XLA Modules:
  0.0 363.1 jit_solution(8653943114468194058)
XLA Ops:
  3.0 5.1 %collective-permute-start.2 = (bf16[112,768]{1,0:T(8,128)(2,1)S(1)}, bf16[112,768]{1,0:T(8,128)(2,1)S(1)}, u32[]{:S(2)}, u32[]{:S(2)}) collective-permute-start(bf16[112,768]{1,0:T(8,128)(2,1)S(1)} %pad_maximum_fusion.8), channel_id=1, source_target_pairs={{0,6},{1,7},{2,4},{3,5},{4,2},{5,3},{6,0},{7,1},{8,14},{9,15},{10,... | collective-permute-start | bytes 516104 | tf_op jit(solution)/shard_map/ppermute | solution.py:527
  9.8 3.7 %collective-permute-done.2 = bf16[112,768]{1,0:T(8,128)(2,1)S(1)} collective-permute-done((bf16[112,768]{1,0:T(8,128)(2,1)S(1)}, bf16[112,768]{1,0:T(8,128)(2,1)S(1)}, u32[]{:S(2)}, u32[]{:S(2)}) %collective-permute-start.2) | collective-permute-done | bytes 172064 | tf_op jit(solution)/shard_map/ppermute | solution.py:527
  13.5 9.3 %collective-permute-done.1 = bf16[112,768]{1,0:T(8,128)(2,1)S(1)} collective-permute-done((bf16[112,768]{1,0:T(8,128)(2,1)S(1)}, bf16[112,768]{1,0:T(8,128)(2,1)S(1)}, u32[]{:S(2)}, u32[]{:S(2)}) %collective-permute-start.1) | collective-permute-done | bytes 172064 | tf_op jit(solution)/shard_map/ppermute | solution.py:527
  23.0 2.5 collective-permute-start.15
  31.6 13.5 %collective-permute-done.13 = bf16[192,768]{1,0:T(8,128)(2,1)S(1)} collective-permute-done((bf16[192,768]{1,0:T(8,128)(2,1)S(1)}, bf16[192,768]{1,0:T(8,128)(2,1)S(1)}, u32[]{:S(2)}, u32[]{:S(2)}) %collective-permute-start.13) | collective-permute-done | bytes 294944 | tf_op jit(solution)/shard_map/ppermute | solution.py:527
  47.3 3.2 collective-permute-done.14
  55.7 5.6 %collective-permute-done.4.refs_1_ = bf16[384,768]{1,0:T(8,128)(2,1)S(1)} collective-permute-done((bf16[384,768]{1,0:T(8,128)(2,1)S(1)}, bf16[384,768]{1,0:T(8,128)(2,1)S(1)}, u32[]{:S(2)}, u32[]{:S(2)}) %collective-permute-start.4) | collective-permute-done | bytes 589856 | tf_op jit(solution)/shard_map/ppermute | solution.py:527
  74.3 10.0 %project.1 = (bf16[3,1024,768]{2,1,0:T(8,128)(2,1)}, bf16[3072,768]{1,0:T(8,128)(2,1)}) custom-call(s32[32]{0:T(128)} %add.120.table_ref, f32[2,768]{1,0:T(2,128)} %pad_maximum_fusion.11.bias_ref, bf16[1024,768]{1,0:T(8,128)(2,1)} %token_ref.7, bf16[384,768]{1,0:T(8,128)(2,1)} %copy-done.8, bf16[384,768]{1,0:T(8,128)(2,1)} %copy-done.9, ...), custom_call_target="tpu_custom_call" | custom-call | flops 3623878656 | bytes 15728640 | tf_op jit(solution)/shard_map/project/pallas_call | solution.py:73
  84.3 18.2 %attend.1 = (bf16[1024,768]{1,0:T(8,128)(2,1)}, f32[2,6,2,512]{3,2,1,0:T(2,128)}) custom-call(s32[2]{0:T(128)} %length_ref.9, bf16[3,1024,768]{2,1,0:T(8,128)(2,1)} %get-tuple-element.76.q_ref.k_ref.v_ref, bf16[3,1024,768]{2,1,0:T(8,128)(2,1)} %get-tuple-element.76.q_ref.k_ref.v_ref, bf16[3,1024,768]{2,1,0:T(8,128)(2,1)} %get-tuple-element.76.q_ref.k_ref.v_ref), custom_call_target="tpu_custom_call" | custom-call | flops 3221225472 | bytes 6291456 | tf_op jit(solution)/shard_map/attend/pallas_call | solution.py:124
  112.6 6.9 %middle.1 = (f32[1024,768]{1,0:T(8,128)}, f32[1024,128]{1,0:T(8,128)}, bf16[1024,768]{1,0:T(8,128)(2,1)}, f32[8,768]{1,0:T(8,128)}) custom-call(s32[2]{0:T(128)} %length_ref.9, f32[8,768]{1,0:T(8,128)} %stack.100.vec_ref, bf16[1024,768]{1,0:T(8,128)(2,1)} %get-tuple-element.80.ctx_ref, bf16[3072,768]{1,0:T(8,128)(2,1)} %get-tuple-element.81.weight_ref, ...), custom_call_target="tpu_custom_call" | custom-call | flops 1207959552 | bytes 9437184 | tf_op jit(solution)/shard_map/middle/pallas_call | solution.py:254
  122.8 12.0 %expand_gelu.1 = (bf16[1024,3072]{1,0:T(8,128)(2,1)}, bf16[1024,3072]{1,0:T(8,128)(2,1)}) custom-call(f32[1,3072]{1,0:T(1,128)} %reshape_reshape.11.bias_ref, bf16[1024,768]{1,0:T(8,128)(2,1)} %get-tuple-element.85.low_ref, bf16[768,768]{1,0:T(8,128)(2,1)} %slice_dynamic-update-slice_fusion.refs_0_.refs_8_, bf16[768,768]{1,0:T(8,128)(2,1)} %copy-done.5, ...), custom_call_target="tpu_custom_call" | custom-call | flops 4831838208 | bytes 12582912 | tf_op jit(solution)/shard_map/expand_gelu/pallas_call | solution.py:297
  135.6 14.8 %contract_norm.1 = (bf16[1024,768]{1,0:T(8,128)(2,1)}, f32[1024,768]{1,0:T(8,128)}, bf16[1024,768]{1,0:T(8,128)(2,1)}, f32[8,768]{1,0:T(8,128)}) custom-call(s32[2]{0:T(128)} %length_ref.9, f32[8,768]{1,0:T(8,128)} %stack.100.vec_ref, bf16[1024,3072]{1,0:T(8,128)(2,1)} %get-tuple-element.87.gelu_ref, f32[1024,768]{1,0:T(8,128)} %get-tuple-element.88.n_ref, ...), custom_call_target="tpu_custom_call" | custom-call | flops 4831838208 | bytes 17301504 | tf_op jit(solution)/shard_map/contract_norm/pallas_call | solution.py:333
  150.5 23.7 %inner_back.1 = (bf16[1024,3072]{1,0:T(8,128)(2,1)}, f32[1024,768]{1,0:T(8,128)}, f32[8,3072]{1,0:T(8,128)}) custom-call(bf16[1024,768]{1,0:T(8,128)(2,1)} %get-tuple-element.91.low_ref.grad_ref, bf16[1024,3072]{1,0:T(8,128)(2,1)} %get-tuple-element.92.slope_ref, f32[1024,768]{1,0:T(8,128)} %get-tuple-element.93.grad_ref, ...), custom_call_target="tpu_custom_call" | custom-call | flops 9663676416 | bytes 20447232 | tf_op jit(solution)/shard_map/inner_back/pallas_call | solution.py:372
  174.2 9.8 %feed_weights.2 = bf16[3072,768]{1,0:T(8,128)(2,1)} custom-call(bf16[1024,3072]{1,0:T(8,128)(2,1)} %get-tuple-element.96.inner_ref, bf16[1024,3072]{1,0:T(8,128)(2,1)} %get-tuple-element.87.gelu_ref, bf16[1024,768]{1,0:T(8,128)(2,1)} %get-tuple-element.85.low_ref, bf16[1024,768]{1,0:T(8,128)(2,1)} %get-tuple-element.91.low_ref.grad_ref), custom_call_target="tpu_custom_call" | custom-call | flops 4831838208 | bytes 11010048 | tf_op jit(solution)/shard_map/feed_weights/pallas_call | solution.py:399
  184.5 9.6 %feed_weights.3 = bf16[3072,768]{1,0:T(8,128)(2,1)} custom-call(bf16[1024,3072]{1,0:T(8,128)(2,1)} %get-tuple-element.96.inner_ref, bf16[1024,3072]{1,0:T(8,128)(2,1)} %get-tuple-element.87.gelu_ref, bf16[1024,768]{1,0:T(8,128)(2,1)} %get-tuple-element.85.low_ref, bf16[1024,768]{1,0:T(8,128)(2,1)} %get-tuple-element.91.low_ref.grad_ref), custom_call_target="tpu_custom_call" | custom-call | flops 4831838208 | bytes 11010048 | tf_op jit(solution)/shard_map/feed_weights/pallas_call | solution.py:399
  194.1 5.0 %add_convert_fusion = bf16[3072,768]{1,0:T(8,128)(2,1)S(1)} fusion(bf16[3072,768]{1,0:T(8,128)(2,1)} %collective-permute-done.25, bf16[3072,768]{1,0:T(8,128)(2,1)} %feed_weights.3), kind=kLoop, calls=%fused_computation | loop fusion | flops 9437184 | bytes 14155776 | tf_op jit(solution)/shard_map/convert_element_type | solution.py:583
  214.3 8.0 %middle_back.1 = (f32[1024,768]{1,0:T(8,128)}, bf16[1024,768]{1,0:T(8,128)(2,1)}, bf16[1024,768]{1,0:T(8,128)(2,1)}, f32[8,768]{1,0:T(8,128)}) custom-call(f32[8,768]{1,0:T(8,128)} %stack.100.vec_ref, f32[1024,768]{1,0:T(8,128)} %get-tuple-element.98.hid_ref, f32[1024,768]{1,0:T(8,128)} %get-tuple-element.88.n_ref, f32[1024,128]{1,0:T(8,128)} %get-tuple-element.99.s_ref, ...), custom_call_target="tpu_custom_call" | custom-call | flops 1207959552 | bytes 12582912 | tf_op jit(solution)/shard_map/middle_back/pallas_call | solution.py:423
  224.9 19.6 %attend_back.2 = (bf16[3,1024,384]{2,1,0:T(8,128)(2,1)}, f32[2,2,384]{2,1,0:T(2,128)}) custom-call(s32[2]{0:T(128)} %length_ref.9, s32[1]{0:T(128)} %bitcast.9._, bf16[3,1024,768]{2,1,0:T(8,128)(2,1)} %get-tuple-element.76.q_ref.k_ref.v_ref, bf16[3,1024,768]{2,1,0:T(8,128)(2,1)} %get-tuple-element.76.q_ref.k_ref.v_ref, ...), custom_call_target="tpu_custom_call" | custom-call | flops 4026531840 | bytes 6291456 | tf_op jit(solution)/shard_map/attend_back/pallas_call | solution.py:181
  244.6 7.9 %attn_weights.2 = bf16[4,4,96,768]{3,2,1,0:T(8,128)(2,1)} custom-call(s32[3]{0:T(128)} %add_add_fusion.table_ref, bf16[3,1024,384]{2,1,0:T(8,128)(2,1)} %get-tuple-element.109.qkv_ref.far_ref, bf16[1024,768]{1,0:T(8,128)(2,1)} %get-tuple-element.110.low_ref, bf16[1024,768]{1,0:T(8,128)(2,1)} %token_ref.7, bf16[1024,768]{1,0:T(8,128)(2,1)} %get-tuple-element.80.ctx_ref), custom_call_target="tpu_custom_call" | custom-call | flops 2415919104 | bytes 8650752 | tf_op jit(solution)/shard_map/attn_weights/pallas_call | solution.py:458
  252.8 2.4 add_convert_fusion.1
  257.4 2.6 collective-permute-start.31
  260.0 19.8 %attend_back.3 = (bf16[3,1024,384]{2,1,0:T(8,128)(2,1)}, f32[2,2,384]{2,1,0:T(2,128)}) custom-call(s32[2]{0:T(128)} %length_ref.9, s32[1]{0:T(128)} %bitcast.8._.core_ref, bf16[3,1024,768]{2,1,0:T(8,128)(2,1)} %get-tuple-element.76.q_ref.k_ref.v_ref, bf16[3,1024,768]{2,1,0:T(8,128)(2,1)} %get-tuple-element.76.q_ref.k_ref.v_ref, ...), custom_call_target="tpu_custom_call" | custom-call | flops 4026531840 | bytes 6291456 | tf_op jit(solution)/shard_map/attend_back/pallas_call | solution.py:181
  280.5 4.9 %collective-permute-done.31 = bf16[192,768]{1,0:T(8,128)(2,1)S(1)} collective-permute-done((bf16[192,768]{1,0:T(8,128)(2,1)S(1)}, bf16[192,768]{1,0:T(8,128)(2,1)S(1)}, u32[]{:S(2)}, u32[]{:S(2)}) %collective-permute-start.31) | collective-permute-done | bytes 294944 | tf_op jit(solution)/shard_map/ppermute | solution.py:527
  285.7 2.8 collective-permute-start.51
  289.4 7.8 %attn_weights.3 = bf16[4,4,96,768]{3,2,1,0:T(8,128)(2,1)} custom-call(s32[3]{0:T(128)} %add_add_fusion.1.table_ref, bf16[3,1024,384]{2,1,0:T(8,128)(2,1)} %get-tuple-element.124.qkv_ref.near_ref, bf16[1024,768]{1,0:T(8,128)(2,1)} %get-tuple-element.110.low_ref, bf16[1024,768]{1,0:T(8,128)(2,1)} %token_ref.7, bf16[1024,768]{1,0:T(8,128)(2,1)} %get-tuple-element.80.ctx_ref), custom_call_target="tpu_custom_call" | custom-call | flops 2415919104 | bytes 8650752 | tf_op jit(solution)/shard_map/attn_weights/pallas_call | solution.py:458
  297.2 4.9 %collective-permute-done.50 = bf16[192,768]{1,0:T(8,128)(2,1)S(1)} collective-permute-done((bf16[192,768]{1,0:T(8,128)(2,1)S(1)}, bf16[192,768]{1,0:T(8,128)(2,1)S(1)}, u32[]{:S(2)}, u32[]{:S(2)}) %collective-permute-start.50) | collective-permute-done | bytes 294944 | tf_op jit(solution)/shard_map/ppermute | solution.py:527
  303.9 2.3 fusion
  310.1 7.7 %collective-permute-done.45 = f32[16,768]{1,0:T(8,128)S(1)} collective-permute-done((f32[16,768]{1,0:T(8,128)S(1)}, f32[16,768]{1,0:T(8,128)S(1)}, u32[]{:S(2)}, u32[]{:S(2)}) %collective-permute-start.45) | collective-permute-done | bytes 49184 | tf_op jit(solution)/shard_map/ppermute | solution.py:527
  323.9 8.5 %input_back.1 = bf16[1024,768]{1,0:T(8,128)(2,1)} custom-call(s32[1]{0:T(128)} %bitcast.8._.core_ref, bf16[3,1024,384]{2,1,0:T(8,128)(2,1)} %get-tuple-element.124.qkv_ref.near_ref, bf16[3,1024,384]{2,1,0:T(8,128)(2,1)} %get-tuple-element.109.qkv_ref.far_ref, bf16[3072,768]{1,0:T(8,128)(2,1)} %get-tuple-element.81.weight_ref, ...), custom_call_target="tpu_custom_call" | custom-call | flops 3623878656 | bytes 12976128 | tf_op jit(solution)/shard_map/input_back/pallas_call | solution.py:492
  333.8 2.4 collective-permute-start.48
  347.0 5.6 %collective-permute-done.39 = bf16[96,768]{1,0:T(8,128)(2,1)S(1)} collective-permute-done((bf16[96,768]{1,0:T(8,128)(2,1)S(1)}, bf16[96,768]{1,0:T(8,128)(2,1)S(1)}, u32[]{:S(2)}, u32[]{:S(2)}) %collective-permute-start.39) | collective-permute-done | bytes 147488 | tf_op jit(solution)/shard_map/ppermute | solution.py:527
  356.8 3.0 collective-permute-done.43
  (277 shorter events, 97.2 us)
Async XLA Ops:
  8.2 14.6 %collective-permute-start.1 = (bf16[112,768]{1,0:T(8,128)(2,1)S(1)}, bf16[112,768]{1,0:T(8,128)(2,1)S(1)}, u32[]{:S(2)}, u32[]{:S(2)}) collective-permute-start(bf16[112,768]{1,0:T(8,128)(2,1)S(1)} %pad_maximum_fusion.8), channel_id=1, source_target_pairs={{0,4},{1,5},{2,6},{3,7},{4,0},{5,1},{6,2},{7,3},{8,12},{9,13},{10,... | collective-permute-start | bytes 516104 | tf_op jit(solution)/shard_map/ppermute | solution.py:527
  8.2 14.6 %collective-permute-start = (bf16[112,768]{1,0:T(8,128)(2,1)S(1)}, bf16[112,768]{1,0:T(8,128)(2,1)S(1)}, u32[]{:S(2)}, u32[]{:S(2)}) collective-permute-start(bf16[112,768]{1,0:T(8,128)(2,1)S(1)} %pad_maximum_fusion.8), channel_id=1, source_target_pairs={{0,2},{1,3},{2,0},{3,1},{4,6},{5,7},{6,4},{7,5},{8,10},{9,11},{10,... | collective-permute-start | bytes 516104 | tf_op jit(solution)/shard_map/ppermute | solution.py:527
  23.0 28.1 %collective-permute-start.15 = (bf16[192,768]{1,0:T(8,128)(2,1)S(1)}, bf16[192,768]{1,0:T(8,128)(2,1)S(1)}, u32[]{:S(2)}, u32[]{:S(2)}) collective-permute-start(bf16[192,768]{1,0:T(8,128)(2,1)S(1)} %pad_maximum_fusion.7), channel_id=1, source_target_pairs={{0,6},{1,7},{2,4},{3,5},{4,2},{5,3},{6,0},{7,1},{8,14},{9,15},{10,... | collective-permute-start | bytes 884744 | tf_op jit(solution)/shard_map/ppermute | solution.py:527
  25.5 24.9 %collective-permute-start.14 = (bf16[192,768]{1,0:T(8,128)(2,1)S(1)}, bf16[192,768]{1,0:T(8,128)(2,1)S(1)}, u32[]{:S(2)}, u32[]{:S(2)}) collective-permute-start(bf16[192,768]{1,0:T(8,128)(2,1)S(1)} %pad_maximum_fusion.7), channel_id=1, source_target_pairs={{0,4},{1,5},{2,6},{3,7},{4,0},{5,1},{6,2},{7,3},{8,12},{9,13},{10,... | collective-permute-start | bytes 884744 | tf_op jit(solution)/shard_map/ppermute | solution.py:527
  25.5 19.6 %collective-permute-start.13 = (bf16[192,768]{1,0:T(8,128)(2,1)S(1)}, bf16[192,768]{1,0:T(8,128)(2,1)S(1)}, u32[]{:S(2)}, u32[]{:S(2)}) collective-permute-start(bf16[192,768]{1,0:T(8,128)(2,1)S(1)} %pad_maximum_fusion.7), channel_id=1, source_target_pairs={{0,2},{1,3},{2,0},{3,1},{4,6},{5,7},{6,4},{7,5},{8,10},{9,11},{10,... | collective-permute-start | bytes 884744 | tf_op jit(solution)/shard_map/ppermute | solution.py:527
  28.2 41.5 %collective-permute-start.8 = (bf16[384,768]{1,0:T(8,128)(2,1)S(1)}, bf16[384,768]{1,0:T(8,128)(2,1)S(1)}, u32[]{:S(2)}, u32[]{:S(2)}) collective-permute-start(bf16[384,768]{1,0:T(8,128)(2,1)S(1)} %pad_maximum_fusion.3.refs_0_), channel_id=1, source_target_pairs={{0,1},{1,0},{2,3},{3,2},{4,5},{5,4},{6,7},{7,6},{8,9},{9,8},{10,11... | collective-permute-start | bytes 1769480 | tf_op jit(solution)/shard_map/ppermute | solution.py:527
  28.3 24.2 %collective-permute-start.5 = (bf16[384,768]{1,0:T(8,128)(2,1)S(1)}, bf16[384,768]{1,0:T(8,128)(2,1)}, u32[]{:S(2)}, u32[]{:S(2)}) collective-permute-start(bf16[384,768]{1,0:T(8,128)(2,1)S(1)} %pad_maximum_fusion.3.refs_0_), channel_id=1, source_target_pairs={{0,16},{1,17},{2,18},{3,19},{4,20},{5,21},{6,22},{7,23},{8,24},{9,... | collective-permute-start | bytes 1769480 | tf_op jit(solution)/shard_map/ppermute | solution.py:527
  45.1 16.2 %collective-permute-start.4 = (bf16[384,768]{1,0:T(8,128)(2,1)S(1)}, bf16[384,768]{1,0:T(8,128)(2,1)S(1)}, u32[]{:S(2)}, u32[]{:S(2)}) collective-permute-start(bf16[384,768]{1,0:T(8,128)(2,1)S(1)} %pad_maximum_fusion.3.refs_0_), channel_id=1, source_target_pairs={{0,8},{1,9},{2,10},{3,11},{4,12},{5,13},{6,14},{7,15},{8,0},{9,1},... | collective-permute-start | bytes 1769480 | tf_op jit(solution)/shard_map/ppermute | solution.py:527
  53.5 12.8 %collective-permute-start.7 = (bf16[192,768]{1,0:T(8,128)(2,1)S(1)}, bf16[192,768]{1,0:T(8,128)(2,1)S(1)}, u32[]{:S(2)}, u32[]{:S(2)}) collective-permute-start(bf16[192,768]{1,0:T(8,128)(2,1)S(1)} %slice.302), channel_id=1, source_target_pairs={{0,8},{1,9},{2,10},{3,11},{4,12},{5,13},{6,14},{7,15},{8,0},{9,1},... | collective-permute-start | bytes 884744 | tf_op jit(solution)/shard_map/ppermute | solution.py:527
  68.2 34.3 %collective-permute-start.17 = (bf16[768,768]{1,0:T(8,128)(2,1)}, bf16[768,768]{1,0:T(8,128)(2,1)S(1)}, u32[]{:S(2)}, u32[]{:S(2)}) collective-permute-start(bf16[768,768]{1,0:T(8,128)(2,1)} %slice_dynamic-update-slice_fusion.refs_0_.refs_8_), channel_id=1, source_target_pairs={{0,16},{1,17},{2,18},{3,19},{4,20},{5,21},{6,22},{7,23},{8,24},{9,... | collective-permute-start | bytes 3538952 | tf_op jit(solution)/shard_map/ppermute | solution.py:527
  70.5 32.0 %collective-permute-start.16 = (bf16[768,768]{1,0:T(8,128)(2,1)}, bf16[768,768]{1,0:T(8,128)(2,1)S(1)}, u32[]{:S(2)}, u32[]{:S(2)}) collective-permute-start(bf16[768,768]{1,0:T(8,128)(2,1)} %slice_dynamic-update-slice_fusion.refs_0_.refs_8_), channel_id=1, source_target_pairs={{0,8},{1,9},{2,10},{3,11},{4,12},{5,13},{6,14},{7,15},{8,0},{9,1},... | collective-permute-start | bytes 3538952 | tf_op jit(solution)/shard_map/ppermute | solution.py:527
  103.4 16.1 %collective-permute-start.19 = (bf16[384,768]{1,0:T(8,128)(2,1)}, bf16[384,768]{1,0:T(8,128)(2,1)S(1)}, u32[]{:S(2)}, u32[]{:S(2)}) collective-permute-start(bf16[384,768]{1,0:T(8,128)(2,1)} %slice.254), channel_id=1, source_target_pairs={{0,8},{1,9},{2,10},{3,11},{4,12},{5,13},{6,14},{7,15},{8,0},{9,1},... | collective-permute-start | bytes 1769480 | tf_op jit(solution)/shard_map/ppermute | solution.py:527
  104.0 15.5 %collective-permute-start.18 = (bf16[384,768]{1,0:T(8,128)(2,1)S(1)}, bf16[384,768]{1,0:T(8,128)(2,1)}, u32[]{:S(2)}, u32[]{:S(2)}) collective-permute-start(bf16[384,768]{1,0:T(8,128)(2,1)S(1)} %slice.253), channel_id=1, source_target_pairs={{0,16},{1,17},{2,18},{3,19},{4,20},{5,21},{6,22},{7,23},{8,24},{9,... | collective-permute-start | bytes 1769480 | tf_op jit(solution)/shard_map/ppermute | solution.py:527
  108.1 14.7 %collective-permute-start.20 = (bf16[768,768]{1,0:T(8,128)(2,1)}, bf16[768,768]{1,0:T(8,128)(2,1)}, u32[]{:S(2)}, u32[]{:S(2)}) collective-permute-start(bf16[768,768]{1,0:T(8,128)(2,1)} %slice_dynamic-update-slice_fusion.refs_0_.refs_8_), channel_id=1, source_target_pairs={{0,1},{1,0},{2,3},{3,2},{4,5},{5,4},{6,7},{7,6},{8,9},{9,8},{10,11... | collective-permute-start | bytes 3538952 | tf_op jit(solution)/shard_map/ppermute | solution.py:527
  108.1 14.7 %collective-permute-start.21 = (bf16[768,768]{1,0:T(8,128)(2,1)S(1)}, bf16[768,768]{1,0:T(8,128)(2,1)}, u32[]{:S(2)}, u32[]{:S(2)}) collective-permute-start(bf16[768,768]{1,0:T(8,128)(2,1)S(1)} %collective-permute-done.16.refs_1_.refs_9_), channel_id=1, source_target_pairs={{0,1},{1,0},{2,3},{3,2},{4,5},{5,4},{6,7},{7,6},{8,9},{9,8},{10,11... | collective-permute-start | bytes 3538952 | tf_op jit(solution)/shard_map/ppermute | solution.py:527
  108.6 14.2 %collective-permute-start.22 = (bf16[768,768]{1,0:T(8,128)(2,1)S(1)}, bf16[768,768]{1,0:T(8,128)(2,1)}, u32[]{:S(2)}, u32[]{:S(2)}) collective-permute-start(bf16[768,768]{1,0:T(8,128)(2,1)S(1)} %collective-permute-done.17.refs_2_.refs_10_), channel_id=1, source_target_pairs={{0,1},{1,0},{2,3},{3,2},{4,5},{5,4},{6,7},{7,6},{8,9},{9,8},{10,11... | collective-permute-start | bytes 3538952 | tf_op jit(solution)/shard_map/ppermute | solution.py:527
  120.7 14.1 %collective-permute-start.24 = (bf16[384,768]{1,0:T(8,128)(2,1)S(1)}, bf16[384,768]{1,0:T(8,128)(2,1)S(1)}, u32[]{:S(2)}, u32[]{:S(2)}) collective-permute-start(bf16[384,768]{1,0:T(8,128)(2,1)S(1)} %collective-permute-done.19.refs_3_), channel_id=1, source_target_pairs={{0,1},{1,0},{2,3},{3,2},{4,5},{5,4},{6,7},{7,6},{8,9},{9,8},{10,11... | collective-permute-start | bytes 1769480 | tf_op jit(solution)/shard_map/ppermute | solution.py:527
  201.2 21.1 %collective-permute-start.27 = (bf16[384,768]{1,0:T(8,128)(2,1)S(1)}, bf16[384,768]{1,0:T(8,128)(2,1)S(1)}, u32[]{:S(2)}, u32[]{:S(2)}) collective-permute-start(bf16[384,768]{1,0:T(8,128)(2,1)S(1)} %get-tuple-element.146), channel_id=1, source_target_pairs={{0,8},{1,9},{2,10},{3,11},{4,12},{5,13},{6,14},{7,15},{8,0},{9,1},... | collective-permute-start | bytes 1769480 | tf_op jit(solution)/shard_map/ppermute | solution.py:527
  203.4 18.9 %collective-permute-start.26 = (bf16[384,768]{1,0:T(8,128)(2,1)S(1)}, bf16[384,768]{1,0:T(8,128)(2,1)S(1)}, u32[]{:S(2)}, u32[]{:S(2)}) collective-permute-start(bf16[384,768]{1,0:T(8,128)(2,1)S(1)} %get-tuple-element.147), channel_id=1, source_target_pairs={{0,16},{1,17},{2,18},{3,19},{4,20},{5,21},{6,22},{7,23},{8,24},{9,... | collective-permute-start | bytes 1769480 | tf_op jit(solution)/shard_map/ppermute | solution.py:527
  224.0 28.5 %collective-permute-start.28 = (bf16[768,768]{1,0:T(8,128)(2,1)S(1)}, bf16[768,768]{1,0:T(8,128)(2,1)}, u32[]{:S(2)}, u32[]{:S(2)}) collective-permute-start(bf16[768,768]{1,0:T(8,128)(2,1)S(1)} %pad_maximum_fusion), channel_id=1, source_target_pairs={{0,8},{1,9},{2,10},{3,11},{4,12},{5,13},{6,14},{7,15},{8,0},{9,1},... | collective-permute-start | bytes 3538952 | tf_op jit(solution)/shard_map/ppermute | solution.py:527
  224.1 28.4 %collective-permute-start.29 = (bf16[768,768]{1,0:T(8,128)(2,1)S(1)}, bf16[768,768]{1,0:T(8,128)(2,1)}, u32[]{:S(2)}, u32[]{:S(2)}) collective-permute-start(bf16[768,768]{1,0:T(8,128)(2,1)S(1)} %pad_maximum_fusion.1), channel_id=1, source_target_pairs={{0,16},{1,17},{2,18},{3,19},{4,20},{5,21},{6,22},{7,23},{8,24},{9,... | collective-permute-start | bytes 3538952 | tf_op jit(solution)/shard_map/ppermute | solution.py:527
  252.5 49.9 %collective-permute-start.33 = (bf16[1536,768]{1,0:T(8,128)(2,1)}, bf16[1536,768]{1,0:T(8,128)(2,1)}, u32[]{:S(2)}, u32[]{:S(2)}) collective-permute-start(bf16[1536,768]{1,0:T(8,128)(2,1)} %bitcast.77), channel_id=1, source_target_pairs={{0,1},{1,0},{2,3},{3,2},{4,5},{5,4},{6,7},{7,6},{8,9},{9,8},{10,11... | collective-permute-start | bytes 7077896 | tf_op jit(solution)/shard_map/ppermute | solution.py:527
  255.3 25.3 %collective-permute-start.32 = (bf16[192,768]{1,0:T(8,128)(2,1)S(1)}, bf16[192,768]{1,0:T(8,128)(2,1)S(1)}, u32[]{:S(2)}, u32[]{:S(2)}) collective-permute-start(bf16[192,768]{1,0:T(8,128)(2,1)S(1)} %bitcast.85), channel_id=1, source_target_pairs={{0,6},{1,7},{2,4},{3,5},{4,2},{5,3},{6,0},{7,1},{8,14},{9,15},{10,... | collective-permute-start | bytes 884744 | tf_op jit(solution)/shard_map/ppermute | solution.py:527
  257.4 28.1 %collective-permute-start.31 = (bf16[192,768]{1,0:T(8,128)(2,1)S(1)}, bf16[192,768]{1,0:T(8,128)(2,1)S(1)}, u32[]{:S(2)}, u32[]{:S(2)}) collective-permute-start(bf16[192,768]{1,0:T(8,128)(2,1)S(1)} %bitcast.83), channel_id=1, source_target_pairs={{0,4},{1,5},{2,6},{3,7},{4,0},{5,1},{6,2},{7,3},{8,12},{9,13},{10,... | collective-permute-start | bytes 884744 | tf_op jit(solution)/shard_map/ppermute | solution.py:527
  260.0 25.5 %collective-permute-start.30 = (bf16[192,768]{1,0:T(8,128)(2,1)S(1)}, bf16[192,768]{1,0:T(8,128)(2,1)S(1)}, u32[]{:S(2)}, u32[]{:S(2)}) collective-permute-start(bf16[192,768]{1,0:T(8,128)(2,1)S(1)} %bitcast.82), channel_id=1, source_target_pairs={{0,2},{1,3},{2,0},{3,1},{4,6},{5,7},{6,4},{7,5},{8,10},{9,11},{10,... | collective-permute-start | bytes 884744 | tf_op jit(solution)/shard_map/ppermute | solution.py:527
  285.7 11.5 %collective-permute-start.51 = (bf16[192,768]{1,0:T(8,128)(2,1)S(1)}, bf16[192,768]{1,0:T(8,128)(2,1)S(1)}, u32[]{:S(2)}, u32[]{:S(2)}) collective-permute-start(bf16[192,768]{1,0:T(8,128)(2,1)S(1)} %fusion.3), channel_id=1, source_target_pairs={{0,24},{1,25},{2,26},{3,27},{4,28},{5,29},{6,30},{7,31},{8,16},{9,... | collective-permute-start | bytes 884744 | tf_op jit(solution)/shard_map/ppermute | solution.py:527
  288.5 13.6 %collective-permute-start.50 = (bf16[192,768]{1,0:T(8,128)(2,1)S(1)}, bf16[192,768]{1,0:T(8,128)(2,1)S(1)}, u32[]{:S(2)}, u32[]{:S(2)}) collective-permute-start(bf16[192,768]{1,0:T(8,128)(2,1)S(1)} %fusion.3), channel_id=1, source_target_pairs={{0,16},{1,17},{2,18},{3,19},{4,20},{5,21},{6,22},{7,23},{8,24},{9,... | collective-permute-start | bytes 884744 | tf_op jit(solution)/shard_map/ppermute | solution.py:527
  289.1 12.9 %collective-permute-start.49 = (bf16[192,768]{1,0:T(8,128)(2,1)S(1)}, bf16[192,768]{1,0:T(8,128)(2,1)S(1)}, u32[]{:S(2)}, u32[]{:S(2)}) collective-permute-start(bf16[192,768]{1,0:T(8,128)(2,1)S(1)} %fusion.3), channel_id=1, source_target_pairs={{0,8},{1,9},{2,10},{3,11},{4,12},{5,13},{6,14},{7,15},{8,0},{9,1},... | collective-permute-start | bytes 884744 | tf_op jit(solution)/shard_map/ppermute | solution.py:527
  306.3 12.3 %collective-permute-start.34 = (bf16[192,768]{1,0:T(8,128)(2,1)S(1)}, bf16[192,768]{1,0:T(8,128)(2,1)S(1)}, u32[]{:S(2)}, u32[]{:S(2)}) collective-permute-start(bf16[192,768]{1,0:T(8,128)(2,1)S(1)} %get-tuple-element.152), channel_id=1, source_target_pairs={{0,16},{1,17},{2,18},{3,19},{4,20},{5,21},{6,22},{7,23},{8,24},{9,... | collective-permute-start | bytes 884744 | tf_op jit(solution)/shard_map/ppermute | solution.py:527
  318.8 17.4 %collective-permute-start.37 = (bf16[384,768]{1,0:T(8,128)(2,1)S(1)}, bf16[384,768]{1,0:T(8,128)(2,1)}, u32[]{:S(2)}, u32[]{:S(2)}) collective-permute-start(bf16[384,768]{1,0:T(8,128)(2,1)S(1)} %pad_maximum_fusion.5), channel_id=1, source_target_pairs={{0,16},{1,17},{2,18},{3,19},{4,20},{5,21},{6,22},{7,23},{8,24},{9,... | collective-permute-start | bytes 1769480 | tf_op jit(solution)/shard_map/ppermute | solution.py:527
  321.0 15.2 %collective-permute-start.35 = (bf16[384,768]{1,0:T(8,128)(2,1)}, bf16[384,768]{1,0:T(8,128)(2,1)}, u32[]{:S(2)}, u32[]{:S(2)}) collective-permute-start(bf16[384,768]{1,0:T(8,128)(2,1)} %pad_maximum_fusion.4), channel_id=1, source_target_pairs={{0,8},{1,9},{2,10},{3,11},{4,12},{5,13},{6,14},{7,15},{8,0},{9,1},... | collective-permute-start | bytes 1769480 | tf_op jit(solution)/shard_map/ppermute | solution.py:527
  339.9 12.7 %collective-permute-start.39 = (bf16[96,768]{1,0:T(8,128)(2,1)S(1)}, bf16[96,768]{1,0:T(8,128)(2,1)S(1)}, u32[]{:S(2)}, u32[]{:S(2)}) collective-permute-start(bf16[96,768]{1,0:T(8,128)(2,1)S(1)} %get-tuple-element.164), channel_id=1, source_target_pairs={{0,4},{1,5},{2,6},{3,7},{4,0},{5,1},{6,2},{7,3},{8,12},{9,13},{10,... | collective-permute-start | bytes 442376 | tf_op jit(solution)/shard_map/ppermute | solution.py:527
  (45 other events, 326.7 us)

commit v4 on v3

--- a/solution.py
+++ b/solution.py
@@ -95,31 +95,38 @@
 
 
 def scores_of(keys, queries, length, head):
-    scores = dot_nt(keys, head_lanes(queries, head))
-    place = lax.broadcasted_iota(jnp.int32, scores.shape, 0)
-    return jnp.where(place < length, scores, NEGATIVE / SCALE)
+    live = lax.broadcasted_iota(jnp.int32, (keys.shape[0], 1), 0) < length
+    factor = jnp.where(live, SCALE * LOG2E, 0.0)
+    shift = jnp.where(live, 0.0, NEGATIVE * LOG2E)
+    return dot_nt(keys, head_lanes(queries, head)) * factor + shift
+
+
+def pairs_per_step(pairs):
+    return 3 if pairs % 3 == 0 else 1
 
 
 def attend_kernel(length_ref, q_ref, k_ref, v_ref, out_ref, log_ref):
     length = length_ref[pl.program_id(0)]
-    keys = k_ref[0]
-    values_t = v_ref[0].T
-    halves = []
-    for head in range(2):
-        scores = scores_of(keys, q_ref[0], length, head)
-        peak = jnp.max(scores, axis=0, keepdims=True) * (SCALE * LOG2E)
-        weights = jnp.exp2(scores * (SCALE * LOG2E) - peak)
-        total = jnp.sum(weights, axis=0, keepdims=True)
-        part = dot_nn(values_t[head * HEAD_DIM : (head + 1) * HEAD_DIM, :], weights.astype(BF))
-        halves.append(part * (1.0 / total))
-        log_ref[0, 0, head : head + 1, :] = peak + jnp.log2(total)
-    out_ref[...] = jnp.concatenate(halves, axis=0).T.astype(BF)
+    for i in range(log_ref.shape[1]):
+        span = slice(i * PAIR, (i + 1) * PAIR)
+        keys, values_t = k_ref[0, :, span], v_ref[0, :, span].T
+        halves = []
+        for head in range(2):
+            scores = scores_of(keys, q_ref[0, :, span], length, head)
+            peak = jnp.max(scores, axis=0, keepdims=True)
+            weights = jnp.exp2(scores - peak)
+            total = jnp.sum(weights, axis=0, keepdims=True)
+            part = dot_nn(values_t[head * HEAD_DIM : (head + 1) * HEAD_DIM, :], weights.astype(BF))
+            halves.append(part * (1.0 / total))
+            log_ref[0, i, head : head + 1, :] = peak + jnp.log2(total)
+        out_ref[:, span] = jnp.concatenate(halves, axis=0).T.astype(BF)
 
 
 def attend(projected, lengths, positions):
     _, count, width = projected.shape
     rows, pairs = count // positions, width // PAIR
-    block = (1, positions, PAIR)
+    group = pairs_per_step(pairs)
+    block = (1, positions, group * PAIR)
     flops = 4 * rows * pairs * 2 * positions * positions * HEAD_DIM
     return call(
         attend_kernel,
@@ -128,11 +135,11 @@
         8 * count * width,
         grid_spec=pltpu.PrefetchScalarGridSpec(
             num_scalar_prefetch=1,
-            grid=(rows, pairs),
+            grid=(rows, pairs // group),
             in_specs=[pl.BlockSpec(block, lambda r, p, _, j=j: (j, r, p)) for j in range(3)],
             out_specs=[
-                pl.BlockSpec((positions, PAIR), lambda r, p, _: (r, p)),
-                pl.BlockSpec((1, 1, 2, positions), lambda r, p, _: (r, p, 0, 0)),
+                pl.BlockSpec((positions, group * PAIR), lambda r, p, _: (r, p)),
+                pl.BlockSpec((1, group, 2, positions), lambda r, p, _: (r, p, 0, 0)),
             ],
         ),
         out_shape=[
@@ -146,37 +153,42 @@
     length_ref, _, q_ref, k_ref, v_ref, grad_ref, ctx_ref, log_ref, out_ref, sum_ref
 ):
     length = length_ref[pl.program_id(0)]
-    queries, keys, values, grad = q_ref[0], k_ref[0], v_ref[0], grad_ref[...]
-    keys_t = keys.T
-    product = grad.astype(F32) * ctx_ref[...].astype(F32)
-    key_grad, value_grad, query_halves = None, None, []
-    for head in range(2):
-        scores = scores_of(keys, queries, length, head)
-        wide = jnp.exp2(scores * (SCALE * LOG2E) - log_ref[0, 0, head : head + 1, :])
-        grad_head = head_lanes(grad, head)
-        value_part = dot_nn(wide.astype(BF), grad_head)
-        weight_grad = dot_nt(values, grad_head)
-        ones = head_lanes(jnp.ones((8, PAIR), F32), head)
-        row_total = dot_nt(ones, product, lax.Precision.HIGHEST)[0:1, :]
-        score_grad = (wide * (weight_grad - row_total)).astype(BF)
-        key_part = dot_nn(score_grad, head_lanes(queries, head))
-        query_halves.append(dot_nn(keys_t[head * HEAD_DIM : (head + 1) * HEAD_DIM, :], score_grad))
-        value_grad = value_part if head == 0 else value_grad + value_part
-        key_grad = key_part if head == 0 else key_grad + key_part
-    query_low = (jnp.concatenate(query_halves, axis=0) * SCALE).T.astype(BF)
-    value_low = value_grad.astype(BF)
-    out_ref[0] = query_low
-    out_ref[1] = (key_grad * SCALE).astype(BF)
-    out_ref[2] = value_low
-    sum_ref[0, 0:1, :] = jnp.sum(query_low.astype(F32), axis=0, keepdims=True)
-    sum_ref[0, 1:2, :] = jnp.sum(value_low.astype(F32), axis=0, keepdims=True)
+    row = lax.broadcasted_iota(jnp.int32, (8, PAIR), 0)
+    lane = lax.broadcasted_iota(jnp.int32, (8, PAIR), 1)
+    chosen = jnp.where((lane >= HEAD_DIM) == (row == 1), 1.0, 0.0).astype(BF)
+    for i in range(log_ref.shape[1]):
+        span = slice(i * PAIR, (i + 1) * PAIR)
+        queries, keys, values, grad = q_ref[0, :, span], k_ref[0, :, span], v_ref[0, :, span], grad_ref[:, span]
+        product = grad.astype(F32) * ctx_ref[:, span].astype(F32)
+        high = product.astype(BF)
+        low = (product - high.astype(F32)).astype(BF)
+        row_totals = dot_nt(chosen, high) + dot_nt(chosen, low)
+        query_grad, key_grad, value_grad = 0.0, 0.0, 0.0
+        for head in range(2):
+            scores = scores_of(keys, queries, length, head)
+            wide = jnp.exp2(scores - log_ref[0, i, head : head + 1, :])
+            grad_head = head_lanes(grad, head)
+            value_grad += dot_nn(wide.astype(BF), grad_head)
+            weight_grad = dot_nt(values, grad_head)
+            score_grad = (wide * (weight_grad - row_totals[head : head + 1, :])).astype(BF)
+            key_grad += dot_nn(score_grad, head_lanes(queries, head))
+            query_grad += dot_tn(score_grad, head_lanes(keys, head))
+        query_low = (query_grad * SCALE).astype(BF)
+        value_low = value_grad.astype(BF)
+        out_ref[0, :, span] = query_low
+        out_ref[1, :, span] = (key_grad * SCALE).astype(BF)
+        out_ref[2, :, span] = value_low
+        sum_ref[0, 0:1, span] = jnp.sum(query_low.astype(F32), axis=0, keepdims=True)
+        sum_ref[0, 1:2, span] = jnp.sum(value_low.astype(F32), axis=0, keepdims=True)
 
 
 def attend_back(projected, lengths, side, context_grad, context, logs, positions):
     _, count, width = projected.shape
     rows, pairs = count // positions, width // PAIR // 2
-    block = (1, positions, PAIR)
-    flat = pl.BlockSpec((positions, PAIR), lambda r, p, _, s: (r, s[0] * pairs + p))
+    group = pairs_per_step(pairs)
+    steps = pairs // group
+    block = (1, positions, group * PAIR)
+    flat = pl.BlockSpec((positions, group * PAIR), lambda r, p, _, s: (r, s[0] * steps + p))
     flops = 10 * rows * pairs * 2 * positions * positions * HEAD_DIM
     return call(
         attend_back_kernel,
@@ -185,18 +197,18 @@
         8 * count * width,
         grid_spec=pltpu.PrefetchScalarGridSpec(
             num_scalar_prefetch=2,
-            grid=(rows, pairs),
+            grid=(rows, steps),
             in_specs=[
-                pl.BlockSpec(block, lambda r, p, _, s, j=j: (j, r, s[0] * pairs + p)) for j in range(3)
+                pl.BlockSpec(block, lambda r, p, _, s, j=j: (j, r, s[0] * steps + p)) for j in range(3)
             ]
             + [
                 flat,
                 flat,
-                pl.BlockSpec((1, 1, 2, positions), lambda r, p, _, s: (r, s[0] * pairs + p, 0, 0)),
+                pl.BlockSpec((1, group, 2, positions), lambda r, p, _, s: (r, s[0] * steps + p, 0, 0)),
             ],
             out_specs=[
-                pl.BlockSpec((3, positions, PAIR), lambda r, p, _, s: (0, r, p)),
-                pl.BlockSpec((1, 2, PAIR), lambda r, p, _, s: (r, 0, p)),
+                pl.BlockSpec((3, positions, group * PAIR), lambda r, p, _, s: (0, r, p)),
+                pl.BlockSpec((1, 2, group * PAIR), lambda r, p, _, s: (r, 0, p)),
             ],
         ),
         out_shape=[
@@ -274,12 +286,17 @@
     return inner * cumulative, cumulative + inner * density
 
 
+def two_by_two(pieces):
+    for first, second in zip(pieces[::2], pieces[1::2]):
+        yield jnp.concatenate([first[...], second[...]], axis=0)
+
+
 def expand_kernel(bias_ref, low_ref, *refs):
     pieces, (gelu_ref, slope_ref) = refs[:-2], refs[-2:]
     low, at = low_ref[...], 0
-    for piece in pieces:
+    for piece in two_by_two(pieces):
         size = piece.shape[0]
-        inner = dot_nt(low, piece[...]) + bias_ref[0:1, at : at + size]
+        inner = dot_nt(low, piece) + bias_ref[0:1, at : at + size]
         gelu, slope = gelu_parts(inner)
         gelu_ref[:, at : at + size] = gelu.astype(BF)
         slope_ref[:, at : at + size] = slope.astype(BF)
@@ -309,9 +326,9 @@
 def contract_kernel(length_ref, vec_ref, gelu_ref, n_ref, cot_ref, *refs, positions):
     pieces, (out_ref, grad_ref, low_ref, sum_ref) = refs[:-4], refs[-4:]
     branch, at = vec_ref[3:4, :], 0
-    for piece in pieces:
+    for piece in two_by_two(pieces):
         size = piece.shape[0]
-        branch = branch + dot_nn(gelu_ref[:, at : at + size], piece[...])
+        branch = branch + dot_nn(gelu_ref[:, at : at + size], piece)
         at += size
     first = n_ref[...] * vec_ref[1:2, :] + vec_ref[2:3, :]
     normed, inverse = normalize(first + branch)
@@ -356,12 +373,12 @@
         sum_ref[...] = jnp.zeros_like(sum_ref)
 
     low, total, at = low_ref[...], grad_ref[...], 0
-    for contract, expand in zip(contracts, expands):
+    for contract, expand in zip(two_by_two(contracts), two_by_two(expands)):
         span = slice(at, at + contract.shape[0])
-        inner = (dot_nt(low, contract[...]) * slope_ref[:, span].astype(F32)).astype(BF)
+        inner = (dot_nt(low, contract) * slope_ref[:, span].astype(F32)).astype(BF)
         inner_ref[:, span] = inner
         sum_ref[0:1, span] += jnp.sum(inner.astype(F32), axis=0, keepdims=True)
-        total = total + dot_nn(inner, expand[...])
+        total = total + dot_nn(inner, expand)
         at += contract.shape[0]
     out_ref[...] = total
 
@@ -386,26 +403,24 @@
     )(low, slope, grad, *[piece[0] for piece in contracts + expands])
 
 
-def feed_weights_kernel(inner_ref, gelu_ref, low_ref, grad_ref, out_ref):
-    size = inner_ref.shape[1]
-    out_ref[0:size, :] = dot_tn(inner_ref[...], low_ref[...]).astype(BF)
-    out_ref[size:, :] = dot_tn(gelu_ref[...], grad_ref[...]).astype(BF)
-
-
-def feed_weights(inner, gelu, low, grad, half, blocks):
-    count, width = low.shape
-    size = inner.shape[1] // (2 * blocks)
-    columns = pl.BlockSpec((count, size), lambda i: (0, half * blocks + i))
+def feed_weights_kernel(left_ref, right_ref, out_ref):
+    out_ref[...] = dot_tn(left_ref[...], right_ref[...]).astype(BF)
+
+
+def feed_weights(left, right, half):
+    count, width = right.shape
+    rows = left.shape[1] // 2
+    size = rows // 2
     return call(
         feed_weights_kernel,
         "feed_weights",
-        4 * count * width * size * blocks,
-        count * size * blocks * 4 + blocks * size * width * 4,
-        grid=(blocks,),
-        in_specs=[columns, columns, resident((count, width)), resident((count, width))],
-        out_specs=pl.BlockSpec((2 * size, width), lambda i: (i, 0)),
-        out_shape=jax.ShapeDtypeStruct((blocks * 2 * size, width), BF),
-    )(inner, gelu, low, grad)
+        2 * count * width * rows,
+        count * rows * 2 + rows * width * 2,
+        grid=(2,),
+        in_specs=[pl.BlockSpec((count, size), lambda i: (0, half * 2 + i)), resident((count, width))],
+        out_specs=pl.BlockSpec((size, width), lambda i: (i, 0)),
+        out_shape=jax.ShapeDtypeStruct((rows, width), BF),
+    )(left, right)
 
 
 def middle_back_kernel(vec_ref, hid_ref, n_ref, s_ref, weight_ref, grad_ref, low_ref, ctx_ref, sum_ref):
@@ -501,6 +516,50 @@
     )(core, near, far, attn_rows, grad)
 
 
+def pack_kernel(place_ref, length_ref, near_ref, far_ref, one_ref, inner_ref, two_ref, middle_ref, out_ref):
+    half = near_ref.shape[2]
+    near_first = place_ref[32] == 0
+    near, far = (jnp.sum(ref[...], axis=0) for ref in (near_ref, far_ref))
+    first, second = jnp.where(near_first, near, far), jnp.where(near_first, far, near)
+    both = jnp.concatenate([first, second], axis=1)
+    rows = [both[0:1, :], both[1:2, :]] + [one_ref[i : i + 1, :] for i in range(3)]
+    rows += [two_ref[i : i + 1, :] for i in (1, 2, 3)]
+    at = 0
+    for row in rows:
+        for lane in range(0, 2 * half, 128):
+            out_ref[at : at + 1, :] = row[:, lane : lane + 128]
+            at += 1
+    size = inner_ref.shape[1] // 32
+    gap = jnp.zeros((1, 128 - size), F32)
+    for i in range(32):
+        part = jnp.concatenate([inner_ref[0:1, i * size : (i + 1) * size], gap], axis=1)
+        out_ref[pl.ds(at + place_ref[i], 1), :] = part
+    at += 32
+    for row in (middle_ref[0:1, :], middle_ref[1:2, :], two_ref[0:1, :]):
+        out_ref[at : at + 1, :] = sum(row[:, lane : lane + 128] for lane in range(0, 2 * half, 128))
+        at += 1
+    live = length_ref[0]
+    for i in range(1, length_ref.shape[0]):
+        live = live + length_ref[i]
+    out_ref[at : at + 1, :] = jnp.full((1, 128), live).astype(F32)
+    out_ref[at + 1 :, :] = jnp.zeros((out_ref.shape[0] - at - 1, 128), F32)
+
+
+def pack(places, lengths, parts):
+    width = parts[2].shape[1]
+    rows = 8 * width // 128 + 32 + 8
+    return call(
+        pack_kernel,
+        "pack",
+        0,
+        rows * 1024,
+        in_specs=[SMEM, SMEM] + [resident(part.shape) for part in parts],
+        out_specs=resident((rows, 128)),
+        out_shape=jax.ShapeDtypeStruct((rows, 128), F32),
+        grid=(1,),
+    )(places, lengths, *parts)
+
+
 def tie(*values):
     return lax.optimization_barrier(values)
 
@@ -579,35 +638,46 @@
     return rows, whole(attvector).astype(F32), whole(feedvector).astype(F32)
 
 
-def reduce_core(links, near, far_got):
-    return add(near, far_got).astype(BF)
-
-
-def reduce_corner(links, mine):
-    block = mine.shape[0] // 4
+def corner_sum(near, got):
+    start = near.shape[0] // 4 * 3
+    return add(near[start:], got[start:]).astype(BF)
+
+
+def send_corner(links, corner):
+    half = corner.shape[0] // 2
+    return links.swap(corner[:half], dp=2), links.swap(corner[half:], dp=1)
+
+
+def side_sums(near, got, corners):
+    block = near.shape[0] // 4
     half = block // 2
-    corner = mine[3 * block :]
-    return links.swap(corner[:half], dp=2), links.swap(corner[half:], dp=1)
-
-
-def reduce_sides(mine, corners):
-    block = mine.shape[0] // 4
-    half = block // 2
-    own, one, two = (mine[m * block : (m + 1) * block] for m in range(3))
-    one = jnp.concatenate([add(one[:half], corners[0]).astype(BF), one[half:]], axis=0)
-    two = jnp.concatenate([two[:half], add(two[half:], corners[1]).astype(BF)], axis=0)
-    return own, one, two
-
-
-def reduce_z(links, summed, size):
-    summed = summed.reshape(-1, 4, size, summed.shape[-1])
-    pieces = [summed[:, k].reshape(-1, summed.shape[-1]) for k in range(4)]
-    return pieces[0], [links.swap(pieces[k], z=k) for k in range(1, 4)]
-
-
-def share_plane(links, final):
-    stacked = jnp.stack([final] + [links.swap(final, dp=m) for m in range(1, 4)])
-    return links.flip(stacked, 0, links.my_dp)
+    one = add(near[block : 2 * block], got[block : 2 * block])
+    two = add(near[2 * block : 3 * block], got[2 * block : 3 * block])
+    one = jnp.concatenate([one[:half] + corners[0].astype(F32), one[half:]], axis=0)
+    two = jnp.concatenate([two[:half], two[half:] + corners[1].astype(F32)], axis=0)
+    return one.astype(BF), two.astype(BF)
+
+
+def send_sides(links, sides):
+    return links.swap(sides[0], dp=1), links.swap(sides[1], dp=2)
+
+
+def own_sum(near, got, sides):
+    block = near.shape[0] // 4
+    return add(near[:block], got[:block], *sides).astype(BF)
+
+
+def send_z(links, summed):
+    size = summed.shape[0] // 4
+    return summed[:size], [links.swap(summed[k * size : (k + 1) * size], z=k) for k in range(1, 4)]
+
+
+def send_share(links, final):
+    return [final] + [links.swap(final, dp=m) for m in range(1, 4)]
+
+
+def quarters(links, shares):
+    return links.flip(jnp.stack(shares), 0, links.my_dp).reshape(-1, shares[0].shape[1]).astype(F32)
 
 
 def per_device(tokens, attention, attvector, expand, contract, feedvector, lengths, cotangent):
@@ -633,21 +703,11 @@
         extras = jnp.concatenate([part[size:] for part in attn_z], axis=0)
         attn_one, attn_two = spread_plane(links, attn_own)
         feed_z = spread_z(links, feed_mine)
-        attn_three = spread_corner(links, attn_one, attn_two)
-        attn_near = [attn_own, attn_one, attn_two, *attn_three]
-        attn_far = [links.swap(part, core=1) for part in attn_near]
         extras = jnp.stack([extras, links.swap(extras, core=1)])
-        attn_pieces = attn_near + attn_far
-        attn_starts = [0, 4, 8, 12, 14, 16, 20, 24, 28, 30]
         extras = extras.reshape(2, 1, 4, 16 * width)[..., : vectors.shape[0]]
         extras = links.flip(links.flip(extras, 0, links.my_core), 2, links.my_z)
         by_owner = extras.transpose(2, 0, 1, 3).reshape(links.fsdp, -1).astype(F32)
         attvec, feedvec = by_owner[:, :att_len].reshape(-1), by_owner[:, att_len:].reshape(-1)
-
-        feed_own = jnp.concatenate([part[:size] for part in feed_z] + [part[size:] for part in feed_z], axis=0)
-        feed_own, *_ = tie(feed_own, *attn_three)
-        feed_one, feed_two = spread_plane(links, feed_own)
-        feed_far = [links.swap(feed_own, core=1)]
     else:
         rows, attvec, feedvec = gather_plain(attention, attvector, expand, contract, feedvector)
         attn_pieces, attn_starts = [rows[0]], [0]
@@ -661,6 +721,20 @@
     vec_rows = [row_of(attvec, i) for i in (2, 3, 4)] + [row_of(feedvec, i, hidden) for i in range(3)]
     vec_rows = jnp.stack(vec_rows + [jnp.zeros((width,), F32)] * 2)
     inner_bias = links.to_exchange(feedvec[:hidden].reshape(4, 2, 4, size)).reshape(1, hidden)
+
+    if links.paired:
+        attn_one, attn_two, project_bias, vec_rows, inner_bias = tie(
+            attn_one, attn_two, project_bias, vec_rows, inner_bias
+        )
+        attn_three = spread_corner(links, attn_one, attn_two)
+        attn_near = [attn_own, attn_one, attn_two, *attn_three]
+        attn_far = [links.swap(part, core=1) for part in attn_near]
+        attn_pieces = attn_near + attn_far
+        attn_starts = [0, 4, 8, 12, 14, 16, 20, 24, 28, 30]
+        feed_own = jnp.concatenate([part[:size] for part in feed_z] + [part[size:] for part in feed_z], axis=0)
+        feed_own, *_ = tie(feed_own, *attn_three)
+        feed_one, feed_two = spread_plane(links, feed_own)
+        feed_far = [links.swap(feed_own, core=1)]
 
     projected, attn_rows = project(tokens, project_bias, links.table(), attn_pieces, attn_starts, size)
     context, logs = attend(projected, lengths, positions)
@@ -683,103 +757,103 @@
     result, grad_two, grad_two_low, sum_two = contract_call(
         lengths, vec_rows, gelu, normed_one, cotangent, contracts, positions
     )
+    tables = [
+        jnp.stack([links.my_core ^ e, links.my_dp, links.my_z]).astype(jnp.int32) for e in range(2)
+    ]
+    places = jnp.concatenate([links.table(), tables[0]])
+
+    cf = feed_weights(gelu, grad_two_low, 1)
+    gelu, cf = tie(gelu, cf)
+    cn = feed_weights(gelu, grad_two_low, 0)
+    if links.paired:
+        cg = links.swap(cf, core=1)
+        corner = corner_sum(cn, cg)
+        slope, corner = tie(slope, corner)
+        c_in = send_corner(links, corner)
+    else:
+        slope, cn = tie(slope, cn)
     inner_grad, hidden_grad, sum_inner = inner_back(grad_two_low, slope, grad_two, contracts, expands)
-    feed_far = feed_weights(inner_grad, gelu, hidden_low, grad_two_low, 1, 4)
-    inner_grad, feed_far = tie(inner_grad, feed_far)
-    feed_near = feed_weights(inner_grad, gelu, hidden_low, grad_two_low, 0, 4)
-    if links.paired:
-        feed_far = links.swap(feed_far, core=1)
-        feed_mine = reduce_core(links, feed_near, feed_far)
-        hidden_grad, feed_mine = tie(hidden_grad, feed_mine)
-        feed_corners = reduce_corner(links, feed_mine)
+    if links.paired:
+        inner_grad, *c_in = tie(inner_grad, *c_in)
+        inner_grad, *c_in = tie(inner_grad, *side_sums(cn, cg, c_in))
+        c_in = send_sides(links, c_in)
+    ef = feed_weights(inner_grad, hidden_low, 1)
+    inner_grad, ef = tie(inner_grad, ef)
+    en = feed_weights(inner_grad, hidden_low, 0)
+    if links.paired:
+        eg = links.swap(ef, core=1)
+        hidden_grad, corner = tie(hidden_grad, corner_sum(en, eg))
+        e_in = send_corner(links, corner)
     else:
-        hidden_grad, feed_near, feed_far = tie(hidden_grad, feed_near, feed_far)
+        hidden_grad, en = tie(hidden_grad, en)
     grad_one, grad_one_low, context_grad, sum_one = middle_back(
         vec_rows, hidden_grad, normed_one, inverse_one, attn_rows
     )
     if links.paired:
-        context_grad, *feed_corners = tie(context_grad, *feed_corners)
-        feed_own, feed_one, feed_two = reduce_sides(feed_mine, feed_corners)
-        context_grad, feed_one, feed_two = tie(context_grad, feed_one, feed_two)
-        feed_one, feed_two = links.swap(feed_one, dp=1), links.swap(feed_two, dp=2)
-
-    def attn_part(e, context_grad):
-        table = jnp.stack([links.my_core ^ e, links.my_dp, links.my_z]).astype(jnp.int32)
-        qkv_grad, sums = attend_back(
-            projected, lengths, table[:1], context_grad, context, logs, positions
+        context_grad, *got = tie(context_grad, *e_in, *c_in)
+        context_grad, c_own, *e_in = tie(
+            context_grad, own_sum(cn, cg, got[2:]), *side_sums(en, eg, got[:2])
         )
-        return qkv_grad, attn_weights(table, qkv_grad, grad_one_low, tokens, context), sums
-
-    qkv_far, attn_far, sum_far = attn_part(1, context_grad)
-    if links.paired:
-        context_grad, feed_one, feed_two, attn_far = tie(context_grad, feed_one, feed_two, attn_far)
-        feed_sum = add(feed_own, feed_one, feed_two).astype(BF)
-        context_grad, feed_sum = tie(context_grad, feed_sum)
-        feed_piece, feed_z = reduce_z(links, feed_sum, size)
-        attn_far = links.swap(attn_far.reshape(-1, width), core=1)
+        e_in = send_sides(links, e_in)
+        c_own, c_in = send_z(links, c_own)
+    qkv_far, sum_far = attend_back(projected, lengths, tables[1][:1], context_grad, context, logs, positions)
+    if links.paired:
+        qkv_far, *got = tie(qkv_far, *e_in, *c_in)
+        qkv_far, e_own, c_own = tie(
+            qkv_far, own_sum(en, eg, got[:2]), add(c_own, *got[2:]).astype(BF)
+        )
+        c_in = send_share(links, c_own)
+        e_own, e_in = send_z(links, e_own)
+    af = attn_weights(tables[1], qkv_far, grad_one_low, tokens, context)
+    context_grad, af = tie(context_grad, af)
+    qkv_near, sum_near = attend_back(
+        projected, lengths, tables[0][:1], context_grad, context, logs, positions
+    )
+    packed = pack(places, lengths, [sum_near, sum_far, sum_one, sum_inner, sum_two, sum_middle])
+    if links.paired:
+        qkv_near, *e_in = tie(qkv_near, *e_in)
+        qkv_near, e_own, packed = tie(qkv_near, add(e_own, *e_in).astype(BF), packed)
+        e_in = send_share(links, e_own)
+        packed_in = links.swap(packed, core=1)
+    an = attn_weights(tables[0], qkv_near, grad_one_low, tokens, context)
+    if links.paired:
+        an, af = an.reshape(-1, width), af.reshape(-1, width)
+        ag = links.swap(af, core=1)
+        an, packed_in = tie(an, packed_in)
+        qkv_near, corner, packed = tie(qkv_near, corner_sum(an, ag), packed + packed_in)
+        a_in, packed_in = send_corner(links, corner), links.swap(packed, dp=1)
+        qkv_near, packed, *a_in = tie(qkv_near, packed + packed_in, *side_sums(an, ag, a_in))
+        a_in, packed_in = send_sides(links, a_in), links.swap(packed, dp=2)
+        input_grad = input_back(tables[0][:1], qkv_near, qkv_far, attn_rows, grad_one)
+        input_grad, packed_in, *a_in = tie(input_grad, packed_in, *a_in)
+        input_grad, packed, a_own = tie(input_grad, packed + packed_in, own_sum(an, ag, a_in))
+        packed_in = links.swap(packed, z=1)
+        a_own, a_in = send_z(links, a_own)
+        packed, a_own = tie(packed + packed_in, add(a_own, *a_in).astype(BF))
+        packed = packed + links.swap(packed, z=2)
+        attn_sum = quarters(links, send_share(links, a_own)).T
+        expand_sum, contract_sum = quarters(links, e_in).T, quarters(links, c_in)
     else:
-        context_grad, attn_far = tie(context_grad, attn_far)
-    qkv_near, sum_near = attend_back(
-        projected, lengths, links.my_core.reshape(1).astype(jnp.int32), context_grad, context, logs, positions
-    )
-    table = jnp.stack([links.my_core, links.my_dp, links.my_z]).astype(jnp.int32)
-    if links.paired:
-        qkv_near, *feed_z = tie(qkv_near, *feed_z)
-        feed_final = add(feed_piece, *feed_z).astype(BF)
-        qkv_near, feed_final = tie(qkv_near, feed_final)
-        feed_shared = share_plane(links, feed_final)
-    attn_near = attn_weights(table, qkv_near, grad_one_low, tokens, context)
-    if links.paired:
-        attn_mine = reduce_core(links, attn_near.reshape(-1, width), attn_far)
-        qkv_last, attn_mine = tie(qkv_near, attn_mine)
-        input_grad = input_back(table[:1], qkv_last, qkv_far, attn_rows, grad_one)
-        corners = reduce_corner(links, attn_mine)
-        attn_own, attn_one, attn_two = reduce_sides(attn_mine, corners)
-        attn_one, attn_two = links.swap(attn_one, dp=1), links.swap(attn_two, dp=2)
-        attn_sum = add(attn_own, attn_one, attn_two).astype(BF)
-        attn_sum, input_grad = tie(attn_sum, input_grad)
-        attn_piece, attn_z = reduce_z(links, attn_sum, size)
-        attn_final = add(attn_piece, *attn_z).astype(BF)
-        attn_sum = share_plane(links, attn_final).reshape(quad, width).astype(F32).T
-        expand_sum = feed_shared[:, :size].reshape(quad, width).astype(F32).T
-        contract_sum = feed_shared[:, size:].reshape(quad, width).astype(F32)
-    else:
-        input_grad = input_back(table[:1], qkv_near, qkv_far, attn_rows, grad_one)
+        input_grad = input_back(tables[0][:1], qkv_near, qkv_far, attn_rows, grad_one)
 
         def finish(natural):
             shard = lax.psum_scatter(natural, "fsdp", scatter_dimension=0, tiled=True)
             return lax.psum(shard, "dp").astype(F32)
 
-        feed = jnp.concatenate([feed_near, feed_far], axis=0).reshape(8, 2, quad, width)
-        expand_sum = finish(feed[:, 0].reshape(hidden, width)).T
-        contract_sum = finish(feed[:, 1].reshape(hidden, width))
-        both = jnp.stack([attn_near, attn_far])
-        attn_sum = finish(both.transpose(2, 0, 1, 3, 4).reshape(4 * width, width)).T
-
-    sums = [jnp.sum(part, axis=0) for part in (sum_near, sum_far)]
-    near_first = links.my_core == 0
-    sum_rows = jnp.concatenate(
-        [jnp.where(near_first, *sums), jnp.where(near_first, sums[1], sums[0])], axis=1
+        expand_sum = finish(jnp.concatenate([en, ef], axis=0)).T
+        contract_sum = finish(jnp.concatenate([cn, cf], axis=0))
+        attn_sum = finish(jnp.stack([an, af]).transpose(2, 0, 1, 3, 4).reshape(4 * width, width)).T
+        packed = lax.psum(packed, AXES)
+
+    att_rows = att_len * links.fsdp // 128
+    inner_at = att_rows + (feed_len * links.fsdp - hidden) // 128
+    att_sum = lax.dynamic_slice_in_dim(packed[:att_rows].reshape(-1), links.my_fsdp * att_len, att_len, 0)
+    feed_flat = jnp.concatenate(
+        [packed[inner_at : inner_at + 32, : hidden // 32].reshape(-1), packed[att_rows:inner_at].reshape(-1)]
     )
-    inner_sum = links.to_natural(sum_inner[0].reshape(2, 4, 4, size)).reshape(hidden // width, width)
-    count_row = jnp.pad(jnp.sum(lengths).astype(F32).reshape(1, 1), ((0, 0), (0, width - 1)))
-    packed = jnp.concatenate(
-        [sum_rows, sum_one[:3], inner_sum, sum_two[1:4], sum_middle[:2], sum_two[:1], count_row], axis=0
-    )
-    if links.paired:
-        packed, attn_mine = tie(packed, attn_mine)
-        for step in ({"core": 1}, {"dp": 1}, {"dp": 2}, {"z": 1}, {"z": 2}):
-            packed = packed + links.swap(packed, **step)
-    else:
-        packed = lax.psum(packed, AXES)
-    flat = packed.reshape(-1)
-    att_total, feed_total = att_len * links.fsdp, feed_len * links.fsdp
-    att_sum = lax.dynamic_slice_in_dim(flat[:att_total], links.my_fsdp * att_len, att_len, 0)
-    feed_vec_sum = lax.dynamic_slice_in_dim(
-        flat[att_total : att_total + feed_total], links.my_fsdp * feed_len, feed_len, 0
-    )
-    squares = jnp.sum(packed[12:15], axis=1)
-    root_squares = jnp.sqrt(squares / (packed[15, 0] * width))
+    feed_vec_sum = lax.dynamic_slice_in_dim(feed_flat, links.my_fsdp * feed_len, feed_len, 0)
+    squares = jnp.sum(packed[inner_at + 32 : inner_at + 35], axis=1)
+    root_squares = jnp.sqrt(squares / (packed[inner_at + 35, 0] * width))
     return (result, input_grad, attn_sum, att_sum, expand_sum, contract_sum, feed_vec_sum, root_squares)
 
 

time: 365 us -> 350 us (0.959)
  Pallas kernels: 177 us -> 159 us
  local copies, waits for them, and re-layouts: 38.9 us -> 20.9 us
  starting transfers between devices: 51.8 us -> 66 us
  other arithmetic: 25.6 us -> 30.3 us
    ppermute x52 -> x63, starting transfers between devices: 51.8 us -> 66 us  [swap(): return lax.ppermute(values, AXES, pairs)]
    pallas_call x2, Pallas kernels: 39.4 us -> 26.2 us  [attend_back(): call(attend_back_kernel, 'attend_back', 2 * flops, 8 * count * width, gri...]
    pallas_call x1, Pallas kernels: 23.7 us -> 17.5 us  [inner_back(): call(functools.partial(inner_kernel, count=len(contracts)), 'inner_back',...]
    add x5 -> x8, other arithmetic: 2.92 us -> 8.66 us  [the longest x3 6.43 us: add(): return sum((part.astype(F32) for part in parts))]
    convert_element_type x9 -> x7, other arithmetic: 14.1 us -> 8.53 us  [the longest x3 5.13 us: own_sum(): return add(near[:block], got[:block], *sides).astype(BF)]
    pallas_call x2 -> x5, Pallas kernels: 19.4 us -> 25 us  [the longest x4 23.4 us: feed_weights(): call(feed_weights_kernel, 'feed_weights', 2 * count * width * rows, count...]
    another operation x8, local copies, waits for them, and re-layouts: 5.49 us -> 0.67 us  [per_device(): vec_rows = jnp.stack(vec_rows + [jnp.zeros((width,), F32)] * 2)]
    another operation x4 -> x10, other arithmetic: 1.51 us -> 5.92 us  [the longest x1 0.64 us: per_device(): jnp.stack([links.my_core, links.my_dp, links.my_z]).astype(jnp.int32)]
  transfers between devices with their start and end apart: 52 -> 63, of which waited for: 15 -> 18; matrix products, arithmetic and copies ran while one was open for 12% -> 9% of each run, Pallas kernels for 35% -> 37%
where the time goes in v4:
time: 350 us; the launch traced here: 346 us
  Pallas kernels  159 us (45%)
  waiting for transfers between devices  67.1 us (19%)
  starting transfers between devices  66 us (19%)
  other arithmetic  30.3 us (9%)
  local copies, waits for them, and re-layouts  20.9 us (6%)
    ppermute x63, waiting for transfers between devices, swap(): return lax.ppermute(values, AXES, pairs)  67.1 us
    ppermute x63, starting transfers between devices, swap(): return lax.ppermute(values, AXES, pairs)  66 us
    pallas_call x2, Pallas kernels, attend_back(): call(attend_back_kernel, 'attend_back', 2 * flops, 8 * count * width, gri...  26.2 us
    pallas_call x4, Pallas kernels, feed_weights(): call(feed_weights_kernel, 'feed_weights', 2 * count * width * rows, count...  23.4 us
    pallas_call x1, Pallas kernels, inner_back(): call(functools.partial(inner_kernel, count=len(contracts)), 'inner_back',...  17.5 us
    pallas_call x2, Pallas kernels, attn_weights(): call(functools.partial(attn_weights_kernel, quarters=4), 'attn_weights',...  15.7 us
    pallas_call x1, Pallas kernels, attend(): call(attend_kernel, 'attend', 2 * flops, 8 * count * width, grid_spec=plt...  15 us
    pallas_call x1, Pallas kernels, contract_call(): call(functools.partial(contract_kernel, positions=positions), 'contract_n...  13.3 us
  transfers between devices with their start and end apart: 63, of which 18 were waited for; matrix products, arithmetic and copies ran while one was open for 9% of the time, Pallas kernels for 37%

profile of v4, /device:TPU:0, one launch (start us, length us, event | category | flops | bytes accessed | tf_op | source)
XLA Modules:
  0.0 346.0 jit_solution(11450703792622068929)
XLA Ops:
  3.0 3.1 collective-permute-start
  6.1 2.6 collective-permute-start.1
  9.0 4.3 %collective-permute-done = bf16[112,768]{1,0:T(8,128)(2,1)S(1)} collective-permute-done((bf16[112,768]{1,0:T(8,128)(2,1)S(1)}, bf16[112,768]{1,0:T(8,128)(2,1)S(1)}, u32[]{:S(2)}, u32[]{:S(2)}) %collective-permute-start) | collective-permute-done | bytes 172064 | tf_op jit(solution)/shard_map/ppermute | solution.py:586
  13.3 8.4 %collective-permute-done.1 = bf16[112,768]{1,0:T(8,128)(2,1)S(1)} collective-permute-done((bf16[112,768]{1,0:T(8,128)(2,1)S(1)}, bf16[112,768]{1,0:T(8,128)(2,1)S(1)}, u32[]{:S(2)}, u32[]{:S(2)}) %collective-permute-start.1) | collective-permute-done | bytes 172064 | tf_op jit(solution)/shard_map/ppermute | solution.py:586
  21.7 2.9 collective-permute-start.13
  35.9 12.8 %collective-permute-done.14 = bf16[192,768]{1,0:T(8,128)(2,1)S(1)} collective-permute-done((bf16[192,768]{1,0:T(8,128)(2,1)S(1)}, bf16[192,768]{1,0:T(8,128)(2,1)S(1)}, u32[]{:S(2)}, u32[]{:S(2)}) %collective-permute-start.14) | collective-permute-done | bytes 294944 | tf_op jit(solution)/shard_map/ppermute | solution.py:586
  59.2 2.6 collective-permute-done.7.refs_4_
  66.4 10.5 %project.1 = (bf16[3,1024,768]{2,1,0:T(8,128)(2,1)}, bf16[3072,768]{1,0:T(8,128)(2,1)}) custom-call(s32[32]{0:T(128)} %add.183.table_ref, f32[2,768]{1,0:T(2,128)} %pad_maximum_fusion.14.bias_ref, bf16[1024,768]{1,0:T(8,128)(2,1)} %token_ref.7, bf16[384,768]{1,0:T(8,128)(2,1)} %copy-done.6, bf16[384,768]{1,0:T(8,128)(2,1)} %collective-permute-done.3.refs_1_, ...), custom_call_target="tpu_custom_call" | custom-call | flops 3623878656 | bytes 15728640 | tf_op jit(solution)/shard_map/project/pallas_call | solution.py:73
  76.9 15.0 %attend.1 = (bf16[1024,768]{1,0:T(8,128)(2,1)}, f32[2,6,2,512]{3,2,1,0:T(2,128)}) custom-call(s32[2]{0:T(128)} %length_ref.11, bf16[3,1024,768]{2,1,0:T(8,128)(2,1)} %get-tuple-element.118.q_ref.k_ref.v_ref, bf16[3,1024,768]{2,1,0:T(8,128)(2,1)} %get-tuple-element.118.q_ref.k_ref.v_ref, bf16[3,1024,768]{2,1,0:T(8,128)(2,1)} %get-tuple-element.118.q_ref.k_ref.v_ref), custom_call_target="tpu_custom_call" | custom-call | flops 3221225472 | bytes 6291456 | tf_op jit(solution)/shard_map/attend/pallas_call | solution.py:131
  95.6 6.8 %middle.1 = (f32[1024,768]{1,0:T(8,128)}, f32[1024,128]{1,0:T(8,128)}, bf16[1024,768]{1,0:T(8,128)(2,1)}, f32[8,768]{1,0:T(8,128)}) custom-call(s32[2]{0:T(128)} %length_ref.11, f32[8,768]{1,0:T(8,128)} %stack.120.vec_ref, bf16[1024,768]{1,0:T(8,128)(2,1)} %get-tuple-element.122.ctx_ref, bf16[3072,768]{1,0:T(8,128)(2,1)} %get-tuple-element.123.weight_ref, ...), custom_call_target="tpu_custom_call" | custom-call | flops 1207959552 | bytes 9437184 | tf_op jit(solution)/shard_map/middle/pallas_call | solution.py:266
  102.4 5.1 %collective-permute-done.18.refs_3_.refs_11_ = bf16[384,768]{1,0:T(8,128)(2,1)} collective-permute-done((bf16[384,768]{1,0:T(8,128)(2,1)S(1)}, bf16[384,768]{1,0:T(8,128)(2,1)}, u32[]{:S(2)}, u32[]{:S(2)}) %collective-permute-start.18) | collective-permute-done | bytes 589856 | tf_op jit(solution)/shard_map/ppermute | solution.py:586
  112.7 12.7 %expand_gelu.1 = (bf16[1024,3072]{1,0:T(8,128)(2,1)}, bf16[1024,3072]{1,0:T(8,128)(2,1)}) custom-call(f32[1,3072]{1,0:T(1,128)} %reshape_reshape.10.bias_ref, bf16[1024,768]{1,0:T(8,128)(2,1)} %get-tuple-element.127.low_ref.right_ref, bf16[768,768]{1,0:T(8,128)(2,1)} %slice_dynamic-update-slice_fusion.refs_0_.refs_8_, bf16[768,768]{1,0:T(8,128)(2,1)} %copy-done.2, ...), custom_call_target="tpu_custom_call" | custom-call | flops 4831838208 | bytes 12582912 | tf_op jit(solution)/shard_map/expand_gelu/pallas_call | solution.py:314
  126.2 13.3 %contract_norm.1 = (bf16[1024,768]{1,0:T(8,128)(2,1)}, f32[1024,768]{1,0:T(8,128)}, bf16[1024,768]{1,0:T(8,128)(2,1)}, f32[8,768]{1,0:T(8,128)}) custom-call(s32[2]{0:T(128)} %length_ref.11, f32[8,768]{1,0:T(8,128)} %stack.120.vec_ref, bf16[1024,3072]{1,0:T(8,128)(2,1)} %get-tuple-element.135.gelu_ref.left_ref, f32[1024,768]{1,0:T(8,128)} %get-tuple-element.130.n_ref, ...), custom_call_target="tpu_custom_call" | custom-call | flops 4831838208 | bytes 17301504 | tf_op jit(solution)/shard_map/contract_norm/pallas_call | solution.py:350
  139.5 5.8 %feed_weights.4 = bf16[1536,768]{1,0:T(8,128)(2,1)} custom-call(bf16[1024,3072]{1,0:T(8,128)(2,1)} %get-tuple-element.135.gelu_ref.left_ref, bf16[1024,768]{1,0:T(8,128)(2,1)} %get-tuple-element.133.right_ref.low_ref), custom_call_target="tpu_custom_call" | custom-call | flops 2415919104 | bytes 5505024 | tf_op jit(solution)/shard_map/feed_weights/pallas_call | solution.py:414
  145.5 6.0 %feed_weights.5 = bf16[1536,768]{1,0:T(8,128)(2,1)} custom-call(bf16[1024,3072]{1,0:T(8,128)(2,1)} %get-tuple-element.135.gelu_ref.left_ref, bf16[1024,768]{1,0:T(8,128)(2,1)} %get-tuple-element.133.right_ref.low_ref), custom_call_target="tpu_custom_call" | custom-call | flops 2415919104 | bytes 5505024 | tf_op jit(solution)/shard_map/feed_weights/pallas_call | solution.py:414
  156.0 17.5 %inner_back.1 = (bf16[1024,3072]{1,0:T(8,128)(2,1)}, f32[1024,768]{1,0:T(8,128)}, f32[8,3072]{1,0:T(8,128)}) custom-call(bf16[1024,768]{1,0:T(8,128)(2,1)} %get-tuple-element.133.right_ref.low_ref, bf16[1024,3072]{1,0:T(8,128)(2,1)} %get-tuple-element.137.slope_ref, f32[1024,768]{1,0:T(8,128)} %get-tuple-element.138.grad_ref, ...), custom_call_target="tpu_custom_call" | custom-call | flops 9663676416 | bytes 20447232 | tf_op jit(solution)/shard_map/inner_back/pallas_call | solution.py:389
  175.6 5.8 %feed_weights.6 = bf16[1536,768]{1,0:T(8,128)(2,1)} custom-call(bf16[1024,3072]{1,0:T(8,128)(2,1)} %get-tuple-element.146.left_ref, bf16[1024,768]{1,0:T(8,128)(2,1)} %get-tuple-element.127.low_ref.right_ref), custom_call_target="tpu_custom_call" | custom-call | flops 2415919104 | bytes 5505024 | tf_op jit(solution)/shard_map/feed_weights/pallas_call | solution.py:414
  184.0 5.8 %feed_weights.7 = bf16[1536,768]{1,0:T(8,128)(2,1)} custom-call(bf16[1024,3072]{1,0:T(8,128)(2,1)} %get-tuple-element.146.left_ref, bf16[1024,768]{1,0:T(8,128)(2,1)} %get-tuple-element.127.low_ref.right_ref), custom_call_target="tpu_custom_call" | custom-call | flops 2415919104 | bytes 5505024 | tf_op jit(solution)/shard_map/feed_weights/pallas_call | solution.py:414
  195.1 8.0 %middle_back.1 = (f32[1024,768]{1,0:T(8,128)}, bf16[1024,768]{1,0:T(8,128)(2,1)}, bf16[1024,768]{1,0:T(8,128)(2,1)}, f32[8,768]{1,0:T(8,128)}) custom-call(f32[8,768]{1,0:T(8,128)} %stack.120.vec_ref, f32[1024,768]{1,0:T(8,128)} %get-tuple-element.148.hid_ref, f32[1024,768]{1,0:T(8,128)} %get-tuple-element.130.n_ref, f32[1024,128]{1,0:T(8,128)} %get-tuple-element.149.s_ref, ...), custom_call_target="tpu_custom_call" | custom-call | flops 1207959552 | bytes 12582912 | tf_op jit(solution)/shard_map/middle_back/pallas_call | solution.py:438
  210.6 3.8 %collective-permute-start.35 = (bf16[96,768]{1,0:T(8,128)(2,1)S(1)}, bf16[96,768]{1,0:T(8,128)(2,1)S(1)}, u32[]{:S(2)}, u32[]{:S(2)}) collective-permute-start(bf16[96,768]{1,0:T(8,128)(2,1)S(1)} %get-tuple-element.237), channel_id=1, source_target_pairs={{0,2},{1,3},{2,0},{3,1},{4,6},{5,7},{6,4},{7,5},{8,10},{9,11},{10,... | collective-permute-start | bytes 442376 | tf_op jit(solution)/shard_map/ppermute | solution.py:586
  217.0 13.1 %attend_back.2 = (bf16[3,1024,384]{2,1,0:T(8,128)(2,1)}, f32[2,2,384]{2,1,0:T(2,128)}) custom-call(s32[2]{0:T(128)} %length_ref.11, s32[1]{0:T(128)} %bitcast.9._, bf16[3,1024,768]{2,1,0:T(8,128)(2,1)} %get-tuple-element.118.q_ref.k_ref.v_ref, bf16[3,1024,768]{2,1,0:T(8,128)(2,1)} %get-tuple-element.118.q_ref.k_ref.v_ref, ...), custom_call_target="tpu_custom_call" | custom-call | flops 4026531840 | bytes 6291456 | tf_op jit(solution)/shard_map/attend_back/pallas_call | solution.py:193
  232.7 7.8 %attn_weights.2 = bf16[4,4,96,768]{3,2,1,0:T(8,128)(2,1)} custom-call(s32[3]{0:T(128)} %get-tuple-element.250.table_ref, bf16[3,1024,384]{2,1,0:T(8,128)(2,1)} %get-tuple-element.171.qkv_ref.far_ref, bf16[1024,768]{1,0:T(8,128)(2,1)} %get-tuple-element.172.low_ref, bf16[1024,768]{1,0:T(8,128)(2,1)} %token_ref.7, bf16[1024,768]{1,0:T(8,128)(2,1)} %get-tuple-element.122.ctx_ref), custom_call_target="tpu_custom_call" | custom-call | flops 2415919104 | bytes 8650752 | tf_op jit(solution)/shard_map/attn_weights/pallas_call | solution.py:473
  245.6 13.1 %attend_back.3 = (bf16[3,1024,384]{2,1,0:T(8,128)(2,1)}, f32[2,2,384]{2,1,0:T(2,128)}) custom-call(s32[2]{0:T(128)} %length_ref.11, s32[1]{0:T(128)} %bitcast.8._.core_ref, bf16[3,1024,768]{2,1,0:T(8,128)(2,1)} %get-tuple-element.118.q_ref.k_ref.v_ref, bf16[3,1024,768]{2,1,0:T(8,128)(2,1)} %get-tuple-element.118.q_ref.k_ref.v_ref, ...), custom_call_target="tpu_custom_call" | custom-call | flops 4026531840 | bytes 6291456 | tf_op jit(solution)/shard_map/attend_back/pallas_call | solution.py:193
  267.4 5.3 %collective-permute-done.61 = bf16[96,768]{1,0:T(8,128)(2,1)S(1)} collective-permute-done((bf16[96,768]{1,0:T(8,128)(2,1)S(1)}, bf16[96,768]{1,0:T(8,128)(2,1)S(1)}, u32[]{:S(2)}, u32[]{:S(2)}) %collective-permute-start.61) | collective-permute-done | bytes 147488 | tf_op jit(solution)/shard_map/ppermute | solution.py:586
  273.9 7.9 %attn_weights.3 = bf16[4,4,96,768]{3,2,1,0:T(8,128)(2,1)} custom-call(s32[3]{0:T(128)} %get-tuple-element.251.table_ref, bf16[3,1024,384]{2,1,0:T(8,128)(2,1)} %get-tuple-element.194.qkv_ref.near_ref, bf16[1024,768]{1,0:T(8,128)(2,1)} %get-tuple-element.172.low_ref, bf16[1024,768]{1,0:T(8,128)(2,1)} %token_ref.7, bf16[1024,768]{1,0:T(8,128)(2,1)} %get-tuple-element.122.ctx_ref), custom_call_target="tpu_custom_call" | custom-call | flops 2415919104 | bytes 8650752 | tf_op jit(solution)/shard_map/attn_weights/pallas_call | solution.py:473
  290.5 4.5 %collective-permute-done.43 = f32[88,128]{1,0:T(8,128)S(1)} collective-permute-done((f32[88,128]{1,0:T(8,128)S(1)}, f32[88,128]{1,0:T(8,128)S(1)}, u32[]{:S(2)}, u32[]{:S(2)}) %collective-permute-start.43) | collective-permute-done | bytes 45088 | tf_op jit(solution)/shard_map/ppermute | solution.py:586
  302.6 8.5 %input_back.1 = bf16[1024,768]{1,0:T(8,128)(2,1)} custom-call(s32[1]{0:T(128)} %bitcast.8._.core_ref, bf16[3,1024,384]{2,1,0:T(8,128)(2,1)} %get-tuple-element.194.qkv_ref.near_ref, bf16[3,1024,384]{2,1,0:T(8,128)(2,1)} %get-tuple-element.171.qkv_ref.far_ref, bf16[3072,768]{1,0:T(8,128)(2,1)} %get-tuple-element.123.weight_ref, ...), custom_call_target="tpu_custom_call" | custom-call | flops 3623878656 | bytes 12976128 | tf_op jit(solution)/shard_map/input_back/pallas_call | solution.py:507
  311.1 4.6 %collective-permute-done.46 = f32[88,128]{1,0:T(8,128)S(1)} collective-permute-done((f32[88,128]{1,0:T(8,128)}, f32[88,128]{1,0:T(8,128)S(1)}, u32[]{:S(2)}, u32[]{:S(2)}) %collective-permute-start.46) | collective-permute-done | bytes 45088 | tf_op jit(solution)/shard_map/ppermute | solution.py:586
  318.3 2.9 collective-permute-start.51
  322.7 5.3 %collective-permute-done.49 = f32[88,128]{1,0:T(8,128)S(1)} collective-permute-done((f32[88,128]{1,0:T(8,128)S(1)}, f32[88,128]{1,0:T(8,128)S(1)}, u32[]{:S(2)}, u32[]{:S(2)}) %collective-permute-start.49) | collective-permute-done | bytes 45088 | tf_op jit(solution)/shard_map/ppermute | solution.py:586
  328.0 2.9 collective-permute-done.51
  331.0 3.3 collective-permute-start.56
  (273 shorter events, 111.8 us)
Async XLA Ops:
  6.1 15.5 %collective-permute-start.1 = (bf16[112,768]{1,0:T(8,128)(2,1)S(1)}, bf16[112,768]{1,0:T(8,128)(2,1)S(1)}, u32[]{:S(2)}, u32[]{:S(2)}) collective-permute-start(bf16[112,768]{1,0:T(8,128)(2,1)S(1)} %pad_maximum_fusion.11), channel_id=1, source_target_pairs={{0,4},{1,5},{2,6},{3,7},{4,0},{5,1},{6,2},{7,3},{8,12},{9,13},{10,... | collective-permute-start | bytes 516104 | tf_op jit(solution)/shard_map/ppermute | solution.py:586
  25.2 23.4 %collective-permute-start.14 = (bf16[192,768]{1,0:T(8,128)(2,1)S(1)}, bf16[192,768]{1,0:T(8,128)(2,1)S(1)}, u32[]{:S(2)}, u32[]{:S(2)}) collective-permute-start(bf16[192,768]{1,0:T(8,128)(2,1)S(1)} %pad_maximum_fusion.10), channel_id=1, source_target_pairs={{0,4},{1,5},{2,6},{3,7},{4,0},{5,1},{6,2},{7,3},{8,12},{9,13},{10,... | collective-permute-start | bytes 884744 | tf_op jit(solution)/shard_map/ppermute | solution.py:586
  26.2 23.1 %collective-permute-start.15 = (bf16[192,768]{1,0:T(8,128)(2,1)S(1)}, bf16[192,768]{1,0:T(8,128)(2,1)S(1)}, u32[]{:S(2)}, u32[]{:S(2)}) collective-permute-start(bf16[192,768]{1,0:T(8,128)(2,1)S(1)} %pad_maximum_fusion.10), channel_id=1, source_target_pairs={{0,6},{1,7},{2,4},{3,5},{4,2},{5,3},{6,0},{7,1},{8,14},{9,15},{10,... | collective-permute-start | bytes 884744 | tf_op jit(solution)/shard_map/ppermute | solution.py:586
  28.0 22.7 %collective-permute-start.3 = (bf16[384,768]{1,0:T(8,128)(2,1)S(1)}, bf16[384,768]{1,0:T(8,128)(2,1)}, u32[]{:S(2)}, u32[]{:S(2)}) collective-permute-start(bf16[384,768]{1,0:T(8,128)(2,1)S(1)} %pad_maximum_fusion.refs_0_), channel_id=1, source_target_pairs={{0,8},{1,9},{2,10},{3,11},{4,12},{5,13},{6,14},{7,15},{8,0},{9,1},... | collective-permute-start | bytes 1769480 | tf_op jit(solution)/shard_map/ppermute | solution.py:586
  29.6 21.1 %collective-permute-start.4 = (bf16[384,768]{1,0:T(8,128)(2,1)S(1)}, bf16[384,768]{1,0:T(8,128)(2,1)}, u32[]{:S(2)}, u32[]{:S(2)}) collective-permute-start(bf16[384,768]{1,0:T(8,128)(2,1)S(1)} %pad_maximum_fusion.refs_0_), channel_id=1, source_target_pairs={{0,16},{1,17},{2,18},{3,19},{4,20},{5,21},{6,22},{7,23},{8,24},{9,... | collective-permute-start | bytes 1769480 | tf_op jit(solution)/shard_map/ppermute | solution.py:586
  35.2 28.0 %collective-permute-start.8 = (bf16[384,768]{1,0:T(8,128)(2,1)S(1)}, bf16[384,768]{1,0:T(8,128)(2,1)}, u32[]{:S(2)}, u32[]{:S(2)}) collective-permute-start(bf16[384,768]{1,0:T(8,128)(2,1)S(1)} %pad_maximum_fusion.refs_0_), channel_id=1, source_target_pairs={{0,1},{1,0},{2,3},{3,2},{4,5},{5,4},{6,7},{7,6},{8,9},{9,8},{10,11... | collective-permute-start | bytes 1769480 | tf_op jit(solution)/shard_map/ppermute | solution.py:586
  61.8 30.1 %collective-permute-start.16 = (bf16[768,768]{1,0:T(8,128)(2,1)}, bf16[768,768]{1,0:T(8,128)(2,1)S(1)}, u32[]{:S(2)}, u32[]{:S(2)}) collective-permute-start(bf16[768,768]{1,0:T(8,128)(2,1)} %slice_dynamic-update-slice_fusion.refs_0_.refs_8_), channel_id=1, source_target_pairs={{0,8},{1,9},{2,10},{3,11},{4,12},{5,13},{6,14},{7,15},{8,0},{9,1},... | collective-permute-start | bytes 3538952 | tf_op jit(solution)/shard_map/ppermute | solution.py:586
  63.2 28.7 %collective-permute-start.17 = (bf16[768,768]{1,0:T(8,128)(2,1)}, bf16[768,768]{1,0:T(8,128)(2,1)S(1)}, u32[]{:S(2)}, u32[]{:S(2)}) collective-permute-start(bf16[768,768]{1,0:T(8,128)(2,1)} %slice_dynamic-update-slice_fusion.refs_0_.refs_8_), channel_id=1, source_target_pairs={{0,16},{1,17},{2,18},{3,19},{4,20},{5,21},{6,22},{7,23},{8,24},{9,... | collective-permute-start | bytes 3538952 | tf_op jit(solution)/shard_map/ppermute | solution.py:586
  92.0 15.5 %collective-permute-start.18 = (bf16[384,768]{1,0:T(8,128)(2,1)S(1)}, bf16[384,768]{1,0:T(8,128)(2,1)}, u32[]{:S(2)}, u32[]{:S(2)}) collective-permute-start(bf16[384,768]{1,0:T(8,128)(2,1)S(1)} %slice.313), channel_id=1, source_target_pairs={{0,16},{1,17},{2,18},{3,19},{4,20},{5,21},{6,22},{7,23},{8,24},{9,... | collective-permute-start | bytes 1769480 | tf_op jit(solution)/shard_map/ppermute | solution.py:586
  94.3 15.3 %collective-permute-start.19 = (bf16[384,768]{1,0:T(8,128)(2,1)}, bf16[384,768]{1,0:T(8,128)(2,1)S(1)}, u32[]{:S(2)}, u32[]{:S(2)}) collective-permute-start(bf16[384,768]{1,0:T(8,128)(2,1)} %slice.314), channel_id=1, source_target_pairs={{0,8},{1,9},{2,10},{3,11},{4,12},{5,13},{6,14},{7,15},{8,0},{9,1},... | collective-permute-start | bytes 1769480 | tf_op jit(solution)/shard_map/ppermute | solution.py:586
  95.0 15.2 %collective-permute-start.20 = (bf16[768,768]{1,0:T(8,128)(2,1)}, bf16[768,768]{1,0:T(8,128)(2,1)}, u32[]{:S(2)}, u32[]{:S(2)}) collective-permute-start(bf16[768,768]{1,0:T(8,128)(2,1)} %slice_dynamic-update-slice_fusion.refs_0_.refs_8_), channel_id=1, source_target_pairs={{0,1},{1,0},{2,3},{3,2},{4,5},{5,4},{6,7},{7,6},{8,9},{9,8},{10,11... | collective-permute-start | bytes 3538952 | tf_op jit(solution)/shard_map/ppermute | solution.py:586
  95.0 16.9 %collective-permute-start.21 = (bf16[768,768]{1,0:T(8,128)(2,1)S(1)}, bf16[768,768]{1,0:T(8,128)(2,1)}, u32[]{:S(2)}, u32[]{:S(2)}) collective-permute-start(bf16[768,768]{1,0:T(8,128)(2,1)S(1)} %collective-permute-done.16.refs_1_.refs_9_), channel_id=1, source_target_pairs={{0,1},{1,0},{2,3},{3,2},{4,5},{5,4},{6,7},{7,6},{8,9},{9,8},{10,11... | collective-permute-start | bytes 3538952 | tf_op jit(solution)/shard_map/ppermute | solution.py:586
  95.5 17.2 %collective-permute-start.22 = (bf16[768,768]{1,0:T(8,128)(2,1)S(1)}, bf16[768,768]{1,0:T(8,128)(2,1)}, u32[]{:S(2)}, u32[]{:S(2)}) collective-permute-start(bf16[768,768]{1,0:T(8,128)(2,1)S(1)} %collective-permute-done.17.refs_2_.refs_10_), channel_id=1, source_target_pairs={{0,1},{1,0},{2,3},{3,2},{4,5},{5,4},{6,7},{7,6},{8,9},{9,8},{10,11... | collective-permute-start | bytes 3538952 | tf_op jit(solution)/shard_map/ppermute | solution.py:586
  109.6 15.7 %collective-permute-start.24 = (bf16[384,768]{1,0:T(8,128)(2,1)S(1)}, bf16[384,768]{1,0:T(8,128)(2,1)S(1)}, u32[]{:S(2)}, u32[]{:S(2)}) collective-permute-start(bf16[384,768]{1,0:T(8,128)(2,1)S(1)} %collective-permute-done.19.refs_3_), channel_id=1, source_target_pairs={{0,1},{1,0},{2,3},{3,2},{4,5},{5,4},{6,7},{7,6},{8,9},{9,8},{10,11... | collective-permute-start | bytes 1769480 | tf_op jit(solution)/shard_map/ppermute | solution.py:586
  154.5 19.0 %collective-permute-start.26 = (bf16[192,768]{1,0:T(8,128)(2,1)}, bf16[192,768]{1,0:T(8,128)(2,1)S(1)}, u32[]{:S(2)}, u32[]{:S(2)}) collective-permute-start(bf16[192,768]{1,0:T(8,128)(2,1)} %get-tuple-element.241), channel_id=1, source_target_pairs={{0,16},{1,17},{2,18},{3,19},{4,20},{5,21},{6,22},{7,23},{8,24},{9,... | collective-permute-start | bytes 884744 | tf_op jit(solution)/shard_map/ppermute | solution.py:586
  155.4 18.2 %collective-permute-start.27 = (bf16[192,768]{1,0:T(8,128)(2,1)S(1)}, bf16[192,768]{1,0:T(8,128)(2,1)}, u32[]{:S(2)}, u32[]{:S(2)}) collective-permute-start(bf16[192,768]{1,0:T(8,128)(2,1)S(1)} %get-tuple-element.240), channel_id=1, source_target_pairs={{0,8},{1,9},{2,10},{3,11},{4,12},{5,13},{6,14},{7,15},{8,0},{9,1},... | collective-permute-start | bytes 884744 | tf_op jit(solution)/shard_map/ppermute | solution.py:586
  181.4 21.7 %collective-permute-start.31 = (bf16[384,768]{1,0:T(8,128)(2,1)}, bf16[384,768]{1,0:T(8,128)(2,1)}, u32[]{:S(2)}, u32[]{:S(2)}) collective-permute-start(bf16[384,768]{1,0:T(8,128)(2,1)} %pad_maximum_fusion.1), channel_id=1, source_target_pairs={{0,8},{1,9},{2,10},{3,11},{4,12},{5,13},{6,14},{7,15},{8,0},{9,1},... | collective-permute-start | bytes 1769480 | tf_op jit(solution)/shard_map/ppermute | solution.py:586
  182.8 20.3 %collective-permute-start.32 = (bf16[384,768]{1,0:T(8,128)(2,1)S(1)}, bf16[384,768]{1,0:T(8,128)(2,1)}, u32[]{:S(2)}, u32[]{:S(2)}) collective-permute-start(bf16[384,768]{1,0:T(8,128)(2,1)S(1)} %pad_maximum_fusion.2), channel_id=1, source_target_pairs={{0,16},{1,17},{2,18},{3,19},{4,20},{5,21},{6,22},{7,23},{8,24},{9,... | collective-permute-start | bytes 1769480 | tf_op jit(solution)/shard_map/ppermute | solution.py:586
  208.7 21.4 %collective-permute-start.33 = (bf16[384,768]{1,0:T(8,128)(2,1)S(1)}, bf16[384,768]{1,0:T(8,128)(2,1)S(1)}, u32[]{:S(2)}, u32[]{:S(2)}) collective-permute-start(bf16[384,768]{1,0:T(8,128)(2,1)S(1)} %pad_maximum_fusion.3), channel_id=1, source_target_pairs={{0,8},{1,9},{2,10},{3,11},{4,12},{5,13},{6,14},{7,15},{8,0},{9,1},... | collective-permute-start | bytes 1769480 | tf_op jit(solution)/shard_map/ppermute | solution.py:586
  209.4 20.7 %collective-permute-start.34 = (bf16[384,768]{1,0:T(8,128)(2,1)S(1)}, bf16[384,768]{1,0:T(8,128)(2,1)S(1)}, u32[]{:S(2)}, u32[]{:S(2)}) collective-permute-start(bf16[384,768]{1,0:T(8,128)(2,1)S(1)} %pad_maximum_fusion.4), channel_id=1, source_target_pairs={{0,16},{1,17},{2,18},{3,19},{4,20},{5,21},{6,22},{7,23},{8,24},{9,... | collective-permute-start | bytes 1769480 | tf_op jit(solution)/shard_map/ppermute | solution.py:586
  210.6 19.5 %collective-permute-start.35 = (bf16[96,768]{1,0:T(8,128)(2,1)S(1)}, bf16[96,768]{1,0:T(8,128)(2,1)S(1)}, u32[]{:S(2)}, u32[]{:S(2)}) collective-permute-start(bf16[96,768]{1,0:T(8,128)(2,1)S(1)} %get-tuple-element.237), channel_id=1, source_target_pairs={{0,2},{1,3},{2,0},{3,1},{4,6},{5,7},{6,4},{7,5},{8,10},{9,11},{10,... | collective-permute-start | bytes 442376 | tf_op jit(solution)/shard_map/ppermute | solution.py:586
  214.4 15.6 %collective-permute-start.36 = (bf16[96,768]{1,0:T(8,128)(2,1)S(1)}, bf16[96,768]{1,0:T(8,128)(2,1)}, u32[]{:S(2)}, u32[]{:S(2)}) collective-permute-start(bf16[96,768]{1,0:T(8,128)(2,1)S(1)} %get-tuple-element.236), channel_id=1, source_target_pairs={{0,4},{1,5},{2,6},{3,7},{4,0},{5,1},{6,2},{7,3},{8,12},{9,13},{10,... | collective-permute-start | bytes 442376 | tf_op jit(solution)/shard_map/ppermute | solution.py:586
  215.6 14.5 %collective-permute-start.37 = (bf16[96,768]{1,0:T(8,128)(2,1)S(1)}, bf16[96,768]{1,0:T(8,128)(2,1)}, u32[]{:S(2)}, u32[]{:S(2)}) collective-permute-start(bf16[96,768]{1,0:T(8,128)(2,1)S(1)} %get-tuple-element.235), channel_id=1, source_target_pairs={{0,6},{1,7},{2,4},{3,5},{4,2},{5,3},{6,0},{7,1},{8,14},{9,15},{10,... | collective-permute-start | bytes 442376 | tf_op jit(solution)/shard_map/ppermute | solution.py:586
  240.5 42.2 %collective-permute-start.42 = (bf16[1536,768]{1,0:T(8,128)(2,1)}, bf16[1536,768]{1,0:T(8,128)(2,1)S(1)}, u32[]{:S(2)}, u32[]{:S(2)}) collective-permute-start(bf16[1536,768]{1,0:T(8,128)(2,1)} %bitcast.57), channel_id=1, source_target_pairs={{0,1},{1,0},{2,3},{3,2},{4,5},{5,4},{6,7},{7,6},{8,9},{9,8},{10,11... | collective-permute-start | bytes 7077896 | tf_op jit(solution)/shard_map/ppermute | solution.py:586
  241.1 20.7 %collective-permute-start.38 = (bf16[96,768]{1,0:T(8,128)(2,1)S(1)}, bf16[96,768]{1,0:T(8,128)(2,1)}, u32[]{:S(2)}, u32[]{:S(2)}) collective-permute-start(bf16[96,768]{1,0:T(8,128)(2,1)S(1)} %get-tuple-element.234), channel_id=1, source_target_pairs={{0,2},{1,3},{2,0},{3,1},{4,6},{5,7},{6,4},{7,5},{8,10},{9,11},{10,... | collective-permute-start | bytes 442376 | tf_op jit(solution)/shard_map/ppermute | solution.py:586
  242.2 20.6 %collective-permute-start.39 = (bf16[96,768]{1,0:T(8,128)(2,1)S(1)}, bf16[96,768]{1,0:T(8,128)(2,1)}, u32[]{:S(2)}, u32[]{:S(2)}) collective-permute-start(bf16[96,768]{1,0:T(8,128)(2,1)S(1)} %get-tuple-element.233), channel_id=1, source_target_pairs={{0,4},{1,5},{2,6},{3,7},{4,0},{5,1},{6,2},{7,3},{8,12},{9,13},{10,... | collective-permute-start | bytes 442376 | tf_op jit(solution)/shard_map/ppermute | solution.py:586
  244.2 19.8 %collective-permute-start.40 = (bf16[96,768]{1,0:T(8,128)(2,1)S(1)}, bf16[96,768]{1,0:T(8,128)(2,1)}, u32[]{:S(2)}, u32[]{:S(2)}) collective-permute-start(bf16[96,768]{1,0:T(8,128)(2,1)S(1)} %get-tuple-element.232), channel_id=1, source_target_pairs={{0,6},{1,7},{2,4},{3,5},{4,2},{5,3},{6,0},{7,1},{8,14},{9,15},{10,... | collective-permute-start | bytes 442376 | tf_op jit(solution)/shard_map/ppermute | solution.py:586
  265.1 22.6 %collective-permute-start.57 = (bf16[96,768]{1,0:T(8,128)(2,1)S(1)}, bf16[96,768]{1,0:T(8,128)(2,1)S(1)}, u32[]{:S(2)}, u32[]{:S(2)}) collective-permute-start(bf16[96,768]{1,0:T(8,128)(2,1)S(1)} %add_convert_fusion.7), channel_id=1, source_target_pairs={{0,8},{1,9},{2,10},{3,11},{4,12},{5,13},{6,14},{7,15},{8,0},{9,1},... | collective-permute-start | bytes 442376 | tf_op jit(solution)/shard_map/ppermute | solution.py:586
  266.6 21.2 %collective-permute-start.58 = (bf16[96,768]{1,0:T(8,128)(2,1)S(1)}, bf16[96,768]{1,0:T(8,128)(2,1)S(1)}, u32[]{:S(2)}, u32[]{:S(2)}) collective-permute-start(bf16[96,768]{1,0:T(8,128)(2,1)S(1)} %add_convert_fusion.7), channel_id=1, source_target_pairs={{0,16},{1,17},{2,18},{3,19},{4,20},{5,21},{6,22},{7,23},{8,24},{9,... | collective-permute-start | bytes 442376 | tf_op jit(solution)/shard_map/ppermute | solution.py:586
  272.7 15.0 %collective-permute-start.59 = (bf16[96,768]{1,0:T(8,128)(2,1)S(1)}, bf16[96,768]{1,0:T(8,128)(2,1)}, u32[]{:S(2)}, u32[]{:S(2)}) collective-permute-start(bf16[96,768]{1,0:T(8,128)(2,1)S(1)} %add_convert_fusion.7), channel_id=1, source_target_pairs={{0,24},{1,25},{2,26},{3,27},{4,28},{5,29},{6,30},{7,31},{8,16},{9,... | collective-permute-start | bytes 442376 | tf_op jit(solution)/shard_map/ppermute | solution.py:586
  298.7 17.0 %collective-permute-start.47 = (bf16[384,768]{1,0:T(8,128)(2,1)}, bf16[384,768]{1,0:T(8,128)(2,1)}, u32[]{:S(2)}, u32[]{:S(2)}) collective-permute-start(bf16[384,768]{1,0:T(8,128)(2,1)} %pad_maximum_fusion.5), channel_id=1, source_target_pairs={{0,8},{1,9},{2,10},{3,11},{4,12},{5,13},{6,14},{7,15},{8,0},{9,1},... | collective-permute-start | bytes 1769480 | tf_op jit(solution)/shard_map/ppermute | solution.py:586
  300.4 15.2 %collective-permute-start.48 = (bf16[384,768]{1,0:T(8,128)(2,1)}, bf16[384,768]{1,0:T(8,128)(2,1)}, u32[]{:S(2)}, u32[]{:S(2)}) collective-permute-start(bf16[384,768]{1,0:T(8,128)(2,1)} %pad_maximum_fusion.6), channel_id=1, source_target_pairs={{0,16},{1,17},{2,18},{3,19},{4,20},{5,21},{6,22},{7,23},{8,24},{9,... | collective-permute-start | bytes 1769480 | tf_op jit(solution)/shard_map/ppermute | solution.py:586
  (44 other events, 339.0 us)

commit v5 on v4

--- a/solution.py
+++ b/solution.py
@@ -102,7 +102,7 @@
 
 
 def pairs_per_step(pairs):
-    return 3 if pairs % 3 == 0 else 1
+    return 2 if pairs % 2 == 0 else 1
 
 
 def attend_kernel(length_ref, q_ref, k_ref, v_ref, out_ref, log_ref):
@@ -150,7 +150,7 @@
 
 
 def attend_back_kernel(
-    length_ref, _, q_ref, k_ref, v_ref, grad_ref, ctx_ref, log_ref, out_ref, sum_ref
+    length_ref, q_ref, k_ref, v_ref, grad_ref, ctx_ref, log_ref, out_ref, sum_ref
 ):
     length = length_ref[pl.program_id(0)]
     row = lax.broadcasted_iota(jnp.int32, (8, PAIR), 0)
@@ -182,40 +182,33 @@
         sum_ref[0, 1:2, span] = jnp.sum(value_low.astype(F32), axis=0, keepdims=True)
 
 
-def attend_back(projected, lengths, side, context_grad, context, logs, positions):
+def attend_back(projected, lengths, context_grad, context, logs, positions):
     _, count, width = projected.shape
-    rows, pairs = count // positions, width // PAIR // 2
+    rows, pairs = count // positions, width // PAIR
     group = pairs_per_step(pairs)
-    steps = pairs // group
     block = (1, positions, group * PAIR)
-    flat = pl.BlockSpec((positions, group * PAIR), lambda r, p, _, s: (r, s[0] * steps + p))
+    flat = pl.BlockSpec((positions, group * PAIR), lambda r, p, _: (r, p))
     flops = 10 * rows * pairs * 2 * positions * positions * HEAD_DIM
     return call(
         attend_back_kernel,
         "attend_back",
         2 * flops,
-        8 * count * width,
+        16 * count * width,
         grid_spec=pltpu.PrefetchScalarGridSpec(
-            num_scalar_prefetch=2,
-            grid=(rows, steps),
-            in_specs=[
-                pl.BlockSpec(block, lambda r, p, _, s, j=j: (j, r, s[0] * steps + p)) for j in range(3)
-            ]
-            + [
-                flat,
-                flat,
-                pl.BlockSpec((1, group, 2, positions), lambda r, p, _, s: (r, s[0] * steps + p, 0, 0)),
-            ],
+            num_scalar_prefetch=1,
+            grid=(rows, pairs // group),
+            in_specs=[pl.BlockSpec(block, lambda r, p, _, j=j: (j, r, p)) for j in range(3)]
+            + [flat, flat, pl.BlockSpec((1, group, 2, positions), lambda r, p, _: (r, p, 0, 0))],
             out_specs=[
-                pl.BlockSpec((3, positions, group * PAIR), lambda r, p, _, s: (0, r, p)),
-                pl.BlockSpec((1, 2, group * PAIR), lambda r, p, _, s: (r, 0, p)),
+                pl.BlockSpec((3, positions, group * PAIR), lambda r, p, _: (0, r, p)),
+                pl.BlockSpec((1, 2, group * PAIR), lambda r, p, _: (r, 0, p)),
             ],
         ),
         out_shape=[
-            jax.ShapeDtypeStruct((3, count, width // 2), BF),
-            jax.ShapeDtypeStruct((rows, 2, width // 2), F32),
+            jax.ShapeDtypeStruct((3, count, width), BF),
+            jax.ShapeDtypeStruct((rows, 2, width), F32),
         ],
-    )(lengths, side, projected, projected, projected, context_grad, context, logs)
+    )(lengths, projected, projected, projected, context_grad, context, logs)
 
 
 def normalize(residual):
@@ -291,16 +284,22 @@
         yield jnp.concatenate([first[...], second[...]], axis=0)
 
 
-def expand_kernel(bias_ref, low_ref, *refs):
+def expand_kernel(bias_ref, low_ref, *refs, groups):
     pieces, (gelu_ref, slope_ref) = refs[:-2], refs[-2:]
-    low, at = low_ref[...], 0
-    for piece in two_by_two(pieces):
-        size = piece.shape[0]
-        inner = dot_nt(low, piece) + bias_ref[0:1, at : at + size]
-        gelu, slope = gelu_parts(inner)
-        gelu_ref[:, at : at + size] = gelu.astype(BF)
-        slope_ref[:, at : at + size] = slope.astype(BF)
-        at += size
+    low = low_ref[...]
+    for first, last, at in groups:
+        weights = jnp.concatenate([piece[...] for piece in pieces[first:last]], axis=0)
+        span = slice(at, at + weights.shape[0])
+        gelu, slope = gelu_parts(dot_nt(low, weights) + bias_ref[0:1, span])
+        gelu_ref[:, span] = gelu.astype(BF)
+        slope_ref[:, span] = slope.astype(BF)
+
+
+def expand_last_kernel(bias_ref, low_ref, near_ref, far_ref, _, __, gelu_ref, slope_ref):
+    weights = jnp.where(pl.program_id(1) == 0, near_ref[...], far_ref[...])
+    gelu, slope = gelu_parts(dot_nt(low_ref[...], weights) + bias_ref[...])
+    gelu_ref[...] = gelu.astype(BF)
+    slope_ref[...] = slope.astype(BF)
 
 
 def picked(piece, width):
@@ -308,19 +307,44 @@
     return pl.BlockSpec((size, width), lambda *_, at=start // size: (at, 0))
 
 
-def expand_call(low, bias, pieces):
+def expand_call(low, bias, pieces, groups):
     count, width = low.shape
     hidden = bias.shape[1]
-    return call(
-        expand_kernel,
+    done = sum(piece[2] for piece in pieces)
+    return call(
+        functools.partial(expand_kernel, groups=groups),
         "expand_gelu",
-        2 * count * width * hidden,
+        2 * count * width * done,
         count * hidden * 4,
         grid=(count // TILE,),
         in_specs=[resident(bias.shape), tiles(width)] + [picked(piece, width) for piece in pieces],
         out_specs=[tiles(hidden), tiles(hidden)],
         out_shape=[jax.ShapeDtypeStruct((count, hidden), BF)] * 2,
     )(bias, low, *[piece[0] for piece in pieces])
+
+
+def expand_last(low, bias, pieces, gelu, slope):
+    count, width = low.shape
+    size = pieces[0][2]
+    tall = count // 2
+    spot = pl.BlockSpec((tall, size), lambda t, e: (t, 4 * e + 3))
+    anywhere = pl.BlockSpec(memory_space=pl.ANY)
+    return call(
+        expand_last_kernel,
+        "expand_last",
+        4 * count * width * size,
+        count * size * 8,
+        grid=(2, 2),
+        in_specs=[
+            pl.BlockSpec((1, size), lambda t, e: (0, 4 * e + 3)),
+            pl.BlockSpec((tall, width), lambda t, e: (t, 0)),
+        ]
+        + [picked(piece, width) for piece in pieces]
+        + [anywhere, anywhere],
+        out_specs=[spot, spot],
+        out_shape=[jax.ShapeDtypeStruct(gelu.shape, BF)] * 2,
+        input_output_aliases={4: 0, 5: 1},
+    )(bias, low, *[piece[0] for piece in pieces], gelu, slope)
 
 
 def contract_kernel(length_ref, vec_ref, gelu_ref, n_ref, cot_ref, *refs, positions):
@@ -452,81 +476,92 @@
     )(vectors, hidden_grad, normed, inverse, attn_rows)
 
 
-def attn_weights_kernel(table_ref, qkv_ref, low_ref, token_ref, ctx_ref, out_ref, *, quarters):
-    def put(result):
-        size = result.shape[0] // quarters
-        for d in range(quarters):
-            out_ref[d ^ table_ref[1], 0] = result[d * size : (d + 1) * size, :]
-
-    @pl.when(pl.program_id(0) < 3)
+def attn_weights_kernel(table_ref, qkv_ref, low_ref, token_ref, ctx_ref, far_ref, near_ref, sum_ref):
+    step = pl.program_id(0)
+
+    @pl.when(step % 4 < 3)
     def _():
-        put(dot_tn(qkv_ref[0], token_ref[...]).astype(BF))
-
-    @pl.when(pl.program_id(0) == 3)
+        sum_ref[...] = dot_tn(qkv_ref[0], token_ref[...]).astype(BF)
+
+    @pl.when(step % 4 == 3)
     def _():
-        put(dot_tn(low_ref[...], ctx_ref[...]).astype(BF))
+        sum_ref[...] = dot_tn(low_ref[...], ctx_ref[...]).astype(BF)
+
+    def put(out_ref):
+        size = out_ref.shape[2]
+        for d in range(4):
+            out_ref[d ^ table_ref[1], 0] = sum_ref[d * size : (d + 1) * size, :]
+
+    pl.when(step < 4)(lambda: put(far_ref))
+    pl.when(step >= 4)(lambda: put(near_ref))
 
 
 def attn_weights(table, qkv_grad, out_grad, tokens, context):
     count, width = tokens.shape
     half = width // 2
-    return call(
-        functools.partial(attn_weights_kernel, quarters=4),
+    block = (4, 1, half // 4, width)
+
+    def column(i, t):
+        return jnp.where(i < 4, 1 - t[0], t[0])
+
+    return call(
+        attn_weights_kernel,
         "attn_weights",
-        4 * 2 * count * width * half,
-        count * width * 8 + width * width * 4,
+        8 * 2 * count * width * half,
+        count * width * 8 + width * width * 8,
         grid_spec=pltpu.PrefetchScalarGridSpec(
             num_scalar_prefetch=1,
-            grid=(4,),
+            grid=(8,),
             in_specs=[
-                pl.BlockSpec((1, count, half), lambda i, t: (jnp.minimum(i, 2), 0, 0)),
-                pl.BlockSpec((count, half), lambda i, t: (0, t[0])),
+                pl.BlockSpec((1, count, half), lambda i, t: (jnp.minimum(i % 4, 2), 0, column(i, t))),
+                pl.BlockSpec((count, half), lambda i, t: (0, column(i, t))),
                 resident((count, width)),
                 resident((count, width)),
             ],
-            out_specs=pl.BlockSpec((4, 1, half // 4, width), lambda i, t: (0, i ^ t[2], 0, 0)),
+            out_specs=[
+                pl.BlockSpec(block, lambda i, t: (0, jnp.minimum(i, 3) ^ t[2], 0, 0)),
+                pl.BlockSpec(block, lambda i, t: (0, jnp.maximum(i - 4, 0) ^ t[2], 0, 0)),
+            ],
+            scratch_shapes=[pltpu.VMEM((half, width), BF)],
         ),
-        out_shape=jax.ShapeDtypeStruct((4, 4, half // 4, width), BF),
+        out_shape=[jax.ShapeDtypeStruct((4, 4, half // 4, width), BF)] * 2,
     )(table, qkv_grad, out_grad, tokens, context)
 
 
-def input_kernel(core_ref, near_ref, far_ref, weight_ref, grad_ref, out_ref):
+def input_kernel(qkv_ref, weight_ref, grad_ref, out_ref):
     width = out_ref.shape[1]
-    near_first = core_ref[0] == 0
     total = grad_ref[...]
     for j in range(3):
-        near, far = near_ref[j], far_ref[j]
-        whole = jnp.concatenate([jnp.where(near_first, near, far), jnp.where(near_first, far, near)], axis=1)
-        total = total + dot_nn(whole, weight_ref[j * width : (j + 1) * width, :])
+        total = total + dot_nn(qkv_ref[j], weight_ref[j * width : (j + 1) * width, :])
     out_ref[...] = total.astype(BF)
 
 
-def input_back(core, near, far, attn_rows, grad):
+def input_back(qkv_grad, attn_rows, grad):
     count, width = grad.shape
-    half = pl.BlockSpec((3, TILE, width // 2), lambda t: (0, t, 0))
     return call(
         input_kernel,
         "input_back",
         6 * count * width * width,
         count * width * 12 + width * width * 6,
         grid=(count // TILE,),
-        in_specs=[SMEM, half, half, resident((3 * width, width)), tiles(width)],
+        in_specs=[
+            pl.BlockSpec((3, TILE, width), lambda t: (0, t, 0)),
+            resident((3 * width, width)),
+            tiles(width),
+        ],
         out_specs=tiles(width),
         out_shape=jax.ShapeDtypeStruct((count, width), BF),
-    )(core, near, far, attn_rows, grad)
-
-
-def pack_kernel(place_ref, length_ref, near_ref, far_ref, one_ref, inner_ref, two_ref, middle_ref, out_ref):
-    half = near_ref.shape[2]
-    near_first = place_ref[32] == 0
-    near, far = (jnp.sum(ref[...], axis=0) for ref in (near_ref, far_ref))
-    first, second = jnp.where(near_first, near, far), jnp.where(near_first, far, near)
-    both = jnp.concatenate([first, second], axis=1)
+    )(qkv_grad, attn_rows, grad)
+
+
+def pack_kernel(place_ref, length_ref, qkv_ref, one_ref, inner_ref, two_ref, middle_ref, out_ref):
+    width = qkv_ref.shape[2]
+    both = jnp.sum(qkv_ref[...], axis=0)
     rows = [both[0:1, :], both[1:2, :]] + [one_ref[i : i + 1, :] for i in range(3)]
     rows += [two_ref[i : i + 1, :] for i in (1, 2, 3)]
     at = 0
     for row in rows:
-        for lane in range(0, 2 * half, 128):
+        for lane in range(0, width, 128):
             out_ref[at : at + 1, :] = row[:, lane : lane + 128]
             at += 1
     size = inner_ref.shape[1] // 32
@@ -536,7 +571,7 @@
         out_ref[pl.ds(at + place_ref[i], 1), :] = part
     at += 32
     for row in (middle_ref[0:1, :], middle_ref[1:2, :], two_ref[0:1, :]):
-        out_ref[at : at + 1, :] = sum(row[:, lane : lane + 128] for lane in range(0, 2 * half, 128))
+        out_ref[at : at + 1, :] = sum(row[:, lane : lane + 128] for lane in range(0, width, 128))
         at += 1
     live = length_ref[0]
     for i in range(1, length_ref.shape[0]):
@@ -546,7 +581,7 @@
 
 
 def pack(places, lengths, parts):
-    width = parts[2].shape[1]
+    width = parts[1].shape[1]
     rows = 8 * width // 128 + 32 + 8
     return call(
         pack_kernel,
@@ -639,13 +674,13 @@
 
 
 def corner_sum(near, got):
-    start = near.shape[0] // 4 * 3
-    return add(near[start:], got[start:]).astype(BF)
+    half = near.shape[0] // 8
+    parts = (slice(6 * half, 7 * half), slice(7 * half, 8 * half))
+    return [add(near[part], got[part]).astype(BF) for part in parts]
 
 
 def send_corner(links, corner):
-    half = corner.shape[0] // 2
-    return links.swap(corner[:half], dp=2), links.swap(corner[half:], dp=1)
+    return links.swap(corner[0], dp=2), links.swap(corner[1], dp=1)
 
 
 def side_sums(near, got, corners):
@@ -667,6 +702,11 @@
     return add(near[:block], got[:block], *sides).astype(BF)
 
 
+def send_z_far(links, summed):
+    half = summed.shape[0] // 2
+    return summed[:half], links.swap(summed[half:], z=2)
+
+
 def send_z(links, summed):
     size = summed.shape[0] // 4
     return summed[:size], [links.swap(summed[k * size : (k + 1) * size], z=k) for k in range(1, 4)]
@@ -691,7 +731,7 @@
 
     if links.paired:
         vectors = jnp.concatenate([attvector, feedvector])
-        extra = jnp.pad(vectors, (0, 16 * width - vectors.shape[0])).reshape(16, width)
+        extra = jnp.pad(vectors, (0, 8 * width - vectors.shape[0])).reshape(8, width)
 
         def quarter(shard):
             return lax.dynamic_slice_in_dim(shard, links.my_dp * size, size, 0)
@@ -702,9 +742,11 @@
         attn_own = jnp.concatenate([part[:size] for part in attn_z], axis=0)
         extras = jnp.concatenate([part[size:] for part in attn_z], axis=0)
         attn_one, attn_two = spread_plane(links, attn_own)
+        attn_far, extras_far = links.swap(attn_own, core=1), links.swap(extras, core=1)
+        feed_mine, attn_far, extras_far = tie(feed_mine, attn_far, extras_far)
         feed_z = spread_z(links, feed_mine)
-        extras = jnp.stack([extras, links.swap(extras, core=1)])
-        extras = extras.reshape(2, 1, 4, 16 * width)[..., : vectors.shape[0]]
+        extras = jnp.stack([extras, extras_far])
+        extras = extras.reshape(2, 1, 4, 8 * width)[..., : vectors.shape[0]]
         extras = links.flip(links.flip(extras, 0, links.my_core), 2, links.my_z)
         by_owner = extras.transpose(2, 0, 1, 3).reshape(links.fsdp, -1).astype(F32)
         attvec, feedvec = by_owner[:, :att_len].reshape(-1), by_owner[:, att_len:].reshape(-1)
@@ -726,9 +768,10 @@
         attn_one, attn_two, project_bias, vec_rows, inner_bias = tie(
             attn_one, attn_two, project_bias, vec_rows, inner_bias
         )
+        *feed_z, _ = tie(*feed_z, attn_one)
         attn_three = spread_corner(links, attn_one, attn_two)
         attn_near = [attn_own, attn_one, attn_two, *attn_three]
-        attn_far = [links.swap(part, core=1) for part in attn_near]
+        attn_far = [attn_far] + [links.swap(part, core=1) for part in attn_near[1:]]
         attn_pieces = attn_near + attn_far
         attn_starts = [0, 4, 8, 12, 14, 16, 20, 24, 28, 30]
         feed_own = jnp.concatenate([part[:size] for part in feed_z] + [part[size:] for part in feed_z], axis=0)
@@ -736,7 +779,8 @@
         feed_one, feed_two = spread_plane(links, feed_own)
         feed_far = [links.swap(feed_own, core=1)]
 
-    projected, attn_rows = project(tokens, project_bias, links.table(), attn_pieces, attn_starts, size)
+    places = links.table()
+    projected, attn_rows = project(tokens, project_bias, places, attn_pieces, attn_starts, size)
     context, logs = attend(projected, lengths, positions)
     if links.paired:
         context, feed_one, feed_two = tie(context, feed_one, feed_two)
@@ -746,35 +790,36 @@
         lengths, vec_rows, context, attn_rows, tokens, positions
     )
     if links.paired:
-        hidden_low, *feed_three = tie(hidden_low, *feed_three)
         feed_near = [feed_own, feed_one, feed_two]
+        expands = [(part, 0, quad) for part in feed_near + feed_far]
+        gelu, slope = expand_call(hidden_low, inner_bias, expands, [(0, 3, 0), (3, 6, 4 * quad)])
+        gelu, *feed_three = tie(gelu, *feed_three)
         far_three = [links.swap(part, core=1) for part in feed_three]
-        expands = [(part, 0, quad) for part in feed_near] + [(feed_three[0], 0, quad)]
-        expands += [(part, 0, quad) for part in feed_far] + [(far_three[0], 0, quad)]
+        last = [(feed_three[0], 0, quad), (far_three[0], 0, quad)]
+        gelu, slope = expand_last(hidden_low, inner_bias, last, gelu, slope)
+        expands = expands[:3] + last[:1] + expands[3:] + last[1:]
         contracts = [(part, quad, quad) for part in feed_near] + [(feed_three[1], 0, quad)]
         contracts += [(part, quad, quad) for part in feed_far] + [(far_three[1], 0, quad)]
-    gelu, slope = expand_call(hidden_low, inner_bias, expands)
+    else:
+        groups = [(i, i + 2, i * quad) for i in range(0, 8, 2)]
+        gelu, slope = expand_call(hidden_low, inner_bias, expands, groups)
     result, grad_two, grad_two_low, sum_two = contract_call(
         lengths, vec_rows, gelu, normed_one, cotangent, contracts, positions
     )
-    tables = [
-        jnp.stack([links.my_core ^ e, links.my_dp, links.my_z]).astype(jnp.int32) for e in range(2)
-    ]
-    places = jnp.concatenate([links.table(), tables[0]])
+    table = jnp.stack([links.my_core, links.my_dp, links.my_z]).astype(jnp.int32)
 
     cf = feed_weights(gelu, grad_two_low, 1)
     gelu, cf = tie(gelu, cf)
     cn = feed_weights(gelu, grad_two_low, 0)
     if links.paired:
         cg = links.swap(cf, core=1)
-        corner = corner_sum(cn, cg)
-        slope, corner = tie(slope, corner)
+        slope, *corner = tie(slope, *corner_sum(cn, cg))
         c_in = send_corner(links, corner)
     else:
         slope, cn = tie(slope, cn)
     inner_grad, hidden_grad, sum_inner = inner_back(grad_two_low, slope, grad_two, contracts, expands)
     if links.paired:
-        inner_grad, *c_in = tie(inner_grad, *c_in)
+        inner_grad, cn, cg, *c_in = tie(inner_grad, cn, cg, *c_in)
         inner_grad, *c_in = tie(inner_grad, *side_sums(cn, cg, c_in))
         c_in = send_sides(links, c_in)
     ef = feed_weights(inner_grad, hidden_low, 1)
@@ -782,7 +827,7 @@
     en = feed_weights(inner_grad, hidden_low, 0)
     if links.paired:
         eg = links.swap(ef, core=1)
-        hidden_grad, corner = tie(hidden_grad, corner_sum(en, eg))
+        hidden_grad, *corner = tie(hidden_grad, *corner_sum(en, eg))
         e_in = send_corner(links, corner)
     else:
         hidden_grad, en = tie(hidden_grad, en)
@@ -790,51 +835,54 @@
         vec_rows, hidden_grad, normed_one, inverse_one, attn_rows
     )
     if links.paired:
-        context_grad, *got = tie(context_grad, *e_in, *c_in)
+        context_grad, cn, cg, en, eg, *got = tie(context_grad, cn, cg, en, eg, *e_in, *c_in)
         context_grad, c_own, *e_in = tie(
             context_grad, own_sum(cn, cg, got[2:]), *side_sums(en, eg, got[:2])
         )
         e_in = send_sides(links, e_in)
         c_own, c_in = send_z(links, c_own)
-    qkv_far, sum_far = attend_back(projected, lengths, tables[1][:1], context_grad, context, logs, positions)
+    qkv_grad, sum_qkv = attend_back(projected, lengths, context_grad, context, logs, positions)
+    packed = pack(places, lengths, [sum_qkv, sum_one, sum_inner, sum_two, sum_middle])
     if links.paired:
-        qkv_far, *got = tie(qkv_far, *e_in, *c_in)
-        qkv_far, e_own, c_own = tie(
-            qkv_far, own_sum(en, eg, got[:2]), add(c_own, *got[2:]).astype(BF)
-        )
-        c_in = send_share(links, c_own)
-        e_own, e_in = send_z(links, e_own)
-    af = attn_weights(tables[1], qkv_far, grad_one_low, tokens, context)
-    context_grad, af = tie(context_grad, af)
-    qkv_near, sum_near = attend_back(
-        projected, lengths, tables[0][:1], context_grad, context, logs, positions
-    )
-    packed = pack(places, lengths, [sum_near, sum_far, sum_one, sum_inner, sum_two, sum_middle])
-    if links.paired:
-        qkv_near, *e_in = tie(qkv_near, *e_in)
-        qkv_near, e_own, packed = tie(qkv_near, add(e_own, *e_in).astype(BF), packed)
-        e_in = send_share(links, e_own)
-        packed_in = links.swap(packed, core=1)
-    an = attn_weights(tables[0], qkv_near, grad_one_low, tokens, context)
+        qkv_grad, c_own, packed, *got = tie(qkv_grad, c_own, packed, *e_in, *c_in)
+        c_own = add(c_own, *got[2:]).astype(BF)
+        qkv_grad, e_own, c_own = tie(qkv_grad, own_sum(en, eg, got[:2]), c_own)
+        c_in, packed_in = send_share(links, c_own), links.swap(packed, core=1)
+        e_own, e_in = send_z_far(links, e_own)
+    af, an = attn_weights(table, qkv_grad, grad_one_low, tokens, context)
     if links.paired:
         an, af = an.reshape(-1, width), af.reshape(-1, width)
+        an, af, packed_in, e_own, e_in, *c_in = tie(an, af, packed_in, e_own, e_in, *c_in)
         ag = links.swap(af, core=1)
-        an, packed_in = tie(an, packed_in)
-        qkv_near, corner, packed = tie(qkv_near, corner_sum(an, ag), packed + packed_in)
-        a_in, packed_in = send_corner(links, corner), links.swap(packed, dp=1)
-        qkv_near, packed, *a_in = tie(qkv_near, packed + packed_in, *side_sums(an, ag, a_in))
-        a_in, packed_in = send_sides(links, a_in), links.swap(packed, dp=2)
-        input_grad = input_back(tables[0][:1], qkv_near, qkv_far, attn_rows, grad_one)
-        input_grad, packed_in, *a_in = tie(input_grad, packed_in, *a_in)
-        input_grad, packed, a_own = tie(input_grad, packed + packed_in, own_sum(an, ag, a_in))
-        packed_in = links.swap(packed, z=1)
+        packed = packed + packed_in
+        packed_in = links.swap(packed, dp=1)
+        e_own = add(e_own, e_in)
+        e_in = e_own[size:].astype(BF)
+        qkv_grad, packed, packed_in, e_in, *got = tie(
+            qkv_grad, packed, packed_in, e_in, *corner_sum(an, ag), *c_in
+        )
+        corner, c_in = got[:2], got[2:]
+        packed = packed + packed_in
+        a_in = send_corner(links, corner)
+        packed_in, e_in = links.swap(packed, dp=2), links.swap(e_in, z=1)
+        an, ag, packed, packed_in, e_in, *a_in = tie(an, ag, packed, packed_in, e_in, *a_in)
+        e_own = add(e_own[:size], e_in).astype(BF)
+        qkv_grad, packed, e_own, *a_in = tie(qkv_grad, packed + packed_in, e_own, *side_sums(an, ag, a_in))
+        a_in, packed_in = send_sides(links, a_in), links.swap(packed, z=1)
+        e_in = links.swap(e_own, dp=1)
+        input_grad = input_back(qkv_grad, attn_rows, grad_one)
+        input_grad, packed_in, e_in, *a_in = tie(input_grad, packed_in, e_in, *a_in)
+        e_near = jnp.concatenate([e_own, e_in], axis=0)
+        packed, a_own, e_near = tie(packed + packed_in, own_sum(an, ag, a_in), e_near)
         a_own, a_in = send_z(links, a_own)
-        packed, a_own = tie(packed + packed_in, add(a_own, *a_in).astype(BF))
-        packed = packed + links.swap(packed, z=2)
-        attn_sum = quarters(links, send_share(links, a_own)).T
-        expand_sum, contract_sum = quarters(links, e_in).T, quarters(links, c_in)
+        packed_in, e_far = links.swap(packed, z=2), links.swap(e_near, dp=2)
+        packed, packed_in, e_far, *a_in = tie(packed, packed_in, e_far, *a_in)
+        a_own, packed, e_far = tie(add(a_own, *a_in).astype(BF), packed + packed_in, e_far)
+        a_in = send_share(links, a_own)
+        attn_sum = quarters(links, a_in).T
+        expand_sum, contract_sum = quarters(links, [e_near[:size], e_near[size:], e_far[:size], e_far[size:]]).T, quarters(links, c_in)
     else:
-        input_grad = input_back(tables[0][:1], qkv_near, qkv_far, attn_rows, grad_one)
+        input_grad = input_back(qkv_grad, attn_rows, grad_one)
 
         def finish(natural):
             shard = lax.psum_scatter(natural, "fsdp", scatter_dimension=0, tiled=True)

time: 350 us -> 330 us (0.943)
  waiting for transfers between devices: 67.1 us -> 59.7 us
  starting transfers between devices: 66 us -> 59.2 us
    ppermute x63 -> x61, waiting for transfers between devices: 67.1 us -> 59.7 us  [swap(): return lax.ppermute(values, AXES, pairs)]
    ppermute x63 -> x61, starting transfers between devices: 66 us -> 59.2 us  [swap(): return lax.ppermute(values, AXES, pairs)]
    convert_element_type x3 -> x6, other arithmetic: 2.27 us -> 6.21 us  [the longest x3 5.35 us: corner_sum(): return [add(near[part], got[part]).astype(BF) for part in parts]]
    pallas_call x5 -> x4, Pallas kernels: 54.6 us -> 52.9 us  [the longest x1 22.9 us: attend_back(): call(attend_back_kernel, 'attend_back', 2 * flops, 16 * count * width, gr...]
    unnamed x37 -> x63, local copies, waits for them, and re-layouts: 10.1 us -> 10.7 us
  transfers between devices with their start and end apart: 63 -> 61, of which waited for: 18 -> 20; matrix products, arithmetic and copies ran while one was open for 9% -> 7% of each run, Pallas kernels for 37% -> 40%
where the time goes in v5:
time: 330 us; the launch traced here: 329 us
  Pallas kernels  158 us (48%)
  waiting for transfers between devices  59.7 us (18%)
  starting transfers between devices  59.2 us (18%)
  other arithmetic  29.3 us (9%)
  local copies, waits for them, and re-layouts  20.8 us (6%)
    ppermute x61, waiting for transfers between devices, swap(): return lax.ppermute(values, AXES, pairs)  59.7 us
    ppermute x61, starting transfers between devices, swap(): return lax.ppermute(values, AXES, pairs)  59.2 us
    pallas_call x4, Pallas kernels, feed_weights(): call(feed_weights_kernel, 'feed_weights', 2 * count * width * rows, count...  23.3 us
    pallas_call x1, Pallas kernels, attend_back(): call(attend_back_kernel, 'attend_back', 2 * flops, 16 * count * width, gr...  22.9 us
    pallas_call x1, Pallas kernels, inner_back(): call(functools.partial(inner_kernel, count=len(contracts)), 'inner_back',...  17.8 us
    pallas_call x1, Pallas kernels, attend(): call(attend_kernel, 'attend', 2 * flops, 8 * count * width, grid_spec=plt...  15.4 us
    pallas_call x1, Pallas kernels, contract_call(): call(functools.partial(contract_kernel, positions=positions), 'contract_n...  13.3 us
    pallas_call x1, Pallas kernels, attn_weights(): call(attn_weights_kernel, 'attn_weights', 8 * 2 * count * width * half, c...  13 us
  transfers between devices with their start and end apart: 61, of which 20 were waited for; matrix products, arithmetic and copies ran while one was open for 7% of the time, Pallas kernels for 40%

profile of v5, /device:TPU:0, one launch (start us, length us, event | category | flops | bytes accessed | tf_op | source)
XLA Modules:
  0.0 328.8 jit_solution(4297889763229384998)
XLA Ops:
  3.0 5.1 %collective-permute-start.2 = (bf16[104,768]{1,0:T(8,128)(2,1)S(1)}, bf16[104,768]{1,0:T(8,128)(2,1)S(1)}, u32[]{:S(2)}, u32[]{:S(2)}) collective-permute-start(bf16[104,768]{1,0:T(8,128)(2,1)S(1)} %pad_maximum_fusion.12), channel_id=1, source_target_pairs={{0,6},{1,7},{2,4},{3,5},{4,2},{5,3},{6,0},{7,1},{8,14},{9,15},{10,... | collective-permute-start | bytes 479240 | tf_op jit(solution)/shard_map/ppermute | solution.py:621
  9.0 4.2 %collective-permute-done.2 = bf16[104,768]{1,0:T(8,128)(2,1)S(1)} collective-permute-done((bf16[104,768]{1,0:T(8,128)(2,1)S(1)}, bf16[104,768]{1,0:T(8,128)(2,1)S(1)}, u32[]{:S(2)}, u32[]{:S(2)}) %collective-permute-start.2) | collective-permute-done | bytes 159776 | tf_op jit(solution)/shard_map/ppermute | solution.py:621
  13.2 8.5 %collective-permute-done.1 = bf16[104,768]{1,0:T(8,128)(2,1)S(1)} collective-permute-done((bf16[104,768]{1,0:T(8,128)(2,1)S(1)}, bf16[104,768]{1,0:T(8,128)(2,1)S(1)}, u32[]{:S(2)}, u32[]{:S(2)}) %collective-permute-start.1) | collective-permute-done | bytes 159776 | tf_op jit(solution)/shard_map/ppermute | solution.py:621
  26.0 2.5 collective-permute-start.15
  32.8 5.2 %collective-permute-done.4.refs_2_ = bf16[384,768]{1,0:T(8,128)(2,1)} collective-permute-done((bf16[384,768]{1,0:T(8,128)(2,1)S(1)}, bf16[384,768]{1,0:T(8,128)(2,1)}, u32[]{:S(2)}, u32[]{:S(2)}) %collective-permute-start.4) | collective-permute-done | bytes 589856 | tf_op jit(solution)/shard_map/ppermute | solution.py:621
  42.4 10.2 %collective-permute-done.14 = bf16[192,768]{1,0:T(8,128)(2,1)S(1)} collective-permute-done((bf16[192,768]{1,0:T(8,128)(2,1)S(1)}, bf16[192,768]{1,0:T(8,128)(2,1)S(1)}, u32[]{:S(2)}, u32[]{:S(2)}) %collective-permute-start.14) | collective-permute-done | bytes 294944 | tf_op jit(solution)/shard_map/ppermute | solution.py:621
  65.1 10.0 %project.1 = (bf16[3,1024,768]{2,1,0:T(8,128)(2,1)}, bf16[3072,768]{1,0:T(8,128)(2,1)}) custom-call(s32[32]{0:T(128)} %add.175.table_ref.place_ref, f32[2,768]{1,0:T(2,128)} %pad_maximum_fusion.15.bias_ref, bf16[1024,768]{1,0:T(8,128)(2,1)} %token_ref.5, bf16[384,768]{1,0:T(8,128)(2,1)} %copy-done.12, bf16[384,768]{1,0:T(8,128)(2,1)} %collective-permute-done.3.refs_1_, ...), custom_call_target="tpu_custom_call" | custom-call | flops 3623878656 | bytes 15728640 | tf_op jit(solution)/shard_map/project/pallas_call | solution.py:73
  75.1 15.4 %attend.1 = (bf16[1024,768]{1,0:T(8,128)(2,1)}, f32[2,6,2,512]{3,2,1,0:T(2,128)}) custom-call(s32[2]{0:T(128)} %length_ref.9, bf16[3,1024,768]{2,1,0:T(8,128)(2,1)} %get-tuple-element.161.q_ref.k_ref.v_ref, bf16[3,1024,768]{2,1,0:T(8,128)(2,1)} %get-tuple-element.161.q_ref.k_ref.v_ref, bf16[3,1024,768]{2,1,0:T(8,128)(2,1)} %get-tuple-element.161.q_ref.k_ref.v_ref), custom_call_target="tpu_custom_call" | custom-call | flops 3221225472 | bytes 6291456 | tf_op jit(solution)/shard_map/attend/pallas_call | solution.py:131
  94.3 6.9 %middle.1 = (f32[1024,768]{1,0:T(8,128)}, f32[1024,128]{1,0:T(8,128)}, bf16[1024,768]{1,0:T(8,128)(2,1)}, f32[8,768]{1,0:T(8,128)}) custom-call(s32[2]{0:T(128)} %length_ref.9, f32[8,768]{1,0:T(8,128)} %stack.112.vec_ref, bf16[1024,768]{1,0:T(8,128)(2,1)} %get-tuple-element.169.ctx_ref, bf16[3072,768]{1,0:T(8,128)(2,1)} %get-tuple-element.170.weight_ref, ...), custom_call_target="tpu_custom_call" | custom-call | flops 1207959552 | bytes 9437184 | tf_op jit(solution)/shard_map/middle/pallas_call | solution.py:259
  101.2 10.7 %expand_gelu.1 = (bf16[1024,3072]{1,0:T(8,128)(2,1)}, bf16[1024,3072]{1,0:T(8,128)(2,1)}) custom-call(f32[1,3072]{1,0:T(1,128)} %reshape_reshape.10.bias_ref, bf16[1024,768]{1,0:T(8,128)(2,1)} %get-tuple-element.171.low_ref.right_ref, bf16[768,768]{1,0:T(8,128)(2,1)} %slice_dynamic-update-slice_fusion.refs_0_.refs_8_, bf16[768,768]{1,0:T(8,128)(2,1)} %copy-done.4, ...), custom_call_target="tpu_custom_call" | custom-call | flops 3623878656 | bytes 12582912 | tf_op jit(solution)/shard_map/expand_gelu/pallas_call | solution.py:314
  114.8 6.3 %expand_last.1 = (bf16[1024,3072]{1,0:T(8,128)(2,1)}, bf16[1024,3072]{1,0:T(8,128)(2,1)}) custom-call(f32[1,3072]{1,0:T(1,128)} %reshape_reshape.10.bias_ref, bf16[1024,768]{1,0:T(8,128)(2,1)} %get-tuple-element.171.low_ref.right_ref, bf16[384,768]{1,0:T(8,128)(2,1)} %copy-done.9, ...), custom_call_target="tpu_custom_call", output_to_operand_aliasing={{0}: (4, {}), {1}: (5, {})} | custom-call | flops 1207959552 | bytes 3145728 | tf_op jit(solution)/shard_map/expand_last/pallas_call | solution.py:332
  122.0 13.3 %contract_norm.1 = (bf16[1024,768]{1,0:T(8,128)(2,1)}, f32[1024,768]{1,0:T(8,128)}, bf16[1024,768]{1,0:T(8,128)(2,1)}, f32[8,768]{1,0:T(8,128)}) custom-call(s32[2]{0:T(128)} %length_ref.9, f32[8,768]{1,0:T(8,128)} %stack.112.vec_ref, bf16[1024,3072]{1,0:T(8,128)(2,1)} %get-tuple-element.184.gelu_ref.left_ref, f32[1024,768]{1,0:T(8,128)} %get-tuple-element.179.n_ref, ...), custom_call_target="tpu_custom_call" | custom-call | flops 4831838208 | bytes 17301504 | tf_op jit(solution)/shard_map/contract_norm/pallas_call | solution.py:374
  135.3 5.8 %feed_weights.4 = bf16[1536,768]{1,0:T(8,128)(2,1)} custom-call(bf16[1024,3072]{1,0:T(8,128)(2,1)} %get-tuple-element.184.gelu_ref.left_ref, bf16[1024,768]{1,0:T(8,128)(2,1)} %get-tuple-element.182.right_ref.low_ref), custom_call_target="tpu_custom_call" | custom-call | flops 2415919104 | bytes 5505024 | tf_op jit(solution)/shard_map/feed_weights/pallas_call | solution.py:438
  141.3 5.9 %feed_weights.5 = bf16[1536,768]{1,0:T(8,128)(2,1)} custom-call(bf16[1024,3072]{1,0:T(8,128)(2,1)} %get-tuple-element.184.gelu_ref.left_ref, bf16[1024,768]{1,0:T(8,128)(2,1)} %get-tuple-element.182.right_ref.low_ref), custom_call_target="tpu_custom_call" | custom-call | flops 2415919104 | bytes 5505024 | tf_op jit(solution)/shard_map/feed_weights/pallas_call | solution.py:438
  151.4 17.8 %inner_back.1 = (bf16[1024,3072]{1,0:T(8,128)(2,1)}, f32[1024,768]{1,0:T(8,128)}, f32[8,3072]{1,0:T(8,128)}) custom-call(bf16[1024,768]{1,0:T(8,128)(2,1)} %get-tuple-element.182.right_ref.low_ref, bf16[1024,3072]{1,0:T(8,128)(2,1)} %get-tuple-element.186.slope_ref, f32[1024,768]{1,0:T(8,128)} %get-tuple-element.187.grad_ref, ...), custom_call_target="tpu_custom_call" | custom-call | flops 9663676416 | bytes 20447232 | tf_op jit(solution)/shard_map/inner_back/pallas_call | solution.py:413
  171.8 5.9 %feed_weights.6 = bf16[1536,768]{1,0:T(8,128)(2,1)} custom-call(bf16[1024,3072]{1,0:T(8,128)(2,1)} %get-tuple-element.198.left_ref, bf16[1024,768]{1,0:T(8,128)(2,1)} %get-tuple-element.171.low_ref.right_ref), custom_call_target="tpu_custom_call" | custom-call | flops 2415919104 | bytes 5505024 | tf_op jit(solution)/shard_map/feed_weights/pallas_call | solution.py:438
  179.2 5.8 %feed_weights.7 = bf16[1536,768]{1,0:T(8,128)(2,1)} custom-call(bf16[1024,3072]{1,0:T(8,128)(2,1)} %get-tuple-element.198.left_ref, bf16[1024,768]{1,0:T(8,128)(2,1)} %get-tuple-element.171.low_ref.right_ref), custom_call_target="tpu_custom_call" | custom-call | flops 2415919104 | bytes 5505024 | tf_op jit(solution)/shard_map/feed_weights/pallas_call | solution.py:438
  184.9 2.2 add_convert_fusion.5
  190.4 7.9 %middle_back.1 = (f32[1024,768]{1,0:T(8,128)}, bf16[1024,768]{1,0:T(8,128)(2,1)}, bf16[1024,768]{1,0:T(8,128)(2,1)}, f32[8,768]{1,0:T(8,128)}) custom-call(f32[8,768]{1,0:T(8,128)} %stack.112.vec_ref, f32[1024,768]{1,0:T(8,128)} %get-tuple-element.200.hid_ref, f32[1024,768]{1,0:T(8,128)} %get-tuple-element.179.n_ref, f32[1024,128]{1,0:T(8,128)} %get-tuple-element.201.s_ref, ...), custom_call_target="tpu_custom_call" | custom-call | flops 1207959552 | bytes 12582912 | tf_op jit(solution)/shard_map/middle_back/pallas_call | solution.py:462
  207.9 3.0 collective-permute-start.35
  213.0 22.9 %attend_back.1 = (bf16[3,1024,768]{2,1,0:T(8,128)(2,1)}, f32[2,2,768]{2,1,0:T(2,128)}) custom-call(s32[2]{0:T(128)} %length_ref.9, bf16[3,1024,768]{2,1,0:T(8,128)(2,1)} %get-tuple-element.161.q_ref.k_ref.v_ref, bf16[3,1024,768]{2,1,0:T(8,128)(2,1)} %get-tuple-element.161.q_ref.k_ref.v_ref, bf16[3,1024,768]{2,1,0:T(8,128)(2,1)} %get-tuple-element.161.q_ref.k_ref.v_ref, ...), custom_call_target="tpu_custom_call" | custom-call | flops 8053063680 | bytes 12582912 | tf_op jit(solution)/shard_map/attend_back/pallas_call | solution.py:192
  242.9 13.0 %attn_weights.1 = (bf16[4,4,96,768]{3,2,1,0:T(8,128)(2,1)}, bf16[4,4,96,768]{3,2,1,0:T(8,128)(2,1)}) custom-call(s32[3]{0:T(128)} %pad_add_fusion.table_ref, bf16[3,1024,768]{2,1,0:T(8,128)(2,1)} %get-tuple-element.263.qkv_ref, bf16[1024,768]{1,0:T(8,128)(2,1)} %get-tuple-element.236.low_ref, bf16[1024,768]{1,0:T(8,128)(2,1)} %token_ref.5, ...), custom_call_target="tpu_custom_call" | custom-call | flops 4831838208 | bytes 11010048 | tf_op jit(solution)/shard_map/attn_weights/pallas_call | solution.py:507
  256.0 3.0 collective-permute-done.39
  260.5 3.4 %collective-permute-done.44 = bf16[1536,768]{1,0:T(8,128)(2,1)S(1)} collective-permute-done((bf16[1536,768]{1,0:T(8,128)(2,1)}, bf16[1536,768]{1,0:T(8,128)(2,1)S(1)}, u32[]{:S(2)}, u32[]{:S(2)}) %collective-permute-start.44) | collective-permute-done | bytes 2359328 | tf_op jit(solution)/shard_map/ppermute | solution.py:621
  269.6 3.3 %collective-permute-done.46 = bf16[96,768]{1,0:T(8,128)(2,1)S(1)} collective-permute-done((bf16[96,768]{1,0:T(8,128)(2,1)S(1)}, bf16[96,768]{1,0:T(8,128)(2,1)S(1)}, u32[]{:S(2)}, u32[]{:S(2)}) %collective-permute-start.46) | collective-permute-done | bytes 147488 | tf_op jit(solution)/shard_map/ppermute | solution.py:621
  272.9 3.2 collective-permute-done.47
  286.5 8.4 %input_back.1 = bf16[1024,768]{1,0:T(8,128)(2,1)} custom-call(bf16[3,1024,768]{2,1,0:T(8,128)(2,1)} %get-tuple-element.263.qkv_ref, bf16[3072,768]{1,0:T(8,128)(2,1)} %get-tuple-element.170.weight_ref, f32[1024,768]{1,0:T(8,128)} %get-tuple-element.264.grad_ref), custom_call_target="tpu_custom_call" | custom-call | flops 3623878656 | bytes 12976128 | tf_op jit(solution)/shard_map/input_back/pallas_call | solution.py:541
  295.0 2.5 collective-permute-done.50
  304.3 2.1 collective-permute-start.57
  306.4 2.3 collective-permute-start.55
  310.6 2.1 collective-permute-done.57
  312.7 5.4 %collective-permute-done.56 = bf16[96,768]{1,0:T(8,128)(2,1)S(1)} collective-permute-done((bf16[96,768]{1,0:T(8,128)(2,1)S(1)}, bf16[96,768]{1,0:T(8,128)(2,1)S(1)}, u32[]{:S(2)}, u32[]{:S(2)}) %collective-permute-start.56) | collective-permute-done | bytes 147488 | tf_op jit(solution)/shard_map/ppermute | solution.py:621
  (298 shorter events, 102.4 us)
Async XLA Ops:
  8.1 13.5 %collective-permute-start.1 = (bf16[104,768]{1,0:T(8,128)(2,1)S(1)}, bf16[104,768]{1,0:T(8,128)(2,1)S(1)}, u32[]{:S(2)}, u32[]{:S(2)}) collective-permute-start(bf16[104,768]{1,0:T(8,128)(2,1)S(1)} %pad_maximum_fusion.12), channel_id=1, source_target_pairs={{0,4},{1,5},{2,6},{3,7},{4,0},{5,1},{6,2},{7,3},{8,12},{9,13},{10,... | collective-permute-start | bytes 479240 | tf_op jit(solution)/shard_map/ppermute | solution.py:621
  8.1 13.5 %collective-permute-start = (bf16[104,768]{1,0:T(8,128)(2,1)S(1)}, bf16[104,768]{1,0:T(8,128)(2,1)S(1)}, u32[]{:S(2)}, u32[]{:S(2)}) collective-permute-start(bf16[104,768]{1,0:T(8,128)(2,1)S(1)} %pad_maximum_fusion.12), channel_id=1, source_target_pairs={{0,2},{1,3},{2,0},{3,1},{4,6},{5,7},{6,4},{7,5},{8,10},{9,11},{10,... | collective-permute-start | bytes 479240 | tf_op jit(solution)/shard_map/ppermute | solution.py:621
  22.5 15.4 %collective-permute-start.4 = (bf16[384,768]{1,0:T(8,128)(2,1)S(1)}, bf16[384,768]{1,0:T(8,128)(2,1)}, u32[]{:S(2)}, u32[]{:S(2)}) collective-permute-start(bf16[384,768]{1,0:T(8,128)(2,1)S(1)} %pad_maximum_fusion.refs_0_), channel_id=1, source_target_pairs={{0,16},{1,17},{2,18},{3,19},{4,20},{5,21},{6,22},{7,23},{8,24},{9,... | collective-permute-start | bytes 1769480 | tf_op jit(solution)/shard_map/ppermute | solution.py:621
  24.1 15.1 %collective-permute-start.3 = (bf16[384,768]{1,0:T(8,128)(2,1)S(1)}, bf16[384,768]{1,0:T(8,128)(2,1)}, u32[]{:S(2)}, u32[]{:S(2)}) collective-permute-start(bf16[384,768]{1,0:T(8,128)(2,1)S(1)} %pad_maximum_fusion.refs_0_), channel_id=1, source_target_pairs={{0,8},{1,9},{2,10},{3,11},{4,12},{5,13},{6,14},{7,15},{8,0},{9,1},... | collective-permute-start | bytes 1769480 | tf_op jit(solution)/shard_map/ppermute | solution.py:621
  26.0 15.8 %collective-permute-start.15 = (bf16[192,768]{1,0:T(8,128)(2,1)S(1)}, bf16[192,768]{1,0:T(8,128)(2,1)S(1)}, u32[]{:S(2)}, u32[]{:S(2)}) collective-permute-start(bf16[192,768]{1,0:T(8,128)(2,1)S(1)} %pad_maximum_fusion.10), channel_id=1, source_target_pairs={{0,6},{1,7},{2,4},{3,5},{4,2},{5,3},{6,0},{7,1},{8,14},{9,15},{10,... | collective-permute-start | bytes 884744 | tf_op jit(solution)/shard_map/ppermute | solution.py:621
  28.5 24.0 %collective-permute-start.14 = (bf16[192,768]{1,0:T(8,128)(2,1)S(1)}, bf16[192,768]{1,0:T(8,128)(2,1)S(1)}, u32[]{:S(2)}, u32[]{:S(2)}) collective-permute-start(bf16[192,768]{1,0:T(8,128)(2,1)S(1)} %pad_maximum_fusion.10), channel_id=1, source_target_pairs={{0,4},{1,5},{2,6},{3,7},{4,0},{5,1},{6,2},{7,3},{8,12},{9,13},{10,... | collective-permute-start | bytes 884744 | tf_op jit(solution)/shard_map/ppermute | solution.py:621
  28.5 24.6 %collective-permute-start.13 = (bf16[192,768]{1,0:T(8,128)(2,1)S(1)}, bf16[192,768]{1,0:T(8,128)(2,1)S(1)}, u32[]{:S(2)}, u32[]{:S(2)}) collective-permute-start(bf16[192,768]{1,0:T(8,128)(2,1)S(1)} %pad_maximum_fusion.10), channel_id=1, source_target_pairs={{0,2},{1,3},{2,0},{3,1},{4,6},{5,7},{6,4},{7,5},{8,10},{9,11},{10,... | collective-permute-start | bytes 884744 | tf_op jit(solution)/shard_map/ppermute | solution.py:621
  40.2 24.3 %collective-permute-start.10 = (bf16[384,768]{1,0:T(8,128)(2,1)}, bf16[384,768]{1,0:T(8,128)(2,1)}, u32[]{:S(2)}, u32[]{:S(2)}) collective-permute-start(bf16[384,768]{1,0:T(8,128)(2,1)} %collective-permute-done.4.refs_2_), channel_id=1, source_target_pairs={{0,1},{1,0},{2,3},{3,2},{4,5},{5,4},{6,7},{7,6},{8,9},{9,8},{10,11... | collective-permute-start | bytes 1769480 | tf_op jit(solution)/shard_map/ppermute | solution.py:621
  41.3 23.2 %collective-permute-start.9 = (bf16[384,768]{1,0:T(8,128)(2,1)}, bf16[384,768]{1,0:T(8,128)(2,1)}, u32[]{:S(2)}, u32[]{:S(2)}) collective-permute-start(bf16[384,768]{1,0:T(8,128)(2,1)} %collective-permute-done.3.refs_1_), channel_id=1, source_target_pairs={{0,1},{1,0},{2,3},{3,2},{4,5},{5,4},{6,7},{7,6},{8,9},{9,8},{10,11... | collective-permute-start | bytes 1769480 | tf_op jit(solution)/shard_map/ppermute | solution.py:621
  41.9 16.0 %collective-permute-start.7 = (bf16[192,768]{1,0:T(8,128)(2,1)S(1)}, bf16[192,768]{1,0:T(8,128)(2,1)S(1)}, u32[]{:S(2)}, u32[]{:S(2)}) collective-permute-start(bf16[192,768]{1,0:T(8,128)(2,1)S(1)} %slice.316), channel_id=1, source_target_pairs={{0,16},{1,17},{2,18},{3,19},{4,20},{5,21},{6,22},{7,23},{8,24},{9,... | collective-permute-start | bytes 884744 | tf_op jit(solution)/shard_map/ppermute | solution.py:621
  60.1 30.4 %collective-permute-start.17 = (bf16[768,768]{1,0:T(8,128)(2,1)}, bf16[768,768]{1,0:T(8,128)(2,1)S(1)}, u32[]{:S(2)}, u32[]{:S(2)}) collective-permute-start(bf16[768,768]{1,0:T(8,128)(2,1)} %slice_dynamic-update-slice_fusion.refs_0_.refs_8_), channel_id=1, source_target_pairs={{0,16},{1,17},{2,18},{3,19},{4,20},{5,21},{6,22},{7,23},{8,24},{9,... | collective-permute-start | bytes 3538952 | tf_op jit(solution)/shard_map/ppermute | solution.py:621
  61.0 29.5 %collective-permute-start.16 = (bf16[768,768]{1,0:T(8,128)(2,1)}, bf16[768,768]{1,0:T(8,128)(2,1)S(1)}, u32[]{:S(2)}, u32[]{:S(2)}) collective-permute-start(bf16[768,768]{1,0:T(8,128)(2,1)} %slice_dynamic-update-slice_fusion.refs_0_.refs_8_), channel_id=1, source_target_pairs={{0,8},{1,9},{2,10},{3,11},{4,12},{5,13},{6,14},{7,15},{8,0},{9,1},... | collective-permute-start | bytes 3538952 | tf_op jit(solution)/shard_map/ppermute | solution.py:621
  64.4 36.8 %collective-permute-start.18 = (bf16[768,768]{1,0:T(8,128)(2,1)}, bf16[768,768]{1,0:T(8,128)(2,1)}, u32[]{:S(2)}, u32[]{:S(2)}) collective-permute-start(bf16[768,768]{1,0:T(8,128)(2,1)} %slice_dynamic-update-slice_fusion.refs_0_.refs_8_), channel_id=1, source_target_pairs={{0,1},{1,0},{2,3},{3,2},{4,5},{5,4},{6,7},{7,6},{8,9},{9,8},{10,11... | collective-permute-start | bytes 3538952 | tf_op jit(solution)/shard_map/ppermute | solution.py:621
  92.9 19.0 %collective-permute-start.22 = (bf16[384,768]{1,0:T(8,128)(2,1)}, bf16[384,768]{1,0:T(8,128)(2,1)S(1)}, u32[]{:S(2)}, u32[]{:S(2)}) collective-permute-start(bf16[384,768]{1,0:T(8,128)(2,1)} %slice.327), channel_id=1, source_target_pairs={{0,8},{1,9},{2,10},{3,11},{4,12},{5,13},{6,14},{7,15},{8,0},{9,1},... | collective-permute-start | bytes 1769480 | tf_op jit(solution)/shard_map/ppermute | solution.py:621
  93.2 18.7 %collective-permute-start.21 = (bf16[384,768]{1,0:T(8,128)(2,1)}, bf16[384,768]{1,0:T(8,128)(2,1)S(1)}, u32[]{:S(2)}, u32[]{:S(2)}) collective-permute-start(bf16[384,768]{1,0:T(8,128)(2,1)} %slice.326), channel_id=1, source_target_pairs={{0,16},{1,17},{2,18},{3,19},{4,20},{5,21},{6,22},{7,23},{8,24},{9,... | collective-permute-start | bytes 1769480 | tf_op jit(solution)/shard_map/ppermute | solution.py:621
  148.7 20.5 %collective-permute-start.26 = (bf16[192,768]{1,0:T(8,128)(2,1)S(1)}, bf16[192,768]{1,0:T(8,128)(2,1)S(1)}, u32[]{:S(2)}, u32[]{:S(2)}) collective-permute-start(bf16[192,768]{1,0:T(8,128)(2,1)S(1)} %get-tuple-element.190), channel_id=1, source_target_pairs={{0,16},{1,17},{2,18},{3,19},{4,20},{5,21},{6,22},{7,23},{8,24},{9,... | collective-permute-start | bytes 884744 | tf_op jit(solution)/shard_map/ppermute | solution.py:621
  149.7 19.5 %collective-permute-start.27 = (bf16[192,768]{1,0:T(8,128)(2,1)S(1)}, bf16[192,768]{1,0:T(8,128)(2,1)S(1)}, u32[]{:S(2)}, u32[]{:S(2)}) collective-permute-start(bf16[192,768]{1,0:T(8,128)(2,1)S(1)} %get-tuple-element.191), channel_id=1, source_target_pairs={{0,8},{1,9},{2,10},{3,11},{4,12},{5,13},{6,14},{7,15},{8,0},{9,1},... | collective-permute-start | bytes 884744 | tf_op jit(solution)/shard_map/ppermute | solution.py:621
  177.7 20.6 %collective-permute-start.31 = (bf16[384,768]{1,0:T(8,128)(2,1)S(1)}, bf16[384,768]{1,0:T(8,128)(2,1)}, u32[]{:S(2)}, u32[]{:S(2)}) collective-permute-start(bf16[384,768]{1,0:T(8,128)(2,1)S(1)} %copy-done.13), channel_id=1, source_target_pairs={{0,8},{1,9},{2,10},{3,11},{4,12},{5,13},{6,14},{7,15},{8,0},{9,1},... | collective-permute-start | bytes 1769480 | tf_op jit(solution)/shard_map/ppermute | solution.py:621
  178.0 20.3 %collective-permute-start.32 = (bf16[384,768]{1,0:T(8,128)(2,1)S(1)}, bf16[384,768]{1,0:T(8,128)(2,1)}, u32[]{:S(2)}, u32[]{:S(2)}) collective-permute-start(bf16[384,768]{1,0:T(8,128)(2,1)S(1)} %pad_maximum_fusion.2), channel_id=1, source_target_pairs={{0,16},{1,17},{2,18},{3,19},{4,20},{5,21},{6,22},{7,23},{8,24},{9,... | collective-permute-start | bytes 1769480 | tf_op jit(solution)/shard_map/ppermute | solution.py:621
  206.5 31.0 %collective-permute-start.37 = (bf16[96,768]{1,0:T(8,128)(2,1)S(1)}, bf16[96,768]{1,0:T(8,128)(2,1)S(1)}, u32[]{:S(2)}, u32[]{:S(2)}) collective-permute-start(bf16[96,768]{1,0:T(8,128)(2,1)S(1)} %get-tuple-element.315), channel_id=1, source_target_pairs={{0,6},{1,7},{2,4},{3,5},{4,2},{5,3},{6,0},{7,1},{8,14},{9,15},{10,... | collective-permute-start | bytes 442376 | tf_op jit(solution)/shard_map/ppermute | solution.py:621
  207.9 29.6 %collective-permute-start.36 = (bf16[96,768]{1,0:T(8,128)(2,1)S(1)}, bf16[96,768]{1,0:T(8,128)(2,1)S(1)}, u32[]{:S(2)}, u32[]{:S(2)}) collective-permute-start(bf16[96,768]{1,0:T(8,128)(2,1)S(1)} %get-tuple-element.316), channel_id=1, source_target_pairs={{0,4},{1,5},{2,6},{3,7},{4,0},{5,1},{6,2},{7,3},{8,12},{9,13},{10,... | collective-permute-start | bytes 442376 | tf_op jit(solution)/shard_map/ppermute | solution.py:621
  207.9 29.6 %collective-permute-start.35 = (bf16[96,768]{1,0:T(8,128)(2,1)S(1)}, bf16[96,768]{1,0:T(8,128)(2,1)S(1)}, u32[]{:S(2)}, u32[]{:S(2)}) collective-permute-start(bf16[96,768]{1,0:T(8,128)(2,1)S(1)} %get-tuple-element.317), channel_id=1, source_target_pairs={{0,2},{1,3},{2,0},{3,1},{4,6},{5,7},{6,4},{7,5},{8,10},{9,11},{10,... | collective-permute-start | bytes 442376 | tf_op jit(solution)/shard_map/ppermute | solution.py:621
  211.0 26.6 %collective-permute-start.33 = (bf16[384,768]{1,0:T(8,128)(2,1)}, bf16[384,768]{1,0:T(8,128)(2,1)S(1)}, u32[]{:S(2)}, u32[]{:S(2)}) collective-permute-start(bf16[384,768]{1,0:T(8,128)(2,1)} %pad_maximum_fusion.3), channel_id=1, source_target_pairs={{0,8},{1,9},{2,10},{3,11},{4,12},{5,13},{6,14},{7,15},{8,0},{9,1},... | collective-permute-start | bytes 1769480 | tf_op jit(solution)/shard_map/ppermute | solution.py:621
  212.7 24.9 %collective-permute-start.34 = (bf16[384,768]{1,0:T(8,128)(2,1)S(1)}, bf16[384,768]{1,0:T(8,128)(2,1)S(1)}, u32[]{:S(2)}, u32[]{:S(2)}) collective-permute-start(bf16[384,768]{1,0:T(8,128)(2,1)S(1)} %pad_maximum_fusion.4), channel_id=1, source_target_pairs={{0,16},{1,17},{2,18},{3,19},{4,20},{5,21},{6,22},{7,23},{8,24},{9,... | collective-permute-start | bytes 1769480 | tf_op jit(solution)/shard_map/ppermute | solution.py:621
  239.2 16.7 %collective-permute-start.42 = (bf16[96,768]{1,0:T(8,128)(2,1)S(1)}, bf16[96,768]{1,0:T(8,128)(2,1)S(1)}, u32[]{:S(2)}, u32[]{:S(2)}) collective-permute-start(bf16[96,768]{1,0:T(8,128)(2,1)S(1)} %add_convert_fusion.10), channel_id=1, source_target_pairs={{0,24},{1,25},{2,26},{3,27},{4,28},{5,29},{6,30},{7,31},{8,16},{9,... | collective-permute-start | bytes 442376 | tf_op jit(solution)/shard_map/ppermute | solution.py:621
  240.8 15.1 %collective-permute-start.41 = (bf16[96,768]{1,0:T(8,128)(2,1)S(1)}, bf16[96,768]{1,0:T(8,128)(2,1)S(1)}, u32[]{:S(2)}, u32[]{:S(2)}) collective-permute-start(bf16[96,768]{1,0:T(8,128)(2,1)S(1)} %add_convert_fusion.10), channel_id=1, source_target_pairs={{0,16},{1,17},{2,18},{3,19},{4,20},{5,21},{6,22},{7,23},{8,24},{9,... | collective-permute-start | bytes 442376 | tf_op jit(solution)/shard_map/ppermute | solution.py:621
  241.9 14.0 %collective-permute-start.40 = (bf16[96,768]{1,0:T(8,128)(2,1)S(1)}, bf16[96,768]{1,0:T(8,128)(2,1)S(1)}, u32[]{:S(2)}, u32[]{:S(2)}) collective-permute-start(bf16[96,768]{1,0:T(8,128)(2,1)S(1)} %add_convert_fusion.10), channel_id=1, source_target_pairs={{0,8},{1,9},{2,10},{3,11},{4,12},{5,13},{6,14},{7,15},{8,0},{9,1},... | collective-permute-start | bytes 442376 | tf_op jit(solution)/shard_map/ppermute | solution.py:621
  242.8 13.1 %collective-permute-start.38 = (f32[88,128]{1,0:T(8,128)S(1)}, f32[88,128]{1,0:T(8,128)S(1)}, u32[]{:S(2)}, u32[]{:S(2)}) collective-permute-start(f32[88,128]{1,0:T(8,128)S(1)} %copy-done.14), channel_id=1, source_target_pairs={{0,1},{1,0},{2,3},{3,2},{4,5},{5,4},{6,7},{7,6},{8,9},{9,8},{10,11... | collective-permute-start | bytes 135176 | tf_op jit(solution)/shard_map/ppermute | solution.py:621
  242.9 16.1 %collective-permute-start.39 = (bf16[192,768]{1,0:T(8,128)(2,1)S(1)}, bf16[192,768]{1,0:T(8,128)(2,1)S(1)}, u32[]{:S(2)}, u32[]{:S(2)}) collective-permute-start(bf16[192,768]{1,0:T(8,128)(2,1)S(1)} %get-tuple-element.313), channel_id=1, source_target_pairs={{0,4},{1,5},{2,6},{3,7},{4,0},{5,1},{6,2},{7,3},{8,12},{9,13},{10,... | collective-permute-start | bytes 884744 | tf_op jit(solution)/shard_map/ppermute | solution.py:621
  280.1 17.5 %collective-permute-start.51 = (bf16[384,768]{1,0:T(8,128)(2,1)}, bf16[384,768]{1,0:T(8,128)(2,1)}, u32[]{:S(2)}, u32[]{:S(2)}) collective-permute-start(bf16[384,768]{1,0:T(8,128)(2,1)} %pad_maximum_fusion.5), channel_id=1, source_target_pairs={{0,8},{1,9},{2,10},{3,11},{4,12},{5,13},{6,14},{7,15},{8,0},{9,1},... | collective-permute-start | bytes 1769480 | tf_op jit(solution)/shard_map/ppermute | solution.py:621
  281.0 16.5 %collective-permute-start.52 = (bf16[384,768]{1,0:T(8,128)(2,1)S(1)}, bf16[384,768]{1,0:T(8,128)(2,1)}, u32[]{:S(2)}, u32[]{:S(2)}) collective-permute-start(bf16[384,768]{1,0:T(8,128)(2,1)S(1)} %pad_maximum_fusion.6), channel_id=1, source_target_pairs={{0,16},{1,17},{2,18},{3,19},{4,20},{5,21},{6,22},{7,23},{8,24},{9,... | collective-permute-start | bytes 1769480 | tf_op jit(solution)/shard_map/ppermute | solution.py:621
  302.8 15.3 %collective-permute-start.54 = (bf16[192,768]{1,0:T(8,128)(2,1)S(1)}, bf16[192,768]{1,0:T(8,128)(2,1)S(1)}, u32[]{:S(2)}, u32[]{:S(2)}) collective-permute-start(bf16[192,768]{1,0:T(8,128)(2,1)S(1)} %pad_maximum_fusion.11), channel_id=1, source_target_pairs={{0,16},{1,17},{2,18},{3,19},{4,20},{5,21},{6,22},{7,23},{8,24},{9,... | collective-permute-start | bytes 884744 | tf_op jit(solution)/shard_map/ppermute | solution.py:621
  (55 other events, 380.8 us)

commit v6 on v5

--- a/solution.py
+++ b/solution.py
@@ -281,14 +281,14 @@
 
 def two_by_two(pieces):
     for first, second in zip(pieces[::2], pieces[1::2]):
-        yield jnp.concatenate([first[...], second[...]], axis=0)
+        yield jnp.concatenate([rows_of(first), rows_of(second)], axis=0)
 
 
 def expand_kernel(bias_ref, low_ref, *refs, groups):
     pieces, (gelu_ref, slope_ref) = refs[:-2], refs[-2:]
     low = low_ref[...]
     for first, last, at in groups:
-        weights = jnp.concatenate([piece[...] for piece in pieces[first:last]], axis=0)
+        weights = jnp.concatenate([rows_of(piece) for piece in pieces[first:last]], axis=0)
         span = slice(at, at + weights.shape[0])
         gelu, slope = gelu_parts(dot_nt(low, weights) + bias_ref[0:1, span])
         gelu_ref[:, span] = gelu.astype(BF)
@@ -296,15 +296,21 @@
 
 
 def expand_last_kernel(bias_ref, low_ref, near_ref, far_ref, _, __, gelu_ref, slope_ref):
-    weights = jnp.where(pl.program_id(1) == 0, near_ref[...], far_ref[...])
+    weights = jnp.where(pl.program_id(1) == 0, rows_of(near_ref), rows_of(far_ref))
     gelu, slope = gelu_parts(dot_nt(low_ref[...], weights) + bias_ref[...])
     gelu_ref[...] = gelu.astype(BF)
     slope_ref[...] = slope.astype(BF)
 
 
 def picked(piece, width):
-    array, start, size = piece
-    return pl.BlockSpec((size, width), lambda *_, at=start // size: (at, 0))
+    array, at, rows = piece
+    if array.ndim == 3:
+        return pl.BlockSpec((4, rows // 4, width), lambda *_: (0, at, 0))
+    return pl.BlockSpec((rows, width), lambda *_: (at, 0))
+
+
+def rows_of(piece):
+    return piece[...].reshape(-1, piece.shape[-1])
 
 
 def expand_call(low, bias, pieces, groups):
@@ -753,8 +759,8 @@
     else:
         rows, attvec, feedvec = gather_plain(attention, attvector, expand, contract, feedvector)
         attn_pieces, attn_starts = [rows[0]], [0]
-        expands = [(rows[1], i * quad, quad) for i in range(8)]
-        contracts = [(rows[2], i * quad, quad) for i in range(8)]
+        expands = [(rows[1], i, quad) for i in range(8)]
+        contracts = [(rows[2], i, quad) for i in range(8)]
 
     def row_of(vector, i, start=0):
         return vector[start + i * width : start + (i + 1) * width]
@@ -774,7 +780,7 @@
         attn_far = [attn_far] + [links.swap(part, core=1) for part in attn_near[1:]]
         attn_pieces = attn_near + attn_far
         attn_starts = [0, 4, 8, 12, 14, 16, 20, 24, 28, 30]
-        feed_own = jnp.concatenate([part[:size] for part in feed_z] + [part[size:] for part in feed_z], axis=0)
+        feed_own = jnp.stack(feed_z)
         feed_own, *_ = tie(feed_own, *attn_three)
         feed_one, feed_two = spread_plane(links, feed_own)
         feed_far = [links.swap(feed_own, core=1)]
@@ -784,7 +790,7 @@
     context, logs = attend(projected, lengths, positions)
     if links.paired:
         context, feed_one, feed_two = tie(context, feed_one, feed_two)
-        feed_three = spread_corner(links, feed_one, feed_two)
+        feed_three = links.swap(feed_one[:, :size], dp=2), links.swap(feed_two[:, size:], dp=1)
         feed_far += [links.swap(feed_one, core=1), links.swap(feed_two, core=1)]
     normed_one, inverse_one, hidden_low, sum_middle = middle(
         lengths, vec_rows, context, attn_rows, tokens, positions
@@ -798,8 +804,8 @@
         last = [(feed_three[0], 0, quad), (far_three[0], 0, quad)]
         gelu, slope = expand_last(hidden_low, inner_bias, last, gelu, slope)
         expands = expands[:3] + last[:1] + expands[3:] + last[1:]
-        contracts = [(part, quad, quad) for part in feed_near] + [(feed_three[1], 0, quad)]
-        contracts += [(part, quad, quad) for part in feed_far] + [(far_three[1], 0, quad)]
+        contracts = [(part, 1, quad) for part in feed_near] + [(feed_three[1], 0, quad)]
+        contracts += [(part, 1, quad) for part in feed_far] + [(far_three[1], 0, quad)]
     else:
         groups = [(i, i + 2, i * quad) for i in range(0, 8, 2)]
         gelu, slope = expand_call(hidden_low, inner_bias, expands, groups)

time: 330 us -> 324 us (0.982)
  local copies, waits for them, and re-layouts: 20.8 us -> 16.9 us
    unnamed x63 -> x56, local copies, waits for them, and re-layouts: 10.7 us -> 6.67 us
  transfers between devices with their start and end apart: 61 -> 61, of which waited for: 20 -> 18; matrix products, arithmetic and copies ran while one was open for 7% -> 6% of each run, Pallas kernels for 40% -> 41%
where the time goes in v6:
time: 324 us; the launch traced here: 323 us
  Pallas kernels  157 us (48%)
  starting transfers between devices  59.5 us (18%)
  waiting for transfers between devices  57.2 us (18%)
  other arithmetic  29.4 us (9%)
  local copies, waits for them, and re-layouts  16.9 us (5%)
    ppermute x61, starting transfers between devices, swap(): return lax.ppermute(values, AXES, pairs)  59.5 us
    ppermute x61, waiting for transfers between devices, swap(): return lax.ppermute(values, AXES, pairs)  57.2 us
    pallas_call x4, Pallas kernels, feed_weights(): call(feed_weights_kernel, 'feed_weights', 2 * count * width * rows, count...  23.3 us
    pallas_call x1, Pallas kernels, attend_back(): call(attend_back_kernel, 'attend_back', 2 * flops, 16 * count * width, gr...  22.9 us
    pallas_call x1, Pallas kernels, inner_back(): call(functools.partial(inner_kernel, count=len(contracts)), 'inner_back',...  17.5 us
    pallas_call x1, Pallas kernels, attend(): call(attend_kernel, 'attend', 2 * flops, 8 * count * width, grid_spec=plt...  15.4 us
    pallas_call x1, Pallas kernels, contract_call(): call(functools.partial(contract_kernel, positions=positions), 'contract_n...  13.2 us
    pallas_call x1, Pallas kernels, attn_weights(): call(attn_weights_kernel, 'attn_weights', 8 * 2 * count * width * half, c...  13 us
  transfers between devices with their start and end apart: 61, of which 18 were waited for; matrix products, arithmetic and copies ran while one was open for 6% of the time, Pallas kernels for 41%

profile of v6, /device:TPU:0, one launch (start us, length us, event | category | flops | bytes accessed | tf_op | source)
XLA Modules:
  0.0 322.7 jit_solution(5610399395678285323)
XLA Ops:
  3.0 5.1 %collective-permute-start.2 = (bf16[104,768]{1,0:T(8,128)(2,1)S(1)}, bf16[104,768]{1,0:T(8,128)(2,1)S(1)}, u32[]{:S(2)}, u32[]{:S(2)}) collective-permute-start(bf16[104,768]{1,0:T(8,128)(2,1)S(1)} %pad_maximum_fusion.13), channel_id=1, source_target_pairs={{0,6},{1,7},{2,4},{3,5},{4,2},{5,3},{6,0},{7,1},{8,14},{9,15},{10,... | collective-permute-start | bytes 479240 | tf_op jit(solution)/shard_map/ppermute | solution.py:627
  9.0 4.2 %collective-permute-done.2 = bf16[104,768]{1,0:T(8,128)(2,1)S(1)} collective-permute-done((bf16[104,768]{1,0:T(8,128)(2,1)S(1)}, bf16[104,768]{1,0:T(8,128)(2,1)S(1)}, u32[]{:S(2)}, u32[]{:S(2)}) %collective-permute-start.2) | collective-permute-done | bytes 159776 | tf_op jit(solution)/shard_map/ppermute | solution.py:627
  13.2 8.5 %collective-permute-done.1 = bf16[104,768]{1,0:T(8,128)(2,1)S(1)} collective-permute-done((bf16[104,768]{1,0:T(8,128)(2,1)S(1)}, bf16[104,768]{1,0:T(8,128)(2,1)S(1)}, u32[]{:S(2)}, u32[]{:S(2)}) %collective-permute-start.1) | collective-permute-done | bytes 159776 | tf_op jit(solution)/shard_map/ppermute | solution.py:627
  26.3 2.5 collective-permute-start.15
  33.1 4.9 %collective-permute-done.4.refs_2_ = bf16[384,768]{1,0:T(8,128)(2,1)} collective-permute-done((bf16[384,768]{1,0:T(8,128)(2,1)S(1)}, bf16[384,768]{1,0:T(8,128)(2,1)}, u32[]{:S(2)}, u32[]{:S(2)}) %collective-permute-start.4) | collective-permute-done | bytes 589856 | tf_op jit(solution)/shard_map/ppermute | solution.py:627
  43.4 9.4 %collective-permute-done.14 = bf16[192,768]{1,0:T(8,128)(2,1)S(1)} collective-permute-done((bf16[192,768]{1,0:T(8,128)(2,1)S(1)}, bf16[192,768]{1,0:T(8,128)(2,1)S(1)}, u32[]{:S(2)}, u32[]{:S(2)}) %collective-permute-start.14) | collective-permute-done | bytes 294944 | tf_op jit(solution)/shard_map/ppermute | solution.py:627
  58.5 10.0 %project.1 = (bf16[3,1024,768]{2,1,0:T(8,128)(2,1)}, bf16[3072,768]{1,0:T(8,128)(2,1)}) custom-call(s32[32]{0:T(128)} %add.175.table_ref.place_ref, f32[2,768]{1,0:T(2,128)} %pad_maximum_fusion.16.bias_ref, bf16[1024,768]{1,0:T(8,128)(2,1)} %token_ref.5, bf16[384,768]{1,0:T(8,128)(2,1)} %copy-done.12, bf16[384,768]{1,0:T(8,128)(2,1)} %collective-permute-done.3.refs_1_, ...), custom_call_target="tpu_custom_call" | custom-call | flops 3623878656 | bytes 15728640 | tf_op jit(solution)/shard_map/project/pallas_call | solution.py:73
  68.5 15.4 %attend.1 = (bf16[1024,768]{1,0:T(8,128)(2,1)}, f32[2,6,2,512]{3,2,1,0:T(2,128)}) custom-call(s32[2]{0:T(128)} %length_ref.9, bf16[3,1024,768]{2,1,0:T(8,128)(2,1)} %get-tuple-element.161.q_ref.k_ref.v_ref, bf16[3,1024,768]{2,1,0:T(8,128)(2,1)} %get-tuple-element.161.q_ref.k_ref.v_ref, bf16[3,1024,768]{2,1,0:T(8,128)(2,1)} %get-tuple-element.161.q_ref.k_ref.v_ref), custom_call_target="tpu_custom_call" | custom-call | flops 3221225472 | bytes 6291456 | tf_op jit(solution)/shard_map/attend/pallas_call | solution.py:131
  89.2 6.9 %middle.1 = (f32[1024,768]{1,0:T(8,128)}, f32[1024,128]{1,0:T(8,128)}, bf16[1024,768]{1,0:T(8,128)(2,1)}, f32[8,768]{1,0:T(8,128)}) custom-call(s32[2]{0:T(128)} %length_ref.9, f32[8,768]{1,0:T(8,128)} %stack.127.vec_ref, bf16[1024,768]{1,0:T(8,128)(2,1)} %get-tuple-element.169.ctx_ref, bf16[3072,768]{1,0:T(8,128)(2,1)} %get-tuple-element.170.weight_ref, ...), custom_call_target="tpu_custom_call" | custom-call | flops 1207959552 | bytes 9437184 | tf_op jit(solution)/shard_map/middle/pallas_call | solution.py:259
  96.1 10.9 %expand_gelu.1 = (bf16[1024,3072]{1,0:T(8,128)(2,1)}, bf16[1024,3072]{1,0:T(8,128)(2,1)}) custom-call(f32[1,3072]{1,0:T(1,128)} %reshape_reshape.10.bias_ref, bf16[1024,768]{1,0:T(8,128)(2,1)} %get-tuple-element.171.low_ref.right_ref, bf16[4,192,768]{2,1,0:T(8,128)(2,1)} %copy-done.3, bf16[4,192,768]{2,1,0:T(8,128)(2,1)} %collective-permute-done.16.refs_1_.refs_9_, ...), custom_call_target="tpu_custom_call" | custom-call | flops 3623878656 | bytes 12582912 | tf_op jit(solution)/shard_map/expand_gelu/pallas_call | solution.py:320
  109.9 6.3 %expand_last.1 = (bf16[1024,3072]{1,0:T(8,128)(2,1)}, bf16[1024,3072]{1,0:T(8,128)(2,1)}) custom-call(f32[1,3072]{1,0:T(1,128)} %reshape_reshape.10.bias_ref, bf16[1024,768]{1,0:T(8,128)(2,1)} %get-tuple-element.171.low_ref.right_ref, bf16[4,96,768]{2,1,0:T(8,128)(2,1)} %copy-done.9, ...), custom_call_target="tpu_custom_call", output_to_operand_aliasing={{0}: (4, {}), {1}: (5, {})} | custom-call | flops 1207959552 | bytes 3145728 | tf_op jit(solution)/shard_map/expand_last/pallas_call | solution.py:338
  117.1 13.2 %contract_norm.1 = (bf16[1024,768]{1,0:T(8,128)(2,1)}, f32[1024,768]{1,0:T(8,128)}, bf16[1024,768]{1,0:T(8,128)(2,1)}, f32[8,768]{1,0:T(8,128)}) custom-call(s32[2]{0:T(128)} %length_ref.9, f32[8,768]{1,0:T(8,128)} %stack.127.vec_ref, bf16[1024,3072]{1,0:T(8,128)(2,1)} %get-tuple-element.184.gelu_ref.left_ref, f32[1024,768]{1,0:T(8,128)} %get-tuple-element.179.n_ref, ...), custom_call_target="tpu_custom_call" | custom-call | flops 4831838208 | bytes 17301504 | tf_op jit(solution)/shard_map/contract_norm/pallas_call | solution.py:380
  130.3 5.8 %feed_weights.4 = bf16[1536,768]{1,0:T(8,128)(2,1)} custom-call(bf16[1024,3072]{1,0:T(8,128)(2,1)} %get-tuple-element.184.gelu_ref.left_ref, bf16[1024,768]{1,0:T(8,128)(2,1)} %get-tuple-element.182.right_ref.low_ref), custom_call_target="tpu_custom_call" | custom-call | flops 2415919104 | bytes 5505024 | tf_op jit(solution)/shard_map/feed_weights/pallas_call | solution.py:444
  136.2 5.9 %feed_weights.5 = bf16[1536,768]{1,0:T(8,128)(2,1)} custom-call(bf16[1024,3072]{1,0:T(8,128)(2,1)} %get-tuple-element.184.gelu_ref.left_ref, bf16[1024,768]{1,0:T(8,128)(2,1)} %get-tuple-element.182.right_ref.low_ref), custom_call_target="tpu_custom_call" | custom-call | flops 2415919104 | bytes 5505024 | tf_op jit(solution)/shard_map/feed_weights/pallas_call | solution.py:444
  145.8 17.5 %inner_back.1 = (bf16[1024,3072]{1,0:T(8,128)(2,1)}, f32[1024,768]{1,0:T(8,128)}, f32[8,3072]{1,0:T(8,128)}) custom-call(bf16[1024,768]{1,0:T(8,128)(2,1)} %get-tuple-element.182.right_ref.low_ref, bf16[1024,3072]{1,0:T(8,128)(2,1)} %get-tuple-element.186.slope_ref, f32[1024,768]{1,0:T(8,128)} %get-tuple-element.187.grad_ref, ...), custom_call_target="tpu_custom_call" | custom-call | flops 9663676416 | bytes 20447232 | tf_op jit(solution)/shard_map/inner_back/pallas_call | solution.py:419
  165.9 5.9 %feed_weights.6 = bf16[1536,768]{1,0:T(8,128)(2,1)} custom-call(bf16[1024,3072]{1,0:T(8,128)(2,1)} %get-tuple-element.198.left_ref, bf16[1024,768]{1,0:T(8,128)(2,1)} %get-tuple-element.171.low_ref.right_ref), custom_call_target="tpu_custom_call" | custom-call | flops 2415919104 | bytes 5505024 | tf_op jit(solution)/shard_map/feed_weights/pallas_call | solution.py:444
  173.9 5.8 %feed_weights.7 = bf16[1536,768]{1,0:T(8,128)(2,1)} custom-call(bf16[1024,3072]{1,0:T(8,128)(2,1)} %get-tuple-element.198.left_ref, bf16[1024,768]{1,0:T(8,128)(2,1)} %get-tuple-element.171.low_ref.right_ref), custom_call_target="tpu_custom_call" | custom-call | flops 2415919104 | bytes 5505024 | tf_op jit(solution)/shard_map/feed_weights/pallas_call | solution.py:444
  179.6 2.2 add_convert_fusion.5
  184.4 7.9 %middle_back.1 = (f32[1024,768]{1,0:T(8,128)}, bf16[1024,768]{1,0:T(8,128)(2,1)}, bf16[1024,768]{1,0:T(8,128)(2,1)}, f32[8,768]{1,0:T(8,128)}) custom-call(f32[8,768]{1,0:T(8,128)} %stack.127.vec_ref, f32[1024,768]{1,0:T(8,128)} %get-tuple-element.200.hid_ref, f32[1024,768]{1,0:T(8,128)} %get-tuple-element.179.n_ref, f32[1024,128]{1,0:T(8,128)} %get-tuple-element.201.s_ref, ...), custom_call_target="tpu_custom_call" | custom-call | flops 1207959552 | bytes 12582912 | tf_op jit(solution)/shard_map/middle_back/pallas_call | solution.py:468
  202.3 3.0 collective-permute-start.35
  207.4 22.9 %attend_back.1 = (bf16[3,1024,768]{2,1,0:T(8,128)(2,1)}, f32[2,2,768]{2,1,0:T(2,128)}) custom-call(s32[2]{0:T(128)} %length_ref.9, bf16[3,1024,768]{2,1,0:T(8,128)(2,1)} %get-tuple-element.161.q_ref.k_ref.v_ref, bf16[3,1024,768]{2,1,0:T(8,128)(2,1)} %get-tuple-element.161.q_ref.k_ref.v_ref, bf16[3,1024,768]{2,1,0:T(8,128)(2,1)} %get-tuple-element.161.q_ref.k_ref.v_ref, ...), custom_call_target="tpu_custom_call" | custom-call | flops 8053063680 | bytes 12582912 | tf_op jit(solution)/shard_map/attend_back/pallas_call | solution.py:192
  237.4 13.0 %attn_weights.1 = (bf16[4,4,96,768]{3,2,1,0:T(8,128)(2,1)}, bf16[4,4,96,768]{3,2,1,0:T(8,128)(2,1)}) custom-call(s32[3]{0:T(128)} %pad_add_fusion.table_ref, bf16[3,1024,768]{2,1,0:T(8,128)(2,1)} %get-tuple-element.263.qkv_ref, bf16[1024,768]{1,0:T(8,128)(2,1)} %get-tuple-element.236.low_ref, bf16[1024,768]{1,0:T(8,128)(2,1)} %token_ref.5, ...), custom_call_target="tpu_custom_call" | custom-call | flops 4831838208 | bytes 11010048 | tf_op jit(solution)/shard_map/attn_weights/pallas_call | solution.py:513
  250.4 3.0 collective-permute-done.39
  255.2 3.1 collective-permute-done.44
  264.2 2.7 collective-permute-done.46
  266.9 3.4 %collective-permute-done.47 = bf16[192,768]{1,0:T(8,128)(2,1)S(1)} collective-permute-done((bf16[192,768]{1,0:T(8,128)(2,1)S(1)}, bf16[192,768]{1,0:T(8,128)(2,1)S(1)}, u32[]{:S(2)}, u32[]{:S(2)}) %collective-permute-start.47) | collective-permute-done | bytes 294944 | tf_op jit(solution)/shard_map/ppermute | solution.py:627
  280.6 8.4 %input_back.1 = bf16[1024,768]{1,0:T(8,128)(2,1)} custom-call(bf16[3,1024,768]{2,1,0:T(8,128)(2,1)} %get-tuple-element.263.qkv_ref, bf16[3072,768]{1,0:T(8,128)(2,1)} %get-tuple-element.170.weight_ref, f32[1024,768]{1,0:T(8,128)} %get-tuple-element.264.grad_ref), custom_call_target="tpu_custom_call" | custom-call | flops 3623878656 | bytes 12976128 | tf_op jit(solution)/shard_map/input_back/pallas_call | solution.py:547
  289.1 2.9 collective-permute-done.50
  298.3 2.1 collective-permute-start.57
  300.5 2.3 collective-permute-start.55
  302.8 2.7 collective-permute-done.53
  306.8 5.4 %collective-permute-done.56 = bf16[96,768]{1,0:T(8,128)(2,1)S(1)} collective-permute-done((bf16[96,768]{1,0:T(8,128)(2,1)S(1)}, bf16[96,768]{1,0:T(8,128)(2,1)S(1)}, u32[]{:S(2)}, u32[]{:S(2)}) %collective-permute-start.56) | collective-permute-done | bytes 147488 | tf_op jit(solution)/shard_map/ppermute | solution.py:627
  (291 shorter events, 97.3 us)
Async XLA Ops:
  8.1 13.5 %collective-permute-start.1 = (bf16[104,768]{1,0:T(8,128)(2,1)S(1)}, bf16[104,768]{1,0:T(8,128)(2,1)S(1)}, u32[]{:S(2)}, u32[]{:S(2)}) collective-permute-start(bf16[104,768]{1,0:T(8,128)(2,1)S(1)} %pad_maximum_fusion.13), channel_id=1, source_target_pairs={{0,4},{1,5},{2,6},{3,7},{4,0},{5,1},{6,2},{7,3},{8,12},{9,13},{10,... | collective-permute-start | bytes 479240 | tf_op jit(solution)/shard_map/ppermute | solution.py:627
  8.1 13.5 %collective-permute-start = (bf16[104,768]{1,0:T(8,128)(2,1)S(1)}, bf16[104,768]{1,0:T(8,128)(2,1)S(1)}, u32[]{:S(2)}, u32[]{:S(2)}) collective-permute-start(bf16[104,768]{1,0:T(8,128)(2,1)S(1)} %pad_maximum_fusion.13), channel_id=1, source_target_pairs={{0,2},{1,3},{2,0},{3,1},{4,6},{5,7},{6,4},{7,5},{8,10},{9,11},{10,... | collective-permute-start | bytes 479240 | tf_op jit(solution)/shard_map/ppermute | solution.py:627
  22.5 15.4 %collective-permute-start.4 = (bf16[384,768]{1,0:T(8,128)(2,1)S(1)}, bf16[384,768]{1,0:T(8,128)(2,1)}, u32[]{:S(2)}, u32[]{:S(2)}) collective-permute-start(bf16[384,768]{1,0:T(8,128)(2,1)S(1)} %pad_maximum_fusion.1.refs_0_), channel_id=1, source_target_pairs={{0,16},{1,17},{2,18},{3,19},{4,20},{5,21},{6,22},{7,23},{8,24},{9,... | collective-permute-start | bytes 1769480 | tf_op jit(solution)/shard_map/ppermute | solution.py:627
  24.1 15.1 %collective-permute-start.3 = (bf16[384,768]{1,0:T(8,128)(2,1)S(1)}, bf16[384,768]{1,0:T(8,128)(2,1)}, u32[]{:S(2)}, u32[]{:S(2)}) collective-permute-start(bf16[384,768]{1,0:T(8,128)(2,1)S(1)} %pad_maximum_fusion.1.refs_0_), channel_id=1, source_target_pairs={{0,8},{1,9},{2,10},{3,11},{4,12},{5,13},{6,14},{7,15},{8,0},{9,1},... | collective-permute-start | bytes 1769480 | tf_op jit(solution)/shard_map/ppermute | solution.py:627
  26.3 17.0 %collective-permute-start.15 = (bf16[192,768]{1,0:T(8,128)(2,1)S(1)}, bf16[192,768]{1,0:T(8,128)(2,1)S(1)}, u32[]{:S(2)}, u32[]{:S(2)}) collective-permute-start(bf16[192,768]{1,0:T(8,128)(2,1)S(1)} %pad_maximum_fusion.11), channel_id=1, source_target_pairs={{0,6},{1,7},{2,4},{3,5},{4,2},{5,3},{6,0},{7,1},{8,14},{9,15},{10,... | collective-permute-start | bytes 884744 | tf_op jit(solution)/shard_map/ppermute | solution.py:627
  28.8 24.0 %collective-permute-start.14 = (bf16[192,768]{1,0:T(8,128)(2,1)S(1)}, bf16[192,768]{1,0:T(8,128)(2,1)S(1)}, u32[]{:S(2)}, u32[]{:S(2)}) collective-permute-start(bf16[192,768]{1,0:T(8,128)(2,1)S(1)} %pad_maximum_fusion.11), channel_id=1, source_target_pairs={{0,4},{1,5},{2,6},{3,7},{4,0},{5,1},{6,2},{7,3},{8,12},{9,13},{10,... | collective-permute-start | bytes 884744 | tf_op jit(solution)/shard_map/ppermute | solution.py:627
  28.8 24.0 %collective-permute-start.13 = (bf16[192,768]{1,0:T(8,128)(2,1)S(1)}, bf16[192,768]{1,0:T(8,128)(2,1)S(1)}, u32[]{:S(2)}, u32[]{:S(2)}) collective-permute-start(bf16[192,768]{1,0:T(8,128)(2,1)S(1)} %pad_maximum_fusion.11), channel_id=1, source_target_pairs={{0,2},{1,3},{2,0},{3,1},{4,6},{5,7},{6,4},{7,5},{8,10},{9,11},{10,... | collective-permute-start | bytes 884744 | tf_op jit(solution)/shard_map/ppermute | solution.py:627
  40.2 12.6 %collective-permute-start.7 = (bf16[192,768]{1,0:T(8,128)(2,1)S(1)}, bf16[192,768]{1,0:T(8,128)(2,1)S(1)}, u32[]{:S(2)}, u32[]{:S(2)}) collective-permute-start(bf16[192,768]{1,0:T(8,128)(2,1)S(1)} %slice.292), channel_id=1, source_target_pairs={{0,16},{1,17},{2,18},{3,19},{4,20},{5,21},{6,22},{7,23},{8,24},{9,... | collective-permute-start | bytes 884744 | tf_op jit(solution)/shard_map/ppermute | solution.py:627
  43.3 14.3 %collective-permute-start.10 = (bf16[384,768]{1,0:T(8,128)(2,1)}, bf16[384,768]{1,0:T(8,128)(2,1)S(1)}, u32[]{:S(2)}, u32[]{:S(2)}) collective-permute-start(bf16[384,768]{1,0:T(8,128)(2,1)} %collective-permute-done.4.refs_2_), channel_id=1, source_target_pairs={{0,1},{1,0},{2,3},{3,2},{4,5},{5,4},{6,7},{7,6},{8,9},{9,8},{10,11... | collective-permute-start | bytes 1769480 | tf_op jit(solution)/shard_map/ppermute | solution.py:627
  53.5 30.3 %collective-permute-start.17 = (bf16[4,192,768]{2,1,0:T(8,128)(2,1)S(1)}, bf16[4,192,768]{2,1,0:T(8,128)(2,1)S(1)}, u32[]{:S(2)}, u32[]{:S(2)}) collective-permute-start(bf16[4,192,768]{2,1,0:T(8,128)(2,1)S(1)} %pad_maximum_fusion.refs_0_.refs_8_), channel_id=1, source_target_pairs={{0,16},{1,17},{2,18},{3,19},{4,20},{5,21},{6,22},{7,23},{8,24},{9,... | collective-permute-start | bytes 3538952 | tf_op jit(solution)/shard_map/ppermute | solution.py:627
  54.2 29.6 %collective-permute-start.16 = (bf16[4,192,768]{2,1,0:T(8,128)(2,1)S(1)}, bf16[4,192,768]{2,1,0:T(8,128)(2,1)}, u32[]{:S(2)}, u32[]{:S(2)}) collective-permute-start(bf16[4,192,768]{2,1,0:T(8,128)(2,1)S(1)} %pad_maximum_fusion.refs_0_.refs_8_), channel_id=1, source_target_pairs={{0,8},{1,9},{2,10},{3,11},{4,12},{5,13},{6,14},{7,15},{8,0},{9,1},... | collective-permute-start | bytes 3538952 | tf_op jit(solution)/shard_map/ppermute | solution.py:627
  57.5 38.6 %collective-permute-start.18 = (bf16[4,192,768]{2,1,0:T(8,128)(2,1)S(1)}, bf16[4,192,768]{2,1,0:T(8,128)(2,1)}, u32[]{:S(2)}, u32[]{:S(2)}) collective-permute-start(bf16[4,192,768]{2,1,0:T(8,128)(2,1)S(1)} %pad_maximum_fusion.refs_0_.refs_8_), channel_id=1, source_target_pairs={{0,1},{1,0},{2,3},{3,2},{4,5},{5,4},{6,7},{7,6},{8,9},{9,8},{10,11... | collective-permute-start | bytes 3538952 | tf_op jit(solution)/shard_map/ppermute | solution.py:627
  87.2 19.8 %collective-permute-start.22 = (bf16[4,96,768]{2,1,0:T(8,128)(2,1)}, bf16[4,96,768]{2,1,0:T(8,128)(2,1)S(1)}, u32[]{:S(2)}, u32[]{:S(2)}) collective-permute-start(bf16[4,96,768]{2,1,0:T(8,128)(2,1)} %slice.295), channel_id=1, source_target_pairs={{0,8},{1,9},{2,10},{3,11},{4,12},{5,13},{6,14},{7,15},{8,0},{9,1},... | collective-permute-start | bytes 1769480 | tf_op jit(solution)/shard_map/ppermute | solution.py:627
  87.8 19.1 %collective-permute-start.21 = (bf16[4,96,768]{2,1,0:T(8,128)(2,1)}, bf16[4,96,768]{2,1,0:T(8,128)(2,1)S(1)}, u32[]{:S(2)}, u32[]{:S(2)}) collective-permute-start(bf16[4,96,768]{2,1,0:T(8,128)(2,1)} %slice.294), channel_id=1, source_target_pairs={{0,16},{1,17},{2,18},{3,19},{4,20},{5,21},{6,22},{7,23},{8,24},{9,... | collective-permute-start | bytes 1769480 | tf_op jit(solution)/shard_map/ppermute | solution.py:627
  143.7 19.6 %collective-permute-start.26 = (bf16[192,768]{1,0:T(8,128)(2,1)S(1)}, bf16[192,768]{1,0:T(8,128)(2,1)S(1)}, u32[]{:S(2)}, u32[]{:S(2)}) collective-permute-start(bf16[192,768]{1,0:T(8,128)(2,1)S(1)} %get-tuple-element.190), channel_id=1, source_target_pairs={{0,16},{1,17},{2,18},{3,19},{4,20},{5,21},{6,22},{7,23},{8,24},{9,... | collective-permute-start | bytes 884744 | tf_op jit(solution)/shard_map/ppermute | solution.py:627
  144.4 18.9 %collective-permute-start.27 = (bf16[192,768]{1,0:T(8,128)(2,1)S(1)}, bf16[192,768]{1,0:T(8,128)(2,1)S(1)}, u32[]{:S(2)}, u32[]{:S(2)}) collective-permute-start(bf16[192,768]{1,0:T(8,128)(2,1)S(1)} %get-tuple-element.191), channel_id=1, source_target_pairs={{0,8},{1,9},{2,10},{3,11},{4,12},{5,13},{6,14},{7,15},{8,0},{9,1},... | collective-permute-start | bytes 884744 | tf_op jit(solution)/shard_map/ppermute | solution.py:627
  171.8 20.6 %collective-permute-start.31 = (bf16[384,768]{1,0:T(8,128)(2,1)S(1)}, bf16[384,768]{1,0:T(8,128)(2,1)}, u32[]{:S(2)}, u32[]{:S(2)}) collective-permute-start(bf16[384,768]{1,0:T(8,128)(2,1)S(1)} %copy-done.13), channel_id=1, source_target_pairs={{0,8},{1,9},{2,10},{3,11},{4,12},{5,13},{6,14},{7,15},{8,0},{9,1},... | collective-permute-start | bytes 1769480 | tf_op jit(solution)/shard_map/ppermute | solution.py:627
  172.4 19.9 %collective-permute-start.32 = (bf16[384,768]{1,0:T(8,128)(2,1)S(1)}, bf16[384,768]{1,0:T(8,128)(2,1)}, u32[]{:S(2)}, u32[]{:S(2)}) collective-permute-start(bf16[384,768]{1,0:T(8,128)(2,1)S(1)} %pad_maximum_fusion.3), channel_id=1, source_target_pairs={{0,16},{1,17},{2,18},{3,19},{4,20},{5,21},{6,22},{7,23},{8,24},{9,... | collective-permute-start | bytes 1769480 | tf_op jit(solution)/shard_map/ppermute | solution.py:627
  200.9 31.1 %collective-permute-start.37 = (bf16[96,768]{1,0:T(8,128)(2,1)S(1)}, bf16[96,768]{1,0:T(8,128)(2,1)S(1)}, u32[]{:S(2)}, u32[]{:S(2)}) collective-permute-start(bf16[96,768]{1,0:T(8,128)(2,1)S(1)} %get-tuple-element.315), channel_id=1, source_target_pairs={{0,6},{1,7},{2,4},{3,5},{4,2},{5,3},{6,0},{7,1},{8,14},{9,15},{10,... | collective-permute-start | bytes 442376 | tf_op jit(solution)/shard_map/ppermute | solution.py:627
  202.3 29.7 %collective-permute-start.36 = (bf16[96,768]{1,0:T(8,128)(2,1)S(1)}, bf16[96,768]{1,0:T(8,128)(2,1)S(1)}, u32[]{:S(2)}, u32[]{:S(2)}) collective-permute-start(bf16[96,768]{1,0:T(8,128)(2,1)S(1)} %get-tuple-element.316), channel_id=1, source_target_pairs={{0,4},{1,5},{2,6},{3,7},{4,0},{5,1},{6,2},{7,3},{8,12},{9,13},{10,... | collective-permute-start | bytes 442376 | tf_op jit(solution)/shard_map/ppermute | solution.py:627
  202.3 29.7 %collective-permute-start.35 = (bf16[96,768]{1,0:T(8,128)(2,1)S(1)}, bf16[96,768]{1,0:T(8,128)(2,1)S(1)}, u32[]{:S(2)}, u32[]{:S(2)}) collective-permute-start(bf16[96,768]{1,0:T(8,128)(2,1)S(1)} %get-tuple-element.317), channel_id=1, source_target_pairs={{0,2},{1,3},{2,0},{3,1},{4,6},{5,7},{6,4},{7,5},{8,10},{9,11},{10,... | collective-permute-start | bytes 442376 | tf_op jit(solution)/shard_map/ppermute | solution.py:627
  205.4 26.6 %collective-permute-start.33 = (bf16[384,768]{1,0:T(8,128)(2,1)}, bf16[384,768]{1,0:T(8,128)(2,1)S(1)}, u32[]{:S(2)}, u32[]{:S(2)}) collective-permute-start(bf16[384,768]{1,0:T(8,128)(2,1)} %pad_maximum_fusion.4), channel_id=1, source_target_pairs={{0,8},{1,9},{2,10},{3,11},{4,12},{5,13},{6,14},{7,15},{8,0},{9,1},... | collective-permute-start | bytes 1769480 | tf_op jit(solution)/shard_map/ppermute | solution.py:627
  206.8 25.2 %collective-permute-start.34 = (bf16[384,768]{1,0:T(8,128)(2,1)S(1)}, bf16[384,768]{1,0:T(8,128)(2,1)S(1)}, u32[]{:S(2)}, u32[]{:S(2)}) collective-permute-start(bf16[384,768]{1,0:T(8,128)(2,1)S(1)} %pad_maximum_fusion.5), channel_id=1, source_target_pairs={{0,16},{1,17},{2,18},{3,19},{4,20},{5,21},{6,22},{7,23},{8,24},{9,... | collective-permute-start | bytes 1769480 | tf_op jit(solution)/shard_map/ppermute | solution.py:627
  233.7 16.7 %collective-permute-start.42 = (bf16[96,768]{1,0:T(8,128)(2,1)S(1)}, bf16[96,768]{1,0:T(8,128)(2,1)S(1)}, u32[]{:S(2)}, u32[]{:S(2)}) collective-permute-start(bf16[96,768]{1,0:T(8,128)(2,1)S(1)} %add_convert_fusion.10), channel_id=1, source_target_pairs={{0,24},{1,25},{2,26},{3,27},{4,28},{5,29},{6,30},{7,31},{8,16},{9,... | collective-permute-start | bytes 442376 | tf_op jit(solution)/shard_map/ppermute | solution.py:627
  235.2 15.2 %collective-permute-start.41 = (bf16[96,768]{1,0:T(8,128)(2,1)S(1)}, bf16[96,768]{1,0:T(8,128)(2,1)S(1)}, u32[]{:S(2)}, u32[]{:S(2)}) collective-permute-start(bf16[96,768]{1,0:T(8,128)(2,1)S(1)} %add_convert_fusion.10), channel_id=1, source_target_pairs={{0,16},{1,17},{2,18},{3,19},{4,20},{5,21},{6,22},{7,23},{8,24},{9,... | collective-permute-start | bytes 442376 | tf_op jit(solution)/shard_map/ppermute | solution.py:627
  236.6 13.8 %collective-permute-start.40 = (bf16[96,768]{1,0:T(8,128)(2,1)S(1)}, bf16[96,768]{1,0:T(8,128)(2,1)S(1)}, u32[]{:S(2)}, u32[]{:S(2)}) collective-permute-start(bf16[96,768]{1,0:T(8,128)(2,1)S(1)} %add_convert_fusion.10), channel_id=1, source_target_pairs={{0,8},{1,9},{2,10},{3,11},{4,12},{5,13},{6,14},{7,15},{8,0},{9,1},... | collective-permute-start | bytes 442376 | tf_op jit(solution)/shard_map/ppermute | solution.py:627
  237.2 13.1 %collective-permute-start.38 = (f32[88,128]{1,0:T(8,128)S(1)}, f32[88,128]{1,0:T(8,128)S(1)}, u32[]{:S(2)}, u32[]{:S(2)}) collective-permute-start(f32[88,128]{1,0:T(8,128)S(1)} %copy-done.14), channel_id=1, source_target_pairs={{0,1},{1,0},{2,3},{3,2},{4,5},{5,4},{6,7},{7,6},{8,9},{9,8},{10,11... | collective-permute-start | bytes 135176 | tf_op jit(solution)/shard_map/ppermute | solution.py:627
  237.3 16.1 %collective-permute-start.39 = (bf16[192,768]{1,0:T(8,128)(2,1)S(1)}, bf16[192,768]{1,0:T(8,128)(2,1)S(1)}, u32[]{:S(2)}, u32[]{:S(2)}) collective-permute-start(bf16[192,768]{1,0:T(8,128)(2,1)S(1)} %get-tuple-element.313), channel_id=1, source_target_pairs={{0,4},{1,5},{2,6},{3,7},{4,0},{5,1},{6,2},{7,3},{8,12},{9,13},{10,... | collective-permute-start | bytes 884744 | tf_op jit(solution)/shard_map/ppermute | solution.py:627
  274.3 17.7 %collective-permute-start.51 = (bf16[384,768]{1,0:T(8,128)(2,1)}, bf16[384,768]{1,0:T(8,128)(2,1)}, u32[]{:S(2)}, u32[]{:S(2)}) collective-permute-start(bf16[384,768]{1,0:T(8,128)(2,1)} %pad_maximum_fusion.6), channel_id=1, source_target_pairs={{0,8},{1,9},{2,10},{3,11},{4,12},{5,13},{6,14},{7,15},{8,0},{9,1},... | collective-permute-start | bytes 1769480 | tf_op jit(solution)/shard_map/ppermute | solution.py:627
  275.7 16.3 %collective-permute-start.52 = (bf16[384,768]{1,0:T(8,128)(2,1)S(1)}, bf16[384,768]{1,0:T(8,128)(2,1)}, u32[]{:S(2)}, u32[]{:S(2)}) collective-permute-start(bf16[384,768]{1,0:T(8,128)(2,1)S(1)} %pad_maximum_fusion.7), channel_id=1, source_target_pairs={{0,16},{1,17},{2,18},{3,19},{4,20},{5,21},{6,22},{7,23},{8,24},{9,... | collective-permute-start | bytes 1769480 | tf_op jit(solution)/shard_map/ppermute | solution.py:627
  279.2 12.8 %collective-permute-start.50 = (bf16[96,768]{1,0:T(8,128)(2,1)}, bf16[96,768]{1,0:T(8,128)(2,1)S(1)}, u32[]{:S(2)}, u32[]{:S(2)}) collective-permute-start(bf16[96,768]{1,0:T(8,128)(2,1)} %fusion.6), channel_id=1, source_target_pairs={{0,8},{1,9},{2,10},{3,11},{4,12},{5,13},{6,14},{7,15},{8,0},{9,1},... | collective-permute-start | bytes 442376 | tf_op jit(solution)/shard_map/ppermute | solution.py:627
  296.9 15.2 %collective-permute-start.54 = (bf16[192,768]{1,0:T(8,128)(2,1)S(1)}, bf16[192,768]{1,0:T(8,128)(2,1)S(1)}, u32[]{:S(2)}, u32[]{:S(2)}) collective-permute-start(bf16[192,768]{1,0:T(8,128)(2,1)S(1)} %pad_maximum_fusion.12), channel_id=1, source_target_pairs={{0,16},{1,17},{2,18},{3,19},{4,20},{5,21},{6,22},{7,23},{8,24},{9,... | collective-permute-start | bytes 884744 | tf_op jit(solution)/shard_map/ppermute | solution.py:627
  (55 other events, 368.1 us)
